TPU v7x, 32 devices: a whole 2x2x4 slice. The times are simulated.
32 devices in a mesh: dp: 16 (over z, y, core), tensor: 2 (over x).
Axes of the slice: x: 2, y: 2, z: 4, core: 2. Of those that a mesh axis runs over, the one named last changes fastest.
Arguments:
- layer_input: bfloat16 [16384, 1024], P('dp'), may hold values from -6 to 6
- w_norm1: bfloat16 [1024], P('dp'), may hold values from 0.5 to 1.5
- w_zx: bfloat16 [1024, 2, 1536], P('dp', None, 'tensor'), may hold values from -0.1875 to 0.1875
- w_bc: bfloat16 [1024, 256], P('dp'), may hold values from -0.1875 to 0.1875
- w_dt: bfloat16 [1024, 24], P('dp', 'tensor'), may hold values from -0.1875 to 0.1875
- conv_x: bfloat16 [4, 1536], P(None, 'tensor'), may hold values from -3 to 3
- conv_xb: bfloat16 [1536], P('tensor'), may hold values from -3 to 3
- conv_bc: bfloat16 [4, 256], replicated, may hold values from -3 to 3
- conv_bcb: bfloat16 [256], replicated, may hold values from -3 to 3
- dt_bias: bfloat16 [24], P('tensor'), may hold values from -6.875 to -2.296875
- a_log: bfloat16 [24], P('tensor'), may hold values from 0 to 2.765625
- d_skip: bfloat16 [24], P('tensor'), may hold values from 0.5 to 1.5
- w_mnorm: bfloat16 [1536], P('tensor'), may hold values from 0.5 to 1.5
- w_mout: bfloat16 [1536, 1024], P('tensor', 'dp'), may hold values from -0.15625 to 0.15625
- query_key_value_weight: bfloat16 [1024, 2, 384], P('dp', 'tensor'), may hold values from -4 to 4
- output_weight: bfloat16 [2, 256, 1024], P('tensor', None, 'dp'), may hold values from -1 to 1
- w_norm2: bfloat16 [1024], P('dp'), may hold values from 0.5 to 1.5
- w_gu: bfloat16 [1024, 2, 2048], P('dp', None, 'tensor'), may hold values from -0.1875 to 0.1875
- w_down: bfloat16 [2048, 1024], P('tensor', 'dp'), may hold values from -0.125 to 0.125
- grad_output: bfloat16 [16384, 1024], P('dp'), may hold values from -6 to 6
Outputs:
- layer_output: bfloat16 [16384, 1024], P('dp')
- grad_x: float32 [16384, 1024], P('dp')
- grad_norm1: float32 [1024], P('dp')
- grad_zx: float32 [1024, 2, 1536], P('dp', None, 'tensor')
- grad_bc: float32 [1024, 256], P('dp', 'tensor')
- grad_dt: float32 [1024, 24], P('dp', 'tensor')
- grad_conv_x: float32 [4, 1536], P(None, 'tensor')
- grad_conv_xb: float32 [1536], P('tensor')
- grad_conv_bc: float32 [4, 256], P(None, 'tensor')
- grad_conv_bcb: float32 [256], P('tensor')
- grad_dt_bias: float32 [24], P('tensor')
- grad_a_log: float32 [24], P('tensor')
- grad_d_skip: float32 [24], P('tensor')
- grad_mnorm: float32 [1536], P('tensor')
- grad_mout: float32 [1536, 1024], P('tensor', 'dp')
- grad_qkv: float32 [1024, 2, 384], P('dp', 'tensor')
- grad_o: float32 [2, 256, 1024], P('tensor', None, 'dp')
- grad_norm2: float32 [1024], P('dp')
- grad_gu: float32 [1024, 2, 2048], P('dp', None, 'tensor')
- grad_down: float32 [2048, 1024], P('tensor', 'dp')
All inputs are finite; a program needn't handle non-finite values.
Results may differ from a plain program's by a relative error of at most 0.013.
Values may be sent and summed in bfloat16 or wider, within the bound.
A program may use at most 256 MiB of HBM per device.

v0:
```python
import functools
import math

import jax
import jax.numpy as jnp
import numpy as np
from jax import lax
from jax.experimental import pallas as pl
from jax.experimental.pallas import tpu as pltpu
from jax.sharding import PartitionSpec as P

HEAD_SIZE = 64
MP = 64
NS = 128
KCONV = 4
SPAN = 128
QBLK = 256
FINE = 32
TBLK = 256
NBLK = 128
UBLK = 256
LANES = 128
EDGE = 8

EPSILON = 1e-05
HIGHEST = lax.Precision.HIGHEST
LOG_BASE = math.log(100000000000.0)
MASKED = -1e30
MESH = pl.DeviceIdType.MESH
F32 = jnp.float32
BF16 = jnp.bfloat16

NN = ((1,), (0,))
NT = ((1,), (1,))
TN = ((0,), (0,))


def dot(left, right, dims=NN, precision=None):
    return lax.dot_general(
        left, right, (dims, ((), ())), preferred_element_type=F32, precision=precision
    )


def iota(shape, dim):
    return lax.broadcasted_iota(jnp.int32, shape, dim)


def ring_place(chip, chips):
    odd = lax.rem(chip, 2)
    half = lax.div(chip, 2)
    return (1 - odd) * half + odd * (chips - 1 - half)


def ring_chip(place, chips):
    place = lax.rem(place + 4 * chips, chips)
    back = lax.div(place, chips // 2)
    return (1 - back) * (2 * place) + back * (2 * (chips - 1 - place) + 1)


def ring_setup(chips):
    me = lax.axis_index("dp")
    group = lax.axis_index("tensor")
    chip = lax.div(me, 2)
    core = lax.rem(me, 2)
    place = ring_place(chip, chips)
    right = ring_chip(place + 1, chips) * 2 + core
    left = ring_chip(place - 1, chips) * 2 + core
    mate = chip * 2 + (1 - core)
    barrier = pltpu.get_barrier_semaphore()
    for other in (right, left, mate):
        pl.semaphore_signal(barrier, inc=1, device_id=(other, group), device_id_type=MESH)
    pl.semaphore_wait(barrier, 3)
    return me, group, core, place, right, left, mate


class RingGather:
    def __init__(self, devices, x_ref, o_ref, sems):
        self.chips = devices // 2
        self.ahead = self.chips // 2
        self.behind = self.chips - 1 - self.ahead
        self.x_ref, self.o_ref, self.rows = x_ref, o_ref, x_ref.shape[0]
        self.fs, self.fr, self.bs, self.br, self.cs, self.cr, self.own_sem = sems

    def locate(self):
        me = lax.axis_index("dp")
        self.group = lax.axis_index("tensor")
        self.core = lax.rem(me, 2)
        chip = lax.div(me, 2)
        self.place = ring_place(chip, self.chips)
        self.right = ring_chip(self.place + 1, self.chips) * 2 + self.core
        self.left = ring_chip(self.place - 1, self.chips) * 2 + self.core
        self.mate = chip * 2 + (1 - self.core)
        self.me = me

    def slot(self, index):
        return self.o_ref.at[pl.ds(pl.multiple_of(index * self.rows, self.rows), self.rows), :]

    def copy(self, shift, ssem, rsem, target):
        if shift == 0:
            index, source = self.me, self.x_ref
        else:
            index = ring_chip(self.place + shift, self.chips) * 2 + self.core
            source = self.slot(index)
        return pltpu.make_async_remote_copy(
            src_ref=source,
            dst_ref=self.slot(index),
            send_sem=ssem,
            recv_sem=rsem,
            device_id=(target, self.group),
            device_id_type=MESH,
        )

    def fore(self, step):
        return self.copy(-step, self.fs.at[step], self.fr.at[step], self.right)

    def back(self, step):
        return self.copy(step, self.bs.at[step], self.br.at[step], self.left)

    def across(self, shift):
        number = 0 if shift == 0 else 2 * abs(shift) - (1 if shift < 0 else 0)
        return self.copy(shift, self.cs.at[number], self.cr.at[number], self.mate)

    def own(self):
        return pltpu.make_async_copy(self.x_ref, self.slot(self.me), self.own_sem)

    def greet(self):
        self.locate()
        barrier = pltpu.get_barrier_semaphore()
        for other in (self.right, self.left, self.mate):
            pl.semaphore_signal(
                barrier, inc=1, device_id=(other, self.group), device_id_type=MESH
            )
        pl.semaphore_wait(barrier, 3)

    def begin(self):
        self.locate()
        self.fore(0).start()
        self.back(0).start()
        self.across(0).start()
        self.own().start()

    def hop(self, step):
        self.locate()
        self.fore(step - 1).wait_recv()
        if step < self.ahead:
            self.fore(step).start()
        self.across(-step).start()
        if step <= self.behind:
            self.back(step - 1).wait_recv()
            if step < self.behind:
                self.back(step).start()
            self.across(step).start()

    def finish(self):
        self.locate()
        self.own().wait()
        for step in range(self.ahead):
            self.fore(step).wait_send()
        for step in range(self.behind):
            self.back(step).wait_send()
        for shift in range(-self.ahead, self.behind + 1):
            self.across(shift).wait()


def gather_sems(devices):
    dma = pltpu.SemaphoreType.DMA
    return [dma((devices // 2,))] * 6 + [dma(())]


def gather_shape(shard, devices):
    return jax.ShapeDtypeStruct((shard.shape[0] * devices, shard.shape[1]), shard.dtype)


def gather_kernel(devices, count, *refs):
    shards, outs, sems = refs[:count], refs[count : 2 * count], refs[2 * count :]
    each = len(sems) // count
    rings = [
        RingGather(devices, shards[i], outs[i], sems[i * each : (i + 1) * each])
        for i in range(count)
    ]
    rings[0].greet()
    for ring in rings:
        ring.begin()
    for step in range(1, rings[0].ahead + 1):
        for ring in rings:
            ring.hop(step)
    for ring in rings:
        ring.finish()


def cost(micros):
    return pl.CostEstimate(flops=int(micros * 1e9), bytes_accessed=0, transcendentals=0)


def gather_rows(shards, devices, collective):
    count = len(shards)
    anywhere = pl.BlockSpec(memory_space=pl.ANY)
    return pl.pallas_call(
        functools.partial(gather_kernel, devices, count),
        out_shape=tuple(gather_shape(shard, devices) for shard in shards),
        in_specs=[anywhere] * count,
        out_specs=(anywhere,) * count,
        scratch_shapes=gather_sems(devices) * count,
        compiler_params=pltpu.CompilerParams(collective_id=collective, has_side_effects=True),
        cost_estimate=cost(3),
        name="gather_rows",
    )(*shards)


def scatter_order(chips):
    ahead = chips // 2
    behind = chips - 1 - ahead
    order = []
    for step in range(ahead):
        order.append(-(ahead - step))
        if step < behind:
            order.append(behind - step)
    order.append(0)
    return order


class RingScatter:
    def __init__(self, devices, windows, pieces, operands, outs, scratch):
        self.chips = devices // 2
        self.ahead = self.chips // 2
        self.behind = self.chips - 1 - self.ahead
        self.windows, self.pieces, self.operands, self.outs = windows, pieces, operands, outs
        count = len(windows)
        self.mine, self.boxes, rest = scratch[:count], scratch[count : 2 * count], scratch[2 * count :]
        self.fbox, self.bbox, self.fout, self.bout = rest[:4]
        self.os, self.ms, self.mr, self.fs, self.fr, self.bs, self.br = rest[4:]
        self.rows = self.fbox.shape[1]
        widths = [item.shape[2] for item in self.mine]
        self.cols = [slice(sum(widths[:i]), sum(widths[: i + 1])) for i in range(count)]

    def locate(self):
        me = lax.axis_index("dp")
        self.group = lax.axis_index("tensor")
        self.core = lax.rem(me, 2)
        chip = lax.div(me, 2)
        self.place = ring_place(chip, self.chips)
        self.right = ring_chip(self.place + 1, self.chips) * 2 + self.core
        self.left = ring_chip(self.place - 1, self.chips) * 2 + self.core
        self.mate = chip * 2 + (1 - self.core)

    def greet(self):
        self.locate()
        barrier = pltpu.get_barrier_semaphore()
        for other in (self.right, self.left, self.mate):
            pl.semaphore_signal(
                barrier, inc=1, device_id=(other, self.group), device_id_type=MESH
            )
        pl.semaphore_wait(barrier, 3)

    def product(self, i):
        return self.windows[i][1] is not None

    def shift_of(self, slot):
        step = slot // 2
        odd = slot % 2
        return (1 - odd) * (step - self.ahead) + odd * (self.behind - step)

    def half(self, which):
        return pl.ds(pl.multiple_of(which * self.rows, self.rows), self.rows)

    def block(self, i, slot, which):
        index = ring_chip(self.place + self.shift_of(slot), self.chips) * 2 + which
        left, right, first, last = self.windows[i]
        return self.operands[left].at[self.half(index), first:last]

    def remote(self, source, target_ref, ssem, rsem, target):
        return pltpu.make_async_remote_copy(
            src_ref=source,
            dst_ref=target_ref,
            send_sem=ssem,
            recv_sem=rsem,
            device_id=(target, self.group),
            device_id_type=MESH,
        )

    def across(self, i, slot):
        if self.product(i):
            source = self.mine[i].at[slot, self.half(1 - self.core)]
        else:
            source = self.block(i, slot, 1 - self.core)
        return self.remote(
            source, self.boxes[i].at[slot], self.ms.at[i, slot], self.mr.at[i, slot], self.mate
        )

    def own(self, i, slot):
        return pltpu.make_async_copy(
            self.block(i, slot, self.core), self.mine[i].at[slot], self.os.at[i, slot]
        )

    def fore(self, step):
        return self.remote(
            self.fout.at[step], self.fbox.at[step], self.fs.at[step], self.fr.at[step], self.right
        )

    def back(self, step):
        return self.remote(
            self.bout.at[step], self.bbox.at[step], self.bs.at[step], self.br.at[step], self.left
        )

    def begin(self):
        self.locate()
        for i in range(len(self.windows)):
            if not self.product(i):
                for slot in range(self.chips):
                    self.across(i, slot).start()
                    self.own(i, slot).start()

    def produce(self, slot):
        chip = ring_chip(self.place + self.shift_of(slot), self.chips)
        size = 2 * self.rows
        for i, (left, right, first, last) in enumerate(self.windows):
            if right is None:
                continue
            at = pl.multiple_of(chip * size, size)
            terms = dot(self.operands[left][pl.ds(at, size), :], self.operands[right][:, first:last])
            self.mine[i][slot] = terms.astype(BF16)
            self.across(i, slot).start()

    def local_sum(self, i, slot, cols, others):
        rows = self.half(self.core) if self.product(i) else slice(None)
        total = self.mine[i][slot, rows, cols].astype(F32) + self.boxes[i][slot, :, cols].astype(F32)
        whole = slice(self.cols[i].start + cols.start, self.cols[i].start + cols.stop)
        for ref in others:
            total = total + ref[:, whole].astype(F32)
        return total

    def arrive(self, slot):
        for i in range(len(self.windows)):
            if not self.product(i):
                self.own(i, slot).wait()
            self.across(i, slot).wait_recv()

    def put(self, target, slot, others):
        self.arrive(slot)
        for i, cols in enumerate(self.cols):
            total = self.local_sum(i, slot, slice(0, cols.stop - cols.start), others)
            target[:, cols] = total.astype(BF16)

    def hop_back(self, step, later):
        if later:
            self.back(step - 1).wait_recv()
        self.put(self.bout.at[step], 2 * step, [self.bbox.at[step - 1]] if later else [])
        self.back(step).start()

    def hop_fore(self, step, later):
        if later:
            self.fore(step - 1).wait_recv()
        self.put(self.fout.at[step], 2 * step + 1, [self.fbox.at[step - 1]] if later else [])
        self.fore(step).start()

    def hop(self, step):
        self.locate()
        self.hop_back(step, step > 0)
        if step < self.behind:
            self.hop_fore(step, step > 0)

    def run(self, after_first=None):
        def turn(step, carry):
            lax.fori_loop(0, 2, lambda part, kept: (self.produce(2 * step + part), kept)[1], 0)

            @pl.when(step == 0)
            def _():
                self.hop_back(0, False)
                self.hop_fore(0, False)
                if after_first is not None:
                    after_first()

            pl.when(step > 0)(lambda: self.hop_back(step, True))
            pl.when((step > 0) & (step < self.behind))(lambda: self.hop_fore(step, True))
            return carry

        lax.fori_loop(0, self.ahead, turn, 0)

    def finish(self):
        self.locate()
        slot = self.chips - 1
        self.arrive(slot)
        self.fore(self.behind - 1).wait_recv()
        self.back(self.ahead - 1).wait_recv()
        others = [self.fbox.at[self.behind - 1], self.bbox.at[self.ahead - 1]]
        for i, first, last, out, form in self.pieces:
            total = self.local_sum(i, slot, slice(first, last), others)
            if form == "turned":
                self.outs[out][...] = total.T[: self.outs[out].shape[0]]
            elif form is None:
                self.outs[out][...] = total
            else:
                self.outs[out][:, form, :] = total
        for step in range(self.ahead):
            self.back(step).wait_send()
        for step in range(self.behind):
            self.fore(step).wait_send()
        for slot in range(self.chips):
            for i in range(len(self.windows)):
                self.across(i, slot).wait_send()


def scatter_scratch(windows, rows, devices):
    chips = devices // 2
    count = len(windows)
    dma = pltpu.SemaphoreType.DMA
    widths = [last - first for left, right, first, last in windows]
    mine = [
        pltpu.VMEM((chips, rows if right is None else 2 * rows, last - first), BF16)
        for left, right, first, last in windows
    ]
    boxes = [pltpu.VMEM((chips, rows, width), BF16) for width in widths]
    box = pltpu.VMEM((chips // 2, rows, sum(widths)), BF16)
    return mine + boxes + [box] * 4 + [dma((count, chips))] * 3 + [dma((chips,))] * 4


class Total:
    def __init__(self, devices, x_ref, o_ref, scratch):
        self.chips = devices // 2
        self.x_ref, self.o_ref = x_ref, o_ref
        self.mate_box, self.joined, self.boxes, self.ms, self.mr, self.ss, self.sr = scratch
        me = lax.axis_index("dp")
        self.group = lax.axis_index("tensor")
        self.chip = lax.div(me, 2)
        core = lax.rem(me, 2)
        self.mate = self.chip * 2 + (1 - core)
        self.peers = [
            lax.rem(self.chip + shift, self.chips) * 2 + core for shift in range(self.chips)
        ]

    def greet(self):
        barrier = pltpu.get_barrier_semaphore()
        for other in [self.mate] + self.peers[1:]:
            pl.semaphore_signal(
                barrier, inc=1, device_id=(other, self.group), device_id_type=MESH
            )
        pl.semaphore_wait(barrier, self.chips)

    def remote(self, source, target_ref, ssem, rsem, target):
        return pltpu.make_async_remote_copy(
            src_ref=source,
            dst_ref=target_ref,
            send_sem=ssem,
            recv_sem=rsem,
            device_id=(target, self.group),
            device_id_type=MESH,
        )

    def across(self):
        return self.remote(self.x_ref, self.mate_box, self.ms, self.mr, self.mate)

    def copies(self):
        return [
            self.remote(
                self.joined,
                self.boxes.at[self.chip],
                self.ss.at[shift],
                self.sr.at[shift],
                self.peers[shift],
            )
            for shift in range(1, self.chips)
        ]

    def begin(self):
        self.across().start()

    def spread(self):
        self.across().wait_recv()
        self.joined[...] = self.x_ref[...] + self.mate_box[...]
        for copy in self.copies():
            copy.start()
        self.boxes[self.chip] = self.joined[...]

    def finish(self):
        for copy in self.copies():
            copy.wait_recv()
        result = self.boxes[0]
        for other in range(1, self.chips):
            result = result + self.boxes[other]
        self.o_ref[...] = result
        self.across().wait_send()
        for copy in self.copies():
            copy.wait_send()


def total_scratch(values, devices):
    chips = devices // 2
    dma = pltpu.SemaphoreType.DMA
    return [
        pltpu.VMEM(values.shape, F32),
        pltpu.VMEM(values.shape, F32),
        pltpu.VMEM((chips,) + values.shape, F32),
        dma(()),
        dma(()),
        dma((chips,)),
        dma((chips,)),
    ]


def turned_copy(source, target):
    for start in range(0, source.shape[1], LANES):
        target[start : start + LANES, :] = source[:, start : start + LANES].T


def product_kernel(devices, windows, pieces, outs, summed, left_ref, right_ref, *refs):
    values = refs[:summed]
    refs = refs[summed:]
    pieces_out, refs = refs[:outs], refs[outs:]
    totals_out, refs = refs[:summed], refs[summed:]
    turned, scratch = refs[0], refs[1:]
    total = None
    if summed:
        scratch, rest = scratch[:-7], scratch[-7:]
        total = Total(devices, values[0], totals_out[0], rest)
    ring = RingScatter(devices, windows, pieces, (turned, right_ref), pieces_out, scratch)
    if total is None:
        ring.greet()
    else:
        ring.locate()
        total.greet()
        total.begin()
    turned_copy(left_ref, turned)
    ring.run(total.spread if total is not None else None)
    ring.finish()
    if total is not None:
        total.finish()


def scatter_product(left, right, windows, pieces, shapes, devices, collective, values=()):
    vmem = pl.BlockSpec(memory_space=pltpu.VMEM)
    rows = left.shape[1] // devices
    scratch = [pltpu.VMEM(left.shape[::-1], BF16)] + scatter_scratch(windows, rows, devices)
    for item in values:
        scratch += total_scratch(item, devices)
    return pl.pallas_call(
        functools.partial(
            product_kernel, devices, windows, pieces, len(shapes), len(values)
        ),
        out_shape=tuple(jax.ShapeDtypeStruct(shape, F32) for shape in shapes)
        + tuple(jax.ShapeDtypeStruct(item.shape, F32) for item in values),
        in_specs=[vmem] * (2 + len(values)),
        out_specs=(vmem,) * (len(shapes) + len(values)),
        scratch_shapes=scratch,
        compiler_params=pltpu.CompilerParams(collective_id=collective, has_side_effects=True),
        cost_estimate=cost(3),
        name="scatter_product",
    )(left, right, *values)


def head_spread(channels):
    return (iota((LANES, channels), 1) // MP == iota((LANES, channels), 0)).astype(BF16)


def parts(values, count):
    terms = []
    for _ in range(count):
        term = values.astype(BF16)
        terms.append(term)
        values = values - term.astype(F32)
    return terms


def pick(values, mask, count=2):
    return dot(jnp.concatenate(parts(values, count), axis=1), jnp.concatenate([mask] * count, axis=0))


def pick_left(mask, values, count):
    return dot(jnp.concatenate([mask] * count, axis=1), jnp.concatenate(parts(values, count), axis=0))


def gather_heads(values, spread):
    high, low = parts(values, 2)
    return dot(high, spread, NT) + dot(low, spread, NT)


def row_sums(values):
    high, low = parts(values, 2)
    ones = jnp.ones((EDGE, values.shape[1]), BF16)
    return dot(ones, high, NT) + dot(ones, low, NT)


def soft_step(raw):
    return jnp.maximum(raw, 0.0) + jnp.log1p(jnp.exp(-jnp.abs(raw)))


def conv_window(buffer, taps_ref, bias_ref, span):
    total = bias_ref[...] + taps_ref[0:1, :] * buffer[EDGE - 3 : EDGE - 3 + span, :]
    for tap in range(1, KCONV):
        start = EDGE - 3 + tap
        total = total + taps_ref[tap : tap + 1, :] * buffer[start : start + span, :]
    return total


def span_rates(step_ref, bias_ref, decay_ref, spread, span):
    raw = step_ref[...] + bias_ref[...]
    step = soft_step(raw)
    lower = (iota((span, span), 1) <= iota((span, span), 0)).astype(BF16)
    cum = pick_left(lower, step * decay_ref[...], 3)
    tails = jnp.exp(cum[span - 1 : span, :] - cum)
    wide = pick(jnp.concatenate([step, tails, jnp.exp(cum)], axis=0), spread)
    return raw, step, cum, wide[:span], wide[span : 2 * span], wide[2 * span :]


def pair_split(values, low_lanes):
    zero = jnp.zeros_like(values)
    return jnp.concatenate(
        [jnp.where(low_lanes, values, zero), jnp.where(low_lanes, zero, values)], axis=0
    )


def pair_decay(cum, cum_rows, pair, causal):
    parts = []
    for head in (2 * pair, 2 * pair + 1):
        differ = cum[:, head : head + 1] - cum_rows[head : head + 1, :]
        parts.append(jnp.exp(jnp.where(causal, differ, MASKED)))
    return parts


def scan_forward(
    devices, spans,
    z_ref, x_ref, bc_ref, step_ref,
    tap_ref, bias_ref, tapb_ref, biasb_ref, stepb_ref, decay_ref, skip_ref, shard_ref,
    y_ref, gated_ref, square_ref, enter_ref, all_ref,
    state, xbuf, bbuf, *sems,
):
    span, channels = x_ref.shape
    ring = RingGather(devices, shard_ref, all_ref, sems)
    turn = pl.program_id(0)

    @pl.when(turn == 0)
    def _():
        ring.greet()
        ring.begin()


    @pl.when(pl.program_id(0) == 0)
    def _():
        state[...] = jnp.zeros_like(state)
        xbuf[span:, :] = jnp.zeros((EDGE, channels), F32)
        bbuf[span:, :] = jnp.zeros((EDGE, 2 * NS), F32)

    xbuf[:EDGE, :] = xbuf[span:, :]
    bbuf[:EDGE, :] = bbuf[span:, :]
    xbuf[EDGE:, :] = x_ref[...]
    bbuf[EDGE:, :] = bc_ref[...]
    inputs = jax.nn.silu(conv_window(xbuf, tap_ref, bias_ref, span))
    shared = jax.nn.silu(conv_window(bbuf, tapb_ref, biasb_ref, span))
    spread = head_spread(channels)
    raw, step, cum, step_w, tails_w, grown_w = span_rates(
        step_ref, stepb_ref, decay_ref, spread, span
    )
    cum_rows = cum.T
    b_low = shared[:, :NS].astype(BF16)
    c_low = shared[:, NS:].astype(BF16)
    scaled = inputs * step_w
    scaled_low = scaled.astype(BF16)
    enter_ref[0] = state[...]
    outer = dot(c_low, state[...].astype(BF16)) * grown_w
    fresh = dot(b_low, (scaled * tails_w).astype(BF16), TN)
    state[...] = state[...] * grown_w[span - 1 : span, :] + fresh
    cross = dot(c_low, b_low, NT)
    causal = iota((span, span), 1) <= iota((span, span), 0)
    low_lanes = iota((span, LANES), 1) < MP
    for pair in range(channels // LANES):
        lanes = slice(pair * LANES, (pair + 1) * LANES)
        first, second = pair_decay(cum, cum_rows, pair, causal)
        weights = jnp.concatenate(
            [(cross * first).astype(BF16), (cross * second).astype(BF16)], axis=1
        )
        y_ref[:, lanes] = dot(weights, pair_split(scaled_low[:, lanes], low_lanes))
    y = y_ref[...] + outer + skip_ref[...] * inputs
    y_ref[...] = y
    gated = y * jax.nn.silu(z_ref[...])
    gated_ref[...] = gated
    square_ref[...] = row_sums(gated * gated)

    count = spans
    for step in range(1, ring.ahead + 1):
        pl.when(turn == min(count - 1, count * step // ring.ahead))(
            functools.partial(ring.hop, step)
        )
    pl.when(turn == count - 1)(ring.finish)


def scan_backward(
    devices, spans, windows, pieces, outs_count, count,
    z_ref, x_ref, xp_ref, bc_ref, bp_ref, step_ref, y_ref, enter_ref,
    dyg_ref, scale_ref, inner_ref, dqkv_ref,
    tap_ref, bias_ref, tapb_ref, biasb_ref, stepb_ref, decay_ref, skip_ref, gain_ref,
    *refs,
):
    sent, refs = refs[:count], refs[count:]
    (grad_ref, gx_ref, gb_ref, gh_ref), refs = refs[:4], refs[4:]
    outs, refs = refs[:outs_count], refs[outs_count:]
    (dstate, xbuf, bbuf, dxbuf, dbbuf, du_buf, col_buf), scratch = refs[:7], refs[7:]
    ring = RingScatter(devices, windows, pieces, sent, outs, scratch)
    span, channels = x_ref.shape
    turn = pl.program_id(0)

    @pl.when(turn == 0)
    def _():
        ring.greet()
        ring.begin()
        dstate[...] = jnp.zeros_like(dstate)
        dxbuf[...] = jnp.zeros_like(dxbuf)
        dbbuf[...] = jnp.zeros_like(dbbuf)
        col_buf[...] = jnp.zeros_like(col_buf)
        gx_ref[...] = jnp.zeros_like(gx_ref)
        gb_ref[...] = jnp.zeros_like(gb_ref)
        gh_ref[...] = jnp.zeros_like(gh_ref)

    inside = (turn < spans - 1).astype(F32)
    xbuf[:EDGE, :] = xp_ref[...] * inside
    bbuf[:EDGE, :] = bp_ref[...] * inside
    xbuf[EDGE:, :] = x_ref[...]
    bbuf[EDGE:, :] = bc_ref[...]
    conv = conv_window(xbuf, tap_ref, bias_ref, span)
    sig = jax.nn.sigmoid(conv)
    inputs = conv * sig
    convb = conv_window(bbuf, tapb_ref, biasb_ref, span)
    sigb = jax.nn.sigmoid(convb)
    shared = convb * sigb
    b_low = shared[:, :NS].astype(BF16)
    c_low = shared[:, NS:].astype(BF16)
    spread = head_spread(channels)
    raw, step, cum, step_w, tails_w, grown_w = span_rates(
        step_ref, stepb_ref, decay_ref, spread, span
    )
    cum_rows = cum.T
    scaled = inputs * step_w
    scaled_low = scaled.astype(BF16)

    z = z_ref[...]
    sig_z = jax.nn.sigmoid(z)
    swish = z * sig_z
    y = y_ref[...]
    scale = scale_ref[...].T[:, :1]
    normed = y * swish * scale
    dyg = dyg_ref[...]
    gain_grad = jnp.sum(dyg * normed, axis=0, keepdims=True)
    dgated = scale * (dyg * gain_ref[...] - normed * inner_ref[...].T[:, :1])
    dy = dgated * swish
    grad_ref[:, :channels] = (dgated * y * (sig_z * (1.0 + z * (1.0 - sig_z)))).astype(BF16)

    state_low = enter_ref[0].astype(BF16)
    dstate_low = dstate[...].astype(BF16)
    grown_low = (dy * grown_w).astype(BF16)
    dy_low = dy.astype(BF16)
    tailed = scaled * tails_w
    outer = dot(c_low, state_low) * grown_w
    from_state = dot(b_low, dstate_low)
    dc = dot(grown_low, state_low, NT)
    db = dot(tailed.astype(BF16), dstate_low, NT)
    leak = from_state * tailed
    last_w = grown_w[span - 1 : span, :]
    ends = (
        jnp.sum(leak, axis=0, keepdims=True)
        + jnp.sum(enter_ref[0] * dstate[...], axis=0, keepdims=True) * last_w
    )
    skips = jnp.sum(dy * inputs, axis=0, keepdims=True)
    dstate[...] = dstate[...] * last_w + dot(c_low, grown_low, TN)

    cross = dot(c_low, b_low, NT)
    causal = iota((span, span), 1) <= iota((span, span), 0)
    low_lanes = iota((span, LANES), 1) < MP
    lane = iota((span, LANES), 1)
    dcross = jnp.zeros((span, span), F32)
    row_part = jnp.zeros((span, LANES), F32)
    for pair in range(channels // LANES):
        lanes = slice(pair * LANES, (pair + 1) * LANES)
        decays = pair_decay(cum, cum_rows, pair, causal)
        dy_pair = pair_split(dy_low[:, lanes], low_lanes)
        dweights = dot(dy_pair, scaled_low[:, lanes], NT)
        both = []
        for part in range(2):
            head = 2 * pair + part
            dterm = dweights[part * span : (part + 1) * span] * decays[part]
            dcross = dcross + dterm
            flow = dterm * cross
            row_part = row_part + jnp.where(
                lane == head, jnp.sum(flow, axis=1, keepdims=True), 0.0
            )
            col_buf[head : head + 1, :] = jnp.sum(flow, axis=0, keepdims=True)
            both.append((cross * decays[part]).astype(BF16))
        du_buf[:, lanes] = dot(jnp.concatenate(both, axis=0), dy_pair, TN)
    du = du_buf[...] + from_state * tails_w
    dcross_low = dcross.astype(BF16)
    dc = dc + dot(dcross_low, b_low)
    db = db + dot(dcross_low, c_low, TN)

    sums = gather_heads(
        jnp.concatenate(
            [dy * outer - leak, du * inputs, ends, skips, jnp.zeros((EDGE - 2, channels), F32)],
            axis=0,
        ),
        spread,
    )
    at_end = sums[2 * span : 2 * span + 1, :]
    dcum = sums[:span] + row_part - col_buf[...].T
    upper = (iota((span, span), 1) >= iota((span, span), 0)).astype(BF16)
    drate = pick_left(upper, dcum, 3) + at_end
    dstep = drate * decay_ref[...] + sums[span : 2 * span]
    draw = dstep * jax.nn.sigmoid(raw)
    gh_ref[0:1, :] += jnp.sum(draw, axis=0, keepdims=True)
    gh_ref[1:2, :] += jnp.sum(drate * step, axis=0, keepdims=True) * decay_ref[...]
    gh_ref[2:3, :] += sums[2 * span + 1 : 2 * span + 2, :]

    dinputs = du * step_w + skip_ref[...] * dy
    dxbuf[span:, :] = dxbuf[:EDGE, :]
    dbbuf[span:, :] = dbbuf[:EDGE, :]
    dconv = dinputs * (sig * (1.0 + conv * (1.0 - sig)))
    dconvb = jnp.concatenate([db, dc], axis=1) * (sigb * (1.0 + convb * (1.0 - sigb)))
    dxbuf[:span, :] = dconv
    dbbuf[:span, :] = dconvb
    dx = jnp.zeros_like(dconv)
    dbc = jnp.zeros_like(dconvb)
    for tap in range(KCONV):
        back = KCONV - 1 - tap
        start = EDGE - 3 + tap
        dx = dx + tap_ref[tap : tap + 1, :] * dxbuf[back : back + span, :]
        dbc = dbc + tapb_ref[tap : tap + 1, :] * dbbuf[back : back + span, :]
        gx_ref[tap : tap + 1, :] += jnp.sum(
            dconv * xbuf[start : start + span, :], axis=0, keepdims=True
        )
        gb_ref[tap : tap + 1, :] += jnp.sum(
            dconvb * bbuf[start : start + span, :], axis=0, keepdims=True
        )
    gx_ref[KCONV : KCONV + 1, :] += jnp.sum(dconv, axis=0, keepdims=True)
    gb_ref[KCONV : KCONV + 1, :] += jnp.sum(dconvb, axis=0, keepdims=True)
    gx_ref[KCONV + 1 : KCONV + 2, :] += gain_grad
    width = 2 * channels + 2 * NS
    grad_ref[:, channels : 2 * channels] = dx.astype(BF16)
    grad_ref[:, 2 * channels : width] = dbc.astype(BF16)
    grad_ref[:, width : width + dqkv_ref.shape[1]] = dqkv_ref[...]
    grad_ref[:, width + dqkv_ref.shape[1] :] = draw.astype(BF16)
    for step in range(ring.ahead):
        pl.when(turn == spans * step // ring.ahead)(functools.partial(ring.hop, step))
    pl.when(turn == spans - 1)(ring.finish)


def scan_params(conv_x, conv_xb, conv_bc, conv_bcb, dt_bias, a_log, d_skip):
    heads = dt_bias.shape[0]

    def wide(row):
        return jnp.pad(row, (0, LANES - heads))[None, :]

    f32 = lambda value: value.astype(F32)
    return (
        f32(conv_x),
        f32(conv_xb)[None, :],
        f32(conv_bc),
        f32(conv_bcb)[None, :],
        wide(f32(dt_bias)),
        wide(-jnp.exp(f32(a_log))),
        jnp.repeat(f32(d_skip), MP)[None, :],
    )


def whole_spec(array):
    return pl.BlockSpec(array.shape, lambda turn: (0,) * array.ndim)


def run_scan_forward(proj, qkv_width, params, shard, devices):
    tokens = proj.shape[0]
    channels = params[1].shape[1]
    step_at = (2 * channels + 2 * NS + qkv_width) // LANES
    spans = tokens // SPAN
    bc_at = 2 * channels // (2 * NS)
    rows = lambda width, at: pl.BlockSpec((SPAN, width), lambda turn: (turn, at))
    anywhere = pl.BlockSpec(memory_space=pl.ANY)
    return pl.pallas_call(
        functools.partial(scan_forward, devices, spans),
        grid=(spans,),
        out_shape=(
            jax.ShapeDtypeStruct((tokens, channels), F32),
            jax.ShapeDtypeStruct((tokens, channels), F32),
            jax.ShapeDtypeStruct((EDGE, tokens), F32),
            jax.ShapeDtypeStruct((spans, NS, channels), F32),
            gather_shape(shard, devices),
        ),
        in_specs=[rows(channels, 0), rows(channels, 1), rows(2 * NS, bc_at), rows(LANES, step_at)]
        + [whole_spec(item) for item in params]
        + [anywhere],
        out_specs=(
            rows(channels, 0),
            rows(channels, 0),
            pl.BlockSpec((EDGE, SPAN), lambda turn: (0, turn)),
            pl.BlockSpec((1, NS, channels), lambda turn: (turn, 0, 0)),
            anywhere,
        ),
        scratch_shapes=[
            pltpu.VMEM((NS, channels), F32),
            pltpu.VMEM((SPAN + EDGE, channels), F32),
            pltpu.VMEM((SPAN + EDGE, 2 * NS), F32),
        ]
        + gather_sems(devices),
        compiler_params=pltpu.CompilerParams(collective_id=2, has_side_effects=True),
        cost_estimate=cost(20),
        name="scan_forward",
    )(proj, proj, proj, proj, *params, shard)


def run_scan_backward(
    proj, y, entering, dyg, scale, inner, dqkv, params, gain, sent, windows, pieces,
    shapes, devices,
):
    tokens, width = proj.shape
    channels = params[1].shape[1]
    qkv_width = dqkv.shape[1]
    step_at = (2 * channels + 2 * NS + qkv_width) // LANES
    spans = tokens // SPAN
    bc_at = 2 * channels // (2 * NS)
    edges = SPAN // EDGE
    rows = lambda size, at: pl.BlockSpec((SPAN, size), lambda turn: (spans - 1 - turn, at))
    edge = lambda size, at: pl.BlockSpec(
        (EDGE, size), lambda turn: (jnp.maximum((spans - 1 - turn) * edges - 1, 0), at)
    )
    keep = lambda shape: pl.BlockSpec(shape, lambda turn: (0, 0))
    shapes = tuple(jax.ShapeDtypeStruct(shape, F32) for shape in shapes)
    return pl.pallas_call(
        functools.partial(
            scan_backward, devices, spans, windows, pieces, len(shapes), len(sent)
        ),
        grid=(spans,),
        out_shape=(
            jax.ShapeDtypeStruct((tokens, width), BF16),
            jax.ShapeDtypeStruct((EDGE, channels), F32),
            jax.ShapeDtypeStruct((EDGE, 2 * NS), F32),
            jax.ShapeDtypeStruct((EDGE, LANES), F32),
        )
        + shapes,
        in_specs=[
            rows(channels, 0),
            rows(channels, 1),
            edge(channels, 1),
            rows(2 * NS, bc_at),
            edge(2 * NS, bc_at),
            rows(LANES, step_at),
            rows(channels, 0),
            pl.BlockSpec((1, NS, channels), lambda turn: (spans - 1 - turn, 0, 0)),
            rows(channels, 0),
            pl.BlockSpec((EDGE, SPAN), lambda turn: (0, spans - 1 - turn)),
            pl.BlockSpec((EDGE, SPAN), lambda turn: (0, spans - 1 - turn)),
            rows(qkv_width, 0),
        ]
        + [whole_spec(item) for item in params]
        + [whole_spec(gain)]
        + [pl.BlockSpec(memory_space=pl.ANY)] * len(sent),
        out_specs=(
            rows(width, 0),
            keep((EDGE, channels)),
            keep((EDGE, 2 * NS)),
            keep((EDGE, LANES)),
        )
        + tuple(keep(item.shape) for item in shapes),
        scratch_shapes=[
            pltpu.VMEM((NS, channels), F32),
            pltpu.VMEM((SPAN + EDGE, channels), F32),
            pltpu.VMEM((SPAN + EDGE, 2 * NS), F32),
            pltpu.VMEM((SPAN + EDGE, channels), F32),
            pltpu.VMEM((SPAN + EDGE, 2 * NS), F32),
            pltpu.VMEM((SPAN, channels), F32),
            pltpu.VMEM((LANES, SPAN), F32),
        ]
        + scatter_scratch(windows, sent[0].shape[0] // devices, devices),
        compiler_params=pltpu.CompilerParams(collective_id=6, has_side_effects=True),
        cost_estimate=cost(47),
        name="scan_backward",
    )(
        proj, proj, proj, proj, proj, proj, y, entering, dyg, scale, inner, dqkv, *params, gain,
        *sent,
    )


def rotary_tables(tokens):
    half = HEAD_SIZE // 2
    exponent = np.arange(half, dtype=np.float64) * (-2.0 * LOG_BASE / HEAD_SIZE)
    rates = np.tile(np.exp(exponent.astype(np.float32)).astype(np.float64), LANES // half)
    tables = []
    for places in (np.arange(FINE), np.arange(0, tokens, FINE)):
        angles = places[:, None] * rates[None, :]
        tables += [np.cos(angles).astype(np.float32), np.sin(angles).astype(np.float32)]
    return tables


def fill_rotary(fine_cos, fine_sin, coarse_cos, coarse_sin, cosine, sine):
    small_cos, small_sin = fine_cos[...], fine_sin[...]
    for turn in range(coarse_cos.shape[0]):
        big_cos, big_sin = coarse_cos[turn : turn + 1, :], coarse_sin[turn : turn + 1, :]
        rows = slice(turn * FINE, (turn + 1) * FINE)
        cosine[rows, :] = small_cos * big_cos - small_sin * big_sin
        sine[rows, :] = small_sin * big_cos + small_cos * big_sin


def head_masks():
    half = HEAD_SIZE // 2
    row, col = iota((LANES, LANES), 0), iota((LANES, LANES), 1)
    place = col % HEAD_SIZE
    ahead = jnp.where(place < half, -1.0, 0.0)
    behind = jnp.where(place < half, 0.0, 1.0)

    def turn(start):
        return jnp.where(row == start + half, ahead, jnp.where(row == start - half, behind, 0.0))

    first = row < HEAD_SIZE
    left = col < HEAD_SIZE
    low = lambda mask: mask.astype(BF16)
    within = low(turn(col))
    copy = low(jnp.where(row == place, 1.0, 0.0))
    copy_turn = low(jnp.where(first, turn(place), 0.0))
    value = low(jnp.where(row == place + HEAD_SIZE, 1.0, 0.0))
    fold = low(jnp.where(left & (row % HEAD_SIZE == place), 1.0, 0.0))
    other = row % HEAD_SIZE
    fold_turn = low(
        jnp.where(
            left,
            jnp.where(other == place + half, ahead, jnp.where(other == place - half, behind, 0.0)),
            0.0,
        )
    )
    fold_value = low(jnp.where(left, 0.0, jnp.where(other == place, 1.0, 0.0)))
    return within, copy, copy_turn, value, fold, fold_turn, fold_value


def attend_forward(
    q_ref, kv_ref, fine_cos, fine_sin, coarse_cos, coarse_sin,
    qkv_ref, lse_ref, o_ref, vt, cos_ref, sin_ref,
):
    fill_rotary(fine_cos, fine_sin, coarse_cos, coarse_sin, cos_ref, sin_ref)
    tokens, query_width = q_ref.shape
    pairs = query_width // LANES
    within, copy, copy_turn, value = head_masks()[:4]

    def turn_rows(i, carry):
        rows = pl.ds(pl.multiple_of(i * QBLK, QBLK), QBLK)
        cosine, sine = cos_ref[rows, :], sin_ref[rows, :]
        for pair in range(pairs):
            lanes = slice(pair * LANES, (pair + 1) * LANES)
            query = q_ref[rows, lanes]
            turned = query * cosine + pick(query, within) * sine
            qkv_ref[rows, lanes] = (turned * HEAD_SIZE**-0.5).astype(BF16)
        kv = kv_ref[rows, :]
        keys = pick(kv, copy) * cosine + pick(kv, copy_turn) * sine
        qkv_ref[rows, query_width : query_width + LANES] = keys.astype(BF16)
        qkv_ref[rows, query_width + LANES :] = dot(kv.astype(BF16), value).astype(BF16)
        vt[:, rows] = kv.T[HEAD_SIZE:, :].astype(BF16)
        return carry

    lax.fori_loop(0, tokens // QBLK, turn_rows, 0)
    low_lanes = iota((QBLK, LANES), 1) < HEAD_SIZE
    wide = (QBLK, 2 * QBLK)
    visible = iota(wide, 0) <= iota(wide, 1) % QBLK

    def block(i, carry):
        here = pl.ds(pl.multiple_of(i * QBLK, QBLK), QBLK)
        queries = [
            pair_split(qkv_ref[here, pair * LANES : (pair + 1) * LANES], low_lanes)
            for pair in range(pairs)
        ]

        def tile(there, state, edge):
            keys = qkv_ref[there, query_width : query_width + LANES]
            result = []
            for pair in range(pairs):
                top, total, out = state[3 * pair : 3 * pair + 3]
                scores = dot(keys, queries[pair], NT)
                if edge:
                    scores = jnp.where(visible, scores, MASKED)
                higher = jnp.maximum(top, jnp.max(scores, axis=0, keepdims=True))
                probs = jnp.exp(scores - higher)
                fade = jnp.exp(top - higher)
                total = total * fade + jnp.sum(probs, axis=0, keepdims=True)
                out = out * fade + dot(vt[:, there], probs.astype(BF16))
                result += [higher, total, out]
            return tuple(result)

        state = (
            jnp.full((1, 2 * QBLK), MASKED, F32),
            jnp.zeros((1, 2 * QBLK), F32),
            jnp.zeros((HEAD_SIZE, 2 * QBLK), F32),
        ) * pairs
        state = lax.fori_loop(
            0,
            i,
            lambda j, state: tile(pl.ds(pl.multiple_of(j * QBLK, QBLK), QBLK), state, False),
            state,
        )
        state = tile(here, state, True)
        for pair in range(pairs):
            top, total, out = state[3 * pair : 3 * pair + 3]
            out = out / total
            lse = top + jnp.log(total)
            lse_ref[2 * pair : 2 * pair + 1, here] = lse[:, :QBLK]
            lse_ref[2 * pair + 1 : 2 * pair + 2, here] = lse[:, QBLK:]
            both = jnp.concatenate([out[:, :QBLK], out[:, QBLK:]], axis=0)
            o_ref[here, pair * LANES : (pair + 1) * LANES] = both.T.astype(BF16)
        return carry

    lax.fori_loop(0, tokens // QBLK, block, 0)


def attend_backward(
    qkv_ref, lse_ref, o_ref, do_ref, fine_cos, fine_sin, coarse_cos, coarse_sin,
    dqkv_ref,
    dq, kt, dk, dv, cos_ref, sin_ref,
):
    fill_rotary(fine_cos, fine_sin, coarse_cos, coarse_sin, cos_ref, sin_ref)
    tokens, query_width = o_ref.shape
    pairs = query_width // LANES
    key_lanes = slice(query_width, query_width + LANES)
    value_lanes = slice(query_width + LANES, query_width + 2 * LANES)

    def turn_keys(i, carry):
        rows = pl.ds(pl.multiple_of(i * QBLK, QBLK), QBLK)
        kt[:, rows] = qkv_ref[rows, key_lanes].astype(F32).T[:HEAD_SIZE, :].astype(BF16)
        return carry

    lax.fori_loop(0, tokens // QBLK, turn_keys, 0)
    dk[...] = jnp.zeros_like(dk)
    dv[...] = jnp.zeros_like(dv)
    low_lanes = iota((QBLK, LANES), 1) < HEAD_SIZE
    wide = (QBLK, 2 * QBLK)
    visible = iota(wide, 0) <= iota(wide, 1) % QBLK
    ones = jnp.ones((EDGE, LANES), BF16)

    def block(i, carry):
        here = pl.ds(pl.multiple_of(i * QBLK, QBLK), QBLK)
        queries, grads, inners, lses = [], [], [], []
        for pair in range(pairs):
            lanes = slice(pair * LANES, (pair + 1) * LANES)
            queries.append(pair_split(qkv_ref[here, lanes], low_lanes))
            grad = do_ref[here, lanes]
            grads.append(pair_split(grad, low_lanes))
            both = pair_split(grad.astype(F32) * o_ref[here, lanes].astype(F32), low_lanes)
            high, low = parts(both, 2)
            inners.append((dot(ones, high, NT) + dot(ones, low, NT))[:1])
            lses.append(
                jnp.concatenate(
                    [
                        lse_ref[2 * pair : 2 * pair + 1, here],
                        lse_ref[2 * pair + 1 : 2 * pair + 2, here],
                    ],
                    axis=1,
                )
            )
        query_all = jnp.concatenate(queries, axis=0)
        grad_all = jnp.concatenate(grads, axis=0)

        def tile(there, state, edge):
            keys = qkv_ref[there, key_lanes]
            values = qkv_ref[there, value_lanes]
            all_probs, all_dscores, result = [], [], []
            for pair in range(pairs):
                probs = dot(keys, queries[pair], NT) - lses[pair]
                if edge:
                    probs = jnp.where(visible, probs, MASKED)
                probs = jnp.exp(probs)
                dprobs = dot(values, grads[pair], NT)
                dscores = (probs * (dprobs - inners[pair])).astype(BF16)
                all_probs.append(probs.astype(BF16))
                all_dscores.append(dscores)
                result.append(state[pair] + dot(kt[:, there], dscores))
            dv[there, :] += dot(jnp.concatenate(all_probs, axis=1), grad_all)
            dk[there, :] += dot(jnp.concatenate(all_dscores, axis=1), query_all)
            return tuple(result)

        state = (jnp.zeros((HEAD_SIZE, 2 * QBLK), F32),) * pairs
        state = lax.fori_loop(
            0,
            i,
            lambda j, state: tile(pl.ds(pl.multiple_of(j * QBLK, QBLK), QBLK), state, False),
            state,
        )
        state = tile(here, state, True)
        for pair in range(pairs):
            both = jnp.concatenate([state[pair][:, :QBLK], state[pair][:, QBLK:]], axis=0)
            dq[here, pair * LANES : (pair + 1) * LANES] = both.T
        return carry

    lax.fori_loop(0, tokens // QBLK, block, 0)
    masks = head_masks()
    within, (fold, fold_turn, fold_value) = masks[0], masks[4:]

    def turn_back(i, carry):
        rows = pl.ds(pl.multiple_of(i * QBLK, QBLK), QBLK)
        cosine, sine = cos_ref[rows, :], sin_ref[rows, :]
        for pair in range(pairs):
            lanes = slice(pair * LANES, (pair + 1) * LANES)
            grad = dq[rows, lanes]
            grad = grad * cosine - pick(grad, within) * sine
            dqkv_ref[rows, lanes] = (grad * HEAD_SIZE**-0.5).astype(BF16)
        grad = dk[rows, :]
        grad = pick(grad, fold) * cosine - pick(grad, fold_turn) * sine
        grad = grad + pick(dv[rows, :], fold_value)
        dqkv_ref[rows, query_width:] = grad.astype(BF16)
        return carry

    lax.fori_loop(0, tokens // QBLK, turn_back, 0)


def run_attend_forward(proj, query_at, query_width, tables):
    tokens = proj.shape[0]
    cols = lambda size, at: pl.BlockSpec((tokens, size), lambda turn: (0, at // size))
    return pl.pallas_call(
        attend_forward,
        grid=(1,),
        out_shape=(
            jax.ShapeDtypeStruct((tokens, query_width + 2 * LANES), BF16),
            jax.ShapeDtypeStruct((EDGE, tokens), F32),
            jax.ShapeDtypeStruct((tokens, query_width), BF16),
        ),
        in_specs=[
            cols(query_width, query_at),
            cols(2 * HEAD_SIZE, query_at + query_width),
        ]
        + [whole_spec(table) for table in tables],
        out_specs=(
            cols(query_width + 2 * LANES, 0),
            pl.BlockSpec((EDGE, tokens), lambda turn: (0, 0)),
            cols(query_width, 0),
        ),
        scratch_shapes=[
            pltpu.VMEM((HEAD_SIZE, tokens), BF16),
            pltpu.VMEM((tokens, LANES), F32),
            pltpu.VMEM((tokens, LANES), F32),
        ],
        cost_estimate=cost(15),
        name="attend_forward",
    )(proj, proj, *tables)


def run_attend_backward(qkv, lse, attended, grads, grad_at, tables):
    tokens, query_width = attended.shape
    vmem = pl.BlockSpec(memory_space=pltpu.VMEM)
    cols = lambda size, at: pl.BlockSpec((tokens, size), lambda turn: (0, at // size))
    return pl.pallas_call(
        attend_backward,
        grid=(1,),
        out_shape=jax.ShapeDtypeStruct((tokens, query_width + 2 * HEAD_SIZE), BF16),
        in_specs=[
            whole_spec(qkv),
            whole_spec(lse),
            whole_spec(attended),
            cols(query_width, grad_at),
        ]
        + [whole_spec(table) for table in tables],
        out_specs=cols(query_width + 2 * HEAD_SIZE, 0),
        scratch_shapes=[
            pltpu.VMEM((tokens, query_width), F32),
            pltpu.VMEM((HEAD_SIZE, tokens), BF16),
            pltpu.VMEM((tokens, LANES), F32),
            pltpu.VMEM((tokens, LANES), F32),
            pltpu.VMEM((tokens, LANES), F32),
            pltpu.VMEM((tokens, LANES), F32),
        ],
        cost_estimate=cost(16),
        name="attend_backward",
    )(qkv, lse, attended, grads, *tables)


def feed_forward(
    x_ref, mixed_ref, other_ref, top_ref, gain_ref, gu_ref, down_ref,
    after_ref, scale_ref, hidden_ref, act_ref, dgu_ref, part_ref, back_ref,
):
    units = down_ref.shape[1]
    after = x_ref[...].astype(F32) + (mixed_ref[...].astype(F32) + other_ref[...].astype(F32))
    after_ref[...] = after
    scale = lax.rsqrt(jnp.mean(after * after, axis=-1, keepdims=True) + EPSILON)
    scale_ref[...] = scale
    hidden = (after * scale * gain_ref[...]).astype(BF16)
    hidden_ref[...] = hidden
    top = top_ref[...]
    for start in range(0, units, UBLK):
        cols = slice(start, start + UBLK)
        up_cols = slice(units + start, units + start + UBLK)
        gate = dot(hidden, gu_ref[:, cols])
        upward = dot(hidden, gu_ref[:, up_cols])
        grad = dot(top, down_ref[:, cols])
        sigma = jax.nn.sigmoid(gate)
        swish = gate * sigma
        act_ref[:, cols] = (swish * upward).astype(BF16)
        slope = sigma * (1.0 + gate * (1.0 - sigma))
        dgu_ref[:, cols] = (grad * upward * slope).astype(BF16)
        dgu_ref[:, up_cols] = (grad * swish).astype(BF16)
    back_ref[...] = dot(dgu_ref[...], gu_ref[...], NT).astype(BF16)
    part_ref[...] = dot(act_ref[...], down_ref[...], NT).astype(BF16)


def once(item):
    return pl.BlockSpec(item.shape, lambda turn: (0,) * item.ndim, pipeline_mode=pl.Buffered(1))


def run_feed_forward(x, mixed, other, top, gain, w_gate_up, w_down_t):
    tokens, width = x.shape
    units = w_down_t.shape[1]
    rows = lambda size: pl.BlockSpec((TBLK, size), lambda turn: (turn, 0))
    shape = jax.ShapeDtypeStruct
    return pl.pallas_call(
        feed_forward,
        grid=(tokens // TBLK,),
        out_shape=(
            shape((tokens, width), F32),
            shape((tokens, 1), F32),
            shape((tokens, width), BF16),
            shape((tokens, units), BF16),
            shape((tokens, 2 * units), BF16),
            shape((tokens, width), BF16),
            shape((tokens, width), BF16),
        ),
        in_specs=[rows(width)] * 4 + [once(gain), once(w_gate_up), once(w_down_t)],
        out_specs=(
            rows(width), rows(1), rows(width), rows(units), rows(2 * units), rows(width),
            rows(width),
        ),
        cost_estimate=cost(20),
        name="feed_forward",
    )(x, mixed, other, top, gain, w_gate_up, w_down_t)


def mixer_forward(gated_ref, scale_ref, gain_ref, attended_ref, w_ref, low_ref, mixed_ref):
    channels = gated_ref.shape[1]
    scale = scale_ref[...].T[:, :1]
    low_ref[:, :channels] = (gated_ref[...] * scale * gain_ref[...]).astype(BF16)
    low_ref[:, channels:] = attended_ref[...]
    mixed_ref[...] = dot(low_ref[...], w_ref[...], NT).astype(BF16)


def run_mixer_forward(gated, scale, gain, attended, w_out):
    tokens, channels = gated.shape
    width, inner = w_out.shape
    rows = lambda size: pl.BlockSpec((TBLK, size), lambda turn: (turn, 0))
    return pl.pallas_call(
        mixer_forward,
        grid=(tokens // TBLK,),
        out_shape=(
            jax.ShapeDtypeStruct((tokens, inner), BF16),
            jax.ShapeDtypeStruct((tokens, width), BF16),
        ),
        in_specs=[
            rows(channels),
            pl.BlockSpec((EDGE, TBLK), lambda turn: (0, turn)),
            once(gain),
            rows(attended.shape[1]),
            once(w_out),
        ],
        out_specs=(rows(inner), rows(width)),
        cost_estimate=cost(5),
        name="mixer_forward",
    )(gated, scale, gain, attended, w_out)


def mixer_backward(
    part_ref, other_ref, after_ref, scale_ref, top_ref, gain_ref,
    w_ref, gated_ref, scale_m_ref, gain_m_ref,
    grad_ref, low_ref, mamba_ref, attended_ref, inner_ref, gain_grad_ref,
):
    channels = gated_ref.shape[1]

    @pl.when(pl.program_id(0) == 0)
    def _():
        gain_grad_ref[...] = jnp.zeros_like(gain_grad_ref)

    grad = part_ref[...].astype(F32) + other_ref[...].astype(F32)
    scale = scale_ref[...]
    normed = after_ref[...] * scale
    gain_grad_ref[:1, :] += jnp.sum(grad * normed, axis=0, keepdims=True)
    weighted = grad * gain_ref[...]
    mean = jnp.mean(weighted * normed, axis=-1, keepdims=True)
    total = top_ref[...].astype(F32) + scale * (weighted - normed * mean)
    grad_ref[...] = total
    low_ref[...] = total.astype(BF16)
    back = dot(low_ref[...], w_ref[...])
    mamba = back[:, :channels]
    mamba_ref[...] = mamba
    attended_ref[...] = back[:, channels:].astype(BF16)
    inner_ref[...] = row_sums(mamba * gain_m_ref[...] * gated_ref[...]) * scale_m_ref[...]


def run_mixer_backward(part, other, after, scale, top, gain, w_out, gated, scale_m, gain_m):
    tokens, width = after.shape
    channels = gated.shape[1]
    inner = w_out.shape[1]
    shape = jax.ShapeDtypeStruct
    rows = lambda size: pl.BlockSpec((NBLK, size), lambda turn: (turn, 0))
    lanes = pl.BlockSpec((EDGE, NBLK), lambda turn: (0, turn))
    return pl.pallas_call(
        mixer_backward,
        grid=(tokens // NBLK,),
        out_shape=(
            shape((tokens, width), F32),
            shape((tokens, width), BF16),
            shape((tokens, channels), F32),
            shape((tokens, inner - channels), BF16),
            shape((EDGE, tokens), F32),
            shape((EDGE, width), F32),
        ),
        in_specs=[rows(width)] * 3
        + [rows(1), rows(width), once(gain), once(w_out), rows(channels), lanes, once(gain_m)],
        out_specs=(
            rows(width), rows(width), rows(channels), rows(inner - channels), lanes,
            pl.BlockSpec((EDGE, width), lambda turn: (0, 0)),
        ),
        cost_estimate=cost(8),
        name="mixer_backward",
    )(part, other, after, scale, top, gain, w_out, gated, scale_m, gain_m)


def weight_grad(left_ref, right_ref, out_ref):
    out_ref[...] = dot(left_ref[...], right_ref[...], TN).astype(BF16)


def run_weight_grad(left, right):
    tokens, rows = left.shape
    cols = right.shape[1]
    return pl.pallas_call(
        weight_grad,
        grid=(rows // LANES,),
        out_shape=jax.ShapeDtypeStruct((rows, cols), BF16),
        in_specs=[pl.BlockSpec((tokens, LANES), lambda turn: (0, turn)), once(right)],
        out_specs=pl.BlockSpec((LANES, cols), lambda turn: (turn, 0)),
        cost_estimate=cost(5),
        name="weight_grad",
    )(left, right)


def finish_layer(
    x_ref, gain_ref, part_ref, other_ref, grad_ref, after_ref, ffn_ref, ffn_other_ref,
    out_ref, result_ref,
):
    x = x_ref[...].astype(F32)
    scale = lax.rsqrt(jnp.mean(x * x, axis=-1, keepdims=True) + EPSILON)
    normed = x * scale
    weighted = (part_ref[...].astype(F32) + other_ref[...].astype(F32)) * gain_ref[...]
    mean = jnp.mean(weighted * normed, axis=-1, keepdims=True)
    out_ref[...] = grad_ref[...] + scale * (weighted - normed * mean)
    ffn = ffn_ref[...].astype(F32) + ffn_other_ref[...].astype(F32)
    result_ref[...] = (after_ref[...] + ffn).astype(BF16)


def run_finish(x, gain, part, other, grad, after, ffn, ffn_other):
    tokens, width = x.shape
    rows = pl.BlockSpec((NBLK, width), lambda turn: (turn, 0))
    return pl.pallas_call(
        finish_layer,
        grid=(tokens // NBLK,),
        out_shape=(
            jax.ShapeDtypeStruct((tokens, width), F32),
            jax.ShapeDtypeStruct((tokens, width), BF16),
        ),
        in_specs=[rows, once(gain)] + [rows] * 6,
        out_specs=(rows, rows),
        cost_estimate=cost(8),
        name="finish_layer",
    )(x, gain, part, other, grad, after, ffn, ffn_other)


def swap(partial):
    return lax.ppermute(partial, "tensor", [(0, 1), (1, 0)])


def join(mine, other):
    return mine.astype(F32) + other.astype(F32)


def tensor_sum(partial):
    return join(partial, swap(partial))


def local(
    layer_input, w_norm1, w_zx, w_bc, w_dt, conv_x, conv_xb, conv_bc, conv_bcb, dt_bias, a_log,
    d_skip, w_mnorm, w_mout, query_key_value_weight, output_weight, w_norm2, w_gu, w_down,
    grad_output,
):
    devices = lax.axis_size("dp")
    tokens, width = layer_input.shape
    shard = w_zx.shape[0]
    channels = conv_xb.shape[0]
    heads = dt_bias.shape[0]
    qkv_width = query_key_value_weight.shape[2]
    units = w_down.shape[0]
    attn_width = output_weight.shape[1]
    tail = jnp.concatenate(
        [w_dt, w_norm1[:, None], w_norm2[:, None], jnp.zeros((shard, LANES - heads - 2), BF16)],
        axis=1,
    )
    mixer_in = jnp.concatenate(
        [w_zx.reshape(shard, -1), w_bc, query_key_value_weight.reshape(shard, -1), tail], axis=1
    )
    in_width = mixer_in.shape[1]
    (w_in,) = gather_rows([mixer_in], devices, 0)
    norm1 = w_in[:, in_width - LANES + heads].astype(F32)
    norm2 = w_in[:, in_width - LANES + heads + 1].astype(F32)

    source = layer_input.astype(F32)
    scale_one = lax.rsqrt(jnp.mean(source * source, axis=-1, keepdims=True) + EPSILON)
    normed_one = source * scale_one
    hidden_one = lax.optimization_barrier((normed_one * norm1).astype(BF16))
    proj = dot(hidden_one, w_in)
    params = scan_params(conv_x, conv_xb, conv_bc, conv_bcb, dt_bias, a_log, d_skip)
    out_shard = jnp.concatenate([w_mout.T, output_weight.reshape(attn_width, -1).T], axis=1)
    y, gated, square_sum, entering, w_out = run_scan_forward(
        proj, qkv_width, params, out_shard, devices
    )
    channels_all = channels * lax.axis_size("tensor")
    scale_m = lax.rsqrt(tensor_sum(square_sum) / channels_all + EPSILON)
    tables = rotary_tables(tokens)
    qkv_at = 2 * channels + 2 * NS
    qkv, lse, attended = run_attend_forward(proj, qkv_at, attn_width, tables)
    gain_m = w_mnorm.astype(F32)[None, :]
    mixer_out, mixed = run_mixer_forward(gated, scale_m, gain_m, attended, w_out)
    mixed, gate_up_shard, down_shard = lax.optimization_barrier(
        (mixed, w_gu.reshape(shard, -1), w_down.T)
    )
    other = swap(mixed)
    w_gate_up, w_down_t = gather_rows([gate_up_shard, down_shard], devices, 3)
    other, w_gate_up, w_down_t = lax.optimization_barrier((other, w_gate_up, w_down_t))
    after, scale_two, hidden_two, activated, grad_gu_low, ffn_part, partial_two = run_feed_forward(
        layer_input, mixed, other, grad_output, norm2[None, :], w_gate_up, w_down_t
    )
    other = swap(partial_two)
    grad_down = run_weight_grad(grad_output, activated)
    (mine_gu,) = scatter_product(
        hidden_two,
        grad_gu_low,
        [(0, 1, 0, 2 * units)],
        [(0, 0, units, 0, 0), (0, units, 2 * units, 0, 1)],
        [(shard, 2, units)],
        devices,
        1,
    )
    other, mine_gu, grad_down, ffn_part = lax.optimization_barrier(
        (other, mine_gu, grad_down, ffn_part)
    )
    ffn_other = swap(ffn_part)
    grad_after, grad_mix_low, grad_mamba, grad_attended, inner_m, grad_norm2 = run_mixer_backward(
        partial_two, other, after, scale_two, grad_output, norm2[None, :], w_out, gated, scale_m,
        gain_m,
    )
    inner_m = tensor_sum(inner_m) / channels_all
    dqkv = run_attend_backward(qkv, lse, attended, grad_attended, 0, tables)
    grad_out = run_weight_grad(grad_mix_low, mixer_out)
    windows = [(0, None, 0, channels + attn_width), (1, None, 0, units)]
    pieces = [
        (0, 0, channels, 0, None),
        (0, channels, channels + attn_width, 1, None),
        (1, 0, units, 2, None),
    ]
    shapes = [(shard, channels), (shard, attn_width), (shard, units)]
    grad_proj, small_x, small_b, small_h, mine_mout, mine_o, mine_down = run_scan_backward(
        proj, y, entering, grad_mamba, scale_m, inner_m, dqkv, params, gain_m,
        [grad_out, grad_down], windows, pieces, shapes, devices,
    )
    ffn_other, grad_proj = lax.optimization_barrier((ffn_other, grad_proj))
    partial_one, grad_proj = lax.optimization_barrier(
        (dot(grad_proj, w_in, NT).astype(BF16), grad_proj)
    )
    crossing = jnp.concatenate(
        [
            small_b[: KCONV + 1].reshape(-1, LANES),
            jnp.sum(partial_one.astype(F32) * normed_one, axis=0).reshape(-1, LANES),
        ],
        axis=0,
    )
    crossing = tensor_sum(crossing)
    partial_one, crossing = lax.optimization_barrier((partial_one, crossing))
    other = swap(partial_one)
    small = jnp.concatenate(
        [
            small_x[: KCONV + 2].reshape(-1, LANES),
            small_h[:3],
            crossing,
            grad_norm2[0].reshape(-1, LANES),
        ],
        axis=0,
    )
    small_rows = small.shape[0]
    small = jnp.pad(small, ((0, -small_rows % EDGE), (0, 0)))
    shared_at = 2 * channels
    step_at = qkv_at + qkv_width
    mine_zx, mine_bc, mine_qkv, mine_step, small = scatter_product(
        hidden_one,
        grad_proj,
        [(0, 1, 0, in_width)],
        [
            (0, 0, channels, 0, 0),
            (0, channels, shared_at, 0, 1),
            (0, shared_at, qkv_at, 1, None),
            (0, qkv_at, step_at, 2, 0),
            (0, step_at, in_width, 3, "turned"),
        ],
        [
            (shard, 2, channels),
            (shard, 2 * NS),
            (shard, 1, qkv_width),
            (heads, shard),
        ],
        devices,
        5,
        (small,),
    )
    other, mine_bc = lax.optimization_barrier((other, mine_bc))
    grad_source, result = run_finish(
        layer_input, norm1[None, :], partial_one, other, grad_after, after, ffn_part, ffn_other
    )

    half = NS * 2 // lax.axis_size("tensor")
    shared_cols = tensor_sum(mine_bc)
    begin = lax.axis_index("tensor") * half
    grad_bc = lax.dynamic_slice_in_dim(shared_cols, begin, half, 1)
    small = small[:small_rows].reshape(-1)
    x_size = (KCONV + 2) * channels
    h_size = 3 * LANES
    b_size = (KCONV + 1) * 2 * NS
    total_x = small[:x_size].reshape(KCONV + 2, channels)
    total_h = small[x_size : x_size + h_size].reshape(3, LANES)
    total_b = small[x_size + h_size : x_size + h_size + b_size].reshape(KCONV + 1, 2 * NS)
    total_b = lax.dynamic_slice_in_dim(total_b, begin, half, 1)
    norms = small[x_size + h_size + b_size :].reshape(2, width)
    norms = lax.dynamic_slice_in_dim(norms, lax.axis_index("dp") * shard, shard, 1)
    return (
        result,
        grad_source,
        norms[0],
        mine_zx,
        grad_bc,
        mine_step.T,
        total_x[:KCONV],
        total_x[KCONV],
        total_b[:KCONV],
        total_b[KCONV],
        total_h[0, :heads],
        total_h[1, :heads],
        total_h[2, :heads],
        total_x[KCONV + 1],
        mine_mout.T,
        mine_qkv,
        mine_o.T.reshape(output_weight.shape),
        norms[1],
        mine_gu,
        mine_down.T,
    )


def solution(mesh):
    return jax.shard_map(
        local,
        mesh=mesh,
        in_specs=(
            P("dp", None),
            P("dp"),
            P("dp", None, "tensor"),
            P("dp", None),
            P("dp", "tensor"),
            P(None, "tensor"),
            P("tensor"),
            P(),
            P(),
            P("tensor"),
            P("tensor"),
            P("tensor"),
            P("tensor"),
            P("tensor", "dp"),
            P("dp", "tensor", None),
            P("tensor", None, "dp"),
            P("dp"),
            P("dp", None, "tensor"),
            P("tensor", "dp"),
            P("dp", None),
        ),
        out_specs=(
            P("dp", None),
            P("dp", None),
            P("dp"),
            P("dp", None, "tensor"),
            P("dp", "tensor"),
            P("dp", "tensor"),
            P(None, "tensor"),
            P("tensor"),
            P(None, "tensor"),
            P("tensor"),
            P("tensor"),
            P("tensor"),
            P("tensor"),
            P("tensor"),
            P("tensor", "dp"),
            P("dp", "tensor", None),
            P("tensor", None, "dp"),
            P("dp"),
            P("dp", None, "tensor"),
            P("tensor", "dp"),
        ),
        check_vma=False,
    )
```

profile of v0, /device:TPU:0, one launch (start us, length us, event | category | flops | bytes accessed | tf_op | source)
XLA Modules:
  0.0 391.1 jit_solution(469733952942355685)
XLA Ops:
  3.9 1.6 concatenate.12.refs_0_
  5.6 36.8 %gather_rows.2 = bf16[1024,2304]{1,0:T(8,128)(2,1)} custom-call(bf16[64,2304]{1,0:T(8,128)(2,1)} %concatenate.12.refs_0_), custom_call_target="tpu_custom_call" | custom-call | flops 3000000000 | tf_op jit(solution)/shard_map/gather_rows/pallas_call | solution.py:198
  42.4 2.0 convert_reduce_fusion
  46.9 7.4 %fusion.6.z_ref.x_ref.bc_ref.step_ref.q_ref.kv_ref.xp_ref.bp_ref = f32[1024,2304]{1,0:T(8,128)} fusion(bf16[1024,1024]{1,0:T(8,128)(2,1)S(1)} %fusion.2.left_ref, bf16[1024,2304]{1,0:T(8,128)(2,1)S(1)} %copy-done.11), kind=kOutput, calls=%fused_computation.34 | convolution fusion | flops 4831838208 | bytes 16252928 | tf_op jit(solution)/shard_map/dot_general | solution.py:39
  59.1 22.0 %scan_forward.1 = (f32[1024,768]{1,0:T(8,128)}, f32[1024,768]{1,0:T(8,128)}, f32[8,1024]{1,0:T(8,128)}, f32[8,128,768]{2,1,0:T(8,128)}, bf16[1024,1024]{1,0:T(8,128)(2,1)}) custom-call(f32[1024,2304]{1,0:T(8,128)} %fusion.6.z_ref.x_ref.bc_ref.step_ref.q_ref.kv_ref.xp_ref.bp_ref, f32[1024,2304]{1,0:T(8,128)} %fusion.6.z_ref.x_ref.bc_ref.step_ref.q_ref.kv_ref.xp_ref.bp_ref, ...), custom_call_target="tpu_custom_call" | custom-call | flops 20000000000 | tf_op jit(solution)/shard_map/scan_forward/pallas_call | solution.py:871
  81.1 1.6 collective-permute-start
  82.7 12.5 %attend_forward.1 = (bf16[1024,512]{1,0:T(8,128)(2,1)}, f32[8,1024]{1,0:T(8,128)}, bf16[1024,256]{1,0:T(8,128)(2,1)}) custom-call(f32[1024,2304]{1,0:T(8,128)} %fusion.6.z_ref.x_ref.bc_ref.step_ref.q_ref.kv_ref.xp_ref.bp_ref, f32[1024,2304]{1,0:T(8,128)} %fusion.6.z_ref.x_ref.bc_ref.step_ref.q_ref.kv_ref.xp_ref.bp_ref, f32[32,128]{1,0:T(8,128)} %constant.42.clone.fine_cos, ...), custom_call_target="tpu_custom_call" | custom-call | flops 15000000512 | tf_op jit(solution)/shard_map/attend_forward/pallas_call | solution.py:1204
  97.2 7.0 %mixer_forward.1 = (bf16[1024,1024]{1,0:T(8,128)(2,1)}, bf16[1024,1024]{1,0:T(8,128)(2,1)}) custom-call(f32[1024,768]{1,0:T(8,128)} %get-tuple-element.77.gated_ref, f32[8,1024]{1,0:T(8,128)} %add_rsqrt_fusion.scale_ref.scale_m_ref, f32[1,768]{1,0:T(1,128)} %reshape.136.gain_ref.gain_m_ref, bf16[1024,256]{1,0:T(8,128)(2,1)} %get-tuple-element.79.attended_ref.o_ref, ...), custom_call_target="tpu_custom_call" | custom-call | flops 5000000000 | tf_op jit(solution)/shard_map/mixer_forward/pallas_call | solution.py:1332
  104.7 38.8 %gather_rows.3 = (bf16[1024,2048]{1,0:T(8,128)(2,1)}, bf16[1024,1024]{1,0:T(8,128)(2,1)}) custom-call(bf16[64,2048]{1,0:T(8,128)(2,1)} %bitcast.53, bf16[64,1024]{1,0:T(8,128)(2,1)} %bitcast.71), custom_call_target="tpu_custom_call" | custom-call | flops 3000000000 | tf_op jit(solution)/shard_map/gather_rows/pallas_call | solution.py:198
  143.5 8.5 %collective-permute-done.1.other_ref = bf16[1024,1024]{1,0:T(8,128)(2,1)S(1)} collective-permute-done((bf16[1024,1024]{1,0:T(8,128)(2,1)}, bf16[1024,1024]{1,0:T(8,128)(2,1)S(1)}, u32[]{:S(2)}, u32[]{:S(2)}) %collective-permute-start.1) | collective-permute-done | bytes 2097184 | tf_op jit(solution)/shard_map/ppermute | solution.py:1458
  153.3 20.0 %feed_forward.1 = (f32[1024,1024]{1,0:T(8,128)}, f32[1024,1]{1,0:T(8,128)}, bf16[1024,1024]{1,0:T(8,128)(2,1)}, bf16[1024,1024]{1,0:T(8,128)(2,1)}, bf16[1024,20...) custom-call(bf16[1024,1024]{1,0:T(8,128)(2,1)} %x_ref.3, ...), custom_call_target="tpu_custom_call" | custom-call | flops 20000000000 | tf_op jit(solution)/shard_map/feed_forward/pallas_call | solution.py:1298
  173.9 38.4 %scatter_product.2 = f32[64,2,1024]{2,1,0:T(2,128)} custom-call(bf16[1024,1024]{1,0:T(8,128)(2,1)} %get-tuple-element.91.left_ref, bf16[1024,2048]{1,0:T(8,128)(2,1)} %get-tuple-element.92.right_ref), custom_call_target="tpu_custom_call" | custom-call | flops 3000000000 | tf_op jit(solution)/shard_map/scatter_product/pallas_call | solution.py:535
  212.2 8.1 %weight_grad.2.refs_1_ = bf16[1024,1024]{1,0:T(8,128)(2,1)} custom-call(bf16[1024,1024]{1,0:T(8,128)(2,1)} %top_ref.3, bf16[1024,1024]{1,0:T(8,128)(2,1)} %get-tuple-element.93.right_ref), custom_call_target="tpu_custom_call" | custom-call | flops 5000000000 | tf_op jit(solution)/shard_map/weight_grad/pallas_call | solution.py:1415
  221.7 13.3 %mixer_backward.1 = (f32[1024,1024]{1,0:T(8,128)}, bf16[1024,1024]{1,0:T(8,128)(2,1)}, f32[1024,768]{1,0:T(8,128)}, bf16[1024,256]{1,0:T(8,128)(2,1)}, f32[8,1024]{1,0:T(8,128)}, /*index=5*/f32[8,1024]{1,0:T(8,128)}) custom-call(bf16[1024,1024]{1,0:T(8,128)(2,1)} %get-tuple-element.90.part_ref, bf16[1024,1024]{1,0:T(8,128)(2,1)} %copy-done.29, ...), custom_call_target="tpu_custom_call" | custom-call | flops 8000000000 | tf_op jit(solution)/shard_map/mixer_backward/pallas_call | solution.py:1386
  235.1 1.6 collective-permute-start.4
  237.1 16.2 %attend_backward.1.dqkv_ref = bf16[1024,384]{1,0:T(8,128)(2,1)} custom-call(bf16[1024,512]{1,0:T(8,128)(2,1)} %get-tuple-element.103.qkv_ref, f32[8,1024]{1,0:T(8,128)} %get-tuple-element.104.lse_ref, bf16[1024,256]{1,0:T(8,128)(2,1)} %get-tuple-element.79.attended_ref.o_ref, bf16[1024,256]{1,0:T(8,128)(2,1)} %get-tuple-element.105.do_ref, ...), custom_call_target="tpu_custom_call" | custom-call | flops 16000000000 | tf_op jit(solution)/shard_map/attend_backward/pallas_call | solution.py:1236
  253.3 8.1 %weight_grad.3.refs_0_ = bf16[1024,1024]{1,0:T(8,128)(2,1)} custom-call(bf16[1024,1024]{1,0:T(8,128)(2,1)} %get-tuple-element.106.left_ref, bf16[1024,1024]{1,0:T(8,128)(2,1)} %get-tuple-element.107.right_ref), custom_call_target="tpu_custom_call" | custom-call | flops 5000000000 | tf_op jit(solution)/shard_map/weight_grad/pallas_call | solution.py:1415
  262.1 38.5 %scan_backward.1 = (bf16[1024,2304]{1,0:T(8,128)(2,1)}, f32[8,768]{1,0:T(8,128)}, f32[8,256]{1,0:T(8,128)}, f32[8,128]{1,0:T(8,128)}, f32[64,768]{1,0:T(8,128)}, /*index=5*/f32[64,256]{1,0:T(8,128)}, f32[64,1024]{1,0:T(8,128)}) custom-call(f32[1024,2304]{1,0:T(8,128)} %fusion.6.z_ref.x_ref.bc_ref.step_ref.q_ref.kv_ref.xp_ref.bp_ref, ...), custom_call_target="tpu_custom_call" | custom-call | flops 46999998464 | tf_op jit(solution)/shard_map/scan_backward/pallas_call | solution.py:920
  301.2 9.5 %convolution_convert_fusion.part_ref = bf16[1024,1024]{1,0:T(8,128)(2,1)} fusion(bf16[1024,2304]{1,0:T(8,128)(2,1)} %get-tuple-element.114.right_ref, bf16[1024,2304]{1,0:T(8,128)(2,1)} %gather_rows.2), kind=kOutput, calls=%fused_computation.7 | convolution fusion | flops 4832886784 | bytes 11534336 | tf_op jit(solution)/shard_map/dot_general | solution.py:39
  310.8 2.4 fusion.3
  313.7 3.2 collective-permute-done.5
  318.9 45.8 %scatter_product.3 = (f32[64,2,768]{2,1,0:T(2,128)}, f32[64,256]{1,0:T(8,128)}, f32[64,1,384]{2,1,0:T(1,128)}, f32[12,64]{1,0:T(8,128)}, f32[72,128]{1,0:T(8,128)}) custom-call(bf16[1024,1024]{1,0:T(8,128)(2,1)} %copy-done.2, bf16[1024,2304]{1,0:T(8,128)(2,1)} %get-tuple-element.114.right_ref, f32[72,128]{1,0:T(8,128)} %select_maximum_fusion.refs_0_), custom_call_target="tpu_custom_call" | custom-call | flops 3000000000 | tf_op jit(solution)/shard_map/scatter_product/pallas_call | solution.py:535
  371.8 1.4 copy-done.28
  374.3 11.3 %finish_layer.1 = (f32[1024,1024]{1,0:T(8,128)}, bf16[1024,1024]{1,0:T(8,128)(2,1)}) custom-call(bf16[1024,1024]{1,0:T(8,128)(2,1)} %x_ref.3, f32[1,1024]{1,0:T(1,128)} %bitcast.64, bf16[1024,1024]{1,0:T(8,128)(2,1)} %convolution_convert_fusion.part_ref, bf16[1024,1024]{1,0:T(8,128)(2,1)} %copy-done.28, f32[1024,1024]{1,0:T(8,128)} %get-tuple-element.121.grad_ref, ...), custom_call_target="tpu_custom_call" | custom-call | flops 8000000000 | tf_op jit(solution)/shard_map/finish_layer/pallas_call | solution.py:1443
  (129 shorter events, 34.2 us)
Async XLA Ops:
  5.6 38.9 %copy-start = (bf16[1024,1024]{1,0:T(8,128)(2,1)S(1)}, bf16[1024,1024]{1,0:T(8,128)(2,1)}, u32[]{:S(2)}) copy-start(bf16[1024,1024]{1,0:T(8,128)(2,1)} %x_ref.3) | copy-start | bytes 6291460
  46.8 11.1 %copy-start.33 = (bf16[12]{0:T(256)(128)(2,1)S(1)}, bf16[12]{0:T(256)(128)(2,1)}, u32[]{:S(2)}) copy-start(bf16[12]{0:T(256)(128)(2,1)} %param.33) | copy-start | bytes 76
  46.8 11.6 %copy-start.9 = (bf16[768,64]{0,1:T(8,128)(2,1)S(1)}, bf16[768,64]{0,1:T(8,128)(2,1)}, u32[]{:S(2)}) copy-start(bf16[768,64]{0,1:T(8,128)(2,1)} %param.37) | copy-start | bytes 294916
  46.8 11.6 %copy-start.16 = (bf16[1,256,64]{1,2,0:T(8,128)(2,1)S(1)}, bf16[1,256,64]{1,2,0:T(8,128)(2,1)}, u32[]{:S(2)}) copy-start(bf16[1,256,64]{1,2,0:T(8,128)(2,1)} %param.39) | copy-start | bytes 98308
  81.1 14.1 %copy-start.24 = (bf16[768]{0:T(1024)(128)(2,1)S(1)}, bf16[768]{0:T(1024)(128)(2,1)}, u32[]{:S(2)}) copy-start(bf16[768]{0:T(1024)(128)(2,1)} %param.36) | copy-start | bytes 4612
  81.1 14.7 %copy-start.5 = (bf16[64,2,1024]{2,1,0:T(2,128)(2,1)S(1)}, bf16[64,2,1024]{2,1,0:T(2,128)(2,1)}, u32[]{:S(2)}) copy-start(bf16[64,2,1024]{2,1,0:T(2,128)(2,1)} %param.41) | copy-start | bytes 786436
  81.1 15.4 %copy-start.15 = (f32[8,1024]{1,0:T(8,128)S(1)}, f32[8,1024]{1,0:T(8,128)}, u32[]{:S(2)}) copy-start(f32[8,1024]{1,0:T(8,128)} %get-tuple-element.78) | copy-start | bytes 98308
  81.1 15.4 %collective-permute-start = (f32[8,1024]{1,0:T(8,128)}, f32[8,1024]{1,0:T(8,128)S(1)}, u32[]{:S(2)}, u32[]{:S(2)}) collective-permute-start(f32[8,1024]{1,0:T(8,128)} %get-tuple-element.78), channel_id=1, source_target_pairs={{0,1},{1,0},{2,3},{3,2},{4,5},{5,4},{6,7},{7,6},{8,9},{9,8},{10,11... | collective-permute-start | bytes 98312 | tf_op jit(solution)/shard_map/ppermute | solution.py:1458
  104.2 47.8 %collective-permute-start.1 = (bf16[1024,1024]{1,0:T(8,128)(2,1)}, bf16[1024,1024]{1,0:T(8,128)(2,1)S(1)}, u32[]{:S(2)}, u32[]{:S(2)}) collective-permute-start(bf16[1024,1024]{1,0:T(8,128)(2,1)} %get-tuple-element.82.mixed_ref), channel_id=1, source_target_pairs={{0,1},{1,0},{2,3},{3,2},{4,5},{5,4},{6,7},{7,6},{8,9},{9,8},{10,11... | collective-permute-start | bytes 6291464 | tf_op jit(solution)/shard_map/ppermute | solution.py:1458
  173.3 47.1 %collective-permute-start.2 = (bf16[1024,1024]{1,0:T(8,128)(2,1)}, bf16[1024,1024]{1,0:T(8,128)(2,1)S(1)}, u32[]{:S(2)}, u32[]{:S(2)}) collective-permute-start(bf16[1024,1024]{1,0:T(8,128)(2,1)} %get-tuple-element.90.part_ref), channel_id=1, source_target_pairs={{0,1},{1,0},{2,3},{3,2},{4,5},{5,4},{6,7},{7,6},{8,9},{9,8},{10,11... | collective-permute-start | bytes 6291464 | tf_op jit(solution)/shard_map/ppermute | solution.py:1458
  221.7 14.9 %copy-start.27 = (bf16[1024,1024]{1,0:T(8,128)(2,1)S(1)}, bf16[1024,1024]{1,0:T(8,128)(2,1)}, u32[]{:S(2)}) copy-start(bf16[1024,1024]{1,0:T(8,128)(2,1)} %get-tuple-element.95.ffn_ref) | copy-start | bytes 6291460
  235.1 26.4 %collective-permute-start.4 = (f32[8,1024]{1,0:T(8,128)}, f32[8,1024]{1,0:T(8,128)S(1)}, u32[]{:S(2)}, u32[]{:S(2)}) collective-permute-start(f32[8,1024]{1,0:T(8,128)} %get-tuple-element.102), channel_id=1, source_target_pairs={{0,1},{1,0},{2,3},{3,2},{4,5},{5,4},{6,7},{7,6},{8,9},{9,8},{10,11... | collective-permute-start | bytes 98312 | tf_op jit(solution)/shard_map/ppermute | solution.py:1458
  236.6 64.6 %collective-permute-start.3 = (bf16[1024,1024]{1,0:T(8,128)(2,1)S(1)}, bf16[1024,1024]{1,0:T(8,128)(2,1)}, u32[]{:S(2)}, u32[]{:S(2)}) collective-permute-start(bf16[1024,1024]{1,0:T(8,128)(2,1)S(1)} %copy-done.27), channel_id=1, source_target_pairs={{0,1},{1,0},{2,3},{3,2},{4,5},{5,4},{6,7},{7,6},{8,9},{9,8},{10,11... | collective-permute-start | bytes 6291464 | tf_op jit(solution)/shard_map/ppermute | solution.py:1458
  313.2 3.8 collective-permute-start.5
  317.0 54.8 %collective-permute-start.6 = (bf16[1024,1024]{1,0:T(8,128)(2,1)}, bf16[1024,1024]{1,0:T(8,128)(2,1)S(1)}, u32[]{:S(2)}, u32[]{:S(2)}) collective-permute-start(bf16[1024,1024]{1,0:T(8,128)(2,1)} %convolution_convert_fusion.part_ref), channel_id=1, source_target_pairs={{0,1},{1,0},{2,3},{3,2},{4,5},{5,4},{6,7},{7,6},{8,9},{9,8},{10,11... | collective-permute-start | bytes 6291464 | tf_op jit(solution)/shard_map/ppermute | solution.py:1458
  373.1 12.5 %collective-permute-start.7 = (f32[64,256]{1,0:T(8,128)}, f32[64,256]{1,0:T(8,128)S(1)}, u32[]{:S(2)}, u32[]{:S(2)}) collective-permute-start(f32[64,256]{1,0:T(8,128)} %get-tuple-element.127), channel_id=1, source_target_pairs={{0,1},{1,0},{2,3},{3,2},{4,5},{5,4},{6,7},{7,6},{8,9},{9,8},{10,11... | collective-permute-start | bytes 196616 | tf_op jit(solution)/shard_map/ppermute | solution.py:1458
  374.3 11.3 %copy-start.18 = (f32[64,256]{1,0:T(8,128)S(1)}, f32[64,256]{1,0:T(8,128)}, u32[]{:S(2)}) copy-start(f32[64,256]{1,0:T(8,128)} %get-tuple-element.127) | copy-start | bytes 196612
  374.3 12.0 %copy-start.4 = (f32[64,2,768]{2,1,0:T(2,128)S(1)}, f32[64,2,768]{2,1,0:T(2,128)}, u32[]{:S(2)}) copy-start(f32[64,2,768]{2,1,0:T(2,128)} %get-tuple-element.166) | copy-start | bytes 1179652
  374.3 12.7 %copy-start.20 = (f32[12,64]{1,0:T(8,128)S(1)}, f32[12,64]{1,0:T(8,128)}, u32[]{:S(2)}) copy-start(f32[12,64]{1,0:T(8,128)} %get-tuple-element.128) | copy-start | bytes 9220
  374.3 13.3 %copy-start.7 = (f32[64,768]{1,0:T(8,128)S(1)}, f32[64,768]{1,0:T(8,128)}, u32[]{:S(2)}) copy-start(f32[64,768]{1,0:T(8,128)} %get-tuple-element.129) | copy-start | bytes 589828
  374.3 14.0 %copy-start.8 = (f32[64,1,384]{2,1,0:T(1,128)S(1)}, f32[64,1,384]{2,1,0:T(1,128)}, u32[]{:S(2)}) copy-start(f32[64,1,384]{2,1,0:T(1,128)} %get-tuple-element.178) | copy-start | bytes 294916
  374.3 14.6 %copy-start.10 = (f32[64,256]{1,0:T(8,128)S(1)}, f32[64,256]{1,0:T(8,128)}, u32[]{:S(2)}) copy-start(f32[64,256]{1,0:T(8,128)} %get-tuple-element.131) | copy-start | bytes 196612
  374.3 15.3 %copy-start.3 = (f32[64,2,1024]{2,1,0:T(2,128)S(1)}, f32[64,2,1024]{2,1,0:T(2,128)}, u32[]{:S(2)}) copy-start(f32[64,2,1024]{2,1,0:T(2,128)} %scatter_product.2) | copy-start | bytes 1572868
  374.3 16.1 %copy-start.6 = (f32[64,1024]{1,0:T(8,128)S(1)}, f32[64,1024]{1,0:T(8,128)}, u32[]{:S(2)}) copy-start(f32[64,1024]{1,0:T(8,128)} %get-tuple-element.133) | copy-start | bytes 786436
  (18 other events, 111.4 us)
where the time goes:
time: 393 us; the launch traced here: 391 us
  Pallas kernels  317 us (81%)
  local copies, waits for them, and re-layouts  26.9 us (7%)
  matrix products  16.9 us (4%)
  waiting for transfers between devices  11.7 us (3%)
  other arithmetic  10.9 us (3%)
  starting transfers between devices  6.97 us (2%)
    pallas_call x2, Pallas kernels, scatter_product(): pl.pallas_call(functools.partial(product_kernel, devices, windows, pieces...  84.1 us
    pallas_call x2, Pallas kernels, gather_rows(): pl.pallas_call(functools.partial(gather_kernel, devices, count), out_shap...  75.6 us
    pallas_call x1, Pallas kernels, run_scan_backward(): pl.pallas_call(functools.partial(scan_backward, devices, spans, windows,...  38.5 us
    pallas_call x1, Pallas kernels, run_scan_forward(): pl.pallas_call(functools.partial(scan_forward, devices, spans), grid=(spa...  22 us
    pallas_call x1, Pallas kernels, run_feed_forward(): pl.pallas_call(feed_forward, grid=(tokens // TBLK,), out_shape=(shape((to...  20 us
    dot_general x2, matrix products, dot(): lax.dot_general(left, right, (dims, ((), ())), preferred_element_type=F32...  16.9 us
    pallas_call x2, Pallas kernels, run_weight_grad(): pl.pallas_call(weight_grad, grid=(rows // LANES,), out_shape=jax.ShapeDty...  16.3 us
    pallas_call x1, Pallas kernels, run_attend_backward(): pl.pallas_call(attend_backward, grid=(1,), out_shape=jax.ShapeDtypeStruct...  16.2 us
  transfers between devices with their start and end apart: 8, of which 2 were waited for; matrix products, arithmetic and copies ran while one was open for 3% of the time, Pallas kernels for 56%

commit v1 on v0

--- a/solution.py
+++ b/solution.py
@@ -583,19 +583,19 @@
     return jnp.maximum(raw, 0.0) + jnp.log1p(jnp.exp(-jnp.abs(raw)))
 
 
-def conv_window(buffer, taps_ref, bias_ref, span):
-    total = bias_ref[...] + taps_ref[0:1, :] * buffer[EDGE - 3 : EDGE - 3 + span, :]
+def conv_window(buffer, taps_ref, bias, span):
+    total = bias + taps_ref[0:1, :] * buffer[EDGE - 3 : EDGE - 3 + span, :]
     for tap in range(1, KCONV):
         start = EDGE - 3 + tap
         total = total + taps_ref[tap : tap + 1, :] * buffer[start : start + span, :]
     return total
 
 
-def span_rates(step_ref, bias_ref, decay_ref, spread, span):
-    raw = step_ref[...] + bias_ref[...]
+def span_rates(step_ref, bias, decay, spread, span):
+    raw = step_ref[...] + bias
     step = soft_step(raw)
     lower = (iota((span, span), 1) <= iota((span, span), 0)).astype(BF16)
-    cum = pick_left(lower, step * decay_ref[...], 3)
+    cum = pick_left(lower, step * decay, 3)
     tails = jnp.exp(cum[span - 1 : span, :] - cum)
     wide = pick(jnp.concatenate([step, tails, jnp.exp(cum)], axis=0), spread)
     return raw, step, cum, wide[:span], wide[span : 2 * span], wide[2 * span :]
@@ -619,7 +619,7 @@
 def scan_forward(
     devices, spans,
     z_ref, x_ref, bc_ref, step_ref,
-    tap_ref, bias_ref, tapb_ref, biasb_ref, stepb_ref, decay_ref, skip_ref, shard_ref,
+    tap_ref, tapb_ref, row_ref, shard_ref,
     y_ref, gated_ref, square_ref, enter_ref, all_ref,
     state, xbuf, bbuf, *sems,
 ):
@@ -643,12 +643,11 @@
     bbuf[:EDGE, :] = bbuf[span:, :]
     xbuf[EDGE:, :] = x_ref[...]
     bbuf[EDGE:, :] = bc_ref[...]
-    inputs = jax.nn.silu(conv_window(xbuf, tap_ref, bias_ref, span))
-    shared = jax.nn.silu(conv_window(bbuf, tapb_ref, biasb_ref, span))
     spread = head_spread(channels)
-    raw, step, cum, step_w, tails_w, grown_w = span_rates(
-        step_ref, stepb_ref, decay_ref, spread, span
-    )
+    bias, gain, biasb, stepb, decay, skip = unpack_rows(row_ref, spread)
+    inputs = jax.nn.silu(conv_window(xbuf, tap_ref, bias, span))
+    shared = jax.nn.silu(conv_window(bbuf, tapb_ref, biasb, span))
+    raw, step, cum, step_w, tails_w, grown_w = span_rates(step_ref, stepb, decay, spread, span)
     cum_rows = cum.T
     b_low = shared[:, :NS].astype(BF16)
     c_low = shared[:, NS:].astype(BF16)
@@ -668,7 +667,7 @@
             [(cross * first).astype(BF16), (cross * second).astype(BF16)], axis=1
         )
         y_ref[:, lanes] = dot(weights, pair_split(scaled_low[:, lanes], low_lanes))
-    y = y_ref[...] + outer + skip_ref[...] * inputs
+    y = y_ref[...] + outer + skip * inputs
     y_ref[...] = y
     gated = y * jax.nn.silu(z_ref[...])
     gated_ref[...] = gated
@@ -686,7 +685,7 @@
     devices, spans, windows, pieces, outs_count, count,
     z_ref, x_ref, xp_ref, bc_ref, bp_ref, step_ref, y_ref, enter_ref,
     dyg_ref, scale_ref, inner_ref, dqkv_ref,
-    tap_ref, bias_ref, tapb_ref, biasb_ref, stepb_ref, decay_ref, skip_ref, gain_ref,
+    tap_ref, tapb_ref, row_ref,
     *refs,
 ):
     sent, refs = refs[:count], refs[count:]
@@ -714,18 +713,17 @@
     bbuf[:EDGE, :] = bp_ref[...] * inside
     xbuf[EDGE:, :] = x_ref[...]
     bbuf[EDGE:, :] = bc_ref[...]
-    conv = conv_window(xbuf, tap_ref, bias_ref, span)
+    spread = head_spread(channels)
+    bias, gain, biasb, stepb, decay, skip = unpack_rows(row_ref, spread)
+    conv = conv_window(xbuf, tap_ref, bias, span)
     sig = jax.nn.sigmoid(conv)
     inputs = conv * sig
-    convb = conv_window(bbuf, tapb_ref, biasb_ref, span)
+    convb = conv_window(bbuf, tapb_ref, biasb, span)
     sigb = jax.nn.sigmoid(convb)
     shared = convb * sigb
     b_low = shared[:, :NS].astype(BF16)
     c_low = shared[:, NS:].astype(BF16)
-    spread = head_spread(channels)
-    raw, step, cum, step_w, tails_w, grown_w = span_rates(
-        step_ref, stepb_ref, decay_ref, spread, span
-    )
+    raw, step, cum, step_w, tails_w, grown_w = span_rates(step_ref, stepb, decay, spread, span)
     cum_rows = cum.T
     scaled = inputs * step_w
     scaled_low = scaled.astype(BF16)
@@ -738,7 +736,7 @@
     normed = y * swish * scale
     dyg = dyg_ref[...]
     gain_grad = jnp.sum(dyg * normed, axis=0, keepdims=True)
-    dgated = scale * (dyg * gain_ref[...] - normed * inner_ref[...].T[:, :1])
+    dgated = scale * (dyg * gain - normed * inner_ref[...].T[:, :1])
     dy = dgated * swish
     grad_ref[:, :channels] = (dgated * y * (sig_z * (1.0 + z * (1.0 - sig_z)))).astype(BF16)
 
@@ -799,13 +797,13 @@
     dcum = sums[:span] + row_part - col_buf[...].T
     upper = (iota((span, span), 1) >= iota((span, span), 0)).astype(BF16)
     drate = pick_left(upper, dcum, 3) + at_end
-    dstep = drate * decay_ref[...] + sums[span : 2 * span]
+    dstep = drate * decay + sums[span : 2 * span]
     draw = dstep * jax.nn.sigmoid(raw)
     gh_ref[0:1, :] += jnp.sum(draw, axis=0, keepdims=True)
-    gh_ref[1:2, :] += jnp.sum(drate * step, axis=0, keepdims=True) * decay_ref[...]
+    gh_ref[1:2, :] += jnp.sum(drate * step, axis=0, keepdims=True) * decay
     gh_ref[2:3, :] += sums[2 * span + 1 : 2 * span + 2, :]
 
-    dinputs = du * step_w + skip_ref[...] * dy
+    dinputs = du * step_w + skip * dy
     dxbuf[span:, :] = dxbuf[:EDGE, :]
     dbbuf[span:, :] = dbbuf[:EDGE, :]
     dconv = dinputs * (sig * (1.0 + conv * (1.0 - sig)))
@@ -838,21 +836,34 @@
     pl.when(turn == spans - 1)(ring.finish)
 
 
-def scan_params(conv_x, conv_xb, conv_bc, conv_bcb, dt_bias, a_log, d_skip):
+def scan_params(conv_x, conv_xb, conv_bc, conv_bcb, dt_bias, a_log, d_skip, w_mnorm):
     heads = dt_bias.shape[0]
-
-    def wide(row):
-        return jnp.pad(row, (0, LANES - heads))[None, :]
-
-    f32 = lambda value: value.astype(F32)
+    fill = jnp.zeros((LANES - heads,), BF16)
+    flat = [conv_xb, w_mnorm, conv_bcb, dt_bias, fill, a_log, fill, d_skip, fill]
+    size = sum(item.shape[0] for item in flat) // LANES
+    flat.append(jnp.zeros((-size % EDGE * LANES,), BF16))
+    rows = jnp.concatenate(flat).astype(F32).reshape(-1, LANES)
+    return (conv_x.astype(F32), conv_bc.astype(F32), rows)
+
+
+def unpack_rows(row_ref, spread):
+    channels = spread.shape[1]
+    count = channels // LANES
+    at = 2 * count + 2 * NS // LANES
+
+    def join_rows(first, number):
+        return jnp.concatenate(
+            [row_ref[i : i + 1, :] for i in range(first, first + number)], axis=1
+        )
+
+    skip = jnp.broadcast_to(row_ref[at + 2 : at + 3, :], (EDGE, LANES)).astype(BF16)
     return (
-        f32(conv_x),
-        f32(conv_xb)[None, :],
-        f32(conv_bc),
-        f32(conv_bcb)[None, :],
-        wide(f32(dt_bias)),
-        wide(-jnp.exp(f32(a_log))),
-        jnp.repeat(f32(d_skip), MP)[None, :],
+        join_rows(0, count),
+        join_rows(count, count),
+        join_rows(2 * count, 2 * NS // LANES),
+        row_ref[at : at + 1, :],
+        -jnp.exp(row_ref[at + 1 : at + 2, :]),
+        dot(skip, spread)[:1],
     )
 
 
@@ -862,7 +873,7 @@
 
 def run_scan_forward(proj, qkv_width, params, shard, devices):
     tokens = proj.shape[0]
-    channels = params[1].shape[1]
+    channels = params[0].shape[1]
     step_at = (2 * channels + 2 * NS + qkv_width) // LANES
     spans = tokens // SPAN
     bc_at = 2 * channels // (2 * NS)
@@ -901,11 +912,11 @@
 
 
 def run_scan_backward(
-    proj, y, entering, dyg, scale, inner, dqkv, params, gain, sent, windows, pieces,
-    shapes, devices,
+    proj, y, entering, dyg, scale, inner, dqkv, params, sent, windows, pieces, shapes,
+    devices,
 ):
     tokens, width = proj.shape
-    channels = params[1].shape[1]
+    channels = params[0].shape[1]
     qkv_width = dqkv.shape[1]
     step_at = (2 * channels + 2 * NS + qkv_width) // LANES
     spans = tokens // SPAN
@@ -944,7 +955,6 @@
             rows(qkv_width, 0),
         ]
         + [whole_spec(item) for item in params]
-        + [whole_spec(gain)]
         + [pl.BlockSpec(memory_space=pl.ANY)] * len(sent),
         out_specs=(
             rows(width, 0),
@@ -967,8 +977,7 @@
         cost_estimate=cost(47),
         name="scan_backward",
     )(
-        proj, proj, proj, proj, proj, proj, y, entering, dyg, scale, inner, dqkv, *params, gain,
-        *sent,
+        proj, proj, proj, proj, proj, proj, y, entering, dyg, scale, inner, dqkv, *params, *sent,
     )
 
 
@@ -1405,28 +1414,17 @@
     )(part, other, after, scale, top, gain, w_out, gated, scale_m, gain_m)
 
 
-def weight_grad(left_ref, right_ref, out_ref):
-    out_ref[...] = dot(left_ref[...], right_ref[...], TN).astype(BF16)
-
-
-def run_weight_grad(left, right):
-    tokens, rows = left.shape
-    cols = right.shape[1]
-    return pl.pallas_call(
-        weight_grad,
-        grid=(rows // LANES,),
-        out_shape=jax.ShapeDtypeStruct((rows, cols), BF16),
-        in_specs=[pl.BlockSpec((tokens, LANES), lambda turn: (0, turn)), once(right)],
-        out_specs=pl.BlockSpec((LANES, cols), lambda turn: (turn, 0)),
-        cost_estimate=cost(5),
-        name="weight_grad",
-    )(left, right)
-
-
 def finish_layer(
-    x_ref, gain_ref, part_ref, other_ref, grad_ref, after_ref, ffn_ref, ffn_other_ref,
-    out_ref, result_ref,
+    x_ref, gain_ref, part_ref, other_ref, grad_ref, after_ref, ffn_ref, ffn_other_ref, *refs,
 ):
+    count = len(refs) // 2 - 1
+    passed, out_ref, result_ref, handed = refs[:count], refs[count], refs[count + 1], refs[count + 2 :]
+
+    @pl.when(pl.program_id(0) == 0)
+    def _():
+        for source, target in zip(passed, handed):
+            target[...] = source[...]
+
     x = x_ref[...].astype(F32)
     scale = lax.rsqrt(jnp.mean(x * x, axis=-1, keepdims=True) + EPSILON)
     normed = x * scale
@@ -1437,21 +1435,22 @@
     result_ref[...] = (after_ref[...] + ffn).astype(BF16)
 
 
-def run_finish(x, gain, part, other, grad, after, ffn, ffn_other):
+def run_finish(x, gain, part, other, grad, after, ffn, ffn_other, passed):
     tokens, width = x.shape
-    rows = pl.BlockSpec((NBLK, width), lambda turn: (turn, 0))
+    rows = pl.BlockSpec((TBLK, width), lambda turn: (turn, 0))
     return pl.pallas_call(
         finish_layer,
-        grid=(tokens // NBLK,),
+        grid=(tokens // TBLK,),
         out_shape=(
             jax.ShapeDtypeStruct((tokens, width), F32),
             jax.ShapeDtypeStruct((tokens, width), BF16),
-        ),
-        in_specs=[rows, once(gain)] + [rows] * 6,
-        out_specs=(rows, rows),
+        )
+        + tuple(jax.ShapeDtypeStruct(item.shape, F32) for item in passed),
+        in_specs=[rows, once(gain)] + [rows] * 6 + [once(item) for item in passed],
+        out_specs=(rows, rows) + tuple(once(item) for item in passed),
         cost_estimate=cost(8),
         name="finish_layer",
-    )(x, gain, part, other, grad, after, ffn, ffn_other)
+    )(x, gain, part, other, grad, after, ffn, ffn_other, *passed)
 
 
 def swap(partial):
@@ -1496,7 +1495,9 @@
     normed_one = source * scale_one
     hidden_one = lax.optimization_barrier((normed_one * norm1).astype(BF16))
     proj = dot(hidden_one, w_in)
-    params = scan_params(conv_x, conv_xb, conv_bc, conv_bcb, dt_bias, a_log, d_skip)
+    params = scan_params(
+        conv_x, conv_xb, conv_bc, conv_bcb, dt_bias, a_log, d_skip, w_mnorm
+    )
     out_shard = jnp.concatenate([w_mout.T, output_weight.reshape(attn_width, -1).T], axis=1)
     y, gated, square_sum, entering, w_out = run_scan_forward(
         proj, qkv_width, params, out_shard, devices
@@ -1518,7 +1519,7 @@
         layer_input, mixed, other, grad_output, norm2[None, :], w_gate_up, w_down_t
     )
     other = swap(partial_two)
-    grad_down = run_weight_grad(grad_output, activated)
+    grad_down = dot(grad_output, activated, TN).astype(BF16)
     (mine_gu,) = scatter_product(
         hidden_two,
         grad_gu_low,
@@ -1538,7 +1539,7 @@
     )
     inner_m = tensor_sum(inner_m) / channels_all
     dqkv = run_attend_backward(qkv, lse, attended, grad_attended, 0, tables)
-    grad_out = run_weight_grad(grad_mix_low, mixer_out)
+    grad_out = dot(grad_mix_low, mixer_out, TN).astype(BF16)
     windows = [(0, None, 0, channels + attn_width), (1, None, 0, units)]
     pieces = [
         (0, 0, channels, 0, None),
@@ -1547,33 +1548,28 @@
     ]
     shapes = [(shard, channels), (shard, attn_width), (shard, units)]
     grad_proj, small_x, small_b, small_h, mine_mout, mine_o, mine_down = run_scan_backward(
-        proj, y, entering, grad_mamba, scale_m, inner_m, dqkv, params, gain_m,
+        proj, y, entering, grad_mamba, scale_m, inner_m, dqkv, params,
         [grad_out, grad_down], windows, pieces, shapes, devices,
     )
     ffn_other, grad_proj = lax.optimization_barrier((ffn_other, grad_proj))
     partial_one, grad_proj = lax.optimization_barrier(
         (dot(grad_proj, w_in, NT).astype(BF16), grad_proj)
     )
-    crossing = jnp.concatenate(
-        [
-            small_b[: KCONV + 1].reshape(-1, LANES),
-            jnp.sum(partial_one.astype(F32) * normed_one, axis=0).reshape(-1, LANES),
-        ],
-        axis=0,
-    )
-    crossing = tensor_sum(crossing)
-    partial_one, crossing = lax.optimization_barrier((partial_one, crossing))
     other = swap(partial_one)
+    grad_norm1 = jnp.sum(partial_one.astype(F32) * normed_one, axis=0)
     small = jnp.concatenate(
         [
             small_x[: KCONV + 2].reshape(-1, LANES),
             small_h[:3],
-            crossing,
             grad_norm2[0].reshape(-1, LANES),
+            small_b[: KCONV + 1].reshape(-1, LANES),
+            grad_norm1.reshape(-1, LANES),
         ],
         axis=0,
     )
     small_rows = small.shape[0]
+    cross_rows = (KCONV + 1) * 2 * NS // LANES + width // LANES
+    cross_at = small_rows - cross_rows
     small = jnp.pad(small, ((0, -small_rows % EDGE), (0, 0)))
     shared_at = 2 * channels
     step_at = qkv_at + qkv_width
@@ -1599,24 +1595,30 @@
         (small,),
     )
     other, mine_bc = lax.optimization_barrier((other, mine_bc))
-    grad_source, result = run_finish(
-        layer_input, norm1[None, :], partial_one, other, grad_after, after, ffn_part, ffn_other
-    )
+    crossing = tensor_sum(small[cross_at : cross_at + cross_rows])
+    shared_cols = tensor_sum(mine_bc)
+    passed = (mine_zx, mine_qkv, mine_step, mine_mout, mine_o, mine_gu, mine_down)
+    grad_source, result, *passed = run_finish(
+        layer_input, norm1[None, :], partial_one, other, grad_after, after, ffn_part, ffn_other,
+        passed,
+    )
+    mine_zx, mine_qkv, mine_step, mine_mout, mine_o, mine_gu, mine_down = passed
 
     half = NS * 2 // lax.axis_size("tensor")
-    shared_cols = tensor_sum(mine_bc)
     begin = lax.axis_index("tensor") * half
     grad_bc = lax.dynamic_slice_in_dim(shared_cols, begin, half, 1)
-    small = small[:small_rows].reshape(-1)
-    x_size = (KCONV + 2) * channels
-    h_size = 3 * LANES
-    b_size = (KCONV + 1) * 2 * NS
-    total_x = small[:x_size].reshape(KCONV + 2, channels)
-    total_h = small[x_size : x_size + h_size].reshape(3, LANES)
-    total_b = small[x_size + h_size : x_size + h_size + b_size].reshape(KCONV + 1, 2 * NS)
+    x_rows = (KCONV + 2) * channels // LANES
+    norm_rows = width // LANES
+    total_x = small[:x_rows].reshape(KCONV + 2, channels)
+    total_h = small[x_rows : x_rows + 3]
+    norm2_total = small[x_rows + 3 : cross_at].reshape(width)
+    total_b = crossing[: cross_rows - norm_rows].reshape(KCONV + 1, 2 * NS)
     total_b = lax.dynamic_slice_in_dim(total_b, begin, half, 1)
-    norms = small[x_size + h_size + b_size :].reshape(2, width)
-    norms = lax.dynamic_slice_in_dim(norms, lax.axis_index("dp") * shard, shard, 1)
+    norm1_total = crossing[cross_rows - norm_rows :].reshape(width)
+    norms = [
+        lax.dynamic_slice_in_dim(item, lax.axis_index("dp") * shard, shard, 0)
+        for item in (norm1_total, norm2_total)
+    ]
     return (
         result,
         grad_source,

time: 393 us -> 378 us (0.962)
  Pallas kernels: 317 us -> 301 us
  matrix products: 16.9 us -> 28.1 us
  local copies, waits for them, and re-layouts: 26.9 us -> 18.4 us
    pallas_call x3 -> x1, Pallas kernels: 27.6 us -> 10.9 us  [run_finish(): pl.pallas_call(finish_layer, grid=(tokens // TBLK,), out_shape=(jax.Shape...]
    dot_general x2 -> x4, matrix products: 16.9 us -> 28.1 us  [dot(): lax.dot_general(left, right, (dims, ((), ())), preferred_element_type=F32...]
    unnamed x78 -> x57, local copies, waits for them, and re-layouts: 12.7 us -> 5.21 us
  transfers between devices with their start and end apart: 8 -> 8, of which waited for: 2 -> 2; matrix products, arithmetic and copies ran while one was open for 3% -> 7% of each run, Pallas kernels for 56% -> 54%
where the time goes in v1:
time: 378 us; the launch traced here: 377 us
  Pallas kernels  301 us (80%)
  matrix products  28.1 us (7%)
  local copies, waits for them, and re-layouts  18.4 us (5%)
  waiting for transfers between devices  10.7 us (3%)
  other arithmetic  10.5 us (3%)
  starting transfers between devices  7.33 us (2%)
    pallas_call x2, Pallas kernels, scatter_product(): pl.pallas_call(functools.partial(product_kernel, devices, windows, pieces...  85 us
    pallas_call x2, Pallas kernels, gather_rows(): pl.pallas_call(functools.partial(gather_kernel, devices, count), out_shap...  75.5 us
    pallas_call x1, Pallas kernels, run_scan_backward(): pl.pallas_call(functools.partial(scan_backward, devices, spans, windows,...  38.8 us
    dot_general x4, matrix products, dot(): lax.dot_general(left, right, (dims, ((), ())), preferred_element_type=F32...  28.1 us
    pallas_call x1, Pallas kernels, run_scan_forward(): pl.pallas_call(functools.partial(scan_forward, devices, spans), grid=(spa...  21.9 us
    pallas_call x1, Pallas kernels, run_feed_forward(): pl.pallas_call(feed_forward, grid=(tokens // TBLK,), out_shape=(shape((to...  19.9 us
    pallas_call x1, Pallas kernels, run_attend_backward(): pl.pallas_call(attend_backward, grid=(1,), out_shape=jax.ShapeDtypeStruct...  16.2 us
    pallas_call x1, Pallas kernels, run_mixer_backward(): pl.pallas_call(mixer_backward, grid=(tokens // NBLK,), out_shape=(shape((...  13.3 us
  transfers between devices with their start and end apart: 8, of which 2 were waited for; matrix products, arithmetic and copies ran while one was open for 7% of the time, Pallas kernels for 54%

profile of v1, /device:TPU:0, one launch (start us, length us, event | category | flops | bytes accessed | tf_op | source)
XLA Modules:
  0.0 377.1 jit_solution(3099759447056778751)
XLA Ops:
  3.9 1.6 concatenate.12.refs_0_
  5.6 36.8 %gather_rows.2 = bf16[1024,2304]{1,0:T(8,128)(2,1)} custom-call(bf16[64,2304]{1,0:T(8,128)(2,1)} %concatenate.12.refs_0_), custom_call_target="tpu_custom_call" | custom-call | flops 3000000000 | tf_op jit(solution)/shard_map/gather_rows/pallas_call | solution.py:198
  42.4 2.0 convert_reduce_fusion
  46.9 7.4 %fusion.5.z_ref.x_ref.bc_ref.step_ref.q_ref.kv_ref.xp_ref.bp_ref = f32[1024,2304]{1,0:T(8,128)} fusion(bf16[1024,1024]{1,0:T(8,128)(2,1)S(1)} %fusion.2.left_ref, bf16[1024,2304]{1,0:T(8,128)(2,1)S(1)} %copy-done.5), kind=kOutput, calls=%fused_computation.28 | convolution fusion | flops 4831838208 | bytes 16252928 | tf_op jit(solution)/shard_map/dot_general | solution.py:39
  57.0 21.9 %scan_forward.1 = (f32[1024,768]{1,0:T(8,128)}, f32[1024,768]{1,0:T(8,128)}, f32[8,1024]{1,0:T(8,128)}, f32[8,128,768]{2,1,0:T(8,128)}, bf16[1024,1024]{1,0:T(8,128)(2,1)}) custom-call(f32[1024,2304]{1,0:T(8,128)} %fusion.5.z_ref.x_ref.bc_ref.step_ref.q_ref.kv_ref.xp_ref.bp_ref, f32[1024,2304]{1,0:T(8,128)} %fusion.5.z_ref.x_ref.bc_ref.step_ref.q_ref.kv_ref.xp_ref.bp_ref, ...), custom_call_target="tpu_custom_call" | custom-call | flops 20000000000 | tf_op jit(solution)/shard_map/scan_forward/pallas_call | solution.py:882
  78.9 1.6 collective-permute-start
  80.5 12.5 %attend_forward.1 = (bf16[1024,512]{1,0:T(8,128)(2,1)}, f32[8,1024]{1,0:T(8,128)}, bf16[1024,256]{1,0:T(8,128)(2,1)}) custom-call(f32[1024,2304]{1,0:T(8,128)} %fusion.5.z_ref.x_ref.bc_ref.step_ref.q_ref.kv_ref.xp_ref.bp_ref, f32[1024,2304]{1,0:T(8,128)} %fusion.5.z_ref.x_ref.bc_ref.step_ref.q_ref.kv_ref.xp_ref.bp_ref, f32[32,128]{1,0:T(8,128)} %constant.43.clone.fine_cos, ...), custom_call_target="tpu_custom_call" | custom-call | flops 15000000512 | tf_op jit(solution)/shard_map/attend_forward/pallas_call | solution.py:1213
  94.9 7.0 %mixer_forward.1 = (bf16[1024,1024]{1,0:T(8,128)(2,1)}, bf16[1024,1024]{1,0:T(8,128)(2,1)}) custom-call(f32[1024,768]{1,0:T(8,128)} %get-tuple-element.82.gated_ref, f32[8,1024]{1,0:T(8,128)} %add_rsqrt_fusion.scale_ref.scale_m_ref, f32[1,768]{1,0:T(1,128)} %reshape.132.gain_ref.gain_m_ref, bf16[1024,256]{1,0:T(8,128)(2,1)} %get-tuple-element.84.attended_ref.o_ref, ...), custom_call_target="tpu_custom_call" | custom-call | flops 5000000000 | tf_op jit(solution)/shard_map/mixer_forward/pallas_call | solution.py:1341
  102.5 38.6 %gather_rows.3 = (bf16[1024,2048]{1,0:T(8,128)(2,1)}, bf16[1024,1024]{1,0:T(8,128)(2,1)}) custom-call(bf16[64,2048]{1,0:T(8,128)(2,1)} %bitcast.55, bf16[64,1024]{1,0:T(8,128)(2,1)} %bitcast.69), custom_call_target="tpu_custom_call" | custom-call | flops 3000000000 | tf_op jit(solution)/shard_map/gather_rows/pallas_call | solution.py:198
  141.1 8.6 %collective-permute-done.1.other_ref = bf16[1024,1024]{1,0:T(8,128)(2,1)S(1)} collective-permute-done((bf16[1024,1024]{1,0:T(8,128)(2,1)}, bf16[1024,1024]{1,0:T(8,128)(2,1)S(1)}, u32[]{:S(2)}, u32[]{:S(2)}) %collective-permute-start.1) | collective-permute-done | bytes 2097184 | tf_op jit(solution)/shard_map/ppermute | solution.py:1457
  151.1 19.9 %feed_forward.1 = (f32[1024,1024]{1,0:T(8,128)}, f32[1024,1]{1,0:T(8,128)}, bf16[1024,1024]{1,0:T(8,128)(2,1)}, bf16[1024,1024]{1,0:T(8,128)(2,1)}, bf16[1024,20...) custom-call(bf16[1024,1024]{1,0:T(8,128)(2,1)} %x_ref.3, ...), custom_call_target="tpu_custom_call" | custom-call | flops 20000000000 | tf_op jit(solution)/shard_map/feed_forward/pallas_call | solution.py:1307
  171.6 39.3 %scatter_product.2.refs_5_ = f32[64,2,1024]{2,1,0:T(2,128)} custom-call(bf16[1024,1024]{1,0:T(8,128)(2,1)} %get-tuple-element.96.left_ref, bf16[1024,2048]{1,0:T(8,128)(2,1)} %get-tuple-element.97.right_ref), custom_call_target="tpu_custom_call" | custom-call | flops 3000000000 | tf_op jit(solution)/shard_map/scatter_product/pallas_call | solution.py:535
  210.9 5.3 %convert_bitcast_fusion.refs_1_ = bf16[1024,1024]{1,0:T(8,128)(2,1)} fusion(bf16[1024,1024]{1,0:T(8,128)(2,1)} %get-tuple-element.98, bf16[1024,1024]{1,0:T(8,128)(2,1)S(1)} %copy-done.24), kind=kOutput, calls=%fused_computation.7 | convolution fusion | flops 2148532224 | bytes 6291456 | tf_op jit(solution)/shard_map/dot_general | solution.py:39
  216.1 2.0 collective-permute-done.2.other_ref
  218.2 13.3 %mixer_backward.1 = (f32[1024,1024]{1,0:T(8,128)}, bf16[1024,1024]{1,0:T(8,128)(2,1)}, f32[1024,768]{1,0:T(8,128)}, bf16[1024,256]{1,0:T(8,128)(2,1)}, f32[8,1024]{1,0:T(8,128)}, /*index=5*/f32[8,1024]{1,0:T(8,128)}) custom-call(bf16[1024,1024]{1,0:T(8,128)(2,1)} %get-tuple-element.95.part_ref, bf16[1024,1024]{1,0:T(8,128)(2,1)} %collective-permute-done.2.other_ref, ...), custom_call_target="tpu_custom_call" | custom-call | flops 8000000000 | tf_op jit(solution)/shard_map/mixer_backward/pallas_call | solution.py:1395
  232.1 1.5 collective-permute-start.3
  233.6 16.2 %attend_backward.1.dqkv_ref = bf16[1024,384]{1,0:T(8,128)(2,1)} custom-call(bf16[1024,512]{1,0:T(8,128)(2,1)} %get-tuple-element.108.qkv_ref, f32[8,1024]{1,0:T(8,128)} %get-tuple-element.109.lse_ref, bf16[1024,256]{1,0:T(8,128)(2,1)} %get-tuple-element.84.attended_ref.o_ref, bf16[1024,256]{1,0:T(8,128)(2,1)} %get-tuple-element.110.do_ref, ...), custom_call_target="tpu_custom_call" | custom-call | flops 16000000000 | tf_op jit(solution)/shard_map/attend_backward/pallas_call | solution.py:1245
  249.8 6.0 %convolution_convert_fusion.1.refs_0_ = bf16[1024,1024]{1,0:T(8,128)(2,1)} fusion(bf16[1024,1024]{1,0:T(8,128)(2,1)} %get-tuple-element.111, bf16[1024,1024]{1,0:T(8,128)(2,1)} %get-tuple-element.112), kind=kOutput, calls=%fused_computation.9 | convolution fusion | flops 2148532224 | bytes 6291456 | tf_op jit(solution)/shard_map/dot_general | solution.py:39
  256.3 38.8 %scan_backward.1 = (bf16[1024,2304]{1,0:T(8,128)(2,1)}, f32[8,768]{1,0:T(8,128)}, f32[8,256]{1,0:T(8,128)}, f32[8,128]{1,0:T(8,128)}, f32[64,768]{1,0:T(8,128)}, /*index=5*/f32[64,256]{1,0:T(8,128)}, f32[64,1024]{1,0:T(8,128)}) custom-call(f32[1024,2304]{1,0:T(8,128)} %fusion.5.z_ref.x_ref.bc_ref.step_ref.q_ref.kv_ref.xp_ref.bp_ref, ...), custom_call_target="tpu_custom_call" | custom-call | flops 46999998464 | tf_op jit(solution)/shard_map/scan_backward/pallas_call | solution.py:931
  295.2 9.5 %convolution_convert_fusion.part_ref = bf16[1024,1024]{1,0:T(8,128)(2,1)} fusion(bf16[1024,2304]{1,0:T(8,128)(2,1)} %get-tuple-element.117.right_ref, bf16[1024,2304]{1,0:T(8,128)(2,1)} %gather_rows.2), kind=kOutput, calls=%fused_computation.8 | convolution fusion | flops 4832886784 | bytes 11534336 | tf_op jit(solution)/shard_map/dot_general | solution.py:39
  306.1 2.3 fusion.3
  309.3 45.7 %scatter_product.3 = (f32[64,2,768]{2,1,0:T(2,128)}, f32[64,256]{1,0:T(8,128)}, f32[64,1,384]{2,1,0:T(1,128)}, f32[12,64]{1,0:T(8,128)}, f32[72,128]{1,0:T(8,128)}) custom-call(bf16[1024,1024]{1,0:T(8,128)(2,1)} %copy-done.2, bf16[1024,2304]{1,0:T(8,128)(2,1)} %get-tuple-element.117.right_ref, f32[72,128]{1,0:T(8,128)} %pad.4.refs_0_), custom_call_target="tpu_custom_call" | custom-call | flops 3000000000 | tf_op jit(solution)/shard_map/scatter_product/pallas_call | solution.py:535
  355.8 1.5 collective-permute-start.6
  365.5 10.9 %finish_layer.1 = (f32[1024,1024]{1,0:T(8,128)}, bf16[1024,1024]{1,0:T(8,128)(2,1)}, f32[64,2,768]{2,1,0:T(2,128)}, f32[64,1,384]{2,1,0:T(1,128)}, f32[12,64]{1,...) custom-call(bf16[1024,1024]{1,0:T(8,128)(2,1)} %x_ref.3, ...), custom_call_target="tpu_custom_call" | custom-call | flops 8000000000 | tf_op jit(solution)/shard_map/finish_layer/pallas_call | solution.py:1441
  (106 shorter events, 25.7 us)
Async XLA Ops:
  5.6 38.9 %copy-start = (bf16[1024,1024]{1,0:T(8,128)(2,1)S(1)}, bf16[1024,1024]{1,0:T(8,128)(2,1)}, u32[]{:S(2)}) copy-start(bf16[1024,1024]{1,0:T(8,128)(2,1)} %x_ref.3) | copy-start | bytes 6291460
  46.8 7.6 %copy-start.21 = (bf16[12]{0:T(256)(128)(2,1)S(1)}, bf16[12]{0:T(256)(128)(2,1)}, u32[]{:S(2)}) copy-start(bf16[12]{0:T(256)(128)(2,1)} %param.33) | copy-start | bytes 76
  46.8 8.3 %copy-start.16 = (bf16[4,768]{1,0:T(4,128)(2,1)S(1)}, bf16[4,768]{1,0:T(4,128)(2,1)}, u32[]{:S(2)}) copy-start(bf16[4,768]{1,0:T(4,128)(2,1)} %param.29) | copy-start | bytes 18436
  46.9 8.8 %copy-start.17 = (bf16[4,256]{1,0:T(4,128)(2,1)S(1)}, bf16[4,256]{1,0:T(4,128)(2,1)}, u32[]{:S(2)}) copy-start(bf16[4,256]{1,0:T(4,128)(2,1)} %param.31) | copy-start | bytes 6148
  46.9 9.4 %copy-start.4 = (bf16[768,64]{0,1:T(8,128)(2,1)S(1)}, bf16[768,64]{0,1:T(8,128)(2,1)}, u32[]{:S(2)}) copy-start(bf16[768,64]{0,1:T(8,128)(2,1)} %param.37) | copy-start | bytes 294916
  46.9 9.4 %copy-start.10 = (bf16[1,256,64]{1,2,0:T(8,128)(2,1)S(1)}, bf16[1,256,64]{1,2,0:T(8,128)(2,1)}, u32[]{:S(2)}) copy-start(bf16[1,256,64]{1,2,0:T(8,128)(2,1)} %param.39) | copy-start | bytes 98308
  78.9 14.7 %copy-start.3 = (bf16[64,2,1024]{2,1,0:T(2,128)(2,1)S(1)}, bf16[64,2,1024]{2,1,0:T(2,128)(2,1)}, u32[]{:S(2)}) copy-start(bf16[64,2,1024]{2,1,0:T(2,128)(2,1)} %param.41) | copy-start | bytes 786436
  78.9 15.4 %copy-start.9 = (f32[8,1024]{1,0:T(8,128)S(1)}, f32[8,1024]{1,0:T(8,128)}, u32[]{:S(2)}) copy-start(f32[8,1024]{1,0:T(8,128)} %get-tuple-element.83) | copy-start | bytes 98308
  78.9 15.4 %collective-permute-start = (f32[8,1024]{1,0:T(8,128)}, f32[8,1024]{1,0:T(8,128)S(1)}, u32[]{:S(2)}, u32[]{:S(2)}) collective-permute-start(f32[8,1024]{1,0:T(8,128)} %get-tuple-element.83), channel_id=1, source_target_pairs={{0,1},{1,0},{2,3},{3,2},{4,5},{5,4},{6,7},{7,6},{8,9},{9,8},{10,11... | collective-permute-start | bytes 98312 | tf_op jit(solution)/shard_map/ppermute | solution.py:1457
  101.9 47.8 %collective-permute-start.1 = (bf16[1024,1024]{1,0:T(8,128)(2,1)}, bf16[1024,1024]{1,0:T(8,128)(2,1)S(1)}, u32[]{:S(2)}, u32[]{:S(2)}) collective-permute-start(bf16[1024,1024]{1,0:T(8,128)(2,1)} %get-tuple-element.87.mixed_ref), channel_id=1, source_target_pairs={{0,1},{1,0},{2,3},{3,2},{4,5},{5,4},{6,7},{7,6},{8,9},{9,8},{10,11... | collective-permute-start | bytes 6291464 | tf_op jit(solution)/shard_map/ppermute | solution.py:1457
  171.0 47.1 %collective-permute-start.2 = (bf16[1024,1024]{1,0:T(8,128)(2,1)}, bf16[1024,1024]{1,0:T(8,128)(2,1)}, u32[]{:S(2)}, u32[]{:S(2)}) collective-permute-start(bf16[1024,1024]{1,0:T(8,128)(2,1)} %get-tuple-element.95.part_ref), channel_id=1, source_target_pairs={{0,1},{1,0},{2,3},{3,2},{4,5},{5,4},{6,7},{7,6},{8,9},{9,8},{10,11... | collective-permute-start | bytes 6291464 | tf_op jit(solution)/shard_map/ppermute | solution.py:1457
  171.6 39.3 %copy-start.24 = (bf16[1024,1024]{1,0:T(8,128)(2,1)S(1)}, bf16[1024,1024]{1,0:T(8,128)(2,1)}, u32[]{:S(2)}) copy-start(bf16[1024,1024]{1,0:T(8,128)(2,1)} %top_ref.3) | copy-start | bytes 6291460
  218.2 13.9 %copy-start.25 = (bf16[1024,1024]{1,0:T(8,128)(2,1)S(1)}, bf16[1024,1024]{1,0:T(8,128)(2,1)}, u32[]{:S(2)}) copy-start(bf16[1024,1024]{1,0:T(8,128)(2,1)} %get-tuple-element.100.ffn_ref) | copy-start | bytes 6291460
  231.5 24.2 %collective-permute-start.4 = (f32[8,1024]{1,0:T(8,128)}, f32[8,1024]{1,0:T(8,128)S(1)}, u32[]{:S(2)}, u32[]{:S(2)}) collective-permute-start(f32[8,1024]{1,0:T(8,128)} %get-tuple-element.107), channel_id=1, source_target_pairs={{0,1},{1,0},{2,3},{3,2},{4,5},{5,4},{6,7},{7,6},{8,9},{9,8},{10,11... | collective-permute-start | bytes 98312 | tf_op jit(solution)/shard_map/ppermute | solution.py:1457
  232.1 63.0 %collective-permute-start.3 = (bf16[1024,1024]{1,0:T(8,128)(2,1)S(1)}, bf16[1024,1024]{1,0:T(8,128)(2,1)}, u32[]{:S(2)}, u32[]{:S(2)}) collective-permute-start(bf16[1024,1024]{1,0:T(8,128)(2,1)S(1)} %copy-done.25), channel_id=1, source_target_pairs={{0,1},{1,0},{2,3},{3,2},{4,5},{5,4},{6,7},{7,6},{8,9},{9,8},{10,11... | collective-permute-start | bytes 6291464 | tf_op jit(solution)/shard_map/ppermute | solution.py:1457
  295.1 10.8 %copy-start.11 = (f32[8,768]{1,0:T(8,128)S(1)}, f32[8,768]{1,0:T(8,128)}, u32[]{:S(2)}) copy-start(f32[8,768]{1,0:T(8,128)} %get-tuple-element.118) | copy-start | bytes 73732
  295.2 10.8 %copy-start.14 = (f32[8,256]{1,0:T(8,128)S(1)}, f32[8,256]{1,0:T(8,128)}, u32[]{:S(2)}) copy-start(f32[8,256]{1,0:T(8,128)} %get-tuple-element.121) | copy-start | bytes 24580
  295.2 10.8 %copy-start.19 = (f32[8,128]{1,0:T(8,128)S(1)}, f32[8,128]{1,0:T(8,128)}, u32[]{:S(2)}) copy-start(f32[8,128]{1,0:T(8,128)} %get-tuple-element.119) | copy-start | bytes 12292
  295.2 10.9 %copy-start.1 = (bf16[1024,1024]{1,0:T(8,128)(2,1)S(1)}, bf16[1024,1024]{1,0:T(8,128)(2,1)}, u32[]{:S(2)}) copy-start(bf16[1024,1024]{1,0:T(8,128)(2,1)} %x_ref.3) | copy-start | bytes 6291460
  295.2 10.9 %copy-start.7 = (f32[1024]{0:T(1024)S(1)}, f32[1024]{0:T(1024)}, u32[]{:S(2)}) copy-start(f32[1024]{0:T(1024)} %copy-done.6) | copy-start | bytes 12292
  304.7 60.3 %collective-permute-start.5 = (bf16[1024,1024]{1,0:T(8,128)(2,1)}, bf16[1024,1024]{1,0:T(8,128)(2,1)}, u32[]{:S(2)}, u32[]{:S(2)}) collective-permute-start(bf16[1024,1024]{1,0:T(8,128)(2,1)} %convolution_convert_fusion.part_ref), channel_id=1, source_target_pairs={{0,1},{1,0},{2,3},{3,2},{4,5},{5,4},{6,7},{7,6},{8,9},{9,8},{10,11... | collective-permute-start | bytes 6291464 | tf_op jit(solution)/shard_map/ppermute | solution.py:1457
  355.8 6.7 %collective-permute-start.6 = (f32[18,128]{1,0:T(8,128)S(1)}, f32[18,128]{1,0:T(8,128)S(1)}, u32[]{:S(2)}, u32[]{:S(2)}) collective-permute-start(f32[18,128]{1,0:T(8,128)S(1)} %slice.73), channel_id=1, source_target_pairs={{0,1},{1,0},{2,3},{3,2},{4,5},{5,4},{6,7},{7,6},{8,9},{9,8},{10,11... | collective-permute-start | bytes 27656 | tf_op jit(solution)/shard_map/ppermute | solution.py:1457
  365.0 11.4 %collective-permute-start.7 = (f32[64,256]{1,0:T(8,128)}, f32[64,256]{1,0:T(8,128)S(1)}, u32[]{:S(2)}, u32[]{:S(2)}) collective-permute-start(f32[64,256]{1,0:T(8,128)} %get-tuple-element.137), channel_id=1, source_target_pairs={{0,1},{1,0},{2,3},{3,2},{4,5},{5,4},{6,7},{7,6},{8,9},{9,8},{10,11... | collective-permute-start | bytes 196616 | tf_op jit(solution)/shard_map/ppermute | solution.py:1457
  365.5 10.9 %copy-start.12 = (f32[64,256]{1,0:T(8,128)S(1)}, f32[64,256]{1,0:T(8,128)}, u32[]{:S(2)}) copy-start(f32[64,256]{1,0:T(8,128)} %get-tuple-element.137) | copy-start | bytes 196612
  (11 other events, 56.1 us)

commit v2 on v1

--- a/solution.py
+++ b/solution.py
@@ -74,7 +74,8 @@
 
 
 class RingGather:
-    def __init__(self, devices, x_ref, o_ref, sems):
+    def __init__(self, devices, x_ref, o_ref, sems, cols=slice(None)):
+        self.cols = cols
         self.chips = devices // 2
         self.ahead = self.chips // 2
         self.behind = self.chips - 1 - self.ahead
@@ -93,11 +94,12 @@
         self.me = me
 
     def slot(self, index):
-        return self.o_ref.at[pl.ds(pl.multiple_of(index * self.rows, self.rows), self.rows), :]
+        rows = pl.ds(pl.multiple_of(index * self.rows, self.rows), self.rows)
+        return self.o_ref.at[rows, self.cols]
 
     def copy(self, shift, ssem, rsem, target):
         if shift == 0:
-            index, source = self.me, self.x_ref
+            index, source = self.me, self.x_ref.at[:, self.cols]
         else:
             index = ring_chip(self.place + shift, self.chips) * 2 + self.core
             source = self.slot(index)
@@ -121,7 +123,9 @@
         return self.copy(shift, self.cs.at[number], self.cr.at[number], self.mate)
 
     def own(self):
-        return pltpu.make_async_copy(self.x_ref, self.slot(self.me), self.own_sem)
+        return pltpu.make_async_copy(
+            self.x_ref.at[:, self.cols], self.slot(self.me), self.own_sem
+        )
 
     def greet(self):
         self.locate()
@@ -171,12 +175,14 @@
     return jax.ShapeDtypeStruct((shard.shape[0] * devices, shard.shape[1]), shard.dtype)
 
 
-def gather_kernel(devices, count, *refs):
+def gather_kernel(devices, count, windows, *refs):
     shards, outs, sems = refs[:count], refs[count : 2 * count], refs[2 * count :]
-    each = len(sems) // count
+    each = len(sems) // len(windows)
     rings = [
-        RingGather(devices, shards[i], outs[i], sems[i * each : (i + 1) * each])
-        for i in range(count)
+        RingGather(
+            devices, shards[i], outs[i], sems[place * each : (place + 1) * each], slice(first, last)
+        )
+        for place, (i, first, last) in enumerate(windows)
     ]
     rings[0].greet()
     for ring in rings:
@@ -192,15 +198,15 @@
     return pl.CostEstimate(flops=int(micros * 1e9), bytes_accessed=0, transcendentals=0)
 
 
-def gather_rows(shards, devices, collective):
+def gather_rows(shards, devices, collective, windows):
     count = len(shards)
     anywhere = pl.BlockSpec(memory_space=pl.ANY)
     return pl.pallas_call(
-        functools.partial(gather_kernel, devices, count),
+        functools.partial(gather_kernel, devices, count, windows),
         out_shape=tuple(gather_shape(shard, devices) for shard in shards),
         in_specs=[anywhere] * count,
         out_specs=(anywhere,) * count,
-        scratch_shapes=gather_sems(devices) * count,
+        scratch_shapes=gather_sems(devices) * len(windows),
         compiler_params=pltpu.CompilerParams(collective_id=collective, has_side_effects=True),
         cost_estimate=cost(3),
         name="gather_rows",
@@ -358,23 +364,6 @@
         self.hop_back(step, step > 0)
         if step < self.behind:
             self.hop_fore(step, step > 0)
-
-    def run(self, after_first=None):
-        def turn(step, carry):
-            lax.fori_loop(0, 2, lambda part, kept: (self.produce(2 * step + part), kept)[1], 0)
-
-            @pl.when(step == 0)
-            def _():
-                self.hop_back(0, False)
-                self.hop_fore(0, False)
-                if after_first is not None:
-                    after_first()
-
-            pl.when(step > 0)(lambda: self.hop_back(step, True))
-            pl.when((step > 0) & (step < self.behind))(lambda: self.hop_fore(step, True))
-            return carry
-
-        lax.fori_loop(0, self.ahead, turn, 0)
 
     def finish(self):
         self.locate()
@@ -400,6 +389,36 @@
                 self.across(i, slot).wait_send()
 
 
+def run_rings(rings, after_first=None):
+    ahead, behind = rings[0].ahead, rings[0].behind
+
+    def turn(step, carry):
+        def part(odd, kept):
+            for ring in rings:
+                ring.produce(2 * step + odd)
+            return kept
+
+        lax.fori_loop(0, 2, part, 0)
+
+        @pl.when(step == 0)
+        def _():
+            for ring in rings:
+                ring.hop_back(0, False)
+                ring.hop_fore(0, False)
+            if after_first is not None:
+                after_first()
+
+        @pl.when(step > 0)
+        def _():
+            for ring in rings:
+                ring.hop_back(step, True)
+                pl.when(step < behind)(functools.partial(ring.hop_fore, step, True))
+
+        return carry
+
+    lax.fori_loop(0, ahead, turn, 0)
+
+
 def scatter_scratch(windows, rows, devices):
     chips = devices // 2
     count = len(windows)
@@ -502,7 +521,7 @@
         target[start : start + LANES, :] = source[:, start : start + LANES].T
 
 
-def product_kernel(devices, windows, pieces, outs, summed, left_ref, right_ref, *refs):
+def product_kernel(devices, groups, outs, summed, left_ref, right_ref, *refs):
     values = refs[:summed]
     refs = refs[summed:]
     pieces_out, refs = refs[:outs], refs[outs:]
@@ -512,29 +531,40 @@
     if summed:
         scratch, rest = scratch[:-7], scratch[-7:]
         total = Total(devices, values[0], totals_out[0], rest)
-    ring = RingScatter(devices, windows, pieces, (turned, right_ref), pieces_out, scratch)
+    each = len(scratch) // len(groups)
+    rings = [
+        RingScatter(
+            devices, windows, pieces, (turned, right_ref), pieces_out,
+            scratch[place * each : (place + 1) * each],
+        )
+        for place, (windows, pieces) in enumerate(groups)
+    ]
     if total is None:
-        ring.greet()
+        rings[0].greet()
     else:
-        ring.locate()
         total.greet()
         total.begin()
+    for ring in rings:
+        ring.locate()
     turned_copy(left_ref, turned)
-    ring.run(total.spread if total is not None else None)
-    ring.finish()
+    run_rings(rings, total.spread if total is not None else None)
+    for ring in rings:
+        ring.finish()
     if total is not None:
         total.finish()
 
 
-def scatter_product(left, right, windows, pieces, shapes, devices, collective, values=()):
+def scatter_product(left, right, groups, shapes, devices, collective, values=()):
     vmem = pl.BlockSpec(memory_space=pltpu.VMEM)
     rows = left.shape[1] // devices
-    scratch = [pltpu.VMEM(left.shape[::-1], BF16)] + scatter_scratch(windows, rows, devices)
+    scratch = [pltpu.VMEM(left.shape[::-1], BF16)]
+    for windows, pieces in groups:
+        scratch += scatter_scratch(windows, rows, devices)
     for item in values:
         scratch += total_scratch(item, devices)
     return pl.pallas_call(
         functools.partial(
-            product_kernel, devices, windows, pieces, len(shapes), len(values)
+            product_kernel, devices, groups, len(shapes), len(values)
         ),
         out_shape=tuple(jax.ShapeDtypeStruct(shape, F32) for shape in shapes)
         + tuple(jax.ShapeDtypeStruct(item.shape, F32) for item in values),
@@ -1465,6 +1495,11 @@
     return join(partial, swap(partial))
 
 
+def thirds(size):
+    part = size // 3
+    return [(0, part), (part, 2 * part), (2 * part, size)]
+
+
 def local(
     layer_input, w_norm1, w_zx, w_bc, w_dt, conv_x, conv_xb, conv_bc, conv_bcb, dt_bias, a_log,
     d_skip, w_mnorm, w_mout, query_key_value_weight, output_weight, w_norm2, w_gu, w_down,
@@ -1486,7 +1521,7 @@
         [w_zx.reshape(shard, -1), w_bc, query_key_value_weight.reshape(shard, -1), tail], axis=1
     )
     in_width = mixer_in.shape[1]
-    (w_in,) = gather_rows([mixer_in], devices, 0)
+    (w_in,) = gather_rows([mixer_in], devices, 0, [(0, *window) for window in thirds(in_width)])
     norm1 = w_in[:, in_width - LANES + heads].astype(F32)
     norm2 = w_in[:, in_width - LANES + heads + 1].astype(F32)
 
@@ -1513,7 +1548,12 @@
         (mixed, w_gu.reshape(shard, -1), w_down.T)
     )
     other = swap(mixed)
-    w_gate_up, w_down_t = gather_rows([gate_up_shard, down_shard], devices, 3)
+    w_gate_up, w_down_t = gather_rows(
+        [gate_up_shard, down_shard],
+        devices,
+        3,
+        [(0, 0, units), (0, units, 2 * units), (1, 0, units)],
+    )
     other, w_gate_up, w_down_t = lax.optimization_barrier((other, w_gate_up, w_down_t))
     after, scale_two, hidden_two, activated, grad_gu_low, ffn_part, partial_two = run_feed_forward(
         layer_input, mixed, other, grad_output, norm2[None, :], w_gate_up, w_down_t
@@ -1523,8 +1563,10 @@
     (mine_gu,) = scatter_product(
         hidden_two,
         grad_gu_low,
-        [(0, 1, 0, 2 * units)],
-        [(0, 0, units, 0, 0), (0, units, 2 * units, 0, 1)],
+        [
+            ([(0, 1, 0, units)], [(0, 0, units, 0, 0)]),
+            ([(0, 1, units, 2 * units)], [(0, 0, units, 0, 1)]),
+        ],
         [(shard, 2, units)],
         devices,
         1,
@@ -1576,13 +1618,17 @@
     mine_zx, mine_bc, mine_qkv, mine_step, small = scatter_product(
         hidden_one,
         grad_proj,
-        [(0, 1, 0, in_width)],
         [
-            (0, 0, channels, 0, 0),
-            (0, channels, shared_at, 0, 1),
-            (0, shared_at, qkv_at, 1, None),
-            (0, qkv_at, step_at, 2, 0),
-            (0, step_at, in_width, 3, "turned"),
+            ([(0, 1, 0, channels)], [(0, 0, channels, 0, 0)]),
+            ([(0, 1, channels, shared_at)], [(0, 0, channels, 0, 1)]),
+            (
+                [(0, 1, shared_at, in_width)],
+                [
+                    (0, 0, 2 * NS, 1, None),
+                    (0, 2 * NS, 2 * NS + qkv_width, 2, 0),
+                    (0, 2 * NS + qkv_width, in_width - shared_at, 3, "turned"),
+                ],
+            ),
         ],
         [
             (shard, 2, channels),

time: 378 us -> 372 us (0.984)
  Pallas kernels: 301 us -> 289 us
  waiting for transfers between devices: 10.7 us -> 16.5 us
    pallas_call x4, Pallas kernels: 160 us -> 148 us  [the longest x2 75.2 us: scatter_product(): pl.pallas_call(functools.partial(product_kernel, devices, groups, len(sha...]
    ppermute x8, waiting for transfers between devices: 10.7 us -> 16.5 us  [swap(): return lax.ppermute(partial, 'tensor', [(0, 1), (1, 0)])]
  transfers between devices with their start and end apart: 8 -> 8, of which waited for: 2 -> 2; matrix products, arithmetic and copies ran while one was open for 7% -> 7% of each run, Pallas kernels for 54% -> 52%
where the time goes in v2:
time: 372 us; the launch traced here: 371 us
  Pallas kernels  289 us (78%)
  matrix products  28.3 us (8%)
  local copies, waits for them, and re-layouts  18.4 us (5%)
  waiting for transfers between devices  16.5 us (4%)
  other arithmetic  10.5 us (3%)
  starting transfers between devices  7.35 us (2%)
    pallas_call x2, Pallas kernels, scatter_product(): pl.pallas_call(functools.partial(product_kernel, devices, groups, len(sha...  75.2 us
    pallas_call x2, Pallas kernels, gather_rows(): pl.pallas_call(functools.partial(gather_kernel, devices, count, windows),...  72.3 us
    pallas_call x1, Pallas kernels, run_scan_backward(): pl.pallas_call(functools.partial(scan_backward, devices, spans, windows,...  37.6 us
    dot_general x4, matrix products, dot(): lax.dot_general(left, right, (dims, ((), ())), preferred_element_type=F32...  28.3 us
    pallas_call x1, Pallas kernels, run_scan_forward(): pl.pallas_call(functools.partial(scan_forward, devices, spans), grid=(spa...  24.2 us
    pallas_call x1, Pallas kernels, run_feed_forward(): pl.pallas_call(feed_forward, grid=(tokens // TBLK,), out_shape=(shape((to...  19.9 us
    ppermute x8, waiting for transfers between devices, swap(): return lax.ppermute(partial, 'tensor', [(0, 1), (1, 0)])  16.5 us
    pallas_call x1, Pallas kernels, run_attend_backward(): pl.pallas_call(attend_backward, grid=(1,), out_shape=jax.ShapeDtypeStruct...  16.2 us
  transfers between devices with their start and end apart: 8, of which 2 were waited for; matrix products, arithmetic and copies ran while one was open for 7% of the time, Pallas kernels for 52%

profile of v2, /device:TPU:0, one launch (start us, length us, event | category | flops | bytes accessed | tf_op | source)
XLA Modules:
  0.0 371.2 jit_solution(11286297765073855834)
XLA Ops:
  3.9 1.6 concatenate.12.refs_0_
  5.6 33.2 %gather_rows.2 = bf16[1024,2304]{1,0:T(8,128)(2,1)} custom-call(bf16[64,2304]{1,0:T(8,128)(2,1)} %concatenate.12.refs_0_), custom_call_target="tpu_custom_call" | custom-call | flops 3000000000 | tf_op jit(solution)/shard_map/gather_rows/pallas_call | solution.py:204
  38.8 2.0 convert_reduce_fusion
  43.3 7.6 %fusion.5.z_ref.x_ref.bc_ref.step_ref.q_ref.kv_ref.xp_ref.bp_ref = f32[1024,2304]{1,0:T(8,128)} fusion(bf16[1024,1024]{1,0:T(8,128)(2,1)S(1)} %fusion.2.left_ref, bf16[1024,2304]{1,0:T(8,128)(2,1)S(1)} %copy-done.5), kind=kOutput, calls=%fused_computation.28 | convolution fusion | flops 4831838208 | bytes 16252928 | tf_op jit(solution)/shard_map/dot_general | solution.py:39
  53.5 24.2 %scan_forward.1 = (f32[1024,768]{1,0:T(8,128)}, f32[1024,768]{1,0:T(8,128)}, f32[8,1024]{1,0:T(8,128)}, f32[8,128,768]{2,1,0:T(8,128)}, bf16[1024,1024]{1,0:T(8,128)(2,1)}) custom-call(f32[1024,2304]{1,0:T(8,128)} %fusion.5.z_ref.x_ref.bc_ref.step_ref.q_ref.kv_ref.xp_ref.bp_ref, f32[1024,2304]{1,0:T(8,128)} %fusion.5.z_ref.x_ref.bc_ref.step_ref.q_ref.kv_ref.xp_ref.bp_ref, ...), custom_call_target="tpu_custom_call" | custom-call | flops 20000000000 | tf_op jit(solution)/shard_map/scan_forward/pallas_call | solution.py:912
  77.8 1.6 collective-permute-start
  79.3 12.5 %attend_forward.1 = (bf16[1024,512]{1,0:T(8,128)(2,1)}, f32[8,1024]{1,0:T(8,128)}, bf16[1024,256]{1,0:T(8,128)(2,1)}) custom-call(f32[1024,2304]{1,0:T(8,128)} %fusion.5.z_ref.x_ref.bc_ref.step_ref.q_ref.kv_ref.xp_ref.bp_ref, f32[1024,2304]{1,0:T(8,128)} %fusion.5.z_ref.x_ref.bc_ref.step_ref.q_ref.kv_ref.xp_ref.bp_ref, f32[32,128]{1,0:T(8,128)} %constant.43.clone.fine_cos, ...), custom_call_target="tpu_custom_call" | custom-call | flops 15000000512 | tf_op jit(solution)/shard_map/attend_forward/pallas_call | solution.py:1243
  93.8 7.0 %mixer_forward.1 = (bf16[1024,1024]{1,0:T(8,128)(2,1)}, bf16[1024,1024]{1,0:T(8,128)(2,1)}) custom-call(f32[1024,768]{1,0:T(8,128)} %get-tuple-element.82.gated_ref, f32[8,1024]{1,0:T(8,128)} %add_rsqrt_fusion.scale_ref.scale_m_ref, f32[1,768]{1,0:T(1,128)} %reshape.132.gain_ref.gain_m_ref, bf16[1024,256]{1,0:T(8,128)(2,1)} %get-tuple-element.84.attended_ref.o_ref, ...), custom_call_target="tpu_custom_call" | custom-call | flops 5000000000 | tf_op jit(solution)/shard_map/mixer_forward/pallas_call | solution.py:1371
  101.3 39.1 %gather_rows.3 = (bf16[1024,2048]{1,0:T(8,128)(2,1)}, bf16[1024,1024]{1,0:T(8,128)(2,1)}) custom-call(bf16[64,2048]{1,0:T(8,128)(2,1)} %bitcast.55, bf16[64,1024]{1,0:T(8,128)(2,1)} %bitcast.69), custom_call_target="tpu_custom_call" | custom-call | flops 3000000000 | tf_op jit(solution)/shard_map/gather_rows/pallas_call | solution.py:204
  140.4 8.1 %collective-permute-done.1.other_ref = bf16[1024,1024]{1,0:T(8,128)(2,1)S(1)} collective-permute-done((bf16[1024,1024]{1,0:T(8,128)(2,1)}, bf16[1024,1024]{1,0:T(8,128)(2,1)S(1)}, u32[]{:S(2)}, u32[]{:S(2)}) %collective-permute-start.1) | collective-permute-done | bytes 2097184 | tf_op jit(solution)/shard_map/ppermute | solution.py:1487
  149.9 19.9 %feed_forward.1 = (f32[1024,1024]{1,0:T(8,128)}, f32[1024,1]{1,0:T(8,128)}, bf16[1024,1024]{1,0:T(8,128)(2,1)}, bf16[1024,1024]{1,0:T(8,128)(2,1)}, bf16[1024,20...) custom-call(bf16[1024,1024]{1,0:T(8,128)(2,1)} %x_ref.3, ...), custom_call_target="tpu_custom_call" | custom-call | flops 20000000000 | tf_op jit(solution)/shard_map/feed_forward/pallas_call | solution.py:1337
  170.4 32.9 %scatter_product.2.refs_5_ = f32[64,2,1024]{2,1,0:T(2,128)} custom-call(bf16[1024,1024]{1,0:T(8,128)(2,1)} %get-tuple-element.96.left_ref, bf16[1024,2048]{1,0:T(8,128)(2,1)} %get-tuple-element.97.right_ref), custom_call_target="tpu_custom_call" | custom-call | flops 3000000000 | tf_op jit(solution)/shard_map/scatter_product/pallas_call | solution.py:565
  203.3 5.3 %convert_bitcast_fusion.refs_1_ = bf16[1024,1024]{1,0:T(8,128)(2,1)} fusion(bf16[1024,1024]{1,0:T(8,128)(2,1)} %get-tuple-element.98, bf16[1024,1024]{1,0:T(8,128)(2,1)S(1)} %copy-done.24), kind=kOutput, calls=%fused_computation.7 | convolution fusion | flops 2148532224 | bytes 6291456 | tf_op jit(solution)/shard_map/dot_general | solution.py:39
  208.6 8.4 %collective-permute-done.2.other_ref = bf16[1024,1024]{1,0:T(8,128)(2,1)} collective-permute-done((bf16[1024,1024]{1,0:T(8,128)(2,1)}, bf16[1024,1024]{1,0:T(8,128)(2,1)}, u32[]{:S(2)}, u32[]{:S(2)}) %collective-permute-start.2) | collective-permute-done | bytes 2097184 | tf_op jit(solution)/shard_map/ppermute | solution.py:1487
  217.0 13.3 %mixer_backward.1 = (f32[1024,1024]{1,0:T(8,128)}, bf16[1024,1024]{1,0:T(8,128)(2,1)}, f32[1024,768]{1,0:T(8,128)}, bf16[1024,256]{1,0:T(8,128)(2,1)}, f32[8,1024]{1,0:T(8,128)}, /*index=5*/f32[8,1024]{1,0:T(8,128)}) custom-call(bf16[1024,1024]{1,0:T(8,128)(2,1)} %get-tuple-element.95.part_ref, bf16[1024,1024]{1,0:T(8,128)(2,1)} %collective-permute-done.2.other_ref, ...), custom_call_target="tpu_custom_call" | custom-call | flops 8000000000 | tf_op jit(solution)/shard_map/mixer_backward/pallas_call | solution.py:1425
  230.9 1.5 collective-permute-start.3
  232.4 16.2 %attend_backward.1.dqkv_ref = bf16[1024,384]{1,0:T(8,128)(2,1)} custom-call(bf16[1024,512]{1,0:T(8,128)(2,1)} %get-tuple-element.108.qkv_ref, f32[8,1024]{1,0:T(8,128)} %get-tuple-element.109.lse_ref, bf16[1024,256]{1,0:T(8,128)(2,1)} %get-tuple-element.84.attended_ref.o_ref, bf16[1024,256]{1,0:T(8,128)(2,1)} %get-tuple-element.110.do_ref, ...), custom_call_target="tpu_custom_call" | custom-call | flops 16000000000 | tf_op jit(solution)/shard_map/attend_backward/pallas_call | solution.py:1275
  248.6 6.0 %convolution_convert_fusion.1.refs_0_ = bf16[1024,1024]{1,0:T(8,128)(2,1)} fusion(bf16[1024,1024]{1,0:T(8,128)(2,1)} %get-tuple-element.111, bf16[1024,1024]{1,0:T(8,128)(2,1)} %get-tuple-element.112), kind=kOutput, calls=%fused_computation.9 | convolution fusion | flops 2148532224 | bytes 6291456 | tf_op jit(solution)/shard_map/dot_general | solution.py:39
  255.2 37.6 %scan_backward.1 = (bf16[1024,2304]{1,0:T(8,128)(2,1)}, f32[8,768]{1,0:T(8,128)}, f32[8,256]{1,0:T(8,128)}, f32[8,128]{1,0:T(8,128)}, f32[64,768]{1,0:T(8,128)}, /*index=5*/f32[64,256]{1,0:T(8,128)}, f32[64,1024]{1,0:T(8,128)}) custom-call(f32[1024,2304]{1,0:T(8,128)} %fusion.5.z_ref.x_ref.bc_ref.step_ref.q_ref.kv_ref.xp_ref.bp_ref, ...), custom_call_target="tpu_custom_call" | custom-call | flops 46999998464 | tf_op jit(solution)/shard_map/scan_backward/pallas_call | solution.py:961
  292.8 9.5 %convolution_convert_fusion.part_ref = bf16[1024,1024]{1,0:T(8,128)(2,1)} fusion(bf16[1024,2304]{1,0:T(8,128)(2,1)} %get-tuple-element.117.right_ref, bf16[1024,2304]{1,0:T(8,128)(2,1)} %gather_rows.2), kind=kOutput, calls=%fused_computation.8 | convolution fusion | flops 4832886784 | bytes 11534336 | tf_op jit(solution)/shard_map/dot_general | solution.py:39
  303.7 2.3 fusion.3
  307.0 42.3 %scatter_product.3 = (f32[64,2,768]{2,1,0:T(2,128)}, f32[64,256]{1,0:T(8,128)}, f32[64,1,384]{2,1,0:T(1,128)}, f32[12,64]{1,0:T(8,128)}, f32[72,128]{1,0:T(8,128)}) custom-call(bf16[1024,1024]{1,0:T(8,128)(2,1)} %copy-done.2, bf16[1024,2304]{1,0:T(8,128)(2,1)} %get-tuple-element.117.right_ref, f32[72,128]{1,0:T(8,128)} %pad.4.refs_0_), custom_call_target="tpu_custom_call" | custom-call | flops 3000000000 | tf_op jit(solution)/shard_map/scatter_product/pallas_call | solution.py:565
  350.0 1.5 collective-permute-start.6
  359.7 10.9 %finish_layer.1 = (f32[1024,1024]{1,0:T(8,128)}, bf16[1024,1024]{1,0:T(8,128)(2,1)}, f32[64,2,768]{2,1,0:T(2,128)}, f32[64,1,384]{2,1,0:T(1,128)}, f32[12,64]{1,...) custom-call(bf16[1024,1024]{1,0:T(8,128)(2,1)} %x_ref.3, ...), custom_call_target="tpu_custom_call" | custom-call | flops 8000000000 | tf_op jit(solution)/shard_map/finish_layer/pallas_call | solution.py:1471
  (106 shorter events, 25.7 us)
Async XLA Ops:
  5.6 35.3 %copy-start = (bf16[1024,1024]{1,0:T(8,128)(2,1)S(1)}, bf16[1024,1024]{1,0:T(8,128)(2,1)}, u32[]{:S(2)}) copy-start(bf16[1024,1024]{1,0:T(8,128)(2,1)} %x_ref.3) | copy-start | bytes 6291460
  43.2 7.7 %copy-start.21 = (bf16[12]{0:T(256)(128)(2,1)S(1)}, bf16[12]{0:T(256)(128)(2,1)}, u32[]{:S(2)}) copy-start(bf16[12]{0:T(256)(128)(2,1)} %param.33) | copy-start | bytes 76
  43.2 8.4 %copy-start.16 = (bf16[4,768]{1,0:T(4,128)(2,1)S(1)}, bf16[4,768]{1,0:T(4,128)(2,1)}, u32[]{:S(2)}) copy-start(bf16[4,768]{1,0:T(4,128)(2,1)} %param.29) | copy-start | bytes 18436
  43.2 9.0 %copy-start.17 = (bf16[4,256]{1,0:T(4,128)(2,1)S(1)}, bf16[4,256]{1,0:T(4,128)(2,1)}, u32[]{:S(2)}) copy-start(bf16[4,256]{1,0:T(4,128)(2,1)} %param.31) | copy-start | bytes 6148
  43.2 9.6 %copy-start.4 = (bf16[768,64]{0,1:T(8,128)(2,1)S(1)}, bf16[768,64]{0,1:T(8,128)(2,1)}, u32[]{:S(2)}) copy-start(bf16[768,64]{0,1:T(8,128)(2,1)} %param.37) | copy-start | bytes 294916
  43.3 9.6 %copy-start.10 = (bf16[1,256,64]{1,2,0:T(8,128)(2,1)S(1)}, bf16[1,256,64]{1,2,0:T(8,128)(2,1)}, u32[]{:S(2)}) copy-start(bf16[1,256,64]{1,2,0:T(8,128)(2,1)} %param.39) | copy-start | bytes 98308
  77.7 14.7 %copy-start.3 = (bf16[64,2,1024]{2,1,0:T(2,128)(2,1)S(1)}, bf16[64,2,1024]{2,1,0:T(2,128)(2,1)}, u32[]{:S(2)}) copy-start(bf16[64,2,1024]{2,1,0:T(2,128)(2,1)} %param.41) | copy-start | bytes 786436
  77.7 15.4 %copy-start.9 = (f32[8,1024]{1,0:T(8,128)S(1)}, f32[8,1024]{1,0:T(8,128)}, u32[]{:S(2)}) copy-start(f32[8,1024]{1,0:T(8,128)} %get-tuple-element.83) | copy-start | bytes 98308
  77.8 15.4 %collective-permute-start = (f32[8,1024]{1,0:T(8,128)}, f32[8,1024]{1,0:T(8,128)S(1)}, u32[]{:S(2)}, u32[]{:S(2)}) collective-permute-start(f32[8,1024]{1,0:T(8,128)} %get-tuple-element.83), channel_id=1, source_target_pairs={{0,1},{1,0},{2,3},{3,2},{4,5},{5,4},{6,7},{7,6},{8,9},{9,8},{10,11... | collective-permute-start | bytes 98312 | tf_op jit(solution)/shard_map/ppermute | solution.py:1487
  100.8 47.8 %collective-permute-start.1 = (bf16[1024,1024]{1,0:T(8,128)(2,1)}, bf16[1024,1024]{1,0:T(8,128)(2,1)S(1)}, u32[]{:S(2)}, u32[]{:S(2)}) collective-permute-start(bf16[1024,1024]{1,0:T(8,128)(2,1)} %get-tuple-element.87.mixed_ref), channel_id=1, source_target_pairs={{0,1},{1,0},{2,3},{3,2},{4,5},{5,4},{6,7},{7,6},{8,9},{9,8},{10,11... | collective-permute-start | bytes 6291464 | tf_op jit(solution)/shard_map/ppermute | solution.py:1487
  169.8 47.1 %collective-permute-start.2 = (bf16[1024,1024]{1,0:T(8,128)(2,1)}, bf16[1024,1024]{1,0:T(8,128)(2,1)}, u32[]{:S(2)}, u32[]{:S(2)}) collective-permute-start(bf16[1024,1024]{1,0:T(8,128)(2,1)} %get-tuple-element.95.part_ref), channel_id=1, source_target_pairs={{0,1},{1,0},{2,3},{3,2},{4,5},{5,4},{6,7},{7,6},{8,9},{9,8},{10,11... | collective-permute-start | bytes 6291464 | tf_op jit(solution)/shard_map/ppermute | solution.py:1487
  170.4 32.9 %copy-start.24 = (bf16[1024,1024]{1,0:T(8,128)(2,1)S(1)}, bf16[1024,1024]{1,0:T(8,128)(2,1)}, u32[]{:S(2)}) copy-start(bf16[1024,1024]{1,0:T(8,128)(2,1)} %top_ref.3) | copy-start | bytes 6291460
  217.0 13.9 %copy-start.25 = (bf16[1024,1024]{1,0:T(8,128)(2,1)S(1)}, bf16[1024,1024]{1,0:T(8,128)(2,1)}, u32[]{:S(2)}) copy-start(bf16[1024,1024]{1,0:T(8,128)(2,1)} %get-tuple-element.100.ffn_ref) | copy-start | bytes 6291460
  230.3 24.2 %collective-permute-start.4 = (f32[8,1024]{1,0:T(8,128)}, f32[8,1024]{1,0:T(8,128)S(1)}, u32[]{:S(2)}, u32[]{:S(2)}) collective-permute-start(f32[8,1024]{1,0:T(8,128)} %get-tuple-element.107), channel_id=1, source_target_pairs={{0,1},{1,0},{2,3},{3,2},{4,5},{5,4},{6,7},{7,6},{8,9},{9,8},{10,11... | collective-permute-start | bytes 98312 | tf_op jit(solution)/shard_map/ppermute | solution.py:1487
  230.9 61.8 %collective-permute-start.3 = (bf16[1024,1024]{1,0:T(8,128)(2,1)S(1)}, bf16[1024,1024]{1,0:T(8,128)(2,1)}, u32[]{:S(2)}, u32[]{:S(2)}) collective-permute-start(bf16[1024,1024]{1,0:T(8,128)(2,1)S(1)} %copy-done.25), channel_id=1, source_target_pairs={{0,1},{1,0},{2,3},{3,2},{4,5},{5,4},{6,7},{7,6},{8,9},{9,8},{10,11... | collective-permute-start | bytes 6291464 | tf_op jit(solution)/shard_map/ppermute | solution.py:1487
  292.7 10.9 %copy-start.11 = (f32[8,768]{1,0:T(8,128)S(1)}, f32[8,768]{1,0:T(8,128)}, u32[]{:S(2)}) copy-start(f32[8,768]{1,0:T(8,128)} %get-tuple-element.118) | copy-start | bytes 73732
  292.8 10.9 %copy-start.14 = (f32[8,256]{1,0:T(8,128)S(1)}, f32[8,256]{1,0:T(8,128)}, u32[]{:S(2)}) copy-start(f32[8,256]{1,0:T(8,128)} %get-tuple-element.121) | copy-start | bytes 24580
  292.8 10.9 %copy-start.19 = (f32[8,128]{1,0:T(8,128)S(1)}, f32[8,128]{1,0:T(8,128)}, u32[]{:S(2)}) copy-start(f32[8,128]{1,0:T(8,128)} %get-tuple-element.119) | copy-start | bytes 12292
  292.8 10.9 %copy-start.1 = (bf16[1024,1024]{1,0:T(8,128)(2,1)S(1)}, bf16[1024,1024]{1,0:T(8,128)(2,1)}, u32[]{:S(2)}) copy-start(bf16[1024,1024]{1,0:T(8,128)(2,1)} %x_ref.3) | copy-start | bytes 6291460
  292.8 10.9 %copy-start.7 = (f32[1024]{0:T(1024)S(1)}, f32[1024]{0:T(1024)}, u32[]{:S(2)}) copy-start(f32[1024]{0:T(1024)} %copy-done.6) | copy-start | bytes 12292
  302.3 56.9 %collective-permute-start.5 = (bf16[1024,1024]{1,0:T(8,128)(2,1)}, bf16[1024,1024]{1,0:T(8,128)(2,1)}, u32[]{:S(2)}, u32[]{:S(2)}) collective-permute-start(bf16[1024,1024]{1,0:T(8,128)(2,1)} %convolution_convert_fusion.part_ref), channel_id=1, source_target_pairs={{0,1},{1,0},{2,3},{3,2},{4,5},{5,4},{6,7},{7,6},{8,9},{9,8},{10,11... | collective-permute-start | bytes 6291464 | tf_op jit(solution)/shard_map/ppermute | solution.py:1487
  350.0 6.7 %collective-permute-start.6 = (f32[18,128]{1,0:T(8,128)S(1)}, f32[18,128]{1,0:T(8,128)S(1)}, u32[]{:S(2)}, u32[]{:S(2)}) collective-permute-start(f32[18,128]{1,0:T(8,128)S(1)} %slice.73), channel_id=1, source_target_pairs={{0,1},{1,0},{2,3},{3,2},{4,5},{5,4},{6,7},{7,6},{8,9},{9,8},{10,11... | collective-permute-start | bytes 27656 | tf_op jit(solution)/shard_map/ppermute | solution.py:1487
  359.2 11.4 %collective-permute-start.7 = (f32[64,256]{1,0:T(8,128)}, f32[64,256]{1,0:T(8,128)S(1)}, u32[]{:S(2)}, u32[]{:S(2)}) collective-permute-start(f32[64,256]{1,0:T(8,128)} %get-tuple-element.137), channel_id=1, source_target_pairs={{0,1},{1,0},{2,3},{3,2},{4,5},{5,4},{6,7},{7,6},{8,9},{9,8},{10,11... | collective-permute-start | bytes 196616 | tf_op jit(solution)/shard_map/ppermute | solution.py:1487
  359.7 10.9 %copy-start.12 = (f32[64,256]{1,0:T(8,128)S(1)}, f32[64,256]{1,0:T(8,128)}, u32[]{:S(2)}) copy-start(f32[64,256]{1,0:T(8,128)} %get-tuple-element.137) | copy-start | bytes 196612
  (11 other events, 57.2 us)

commit v3 on v2

--- a/solution.py
+++ b/solution.py
@@ -613,11 +613,11 @@
     return jnp.maximum(raw, 0.0) + jnp.log1p(jnp.exp(-jnp.abs(raw)))
 
 
-def conv_window(buffer, taps_ref, bias, span):
-    total = bias + taps_ref[0:1, :] * buffer[EDGE - 3 : EDGE - 3 + span, :]
+def conv_window(buffer, taps, bias, span):
+    total = bias + taps[0:1, :] * buffer[EDGE - 3 : EDGE - 3 + span, :]
     for tap in range(1, KCONV):
         start = EDGE - 3 + tap
-        total = total + taps_ref[tap : tap + 1, :] * buffer[start : start + span, :]
+        total = total + taps[tap : tap + 1, :] * buffer[start : start + span, :]
     return total
 
 
@@ -675,8 +675,9 @@
     bbuf[EDGE:, :] = bc_ref[...]
     spread = head_spread(channels)
     bias, gain, biasb, stepb, decay, skip = unpack_rows(row_ref, spread)
-    inputs = jax.nn.silu(conv_window(xbuf, tap_ref, bias, span))
-    shared = jax.nn.silu(conv_window(bbuf, tapb_ref, biasb, span))
+    taps, tapsb = tap_ref[...].astype(F32), tapb_ref[...].astype(F32)
+    inputs = jax.nn.silu(conv_window(xbuf, taps, bias, span))
+    shared = jax.nn.silu(conv_window(bbuf, tapsb, biasb, span))
     raw, step, cum, step_w, tails_w, grown_w = span_rates(step_ref, stepb, decay, spread, span)
     cum_rows = cum.T
     b_low = shared[:, :NS].astype(BF16)
@@ -700,7 +701,7 @@
     y = y_ref[...] + outer + skip * inputs
     y_ref[...] = y
     gated = y * jax.nn.silu(z_ref[...])
-    gated_ref[...] = gated
+    gated_ref[...] = gated.astype(BF16)
     square_ref[...] = row_sums(gated * gated)
 
     count = spans
@@ -745,10 +746,11 @@
     bbuf[EDGE:, :] = bc_ref[...]
     spread = head_spread(channels)
     bias, gain, biasb, stepb, decay, skip = unpack_rows(row_ref, spread)
-    conv = conv_window(xbuf, tap_ref, bias, span)
+    taps, tapsb = tap_ref[...].astype(F32), tapb_ref[...].astype(F32)
+    conv = conv_window(xbuf, taps, bias, span)
     sig = jax.nn.sigmoid(conv)
     inputs = conv * sig
-    convb = conv_window(bbuf, tapb_ref, biasb, span)
+    convb = conv_window(bbuf, tapsb, biasb, span)
     sigb = jax.nn.sigmoid(convb)
     shared = convb * sigb
     b_low = shared[:, :NS].astype(BF16)
@@ -764,7 +766,7 @@
     y = y_ref[...]
     scale = scale_ref[...].T[:, :1]
     normed = y * swish * scale
-    dyg = dyg_ref[...]
+    dyg = dyg_ref[...].astype(F32)
     gain_grad = jnp.sum(dyg * normed, axis=0, keepdims=True)
     dgated = scale * (dyg * gain - normed * inner_ref[...].T[:, :1])
     dy = dgated * swish
@@ -845,8 +847,8 @@
     for tap in range(KCONV):
         back = KCONV - 1 - tap
         start = EDGE - 3 + tap
-        dx = dx + tap_ref[tap : tap + 1, :] * dxbuf[back : back + span, :]
-        dbc = dbc + tapb_ref[tap : tap + 1, :] * dbbuf[back : back + span, :]
+        dx = dx + taps[tap : tap + 1, :] * dxbuf[back : back + span, :]
+        dbc = dbc + tapsb[tap : tap + 1, :] * dbbuf[back : back + span, :]
         gx_ref[tap : tap + 1, :] += jnp.sum(
             dconv * xbuf[start : start + span, :], axis=0, keepdims=True
         )
@@ -873,7 +875,7 @@
     size = sum(item.shape[0] for item in flat) // LANES
     flat.append(jnp.zeros((-size % EDGE * LANES,), BF16))
     rows = jnp.concatenate(flat).astype(F32).reshape(-1, LANES)
-    return (conv_x.astype(F32), conv_bc.astype(F32), rows)
+    return (conv_x, conv_bc, rows)
 
 
 def unpack_rows(row_ref, spread):
@@ -914,7 +916,7 @@
         grid=(spans,),
         out_shape=(
             jax.ShapeDtypeStruct((tokens, channels), F32),
-            jax.ShapeDtypeStruct((tokens, channels), F32),
+            jax.ShapeDtypeStruct((tokens, channels), BF16),
             jax.ShapeDtypeStruct((EDGE, tokens), F32),
             jax.ShapeDtypeStruct((spans, NS, channels), F32),
             gather_shape(shard, devices),
@@ -1298,23 +1300,22 @@
 
 
 def feed_forward(
-    x_ref, mixed_ref, other_ref, top_ref, gain_ref, gu_ref, down_ref,
-    after_ref, scale_ref, hidden_ref, act_ref, dgu_ref, part_ref, back_ref,
+    x_ref, mixed_ref, other_ref, act_grad_ref, norms_ref, gu_ref,
+    after_ref, scale_ref, hidden_ref, act_ref, dgu_ref, back_ref,
 ):
-    units = down_ref.shape[1]
+    units = act_grad_ref.shape[1]
     after = x_ref[...].astype(F32) + (mixed_ref[...].astype(F32) + other_ref[...].astype(F32))
-    after_ref[...] = after
+    after_ref[...] = after.astype(BF16)
     scale = lax.rsqrt(jnp.mean(after * after, axis=-1, keepdims=True) + EPSILON)
     scale_ref[...] = scale
-    hidden = (after * scale * gain_ref[...]).astype(BF16)
+    hidden = (after * scale * norms_ref[1:2, :]).astype(BF16)
     hidden_ref[...] = hidden
-    top = top_ref[...]
     for start in range(0, units, UBLK):
         cols = slice(start, start + UBLK)
         up_cols = slice(units + start, units + start + UBLK)
         gate = dot(hidden, gu_ref[:, cols])
         upward = dot(hidden, gu_ref[:, up_cols])
-        grad = dot(top, down_ref[:, cols])
+        grad = act_grad_ref[:, cols]
         sigma = jax.nn.sigmoid(gate)
         swish = gate * sigma
         act_ref[:, cols] = (swish * upward).astype(BF16)
@@ -1322,44 +1323,122 @@
         dgu_ref[:, cols] = (grad * upward * slope).astype(BF16)
         dgu_ref[:, up_cols] = (grad * swish).astype(BF16)
     back_ref[...] = dot(dgu_ref[...], gu_ref[...], NT).astype(BF16)
-    part_ref[...] = dot(act_ref[...], down_ref[...], NT).astype(BF16)
+
+
+def product_rows(dims, left_ref, right_ref, out_ref):
+    out_ref[...] = dot(left_ref[...], right_ref[...], dims).astype(out_ref.dtype)
+
+
+def run_product(left, right, dims, dtype):
+    tokens, depth = left.shape
+    cols = right.shape[1 - dims[1][0]]
+    return pl.pallas_call(
+        functools.partial(product_rows, dims),
+        grid=(tokens // TBLK,),
+        out_shape=jax.ShapeDtypeStruct((tokens, cols), dtype),
+        in_specs=[pl.BlockSpec((TBLK, depth), lambda turn: (turn, 0)), once(right)],
+        out_specs=pl.BlockSpec((TBLK, cols), lambda turn: (turn, 0)),
+        cost_estimate=cost(4),
+        name="product_rows",
+    )(left, right)
+
+
+def project(heads, x_ref, w_ref, hidden_ref, proj_ref, norms_ref):
+    @pl.when(pl.program_id(0) == 0)
+    def _():
+        gains = w_ref[:, w_ref.shape[1] - LANES :].astype(F32).T
+        norms_ref[...] = jnp.zeros_like(norms_ref)
+        norms_ref[0:2, :] = gains[heads : heads + 2, :]
+
+    x = x_ref[...].astype(F32)
+    scale = lax.rsqrt(jnp.mean(x * x, axis=-1, keepdims=True) + EPSILON)
+    hidden = (x * scale * norms_ref[0:1, :]).astype(BF16)
+    hidden_ref[...] = hidden
+    proj_ref[...] = dot(hidden, w_ref[...])
+
+
+def run_project(x, w_in, heads):
+    tokens, width = x.shape
+    cols = w_in.shape[1]
+    rows = lambda size: pl.BlockSpec((TBLK, size), lambda turn: (turn, 0))
+    return pl.pallas_call(
+        functools.partial(project, heads),
+        grid=(tokens // TBLK,),
+        out_shape=(
+            jax.ShapeDtypeStruct((tokens, width), BF16),
+            jax.ShapeDtypeStruct((tokens, cols), F32),
+            jax.ShapeDtypeStruct((EDGE, width), F32),
+        ),
+        in_specs=[rows(width), once(w_in)],
+        out_specs=(
+            rows(width), rows(cols), pl.BlockSpec((EDGE, width), lambda turn: (0, 0)),
+        ),
+        cost_estimate=cost(8),
+        name="project",
+    )(x, w_in)
+
+
+def project_back(grad_ref, w_ref, x_ref, part_ref, gain_grad_ref):
+    @pl.when(pl.program_id(0) == 0)
+    def _():
+        gain_grad_ref[...] = jnp.zeros_like(gain_grad_ref)
+
+    x = x_ref[...].astype(F32)
+    normed = x * lax.rsqrt(jnp.mean(x * x, axis=-1, keepdims=True) + EPSILON)
+    part = dot(grad_ref[...], w_ref[...], NT).astype(BF16)
+    part_ref[...] = part
+    gain_grad_ref[:1, :] += jnp.sum(part.astype(F32) * normed, axis=0, keepdims=True)
+
+
+def run_project_back(grads, w_in, x):
+    tokens, width = x.shape
+    cols = w_in.shape[1]
+    rows = lambda size: pl.BlockSpec((TBLK, size), lambda turn: (turn, 0))
+    return pl.pallas_call(
+        project_back,
+        grid=(tokens // TBLK,),
+        out_shape=(
+            jax.ShapeDtypeStruct((tokens, width), BF16),
+            jax.ShapeDtypeStruct((EDGE, width), F32),
+        ),
+        in_specs=[rows(cols), once(w_in), rows(width)],
+        out_specs=(rows(width), pl.BlockSpec((EDGE, width), lambda turn: (0, 0))),
+        cost_estimate=cost(8),
+        name="project_back",
+    )(grads, w_in, x)
 
 
 def once(item):
     return pl.BlockSpec(item.shape, lambda turn: (0,) * item.ndim, pipeline_mode=pl.Buffered(1))
 
 
-def run_feed_forward(x, mixed, other, top, gain, w_gate_up, w_down_t):
+def run_feed_forward(x, mixed, other, act_grad, norms, w_gate_up):
     tokens, width = x.shape
-    units = w_down_t.shape[1]
+    units = act_grad.shape[1]
     rows = lambda size: pl.BlockSpec((TBLK, size), lambda turn: (turn, 0))
     shape = jax.ShapeDtypeStruct
     return pl.pallas_call(
         feed_forward,
         grid=(tokens // TBLK,),
         out_shape=(
-            shape((tokens, width), F32),
+            shape((tokens, width), BF16),
             shape((tokens, 1), F32),
             shape((tokens, width), BF16),
             shape((tokens, units), BF16),
             shape((tokens, 2 * units), BF16),
             shape((tokens, width), BF16),
-            shape((tokens, width), BF16),
         ),
-        in_specs=[rows(width)] * 4 + [once(gain), once(w_gate_up), once(w_down_t)],
-        out_specs=(
-            rows(width), rows(1), rows(width), rows(units), rows(2 * units), rows(width),
-            rows(width),
-        ),
-        cost_estimate=cost(20),
+        in_specs=[rows(width)] * 3 + [rows(units), once(norms), once(w_gate_up)],
+        out_specs=(rows(width), rows(1), rows(width), rows(units), rows(2 * units), rows(width)),
+        cost_estimate=cost(14),
         name="feed_forward",
-    )(x, mixed, other, top, gain, w_gate_up, w_down_t)
+    )(x, mixed, other, act_grad, norms, w_gate_up)
 
 
 def mixer_forward(gated_ref, scale_ref, gain_ref, attended_ref, w_ref, low_ref, mixed_ref):
     channels = gated_ref.shape[1]
     scale = scale_ref[...].T[:, :1]
-    low_ref[:, :channels] = (gated_ref[...] * scale * gain_ref[...]).astype(BF16)
+    low_ref[:, :channels] = (gated_ref[...].astype(F32) * scale * gain_ref[...]).astype(BF16)
     low_ref[:, channels:] = attended_ref[...]
     mixed_ref[...] = dot(low_ref[...], w_ref[...], NT).astype(BF16)
 
@@ -1389,9 +1468,9 @@
 
 
 def mixer_backward(
-    part_ref, other_ref, after_ref, scale_ref, top_ref, gain_ref,
+    part_ref, other_ref, after_ref, scale_ref, top_ref, norms_ref,
     w_ref, gated_ref, scale_m_ref, gain_m_ref,
-    grad_ref, low_ref, mamba_ref, attended_ref, inner_ref, gain_grad_ref,
+    low_ref, mamba_ref, attended_ref, inner_ref, gain_grad_ref,
 ):
     channels = gated_ref.shape[1]
 
@@ -1401,21 +1480,20 @@
 
     grad = part_ref[...].astype(F32) + other_ref[...].astype(F32)
     scale = scale_ref[...]
-    normed = after_ref[...] * scale
+    normed = after_ref[...].astype(F32) * scale
     gain_grad_ref[:1, :] += jnp.sum(grad * normed, axis=0, keepdims=True)
-    weighted = grad * gain_ref[...]
+    weighted = grad * norms_ref[1:2, :]
     mean = jnp.mean(weighted * normed, axis=-1, keepdims=True)
     total = top_ref[...].astype(F32) + scale * (weighted - normed * mean)
-    grad_ref[...] = total
     low_ref[...] = total.astype(BF16)
     back = dot(low_ref[...], w_ref[...])
     mamba = back[:, :channels]
-    mamba_ref[...] = mamba
+    mamba_ref[...] = mamba.astype(BF16)
     attended_ref[...] = back[:, channels:].astype(BF16)
-    inner_ref[...] = row_sums(mamba * gain_m_ref[...] * gated_ref[...]) * scale_m_ref[...]
-
-
-def run_mixer_backward(part, other, after, scale, top, gain, w_out, gated, scale_m, gain_m):
+    inner_ref[...] = row_sums(mamba * gain_m_ref[...] * gated_ref[...].astype(F32)) * scale_m_ref[...]
+
+
+def run_mixer_backward(part, other, after, scale, top, norms, w_out, gated, scale_m, gain_m):
     tokens, width = after.shape
     channels = gated.shape[1]
     inner = w_out.shape[1]
@@ -1426,26 +1504,25 @@
         mixer_backward,
         grid=(tokens // NBLK,),
         out_shape=(
-            shape((tokens, width), F32),
             shape((tokens, width), BF16),
-            shape((tokens, channels), F32),
+            shape((tokens, channels), BF16),
             shape((tokens, inner - channels), BF16),
             shape((EDGE, tokens), F32),
             shape((EDGE, width), F32),
         ),
         in_specs=[rows(width)] * 3
-        + [rows(1), rows(width), once(gain), once(w_out), rows(channels), lanes, once(gain_m)],
+        + [rows(1), rows(width), once(norms), once(w_out), rows(channels), lanes, once(gain_m)],
         out_specs=(
-            rows(width), rows(width), rows(channels), rows(inner - channels), lanes,
+            rows(width), rows(channels), rows(inner - channels), lanes,
             pl.BlockSpec((EDGE, width), lambda turn: (0, 0)),
         ),
         cost_estimate=cost(8),
         name="mixer_backward",
-    )(part, other, after, scale, top, gain, w_out, gated, scale_m, gain_m)
+    )(part, other, after, scale, top, norms, w_out, gated, scale_m, gain_m)
 
 
 def finish_layer(
-    x_ref, gain_ref, part_ref, other_ref, grad_ref, after_ref, ffn_ref, ffn_other_ref, *refs,
+    x_ref, norms_ref, part_ref, other_ref, grad_ref, after_ref, ffn_ref, ffn_other_ref, *refs,
 ):
     count = len(refs) // 2 - 1
     passed, out_ref, result_ref, handed = refs[:count], refs[count], refs[count + 1], refs[count + 2 :]
@@ -1458,14 +1535,14 @@
     x = x_ref[...].astype(F32)
     scale = lax.rsqrt(jnp.mean(x * x, axis=-1, keepdims=True) + EPSILON)
     normed = x * scale
-    weighted = (part_ref[...].astype(F32) + other_ref[...].astype(F32)) * gain_ref[...]
+    weighted = (part_ref[...].astype(F32) + other_ref[...].astype(F32)) * norms_ref[0:1, :]
     mean = jnp.mean(weighted * normed, axis=-1, keepdims=True)
-    out_ref[...] = grad_ref[...] + scale * (weighted - normed * mean)
+    out_ref[...] = grad_ref[...].astype(F32) + scale * (weighted - normed * mean)
     ffn = ffn_ref[...].astype(F32) + ffn_other_ref[...].astype(F32)
-    result_ref[...] = (after_ref[...] + ffn).astype(BF16)
-
-
-def run_finish(x, gain, part, other, grad, after, ffn, ffn_other, passed):
+    result_ref[...] = (after_ref[...].astype(F32) + ffn).astype(BF16)
+
+
+def run_finish(x, norms, part, other, grad, after, ffn, ffn_other, passed):
     tokens, width = x.shape
     rows = pl.BlockSpec((TBLK, width), lambda turn: (turn, 0))
     return pl.pallas_call(
@@ -1476,11 +1553,11 @@
             jax.ShapeDtypeStruct((tokens, width), BF16),
         )
         + tuple(jax.ShapeDtypeStruct(item.shape, F32) for item in passed),
-        in_specs=[rows, once(gain)] + [rows] * 6 + [once(item) for item in passed],
+        in_specs=[rows, once(norms)] + [rows] * 6 + [once(item) for item in passed],
         out_specs=(rows, rows) + tuple(once(item) for item in passed),
         cost_estimate=cost(8),
         name="finish_layer",
-    )(x, gain, part, other, grad, after, ffn, ffn_other, *passed)
+    )(x, norms, part, other, grad, after, ffn, ffn_other, *passed)
 
 
 def swap(partial):
@@ -1522,14 +1599,7 @@
     )
     in_width = mixer_in.shape[1]
     (w_in,) = gather_rows([mixer_in], devices, 0, [(0, *window) for window in thirds(in_width)])
-    norm1 = w_in[:, in_width - LANES + heads].astype(F32)
-    norm2 = w_in[:, in_width - LANES + heads + 1].astype(F32)
-
-    source = layer_input.astype(F32)
-    scale_one = lax.rsqrt(jnp.mean(source * source, axis=-1, keepdims=True) + EPSILON)
-    normed_one = source * scale_one
-    hidden_one = lax.optimization_barrier((normed_one * norm1).astype(BF16))
-    proj = dot(hidden_one, w_in)
+    hidden_one, proj, norms = run_project(layer_input, w_in, heads)
     params = scan_params(
         conv_x, conv_xb, conv_bc, conv_bcb, dt_bias, a_log, d_skip, w_mnorm
     )
@@ -1554,9 +1624,12 @@
         3,
         [(0, 0, units), (0, units, 2 * units), (1, 0, units)],
     )
-    other, w_gate_up, w_down_t = lax.optimization_barrier((other, w_gate_up, w_down_t))
-    after, scale_two, hidden_two, activated, grad_gu_low, ffn_part, partial_two = run_feed_forward(
-        layer_input, mixed, other, grad_output, norm2[None, :], w_gate_up, w_down_t
+    act_grad = run_product(grad_output, w_down_t, NN, F32)
+    other, w_gate_up, w_down_t, act_grad = lax.optimization_barrier(
+        (other, w_gate_up, w_down_t, act_grad)
+    )
+    after, scale_two, hidden_two, activated, grad_gu_low, partial_two = run_feed_forward(
+        layer_input, mixed, other, act_grad, norms, w_gate_up
     )
     other = swap(partial_two)
     grad_down = dot(grad_output, activated, TN).astype(BF16)
@@ -1571,13 +1644,13 @@
         devices,
         1,
     )
+    ffn_part = run_product(activated, w_down_t, NT, BF16)
     other, mine_gu, grad_down, ffn_part = lax.optimization_barrier(
         (other, mine_gu, grad_down, ffn_part)
     )
     ffn_other = swap(ffn_part)
-    grad_after, grad_mix_low, grad_mamba, grad_attended, inner_m, grad_norm2 = run_mixer_backward(
-        partial_two, other, after, scale_two, grad_output, norm2[None, :], w_out, gated, scale_m,
-        gain_m,
+    grad_mix_low, grad_mamba, grad_attended, inner_m, grad_norm2 = run_mixer_backward(
+        partial_two, other, after, scale_two, grad_output, norms, w_out, gated, scale_m, gain_m
     )
     inner_m = tensor_sum(inner_m) / channels_all
     dqkv = run_attend_backward(qkv, lse, attended, grad_attended, 0, tables)
@@ -1594,18 +1667,16 @@
         [grad_out, grad_down], windows, pieces, shapes, devices,
     )
     ffn_other, grad_proj = lax.optimization_barrier((ffn_other, grad_proj))
-    partial_one, grad_proj = lax.optimization_barrier(
-        (dot(grad_proj, w_in, NT).astype(BF16), grad_proj)
-    )
+    partial_one, grad_norm1 = run_project_back(grad_proj, w_in, layer_input)
+    partial_one, grad_proj = lax.optimization_barrier((partial_one, grad_proj))
     other = swap(partial_one)
-    grad_norm1 = jnp.sum(partial_one.astype(F32) * normed_one, axis=0)
     small = jnp.concatenate(
         [
             small_x[: KCONV + 2].reshape(-1, LANES),
             small_h[:3],
             grad_norm2[0].reshape(-1, LANES),
             small_b[: KCONV + 1].reshape(-1, LANES),
-            grad_norm1.reshape(-1, LANES),
+            grad_norm1[0].reshape(-1, LANES),
         ],
         axis=0,
     )
@@ -1645,7 +1716,7 @@
     shared_cols = tensor_sum(mine_bc)
     passed = (mine_zx, mine_qkv, mine_step, mine_mout, mine_o, mine_gu, mine_down)
     grad_source, result, *passed = run_finish(
-        layer_input, norm1[None, :], partial_one, other, grad_after, after, ffn_part, ffn_other,
+        layer_input, norms, partial_one, other, grad_mix_low, after, ffn_part, ffn_other,
         passed,
     )
     mine_zx, mine_qkv, mine_step, mine_mout, mine_o, mine_gu, mine_down = passed

time: 372 us -> 362 us (0.973)
  Pallas kernels: 289 us -> 314 us
  matrix products: 28.3 us -> 11.2 us
  waiting for transfers between devices: 16.5 us -> 4.26 us
  other arithmetic: 10.5 us -> 3.87 us
    pallas_call x0 -> x4, Pallas kernels: none -> 32.6 us  [the longest x2 12.7 us: run_product(): pl.pallas_call(functools.partial(product_rows, dims), grid=(tokens // TBL...]
    dot_general x4 -> x2, matrix products: 28.3 us -> 11.2 us  [dot(): lax.dot_general(left, right, (dims, ((), ())), preferred_element_type=F32...]
    ppermute x8, waiting for transfers between devices: 16.5 us -> 4.26 us  [swap(): return lax.ppermute(partial, 'tensor', [(0, 1), (1, 0)])]
    pallas_call x1, Pallas kernels: 19.9 us -> 16.1 us  [run_feed_forward(): pl.pallas_call(feed_forward, grid=(tokens // TBLK,), out_shape=(shape((to...]
    convert_element_type x4 -> x0, other arithmetic: 3.79 us -> none  [the longest x1 2.05 us: local(): norm2 = w_in[:, in_width - LANES + heads + 1].astype(F32)]
  transfers between devices with their start and end apart: 8 -> 8, of which waited for: 2 -> 2; matrix products, arithmetic and copies ran while one was open for 7% -> 7% of each run, Pallas kernels for 52% -> 56%
where the time goes in v3:
time: 362 us; the launch traced here: 361 us
  Pallas kernels  314 us (87%)
  local copies, waits for them, and re-layouts  18.5 us (5%)
  matrix products  11.2 us (3%)
  starting transfers between devices  7.55 us (2%)
  waiting for transfers between devices  4.26 us (1%)
  other arithmetic  3.87 us (1%)
    pallas_call x2, Pallas kernels, scatter_product(): pl.pallas_call(functools.partial(product_kernel, devices, groups, len(sha...  74.9 us
    pallas_call x2, Pallas kernels, gather_rows(): pl.pallas_call(functools.partial(gather_kernel, devices, count, windows),...  72.4 us
    pallas_call x1, Pallas kernels, run_scan_backward(): pl.pallas_call(functools.partial(scan_backward, devices, spans, windows,...  37.6 us
    pallas_call x1, Pallas kernels, run_scan_forward(): pl.pallas_call(functools.partial(scan_forward, devices, spans), grid=(spa...  24.1 us
    pallas_call x1, Pallas kernels, run_attend_backward(): pl.pallas_call(attend_backward, grid=(1,), out_shape=jax.ShapeDtypeStruct...  16.2 us
    pallas_call x1, Pallas kernels, run_feed_forward(): pl.pallas_call(feed_forward, grid=(tokens // TBLK,), out_shape=(shape((to...  16.1 us
    pallas_call x2, Pallas kernels, run_product(): pl.pallas_call(functools.partial(product_rows, dims), grid=(tokens // TBL...  12.7 us
    pallas_call x1, Pallas kernels, run_attend_forward(): pl.pallas_call(attend_forward, grid=(1,), out_shape=(jax.ShapeDtypeStruct...  12.5 us
  transfers between devices with their start and end apart: 8, of which 2 were waited for; matrix products, arithmetic and copies ran while one was open for 7% of the time, Pallas kernels for 56%

profile of v3, /device:TPU:0, one launch (start us, length us, event | category | flops | bytes accessed | tf_op | source)
XLA Modules:
  0.0 360.8 jit_solution(10735874445904933267)
XLA Ops:
  3.9 1.6 concatenate.12.refs_0_
  5.6 33.2 %gather_rows.2.w_ref = bf16[1024,2304]{1,0:T(8,128)(2,1)} custom-call(bf16[64,2304]{1,0:T(8,128)(2,1)} %concatenate.12.refs_0_), custom_call_target="tpu_custom_call" | custom-call | flops 3000000000 | tf_op jit(solution)/shard_map/gather_rows/pallas_call | solution.py:204
  39.6 10.2 %project.1 = (bf16[1024,1024]{1,0:T(8,128)(2,1)}, f32[1024,2304]{1,0:T(8,128)}, f32[8,1024]{1,0:T(8,128)}) custom-call(bf16[1024,1024]{1,0:T(8,128)(2,1)} %x_ref.7, bf16[1024,2304]{1,0:T(8,128)(2,1)} %gather_rows.2.w_ref), custom_call_target="tpu_custom_call" | custom-call | flops 8000000000 | tf_op jit(solution)/shard_map/project/pallas_call | solution.py:1364
  50.5 24.1 %scan_forward.1 = (f32[1024,768]{1,0:T(8,128)}, bf16[1024,768]{1,0:T(8,128)(2,1)}, f32[8,1024]{1,0:T(8,128)}, f32[8,128,768]{2,1,0:T(8,128)}, bf16[1024,1024]{1,0:T(8,128)(2,1)}) custom-call(f32[1024,2304]{1,0:T(8,128)} %get-tuple-element.87.z_ref.x_ref.bc_ref.step_ref.q_ref.kv_ref.xp_ref.bp_ref, ...), custom_call_target="tpu_custom_call" | custom-call | flops 20000000000 | tf_op jit(solution)/shard_map/scan_forward/pallas_call | solution.py:914
  74.6 1.6 collective-permute-start
  76.2 12.5 %attend_forward.1 = (bf16[1024,512]{1,0:T(8,128)(2,1)}, f32[8,1024]{1,0:T(8,128)}, bf16[1024,256]{1,0:T(8,128)(2,1)}) custom-call(f32[1024,2304]{1,0:T(8,128)} %get-tuple-element.87.z_ref.x_ref.bc_ref.step_ref.q_ref.kv_ref.xp_ref.bp_ref, f32[1024,2304]{1,0:T(8,128)} %get-tuple-element.87.z_ref.x_ref.bc_ref.step_ref.q_ref.kv_ref.xp_ref.bp_ref, ...), custom_call_target="tpu_custom_call" | custom-call | flops 15000000512 | tf_op jit(solution)/shard_map/attend_forward/pallas_call | solution.py:1245
  90.7 6.7 %mixer_forward.1 = (bf16[1024,1024]{1,0:T(8,128)(2,1)}, bf16[1024,1024]{1,0:T(8,128)(2,1)}) custom-call(bf16[1024,768]{1,0:T(8,128)(2,1)} %get-tuple-element.88.gated_ref, f32[8,1024]{1,0:T(8,128)} %add_rsqrt_fusion.scale_ref.scale_m_ref, f32[1,768]{1,0:T(1,128)} %reshape.91.gain_ref.gain_m_ref, bf16[1024,256]{1,0:T(8,128)(2,1)} %get-tuple-element.90.attended_ref.o_ref, ...), custom_call_target="tpu_custom_call" | custom-call | flops 5000000000 | tf_op jit(solution)/shard_map/mixer_forward/pallas_call | solution.py:1450
  97.9 39.1 %gather_rows.3 = (bf16[1024,2048]{1,0:T(8,128)(2,1)}, bf16[1024,1024]{1,0:T(8,128)(2,1)}) custom-call(bf16[64,2048]{1,0:T(8,128)(2,1)} %bitcast.49, bf16[64,1024]{1,0:T(8,128)(2,1)} %bitcast.60), custom_call_target="tpu_custom_call" | custom-call | flops 3000000000 | tf_op jit(solution)/shard_map/gather_rows/pallas_call | solution.py:204
  137.1 6.4 %product_rows.2.act_grad_ref = f32[1024,1024]{1,0:T(8,128)} custom-call(bf16[1024,1024]{1,0:T(8,128)(2,1)} %top_ref.1, bf16[1024,1024]{1,0:T(8,128)(2,1)} %get-tuple-element.105.right_ref), custom_call_target="tpu_custom_call" | custom-call | flops 4000000000 | tf_op jit(solution)/shard_map/product_rows/pallas_call | solution.py:1335
  143.4 1.9 collective-permute-done.1.other_ref
  146.6 16.1 %feed_forward.1 = (bf16[1024,1024]{1,0:T(8,128)(2,1)}, f32[1024,1]{1,0:T(8,128)}, bf16[1024,1024]{1,0:T(8,128)(2,1)}, bf16[1024,1024]{1,0:T(8,128)(2,1)}, bf16[1...) custom-call(bf16[1024,1024]{1,0:T(8,128)(2,1)} %x_ref.7, bf16[1024,1024]{1,0:T(8,128)(2,1)} %get-tuple-element.93.mixed_ref, ...), custom_call_target="tpu_custom_call" | custom-call | flops 14000000000 | tf_op jit(solution)/shard_map/feed_forward/pallas_call | solution.py:1420
  163.2 32.5 %scatter_product.2.refs_5_ = f32[64,2,1024]{2,1,0:T(2,128)} custom-call(bf16[1024,1024]{1,0:T(8,128)(2,1)} %get-tuple-element.102.left_ref, bf16[1024,2048]{1,0:T(8,128)(2,1)} %get-tuple-element.103.right_ref), custom_call_target="tpu_custom_call" | custom-call | flops 3000000000 | tf_op jit(solution)/shard_map/scatter_product/pallas_call | solution.py:565
  195.8 6.4 %product_rows.3.ffn_ref = bf16[1024,1024]{1,0:T(8,128)(2,1)} custom-call(bf16[1024,1024]{1,0:T(8,128)(2,1)} %get-tuple-element.104.left_ref, bf16[1024,1024]{1,0:T(8,128)(2,1)} %get-tuple-element.105.right_ref), custom_call_target="tpu_custom_call" | custom-call | flops 4000000000 | tf_op jit(solution)/shard_map/product_rows/pallas_call | solution.py:1335
  202.1 5.3 %convert_bitcast_fusion.refs_1_ = bf16[1024,1024]{1,0:T(8,128)(2,1)} fusion(bf16[1024,1024]{1,0:T(8,128)(2,1)} %get-tuple-element.104.left_ref, bf16[1024,1024]{1,0:T(8,128)(2,1)S(1)} %copy-done.15), kind=kOutput, calls=%fused_computation | convolution fusion | flops 2148532224 | bytes 6291456 | tf_op jit(solution)/shard_map/dot_general | solution.py:39
  207.4 2.4 collective-permute-done.2.other_ref
  209.8 11.4 %mixer_backward.1 = (bf16[1024,1024]{1,0:T(8,128)(2,1)}, bf16[1024,768]{1,0:T(8,128)(2,1)}, bf16[1024,256]{1,0:T(8,128)(2,1)}, f32[8,1024]{1,0:T(8,128)}, f32[8,1024]{1,0:T(8,128)}) custom-call(bf16[1024,1024]{1,0:T(8,128)(2,1)} %get-tuple-element.101.part_ref, bf16[1024,1024]{1,0:T(8,128)(2,1)} %collective-permute-done.2.other_ref, ...), custom_call_target="tpu_custom_call" | custom-call | flops 8000000000 | tf_op jit(solution)/shard_map/mixer_backward/pallas_call | solution.py:1503
  223.3 16.2 %attend_backward.1.dqkv_ref = bf16[1024,384]{1,0:T(8,128)(2,1)} custom-call(bf16[1024,512]{1,0:T(8,128)(2,1)} %get-tuple-element.114.qkv_ref, f32[8,1024]{1,0:T(8,128)} %get-tuple-element.115.lse_ref, bf16[1024,256]{1,0:T(8,128)(2,1)} %get-tuple-element.90.attended_ref.o_ref, bf16[1024,256]{1,0:T(8,128)(2,1)} %get-tuple-element.116.do_ref, ...), custom_call_target="tpu_custom_call" | custom-call | flops 16000000000 | tf_op jit(solution)/shard_map/attend_backward/pallas_call | solution.py:1277
  239.6 5.9 %convolution_convert_fusion.refs_0_ = bf16[1024,1024]{1,0:T(8,128)(2,1)} fusion(bf16[1024,1024]{1,0:T(8,128)(2,1)} %get-tuple-element.117.grad_ref, bf16[1024,1024]{1,0:T(8,128)(2,1)} %get-tuple-element.118), kind=kOutput, calls=%fused_computation.1 | convolution fusion | flops 2148532224 | bytes 6291456 | tf_op jit(solution)/shard_map/dot_general | solution.py:39
  246.1 37.6 %scan_backward.1 = (bf16[1024,2304]{1,0:T(8,128)(2,1)}, f32[8,768]{1,0:T(8,128)}, f32[8,256]{1,0:T(8,128)}, f32[8,128]{1,0:T(8,128)}, f32[64,768]{1,0:T(8,128)}, /*index=5*/f32[64,256]{1,0:T(8,128)}, f32[64,1024]{1,0:T(8,128)}) custom-call(f32[1024,2304]{1,0:T(8,128)} %get-tuple-element.87.z_ref.x_ref.bc_ref.step_ref.q_ref.kv_ref.xp_ref.bp_ref, ...), custom_call_target="tpu_custom_call" | custom-call | flops 46999998464 | tf_op jit(solution)/shard_map/scan_backward/pallas_call | solution.py:963
  283.8 9.7 %project_back.1 = (bf16[1024,1024]{1,0:T(8,128)(2,1)}, f32[8,1024]{1,0:T(8,128)}) custom-call(bf16[1024,2304]{1,0:T(8,128)(2,1)} %get-tuple-element.125.grad_ref.right_ref, bf16[1024,2304]{1,0:T(8,128)(2,1)} %gather_rows.2.w_ref, bf16[1024,1024]{1,0:T(8,128)(2,1)} %x_ref.7), custom_call_target="tpu_custom_call" | custom-call | flops 8000000000 | tf_op jit(solution)/shard_map/project_back/pallas_call | solution.py:1397
  296.8 42.3 %scatter_product.3 = (f32[64,2,768]{2,1,0:T(2,128)}, f32[64,256]{1,0:T(8,128)}, f32[64,1,384]{2,1,0:T(1,128)}, f32[12,64]{1,0:T(8,128)}, f32[72,128]{1,0:T(8,128)}) custom-call(bf16[1024,1024]{1,0:T(8,128)(2,1)} %get-tuple-element.124.left_ref, bf16[1024,2304]{1,0:T(8,128)(2,1)} %get-tuple-element.125.grad_ref.right_ref, f32[72,128]{1,0:T(8,128)} %pad.4.refs_0_), custom_call_target="tpu_custom_call" | custom-call | flops 3000000000 | tf_op jit(solution)/shard_map/scatter_product/pallas_call | solution.py:565
  341.8 1.3 slice_bitcast_fusion.2
  343.2 1.3 slice_bitcast_fusion.4
  350.2 9.9 %finish_layer.1 = (f32[1024,1024]{1,0:T(8,128)}, bf16[1024,1024]{1,0:T(8,128)(2,1)}, f32[64,2,768]{2,1,0:T(2,128)}, f32[64,1,384]{2,1,0:T(1,128)}, f32[12,64]{1,...) custom-call(bf16[1024,1024]{1,0:T(8,128)(2,1)} %x_ref.7, ...), custom_call_target="tpu_custom_call" | custom-call | flops 8000000000 | tf_op jit(solution)/shard_map/finish_layer/pallas_call | solution.py:1548
  (86 shorter events, 24.0 us)
Async XLA Ops:
  5.6 33.3 %copy-start.8 = (bf16[768]{0:T(1024)(128)(2,1)S(1)}, bf16[768]{0:T(1024)(128)(2,1)}, u32[]{:S(2)}) copy-start(bf16[768]{0:T(1024)(128)(2,1)} %param.36) | copy-start | bytes 4612
  5.6 33.3 %copy-start.9 = (bf16[768]{0:T(1024)(128)(2,1)S(1)}, bf16[768]{0:T(1024)(128)(2,1)}, u32[]{:S(2)}) copy-start(bf16[768]{0:T(1024)(128)(2,1)} %param.30) | copy-start | bytes 4612
  5.6 33.3 %copy-start.11 = (bf16[256]{0:T(256)(128)(2,1)S(1)}, bf16[256]{0:T(256)(128)(2,1)}, u32[]{:S(2)}) copy-start(bf16[256]{0:T(256)(128)(2,1)} %param.32) | copy-start | bytes 1540
  5.6 33.3 %copy-start.12 = (bf16[12]{0:T(256)(128)(2,1)S(1)}, bf16[12]{0:T(256)(128)(2,1)}, u32[]{:S(2)}) copy-start(bf16[12]{0:T(256)(128)(2,1)} %param.33) | copy-start | bytes 76
  5.6 33.3 %copy-start.13 = (bf16[12]{0:T(256)(128)(2,1)S(1)}, bf16[12]{0:T(256)(128)(2,1)}, u32[]{:S(2)}) copy-start(bf16[12]{0:T(256)(128)(2,1)} %param.34) | copy-start | bytes 76
  5.6 33.3 %copy-start.14 = (bf16[12]{0:T(256)(128)(2,1)S(1)}, bf16[12]{0:T(256)(128)(2,1)}, u32[]{:S(2)}) copy-start(bf16[12]{0:T(256)(128)(2,1)} %param.35) | copy-start | bytes 76
  39.6 10.2 %copy-start.1 = (bf16[768,64]{0,1:T(8,128)(2,1)S(1)}, bf16[768,64]{0,1:T(8,128)(2,1)}, u32[]{:S(2)}) copy-start(bf16[768,64]{0,1:T(8,128)(2,1)} %param.37) | copy-start | bytes 294916
  39.6 10.2 %copy-start.4 = (bf16[1,256,64]{1,2,0:T(8,128)(2,1)S(1)}, bf16[1,256,64]{1,2,0:T(8,128)(2,1)}, u32[]{:S(2)}) copy-start(bf16[1,256,64]{1,2,0:T(8,128)(2,1)} %param.39) | copy-start | bytes 98308
  74.6 14.7 %copy-start = (bf16[64,2,1024]{2,1,0:T(2,128)(2,1)S(1)}, bf16[64,2,1024]{2,1,0:T(2,128)(2,1)}, u32[]{:S(2)}) copy-start(bf16[64,2,1024]{2,1,0:T(2,128)(2,1)} %param.41) | copy-start | bytes 786436
  74.6 15.5 %copy-start.3 = (f32[8,1024]{1,0:T(8,128)S(1)}, f32[8,1024]{1,0:T(8,128)}, u32[]{:S(2)}) copy-start(f32[8,1024]{1,0:T(8,128)} %get-tuple-element.89) | copy-start | bytes 98308
  74.6 15.5 %collective-permute-start = (f32[8,1024]{1,0:T(8,128)}, f32[8,1024]{1,0:T(8,128)S(1)}, u32[]{:S(2)}, u32[]{:S(2)}) collective-permute-start(f32[8,1024]{1,0:T(8,128)} %get-tuple-element.89), channel_id=1, source_target_pairs={{0,1},{1,0},{2,3},{3,2},{4,5},{5,4},{6,7},{7,6},{8,9},{9,8},{10,11... | collective-permute-start | bytes 98312 | tf_op jit(solution)/shard_map/ppermute | solution.py:1564
  97.4 47.8 %collective-permute-start.1 = (bf16[1024,1024]{1,0:T(8,128)(2,1)}, bf16[1024,1024]{1,0:T(8,128)(2,1)S(1)}, u32[]{:S(2)}, u32[]{:S(2)}) collective-permute-start(bf16[1024,1024]{1,0:T(8,128)(2,1)} %get-tuple-element.93.mixed_ref), channel_id=1, source_target_pairs={{0,1},{1,0},{2,3},{3,2},{4,5},{5,4},{6,7},{7,6},{8,9},{9,8},{10,11... | collective-permute-start | bytes 6291464 | tf_op jit(solution)/shard_map/ppermute | solution.py:1564
  162.7 47.1 %collective-permute-start.2 = (bf16[1024,1024]{1,0:T(8,128)(2,1)}, bf16[1024,1024]{1,0:T(8,128)(2,1)}, u32[]{:S(2)}, u32[]{:S(2)}) collective-permute-start(bf16[1024,1024]{1,0:T(8,128)(2,1)} %get-tuple-element.101.part_ref), channel_id=1, source_target_pairs={{0,1},{1,0},{2,3},{3,2},{4,5},{5,4},{6,7},{7,6},{8,9},{9,8},{10,11... | collective-permute-start | bytes 6291464 | tf_op jit(solution)/shard_map/ppermute | solution.py:1564
  195.7 6.4 %copy-start.15 = (bf16[1024,1024]{1,0:T(8,128)(2,1)S(1)}, bf16[1024,1024]{1,0:T(8,128)(2,1)}, u32[]{:S(2)}) copy-start(bf16[1024,1024]{1,0:T(8,128)(2,1)} %top_ref.1) | copy-start | bytes 6291460
  209.8 12.3 %copy-start.16 = (bf16[1024,1024]{1,0:T(8,128)(2,1)S(1)}, bf16[1024,1024]{1,0:T(8,128)(2,1)}, u32[]{:S(2)}) copy-start(bf16[1024,1024]{1,0:T(8,128)(2,1)} %product_rows.3.ffn_ref) | copy-start | bytes 6291460
  221.2 24.3 %collective-permute-start.4 = (f32[8,1024]{1,0:T(8,128)}, f32[8,1024]{1,0:T(8,128)S(1)}, u32[]{:S(2)}, u32[]{:S(2)}) collective-permute-start(f32[8,1024]{1,0:T(8,128)} %get-tuple-element.113), channel_id=1, source_target_pairs={{0,1},{1,0},{2,3},{3,2},{4,5},{5,4},{6,7},{7,6},{8,9},{9,8},{10,11... | collective-permute-start | bytes 98312 | tf_op jit(solution)/shard_map/ppermute | solution.py:1564
  222.1 61.7 %collective-permute-start.3 = (bf16[1024,1024]{1,0:T(8,128)(2,1)S(1)}, bf16[1024,1024]{1,0:T(8,128)(2,1)}, u32[]{:S(2)}, u32[]{:S(2)}) collective-permute-start(bf16[1024,1024]{1,0:T(8,128)(2,1)S(1)} %copy-done.16), channel_id=1, source_target_pairs={{0,1},{1,0},{2,3},{3,2},{4,5},{5,4},{6,7},{7,6},{8,9},{9,8},{10,11... | collective-permute-start | bytes 6291464 | tf_op jit(solution)/shard_map/ppermute | solution.py:1564
  283.8 11.3 %copy-start.5 = (f32[8,768]{1,0:T(8,128)S(1)}, f32[8,768]{1,0:T(8,128)}, u32[]{:S(2)}) copy-start(f32[8,768]{1,0:T(8,128)} %get-tuple-element.126) | copy-start | bytes 73732
  283.8 11.3 %copy-start.7 = (f32[8,256]{1,0:T(8,128)S(1)}, f32[8,256]{1,0:T(8,128)}, u32[]{:S(2)}) copy-start(f32[8,256]{1,0:T(8,128)} %get-tuple-element.129) | copy-start | bytes 24580
  283.8 11.3 %copy-start.10 = (f32[8,128]{1,0:T(8,128)S(1)}, f32[8,128]{1,0:T(8,128)}, u32[]{:S(2)}) copy-start(f32[8,128]{1,0:T(8,128)} %get-tuple-element.127) | copy-start | bytes 12292
  293.5 55.3 %collective-permute-start.5 = (bf16[1024,1024]{1,0:T(8,128)(2,1)}, bf16[1024,1024]{1,0:T(8,128)(2,1)S(1)}, u32[]{:S(2)}, u32[]{:S(2)}) collective-permute-start(bf16[1024,1024]{1,0:T(8,128)(2,1)} %get-tuple-element.123.part_ref), channel_id=1, source_target_pairs={{0,1},{1,0},{2,3},{3,2},{4,5},{5,4},{6,7},{7,6},{8,9},{9,8},{10,11... | collective-permute-start | bytes 6291464 | tf_op jit(solution)/shard_map/ppermute | solution.py:1564
  339.9 6.5 %collective-permute-start.6 = (f32[18,128]{1,0:T(8,128)S(1)}, f32[18,128]{1,0:T(8,128)S(1)}, u32[]{:S(2)}, u32[]{:S(2)}) collective-permute-start(f32[18,128]{1,0:T(8,128)S(1)} %slice.69), channel_id=1, source_target_pairs={{0,1},{1,0},{2,3},{3,2},{4,5},{5,4},{6,7},{7,6},{8,9},{9,8},{10,11... | collective-permute-start | bytes 27656 | tf_op jit(solution)/shard_map/ppermute | solution.py:1564
  348.8 11.3 %collective-permute-start.7 = (f32[64,256]{1,0:T(8,128)}, f32[64,256]{1,0:T(8,128)S(1)}, u32[]{:S(2)}, u32[]{:S(2)}) collective-permute-start(f32[64,256]{1,0:T(8,128)} %get-tuple-element.145), channel_id=1, source_target_pairs={{0,1},{1,0},{2,3},{3,2},{4,5},{5,4},{6,7},{7,6},{8,9},{9,8},{10,11... | collective-permute-start | bytes 196616 | tf_op jit(solution)/shard_map/ppermute | solution.py:1564
  350.2 9.9 %copy-start.6 = (f32[64,256]{1,0:T(8,128)S(1)}, f32[64,256]{1,0:T(8,128)}, u32[]{:S(2)}) copy-start(f32[64,256]{1,0:T(8,128)} %get-tuple-element.145) | copy-start | bytes 196612
  (3 other events, 8.7 us)

commit v4 on v3

--- a/solution.py
+++ b/solution.py
@@ -521,16 +521,21 @@
         target[start : start + LANES, :] = source[:, start : start + LANES].T
 
 
-def product_kernel(devices, groups, outs, summed, left_ref, right_ref, *refs):
+def product_kernel(devices, groups, outs, places, summed, left_ref, right_ref, *refs):
     values = refs[:summed]
     refs = refs[summed:]
     pieces_out, refs = refs[:outs], refs[outs:]
-    totals_out, refs = refs[:summed], refs[summed:]
-    turned, scratch = refs[0], refs[1:]
     total = None
     if summed:
-        scratch, rest = scratch[:-7], scratch[-7:]
-        total = Total(devices, values[0], totals_out[0], rest)
+        total_out, refs = refs[0], refs[1:]
+    turned, scratch = refs[0], refs[1:]
+    if summed:
+        scratch, rest = scratch[:-8], scratch[-8:]
+        together = rest[0]
+        together[...] = jnp.zeros_like(together)
+        for at, (which, row, lane) in enumerate(places):
+            together[at : at + 1, :] = values[which][row : row + 1, lane : lane + LANES]
+        total = Total(devices, together, total_out, rest[1:])
     each = len(scratch) // len(groups)
     rings = [
         RingScatter(
@@ -554,22 +559,24 @@
         total.finish()
 
 
-def scatter_product(left, right, groups, shapes, devices, collective, values=()):
+def scatter_product(left, right, groups, shapes, devices, collective, values=(), places=()):
     vmem = pl.BlockSpec(memory_space=pltpu.VMEM)
     rows = left.shape[1] // devices
     scratch = [pltpu.VMEM(left.shape[::-1], BF16)]
     for windows, pieces in groups:
         scratch += scatter_scratch(windows, rows, devices)
-    for item in values:
-        scratch += total_scratch(item, devices)
+    totals = ()
+    if values:
+        total = jax.ShapeDtypeStruct((len(places) + -len(places) % EDGE, LANES), F32)
+        totals = (total,)
+        scratch += [pltpu.VMEM(total.shape, F32)] + total_scratch(total, devices)
     return pl.pallas_call(
         functools.partial(
-            product_kernel, devices, groups, len(shapes), len(values)
+            product_kernel, devices, groups, len(shapes), places, len(values)
         ),
-        out_shape=tuple(jax.ShapeDtypeStruct(shape, F32) for shape in shapes)
-        + tuple(jax.ShapeDtypeStruct(item.shape, F32) for item in values),
+        out_shape=tuple(jax.ShapeDtypeStruct(shape, F32) for shape in shapes) + totals,
         in_specs=[vmem] * (2 + len(values)),
-        out_specs=(vmem,) * (len(shapes) + len(values)),
+        out_specs=(vmem,) * (len(shapes) + len(totals)),
         scratch_shapes=scratch,
         compiler_params=pltpu.CompilerParams(collective_id=collective, has_side_effects=True),
         cost_estimate=cost(3),
@@ -613,11 +620,32 @@
     return jnp.maximum(raw, 0.0) + jnp.log1p(jnp.exp(-jnp.abs(raw)))
 
 
-def conv_window(buffer, taps, bias, span):
-    total = bias + taps[0:1, :] * buffer[EDGE - 3 : EDGE - 3 + span, :]
-    for tap in range(1, KCONV):
-        start = EDGE - 3 + tap
-        total = total + taps[tap : tap + 1, :] * buffer[start : start + span, :]
+def shifted(values, edge, ahead):
+    span = values.shape[0]
+    moves = range(1, KCONV)
+    row, col = iota((span, span), 0), iota((span, span), 1)
+    mask = jnp.concatenate(
+        [(col == (row + move if ahead else row - move)).astype(BF16) for move in moves], axis=0
+    )
+    moved = pick_left(mask, values, 2)
+    place = iota(edge.shape, 0)
+    result = []
+    for move in moves:
+        part = moved[(move - 1) * span : move * span]
+        if ahead:
+            into = jnp.where(place >= EDGE - move, pltpu.roll(edge, EDGE - move, 0), 0.0)
+            part = jnp.concatenate([part[:-EDGE], part[-EDGE:] + into], axis=0)
+        else:
+            into = jnp.where(place < move, pltpu.roll(edge, move, 0), 0.0)
+            part = jnp.concatenate([part[:EDGE] + into, part[EDGE:]], axis=0)
+        result.append(part)
+    return result
+
+
+def apply_taps(values, moved, taps):
+    total = taps[KCONV - 1 : KCONV, :] * values
+    for move, part in enumerate(moved, 1):
+        total = total + taps[KCONV - 1 - move : KCONV - move, :] * part
     return total
 
 
@@ -651,7 +679,7 @@
     z_ref, x_ref, bc_ref, step_ref,
     tap_ref, tapb_ref, row_ref, shard_ref,
     y_ref, gated_ref, square_ref, enter_ref, all_ref,
-    state, xbuf, bbuf, *sems,
+    state, edge, *sems,
 ):
     span, channels = x_ref.shape
     ring = RingGather(devices, shard_ref, all_ref, sems)
@@ -666,18 +694,16 @@
     @pl.when(pl.program_id(0) == 0)
     def _():
         state[...] = jnp.zeros_like(state)
-        xbuf[span:, :] = jnp.zeros((EDGE, channels), F32)
-        bbuf[span:, :] = jnp.zeros((EDGE, 2 * NS), F32)
-
-    xbuf[:EDGE, :] = xbuf[span:, :]
-    bbuf[:EDGE, :] = bbuf[span:, :]
-    xbuf[EDGE:, :] = x_ref[...]
-    bbuf[EDGE:, :] = bc_ref[...]
+        edge[...] = jnp.zeros_like(edge)
+
     spread = head_spread(channels)
     bias, gain, biasb, stepb, decay, skip = unpack_rows(row_ref, spread)
-    taps, tapsb = tap_ref[...].astype(F32), tapb_ref[...].astype(F32)
-    inputs = jax.nn.silu(conv_window(xbuf, taps, bias, span))
-    shared = jax.nn.silu(conv_window(bbuf, tapsb, biasb, span))
+    taps = jnp.concatenate([tap_ref[...], tapb_ref[...]], axis=1).astype(F32)
+    before = jnp.concatenate([x_ref[...], bc_ref[...]], axis=1)
+    conv = apply_taps(before, shifted(before, edge[...], False), taps)
+    edge[...] = before[-EDGE:]
+    conv = jax.nn.silu(conv + jnp.concatenate([bias, biasb], axis=1))
+    inputs, shared = conv[:, :channels], conv[:, channels:]
     raw, step, cum, step_w, tails_w, grown_w = span_rates(step_ref, stepb, decay, spread, span)
     cum_rows = cum.T
     b_low = shared[:, :NS].astype(BF16)
@@ -720,9 +746,9 @@
     *refs,
 ):
     sent, refs = refs[:count], refs[count:]
-    (grad_ref, gx_ref, gb_ref, gh_ref), refs = refs[:4], refs[4:]
+    (grad_ref, gx_ref, gh_ref), refs = refs[:3], refs[3:]
     outs, refs = refs[:outs_count], refs[outs_count:]
-    (dstate, xbuf, bbuf, dxbuf, dbbuf, du_buf, col_buf), scratch = refs[:7], refs[7:]
+    (dstate, dedge, du_buf, col_buf), scratch = refs[:4], refs[4:]
     ring = RingScatter(devices, windows, pieces, sent, outs, scratch)
     span, channels = x_ref.shape
     turn = pl.program_id(0)
@@ -732,27 +758,22 @@
         ring.greet()
         ring.begin()
         dstate[...] = jnp.zeros_like(dstate)
-        dxbuf[...] = jnp.zeros_like(dxbuf)
-        dbbuf[...] = jnp.zeros_like(dbbuf)
+        dedge[...] = jnp.zeros_like(dedge)
         col_buf[...] = jnp.zeros_like(col_buf)
         gx_ref[...] = jnp.zeros_like(gx_ref)
-        gb_ref[...] = jnp.zeros_like(gb_ref)
         gh_ref[...] = jnp.zeros_like(gh_ref)
 
     inside = (turn < spans - 1).astype(F32)
-    xbuf[:EDGE, :] = xp_ref[...] * inside
-    bbuf[:EDGE, :] = bp_ref[...] * inside
-    xbuf[EDGE:, :] = x_ref[...]
-    bbuf[EDGE:, :] = bc_ref[...]
+    before = jnp.concatenate([x_ref[...], bc_ref[...]], axis=1)
+    edge = jnp.concatenate([xp_ref[...], bp_ref[...]], axis=1) * inside
     spread = head_spread(channels)
     bias, gain, biasb, stepb, decay, skip = unpack_rows(row_ref, spread)
-    taps, tapsb = tap_ref[...].astype(F32), tapb_ref[...].astype(F32)
-    conv = conv_window(xbuf, taps, bias, span)
+    taps = jnp.concatenate([tap_ref[...], tapb_ref[...]], axis=1).astype(F32)
+    moved = shifted(before, edge, False)
+    conv = apply_taps(before, moved, taps) + jnp.concatenate([bias, biasb], axis=1)
     sig = jax.nn.sigmoid(conv)
-    inputs = conv * sig
-    convb = conv_window(bbuf, tapsb, biasb, span)
-    sigb = jax.nn.sigmoid(convb)
-    shared = convb * sigb
+    swished = conv * sig
+    inputs, shared = swished[:, :channels], swished[:, channels:]
     b_low = shared[:, :NS].astype(BF16)
     c_low = shared[:, NS:].astype(BF16)
     raw, step, cum, step_w, tails_w, grown_w = span_rates(step_ref, stepb, decay, spread, span)
@@ -836,31 +857,17 @@
     gh_ref[2:3, :] += sums[2 * span + 1 : 2 * span + 2, :]
 
     dinputs = du * step_w + skip * dy
-    dxbuf[span:, :] = dxbuf[:EDGE, :]
-    dbbuf[span:, :] = dbbuf[:EDGE, :]
-    dconv = dinputs * (sig * (1.0 + conv * (1.0 - sig)))
-    dconvb = jnp.concatenate([db, dc], axis=1) * (sigb * (1.0 + convb * (1.0 - sigb)))
-    dxbuf[:span, :] = dconv
-    dbbuf[:span, :] = dconvb
-    dx = jnp.zeros_like(dconv)
-    dbc = jnp.zeros_like(dconvb)
-    for tap in range(KCONV):
-        back = KCONV - 1 - tap
-        start = EDGE - 3 + tap
-        dx = dx + taps[tap : tap + 1, :] * dxbuf[back : back + span, :]
-        dbc = dbc + tapsb[tap : tap + 1, :] * dbbuf[back : back + span, :]
-        gx_ref[tap : tap + 1, :] += jnp.sum(
-            dconv * xbuf[start : start + span, :], axis=0, keepdims=True
-        )
-        gb_ref[tap : tap + 1, :] += jnp.sum(
-            dconvb * bbuf[start : start + span, :], axis=0, keepdims=True
-        )
+    dconv = jnp.concatenate([dinputs, db, dc], axis=1) * (sig * (1.0 + conv * (1.0 - sig)))
+    dbefore = apply_taps(dconv, shifted(dconv, dedge[...], True), taps)
+    dedge[...] = dconv[:EDGE]
+    gx_ref[KCONV - 1 : KCONV, :] += jnp.sum(dconv * before, axis=0, keepdims=True)
+    for move, part in enumerate(moved, 1):
+        tap = KCONV - 1 - move
+        gx_ref[tap : tap + 1, :] += jnp.sum(dconv * part, axis=0, keepdims=True)
     gx_ref[KCONV : KCONV + 1, :] += jnp.sum(dconv, axis=0, keepdims=True)
-    gb_ref[KCONV : KCONV + 1, :] += jnp.sum(dconvb, axis=0, keepdims=True)
-    gx_ref[KCONV + 1 : KCONV + 2, :] += gain_grad
+    gx_ref[KCONV + 1 : KCONV + 2, :channels] += gain_grad
     width = 2 * channels + 2 * NS
-    grad_ref[:, channels : 2 * channels] = dx.astype(BF16)
-    grad_ref[:, 2 * channels : width] = dbc.astype(BF16)
+    grad_ref[:, channels:width] = dbefore.astype(BF16)
     grad_ref[:, width : width + dqkv_ref.shape[1]] = dqkv_ref[...]
     grad_ref[:, width + dqkv_ref.shape[1] :] = draw.astype(BF16)
     for step in range(ring.ahead):
@@ -933,8 +940,7 @@
         ),
         scratch_shapes=[
             pltpu.VMEM((NS, channels), F32),
-            pltpu.VMEM((SPAN + EDGE, channels), F32),
-            pltpu.VMEM((SPAN + EDGE, 2 * NS), F32),
+            pltpu.VMEM((EDGE, channels + 2 * NS), F32),
         ]
         + gather_sems(devices),
         compiler_params=pltpu.CompilerParams(collective_id=2, has_side_effects=True),
@@ -967,8 +973,7 @@
         grid=(spans,),
         out_shape=(
             jax.ShapeDtypeStruct((tokens, width), BF16),
-            jax.ShapeDtypeStruct((EDGE, channels), F32),
-            jax.ShapeDtypeStruct((EDGE, 2 * NS), F32),
+            jax.ShapeDtypeStruct((EDGE, channels + 2 * NS), F32),
             jax.ShapeDtypeStruct((EDGE, LANES), F32),
         )
         + shapes,
@@ -990,17 +995,13 @@
         + [pl.BlockSpec(memory_space=pl.ANY)] * len(sent),
         out_specs=(
             rows(width, 0),
-            keep((EDGE, channels)),
-            keep((EDGE, 2 * NS)),
+            keep((EDGE, channels + 2 * NS)),
             keep((EDGE, LANES)),
         )
         + tuple(keep(item.shape) for item in shapes),
         scratch_shapes=[
             pltpu.VMEM((NS, channels), F32),
-            pltpu.VMEM((SPAN + EDGE, channels), F32),
-            pltpu.VMEM((SPAN + EDGE, 2 * NS), F32),
-            pltpu.VMEM((SPAN + EDGE, channels), F32),
-            pltpu.VMEM((SPAN + EDGE, 2 * NS), F32),
+            pltpu.VMEM((EDGE, channels + 2 * NS), F32),
             pltpu.VMEM((SPAN, channels), F32),
             pltpu.VMEM((LANES, SPAN), F32),
         ]
@@ -1521,16 +1522,38 @@
     )(part, other, after, scale, top, norms, w_out, gated, scale_m, gain_m)
 
 
+def lane_row(ref, first, count):
+    return jnp.concatenate([ref[i : i + 1, :] for i in range(first, first + count)], axis=1)
+
+
+def own_lanes(ref, first, size):
+    start = lax.axis_index("dp") * size
+    row = ref[pl.ds(first + lax.div(start, LANES), 1), :]
+    row = jnp.broadcast_to(row, (EDGE, LANES))
+    return pltpu.roll(row, lax.rem(LANES - lax.rem(start, LANES), LANES), 1)[0, :size]
+
+
 def finish_layer(
-    x_ref, norms_ref, part_ref, other_ref, grad_ref, after_ref, ffn_ref, ffn_other_ref, *refs,
+    norm_at, x_ref, norms_ref, part_ref, other_ref, grad_ref, after_ref, ffn_ref, ffn_other_ref,
+    total_ref, *refs,
 ):
-    count = len(refs) // 2 - 1
+    count = (len(refs) - 9) // 2
     passed, out_ref, result_ref, handed = refs[:count], refs[count], refs[count + 1], refs[count + 2 :]
+    tap_ref, bias_ref, gain_ref, step_ref, log_ref, skip_ref, norm_ref = handed[count:]
 
     @pl.when(pl.program_id(0) == 0)
     def _():
         for source, target in zip(passed, handed):
             target[...] = source[...]
+        rows = tap_ref.shape[1] // LANES
+        for tap in range(KCONV):
+            tap_ref[tap : tap + 1, :] = lane_row(total_ref, tap * rows, rows)
+        bias_ref[...] = lane_row(total_ref, KCONV * rows, rows)[0]
+        gain_ref[...] = lane_row(total_ref, (KCONV + 1) * rows, rows)[0]
+        at = (KCONV + 2) * rows
+        for place, ref in enumerate((step_ref, log_ref, skip_ref)):
+            ref[...] = total_ref[at + place : at + place + 1, :][0, : ref.shape[0]]
+        norm_ref[...] = own_lanes(total_ref, norm_at, norm_ref.shape[0])
 
     x = x_ref[...].astype(F32)
     scale = lax.rsqrt(jnp.mean(x * x, axis=-1, keepdims=True) + EPSILON)
@@ -1542,22 +1565,52 @@
     result_ref[...] = (after_ref[...].astype(F32) + ffn).astype(BF16)
 
 
-def run_finish(x, norms, part, other, grad, after, ffn, ffn_other, passed):
+def run_finish(
+    x, norms, part, other, grad, after, ffn, ffn_other, total, passed, channels, heads, shard,
+    norm_at,
+):
     tokens, width = x.shape
     rows = pl.BlockSpec((TBLK, width), lambda turn: (turn, 0))
+    shape = lambda *sizes: jax.ShapeDtypeStruct(sizes, F32)
+    small = (
+        shape(KCONV, channels), shape(channels), shape(channels), shape(heads), shape(heads),
+        shape(heads), shape(shard),
+    )
     return pl.pallas_call(
-        finish_layer,
+        functools.partial(finish_layer, norm_at),
         grid=(tokens // TBLK,),
-        out_shape=(
-            jax.ShapeDtypeStruct((tokens, width), F32),
-            jax.ShapeDtypeStruct((tokens, width), BF16),
-        )
-        + tuple(jax.ShapeDtypeStruct(item.shape, F32) for item in passed),
-        in_specs=[rows, once(norms)] + [rows] * 6 + [once(item) for item in passed],
-        out_specs=(rows, rows) + tuple(once(item) for item in passed),
+        out_shape=(shape(tokens, width), jax.ShapeDtypeStruct((tokens, width), BF16))
+        + tuple(shape(*item.shape) for item in passed)
+        + small,
+        in_specs=[rows, once(norms)] + [rows] * 6 + [once(total)] + [once(item) for item in passed],
+        out_specs=(rows, rows) + tuple(once(item) for item in passed + small),
         cost_estimate=cost(8),
         name="finish_layer",
-    )(x, norms, part, other, grad, after, ffn, ffn_other, *passed)
+    )(x, norms, part, other, grad, after, ffn, ffn_other, total, *passed)
+
+
+def finish_shared(at, total_ref, cross_ref, mine_ref, other_ref, bc_ref, tap_ref, bias_ref, norm_ref, both):
+    half = lax.axis_index("tensor")
+    cols = pl.ds(pl.multiple_of(half * LANES, LANES), LANES)
+    bc_ref[...] = mine_ref[:, cols] + other_ref[:, cols]
+    both[...] = total_ref[...] + cross_ref[...]
+    for tap in range(KCONV):
+        tap_ref[tap : tap + 1, :] = both[pl.ds(at + 2 * tap + half, 1), :]
+    bias_ref[...] = both[pl.ds(at + 2 * KCONV + half, 1), :][0]
+    norm_ref[...] = own_lanes(both, at + 2 * KCONV + 2, norm_ref.shape[0])
+
+
+def run_finish_shared(total, cross, mine, other, shard, at):
+    vmem = pl.BlockSpec(memory_space=pltpu.VMEM)
+    shape = lambda *sizes: jax.ShapeDtypeStruct(sizes, F32)
+    return pl.pallas_call(
+        functools.partial(finish_shared, at),
+        out_shape=(shape(mine.shape[0], LANES), shape(KCONV, LANES), shape(LANES), shape(shard)),
+        in_specs=[vmem] * 4,
+        out_specs=(vmem,) * 4,
+        scratch_shapes=[pltpu.VMEM(total.shape, F32)],
+        name="finish_shared",
+    )(total, cross, mine, other)
 
 
 def swap(partial):
@@ -1662,7 +1715,7 @@
         (1, 0, units, 2, None),
     ]
     shapes = [(shard, channels), (shard, attn_width), (shard, units)]
-    grad_proj, small_x, small_b, small_h, mine_mout, mine_o, mine_down = run_scan_backward(
+    grad_proj, small_x, small_h, mine_mout, mine_o, mine_down = run_scan_backward(
         proj, y, entering, grad_mamba, scale_m, inner_m, dqkv, params,
         [grad_out, grad_down], windows, pieces, shapes, devices,
     )
@@ -1670,20 +1723,14 @@
     partial_one, grad_norm1 = run_project_back(grad_proj, w_in, layer_input)
     partial_one, grad_proj = lax.optimization_barrier((partial_one, grad_proj))
     other = swap(partial_one)
-    small = jnp.concatenate(
-        [
-            small_x[: KCONV + 2].reshape(-1, LANES),
-            small_h[:3],
-            grad_norm2[0].reshape(-1, LANES),
-            small_b[: KCONV + 1].reshape(-1, LANES),
-            grad_norm1[0].reshape(-1, LANES),
-        ],
-        axis=0,
-    )
-    small_rows = small.shape[0]
-    cross_rows = (KCONV + 1) * 2 * NS // LANES + width // LANES
-    cross_at = small_rows - cross_rows
-    small = jnp.pad(small, ((0, -small_rows % EDGE), (0, 0)))
+    lanes_of = lambda size, start=0: range(start, start + size, LANES)
+    places = [(0, row, lane) for row in range(KCONV + 2) for lane in lanes_of(channels)]
+    places += [(1, row, 0) for row in range(3)]
+    norm_at = len(places)
+    places += [(2, 0, lane) for lane in lanes_of(width)]
+    cross_at = len(places)
+    places += [(0, row, lane) for row in range(KCONV + 1) for lane in lanes_of(2 * NS, channels)]
+    places += [(3, 0, lane) for lane in lanes_of(width)]
     shared_at = 2 * channels
     step_at = qkv_at + qkv_width
     mine_zx, mine_bc, mine_qkv, mine_step, small = scatter_product(
@@ -1709,52 +1756,40 @@
         ],
         devices,
         5,
-        (small,),
+        (small_x, small_h, grad_norm2, grad_norm1),
+        places,
     )
     other, mine_bc = lax.optimization_barrier((other, mine_bc))
-    crossing = tensor_sum(small[cross_at : cross_at + cross_rows])
-    shared_cols = tensor_sum(mine_bc)
     passed = (mine_zx, mine_qkv, mine_step, mine_mout, mine_o, mine_gu, mine_down)
-    grad_source, result, *passed = run_finish(
-        layer_input, norms, partial_one, other, grad_mix_low, after, ffn_part, ffn_other,
-        passed,
-    )
-    mine_zx, mine_qkv, mine_step, mine_mout, mine_o, mine_gu, mine_down = passed
-
-    half = NS * 2 // lax.axis_size("tensor")
-    begin = lax.axis_index("tensor") * half
-    grad_bc = lax.dynamic_slice_in_dim(shared_cols, begin, half, 1)
-    x_rows = (KCONV + 2) * channels // LANES
-    norm_rows = width // LANES
-    total_x = small[:x_rows].reshape(KCONV + 2, channels)
-    total_h = small[x_rows : x_rows + 3]
-    norm2_total = small[x_rows + 3 : cross_at].reshape(width)
-    total_b = crossing[: cross_rows - norm_rows].reshape(KCONV + 1, 2 * NS)
-    total_b = lax.dynamic_slice_in_dim(total_b, begin, half, 1)
-    norm1_total = crossing[cross_rows - norm_rows :].reshape(width)
-    norms = [
-        lax.dynamic_slice_in_dim(item, lax.axis_index("dp") * shard, shard, 0)
-        for item in (norm1_total, norm2_total)
-    ]
+    cross, other_bc = swap(small), swap(mine_bc)
+    grad_source, result, *rest = run_finish(
+        layer_input, norms, partial_one, other, grad_mix_low, after, ffn_part, ffn_other, small,
+        passed, channels, heads, shard, norm_at,
+    )
+    mine_zx, mine_qkv, mine_step, mine_mout, mine_o, mine_gu, mine_down = rest[: len(passed)]
+    grad_taps, grad_bias, grad_gain, grad_steps, grad_log, grad_skip, own_norm2 = rest[len(passed) :]
+    grad_bc, grad_tapsb, grad_biasb, own_norm1 = run_finish_shared(
+        small, cross, mine_bc, other_bc, shard, cross_at
+    )
     return (
         result,
         grad_source,
-        norms[0],
+        own_norm1,
         mine_zx,
         grad_bc,
         mine_step.T,
-        total_x[:KCONV],
-        total_x[KCONV],
-        total_b[:KCONV],
-        total_b[KCONV],
-        total_h[0, :heads],
-        total_h[1, :heads],
-        total_h[2, :heads],
-        total_x[KCONV + 1],
+        grad_taps,
+        grad_bias,
+        grad_tapsb,
+        grad_biasb,
+        grad_steps,
+        grad_log,
+        grad_skip,
+        grad_gain,
         mine_mout.T,
         mine_qkv,
         mine_o.T.reshape(output_weight.shape),
-        norms[1],
+        own_norm2,
         mine_gu,
         mine_down.T,
     )

time: 362 us -> 359 us (level)
  local copies, waits for them, and re-layouts: 18.5 us -> 13.5 us
    slice x8 -> x0, local copies, waits for them, and re-layouts: 4.15 us -> none  [the longest x2 1.32 us: local(): total_x[:KCONV]]
    concatenate x1, local copies, waits for them, and re-layouts: 0.09 us -> 4.12 us  [scan_params(): rows = jnp.concatenate(flat).astype(F32).reshape(-1, LANES)]
    pallas_call x1 -> x2, Pallas kernels: 9.87 us -> 11.6 us  [the longest x1 10 us: run_finish(): pl.pallas_call(functools.partial(finish_layer, norm_at), grid=(tokens //...]
  transfers between devices with their start and end apart: 8 -> 8, of which waited for: 2 -> 3; matrix products, arithmetic and copies ran while one was open for 7% -> 4% of each run, Pallas kernels for 56% -> 57%
where the time goes in v4:
time: 359 us; the launch traced here: 358 us
  Pallas kernels  315 us (88%)
  local copies, waits for them, and re-layouts  13.5 us (4%)
  matrix products  11.2 us (3%)
  starting transfers between devices  7.56 us (2%)
  waiting for transfers between devices  6.91 us (2%)
    pallas_call x2, Pallas kernels, scatter_product(): pl.pallas_call(functools.partial(product_kernel, devices, groups, len(sha...  74.8 us
    pallas_call x2, Pallas kernels, gather_rows(): pl.pallas_call(functools.partial(gather_kernel, devices, count, windows),...  72.3 us
    pallas_call x1, Pallas kernels, run_scan_backward(): pl.pallas_call(functools.partial(scan_backward, devices, spans, windows,...  36.8 us
    pallas_call x1, Pallas kernels, run_scan_forward(): pl.pallas_call(functools.partial(scan_forward, devices, spans), grid=(spa...  24.1 us
    pallas_call x1, Pallas kernels, run_attend_backward(): pl.pallas_call(attend_backward, grid=(1,), out_shape=jax.ShapeDtypeStruct...  16.2 us
    pallas_call x1, Pallas kernels, run_feed_forward(): pl.pallas_call(feed_forward, grid=(tokens // TBLK,), out_shape=(shape((to...  16.1 us
    pallas_call x2, Pallas kernels, run_product(): pl.pallas_call(functools.partial(product_rows, dims), grid=(tokens // TBL...  12.7 us
    pallas_call x1, Pallas kernels, run_attend_forward(): pl.pallas_call(attend_forward, grid=(1,), out_shape=(jax.ShapeDtypeStruct...  12.5 us
  transfers between devices with their start and end apart: 8, of which 3 were waited for; matrix products, arithmetic and copies ran while one was open for 4% of the time, Pallas kernels for 57%

profile of v4, /device:TPU:0, one launch (start us, length us, event | category | flops | bytes accessed | tf_op | source)
XLA Modules:
  0.0 357.7 jit_solution(1233958712372433396)
XLA Ops:
  0.7 4.1 %concatenate.10 = bf16[3072]{0:T(1024)(128)(2,1)S(1)} concatenate(bf16[768]{0:T(1024)(128)(2,1)} %param.30, bf16[768]{0:T(1024)(128)(2,1)} %param.36, bf16[256]{0:T(256)(128)(2,1)} %param.32, bf16[12]{0:T(256)(128)(2,1)} %param.33, bf16[116]{0:T(256)(128)(2,1)S(1)} %broadcast_in_dim.23, bf16[12]{0:T(256)(128)(2,1)} %param.34, bf16[116]{0:T(256)(128)(2,1)S(1)} %broadcast_in_dim.23, ...), dimensions={0} | concatenate | bytes 12288 | tf_op jit(solution)/shard_map/concatenate | solution.py:884
  8.7 1.6 concatenate.9.refs_0_
  10.3 33.2 %gather_rows.2.w_ref = bf16[1024,2304]{1,0:T(8,128)(2,1)} custom-call(bf16[64,2304]{1,0:T(8,128)(2,1)} %concatenate.9.refs_0_), custom_call_target="tpu_custom_call" | custom-call | flops 3000000000 | tf_op jit(solution)/shard_map/gather_rows/pallas_call | solution.py:204
  44.2 10.2 %project.1 = (bf16[1024,1024]{1,0:T(8,128)(2,1)}, f32[1024,2304]{1,0:T(8,128)}, f32[8,1024]{1,0:T(8,128)}) custom-call(bf16[1024,1024]{1,0:T(8,128)(2,1)} %x_ref.7, bf16[1024,2304]{1,0:T(8,128)(2,1)} %gather_rows.2.w_ref), custom_call_target="tpu_custom_call" | custom-call | flops 8000000000 | tf_op jit(solution)/shard_map/project/pallas_call | solution.py:1365
  54.4 24.1 %scan_forward.1 = (f32[1024,768]{1,0:T(8,128)}, bf16[1024,768]{1,0:T(8,128)(2,1)}, f32[8,1024]{1,0:T(8,128)}, f32[8,128,768]{2,1,0:T(8,128)}, bf16[1024,1024]{1,0:T(8,128)(2,1)}) custom-call(f32[1024,2304]{1,0:T(8,128)} %get-tuple-element.97.z_ref.x_ref.bc_ref.step_ref.q_ref.kv_ref.xp_ref.bp_ref, ...), custom_call_target="tpu_custom_call" | custom-call | flops 20000000000 | tf_op jit(solution)/shard_map/scan_forward/pallas_call | solution.py:921
  78.5 1.6 collective-permute-start
  80.1 12.5 %attend_forward.1 = (bf16[1024,512]{1,0:T(8,128)(2,1)}, f32[8,1024]{1,0:T(8,128)}, bf16[1024,256]{1,0:T(8,128)(2,1)}) custom-call(f32[1024,2304]{1,0:T(8,128)} %get-tuple-element.97.z_ref.x_ref.bc_ref.step_ref.q_ref.kv_ref.xp_ref.bp_ref, f32[1024,2304]{1,0:T(8,128)} %get-tuple-element.97.z_ref.x_ref.bc_ref.step_ref.q_ref.kv_ref.xp_ref.bp_ref, ...), custom_call_target="tpu_custom_call" | custom-call | flops 15000000512 | tf_op jit(solution)/shard_map/attend_forward/pallas_call | solution.py:1246
  94.6 6.8 %mixer_forward.1 = (bf16[1024,1024]{1,0:T(8,128)(2,1)}, bf16[1024,1024]{1,0:T(8,128)(2,1)}) custom-call(bf16[1024,768]{1,0:T(8,128)(2,1)} %get-tuple-element.98.gated_ref, f32[8,1024]{1,0:T(8,128)} %add_rsqrt_fusion.scale_ref.scale_m_ref, f32[1,768]{1,0:T(1,128)} %reshape.65.gain_ref.gain_m_ref, bf16[1024,256]{1,0:T(8,128)(2,1)} %get-tuple-element.100.attended_ref.o_ref, ...), custom_call_target="tpu_custom_call" | custom-call | flops 5000000000 | tf_op jit(solution)/shard_map/mixer_forward/pallas_call | solution.py:1451
  101.8 39.1 %gather_rows.3 = (bf16[1024,2048]{1,0:T(8,128)(2,1)}, bf16[1024,1024]{1,0:T(8,128)(2,1)}) custom-call(bf16[64,2048]{1,0:T(8,128)(2,1)} %bitcast.29, bf16[64,1024]{1,0:T(8,128)(2,1)} %bitcast.36), custom_call_target="tpu_custom_call" | custom-call | flops 3000000000 | tf_op jit(solution)/shard_map/gather_rows/pallas_call | solution.py:204
  141.0 6.4 %product_rows.2.act_grad_ref = f32[1024,1024]{1,0:T(8,128)} custom-call(bf16[1024,1024]{1,0:T(8,128)(2,1)} %top_ref.1, bf16[1024,1024]{1,0:T(8,128)(2,1)} %get-tuple-element.115.right_ref), custom_call_target="tpu_custom_call" | custom-call | flops 4000000000 | tf_op jit(solution)/shard_map/product_rows/pallas_call | solution.py:1336
  147.3 1.8 collective-permute-done.1.other_ref
  150.4 16.1 %feed_forward.1 = (bf16[1024,1024]{1,0:T(8,128)(2,1)}, f32[1024,1]{1,0:T(8,128)}, bf16[1024,1024]{1,0:T(8,128)(2,1)}, bf16[1024,1024]{1,0:T(8,128)(2,1)}, bf16[1...) custom-call(bf16[1024,1024]{1,0:T(8,128)(2,1)} %x_ref.7, bf16[1024,1024]{1,0:T(8,128)(2,1)} %get-tuple-element.103.mixed_ref, ...), custom_call_target="tpu_custom_call" | custom-call | flops 14000000000 | tf_op jit(solution)/shard_map/feed_forward/pallas_call | solution.py:1421
  167.1 32.5 %scatter_product.2.refs_5_ = f32[64,2,1024]{2,1,0:T(2,128)} custom-call(bf16[1024,1024]{1,0:T(8,128)(2,1)} %get-tuple-element.112.left_ref, bf16[1024,2048]{1,0:T(8,128)(2,1)} %get-tuple-element.113.right_ref), custom_call_target="tpu_custom_call" | custom-call | flops 3000000000 | tf_op jit(solution)/shard_map/scatter_product/pallas_call | solution.py:573
  199.6 6.4 %product_rows.3.ffn_ref = bf16[1024,1024]{1,0:T(8,128)(2,1)} custom-call(bf16[1024,1024]{1,0:T(8,128)(2,1)} %get-tuple-element.114.left_ref, bf16[1024,1024]{1,0:T(8,128)(2,1)} %get-tuple-element.115.right_ref), custom_call_target="tpu_custom_call" | custom-call | flops 4000000000 | tf_op jit(solution)/shard_map/product_rows/pallas_call | solution.py:1336
  206.0 5.3 %convert_bitcast_fusion.refs_1_ = bf16[1024,1024]{1,0:T(8,128)(2,1)} fusion(bf16[1024,1024]{1,0:T(8,128)(2,1)} %get-tuple-element.114.left_ref, bf16[1024,1024]{1,0:T(8,128)(2,1)S(1)} %copy-done.8), kind=kOutput, calls=%fused_computation | convolution fusion | flops 2148532224 | bytes 6291456 | tf_op jit(solution)/shard_map/dot_general | solution.py:39
  211.3 2.4 collective-permute-done.2.other_ref
  213.7 11.4 %mixer_backward.1 = (bf16[1024,1024]{1,0:T(8,128)(2,1)}, bf16[1024,768]{1,0:T(8,128)(2,1)}, bf16[1024,256]{1,0:T(8,128)(2,1)}, f32[8,1024]{1,0:T(8,128)}, f32[8,1024]{1,0:T(8,128)}) custom-call(bf16[1024,1024]{1,0:T(8,128)(2,1)} %get-tuple-element.111.part_ref, bf16[1024,1024]{1,0:T(8,128)(2,1)} %collective-permute-done.2.other_ref, ...), custom_call_target="tpu_custom_call" | custom-call | flops 8000000000 | tf_op jit(solution)/shard_map/mixer_backward/pallas_call | solution.py:1504
  227.2 16.2 %attend_backward.1.dqkv_ref = bf16[1024,384]{1,0:T(8,128)(2,1)} custom-call(bf16[1024,512]{1,0:T(8,128)(2,1)} %get-tuple-element.124.qkv_ref, f32[8,1024]{1,0:T(8,128)} %get-tuple-element.125.lse_ref, bf16[1024,256]{1,0:T(8,128)(2,1)} %get-tuple-element.100.attended_ref.o_ref, bf16[1024,256]{1,0:T(8,128)(2,1)} %get-tuple-element.126.do_ref, ...), custom_call_target="tpu_custom_call" | custom-call | flops 16000000000 | tf_op jit(solution)/shard_map/attend_backward/pallas_call | solution.py:1278
  243.4 5.9 %convolution_convert_fusion.refs_0_ = bf16[1024,1024]{1,0:T(8,128)(2,1)} fusion(bf16[1024,1024]{1,0:T(8,128)(2,1)} %get-tuple-element.127.grad_ref, bf16[1024,1024]{1,0:T(8,128)(2,1)} %get-tuple-element.128), kind=kOutput, calls=%fused_computation.1 | convolution fusion | flops 2148532224 | bytes 6291456 | tf_op jit(solution)/shard_map/dot_general | solution.py:39
  250.0 36.8 %scan_backward.1 = (bf16[1024,2304]{1,0:T(8,128)(2,1)}, f32[8,1024]{1,0:T(8,128)}, f32[8,128]{1,0:T(8,128)}, f32[64,768]{1,0:T(8,128)}, f32[64,256]{1,0:T(8,128)}, /*index=5*/f32[64,1024]{1,0:T(8,128)}) custom-call(f32[1024,2304]{1,0:T(8,128)} %get-tuple-element.97.z_ref.x_ref.bc_ref.step_ref.q_ref.kv_ref.xp_ref.bp_ref, ...), custom_call_target="tpu_custom_call" | custom-call | flops 46999998464 | tf_op jit(solution)/shard_map/scan_backward/pallas_call | solution.py:969
  286.8 9.6 %project_back.1 = (bf16[1024,1024]{1,0:T(8,128)(2,1)}, f32[8,1024]{1,0:T(8,128)}) custom-call(bf16[1024,2304]{1,0:T(8,128)(2,1)} %get-tuple-element.135.grad_ref.right_ref, bf16[1024,2304]{1,0:T(8,128)(2,1)} %gather_rows.2.w_ref, bf16[1024,1024]{1,0:T(8,128)(2,1)} %x_ref.7), custom_call_target="tpu_custom_call" | custom-call | flops 8000000000 | tf_op jit(solution)/shard_map/project_back/pallas_call | solution.py:1398
  297.2 42.3 %scatter_product.3 = (f32[64,2,768]{2,1,0:T(2,128)}, f32[64,256]{1,0:T(8,128)}, f32[64,1,384]{2,1,0:T(1,128)}, f32[12,64]{1,0:T(8,128)}, f32[72,128]{1,0:T(8,128)}) custom-call(bf16[1024,1024]{1,0:T(8,128)(2,1)} %get-tuple-element.134.left_ref, bf16[1024,2304]{1,0:T(8,128)(2,1)} %get-tuple-element.135.grad_ref.right_ref, ...), custom_call_target="tpu_custom_call" | custom-call | flops 3000000000 | tf_op jit(solution)/shard_map/scatter_product/pallas_call | solution.py:573
  340.8 2.6 collective-permute-done.5.other_ref
  344.9 10.0 %finish_layer.1 = (f32[1024,1024]{1,0:T(8,128)}, bf16[1024,1024]{1,0:T(8,128)(2,1)}, f32[64,2,768]{2,1,0:T(2,128)}, f32[64,1,384]{2,1,0:T(1,128)}, f32[12,64]{1,...) custom-call(bf16[1024,1024]{1,0:T(8,128)(2,1)} %x_ref.7, ...), custom_call_target="tpu_custom_call" | custom-call | flops 8000000000 | tf_op jit(solution)/shard_map/finish_layer/pallas_call | solution.py:1579
  (50 shorter events, 17.8 us)
Async XLA Ops:
  10.3 33.2 %copy-start.1 = (bf16[768,64]{0,1:T(8,128)(2,1)S(1)}, bf16[768,64]{0,1:T(8,128)(2,1)}, u32[]{:S(2)}) copy-start(bf16[768,64]{0,1:T(8,128)(2,1)} %param.37) | copy-start | bytes 294916
  10.3 33.2 %copy-start.6 = (bf16[1,256,64]{1,2,0:T(8,128)(2,1)S(1)}, bf16[1,256,64]{1,2,0:T(8,128)(2,1)}, u32[]{:S(2)}) copy-start(bf16[1,256,64]{1,2,0:T(8,128)(2,1)} %param.39) | copy-start | bytes 98308
  78.4 14.2 %copy-start.7 = (bf16[768]{0:T(1024)(128)(2,1)S(1)}, bf16[768]{0:T(1024)(128)(2,1)}, u32[]{:S(2)}) copy-start(bf16[768]{0:T(1024)(128)(2,1)} %param.36) | copy-start | bytes 4612
  78.5 14.7 %copy-start = (bf16[64,2,1024]{2,1,0:T(2,128)(2,1)S(1)}, bf16[64,2,1024]{2,1,0:T(2,128)(2,1)}, u32[]{:S(2)}) copy-start(bf16[64,2,1024]{2,1,0:T(2,128)(2,1)} %param.41) | copy-start | bytes 786436
  78.5 15.5 %copy-start.5 = (f32[8,1024]{1,0:T(8,128)S(1)}, f32[8,1024]{1,0:T(8,128)}, u32[]{:S(2)}) copy-start(f32[8,1024]{1,0:T(8,128)} %get-tuple-element.99) | copy-start | bytes 98308
  78.5 15.5 %collective-permute-start = (f32[8,1024]{1,0:T(8,128)}, f32[8,1024]{1,0:T(8,128)S(1)}, u32[]{:S(2)}, u32[]{:S(2)}) collective-permute-start(f32[8,1024]{1,0:T(8,128)} %get-tuple-element.99), channel_id=1, source_target_pairs={{0,1},{1,0},{2,3},{3,2},{4,5},{5,4},{6,7},{7,6},{8,9},{9,8},{10,11... | collective-permute-start | bytes 98312 | tf_op jit(solution)/shard_map/ppermute | solution.py:1617
  101.3 47.8 %collective-permute-start.1 = (bf16[1024,1024]{1,0:T(8,128)(2,1)}, bf16[1024,1024]{1,0:T(8,128)(2,1)S(1)}, u32[]{:S(2)}, u32[]{:S(2)}) collective-permute-start(bf16[1024,1024]{1,0:T(8,128)(2,1)} %get-tuple-element.103.mixed_ref), channel_id=1, source_target_pairs={{0,1},{1,0},{2,3},{3,2},{4,5},{5,4},{6,7},{7,6},{8,9},{9,8},{10,11... | collective-permute-start | bytes 6291464 | tf_op jit(solution)/shard_map/ppermute | solution.py:1617
  149.2 1.3 copy-start.11
  166.5 47.1 %collective-permute-start.2 = (bf16[1024,1024]{1,0:T(8,128)(2,1)}, bf16[1024,1024]{1,0:T(8,128)(2,1)}, u32[]{:S(2)}, u32[]{:S(2)}) collective-permute-start(bf16[1024,1024]{1,0:T(8,128)(2,1)} %get-tuple-element.111.part_ref), channel_id=1, source_target_pairs={{0,1},{1,0},{2,3},{3,2},{4,5},{5,4},{6,7},{7,6},{8,9},{9,8},{10,11... | collective-permute-start | bytes 6291464 | tf_op jit(solution)/shard_map/ppermute | solution.py:1617
  199.6 6.4 %copy-start.8 = (bf16[1024,1024]{1,0:T(8,128)(2,1)S(1)}, bf16[1024,1024]{1,0:T(8,128)(2,1)}, u32[]{:S(2)}) copy-start(bf16[1024,1024]{1,0:T(8,128)(2,1)} %top_ref.1) | copy-start | bytes 6291460
  213.6 12.3 %copy-start.9 = (bf16[1024,1024]{1,0:T(8,128)(2,1)S(1)}, bf16[1024,1024]{1,0:T(8,128)(2,1)}, u32[]{:S(2)}) copy-start(bf16[1024,1024]{1,0:T(8,128)(2,1)} %product_rows.3.ffn_ref) | copy-start | bytes 6291460
  225.1 24.2 %collective-permute-start.4 = (f32[8,1024]{1,0:T(8,128)}, f32[8,1024]{1,0:T(8,128)S(1)}, u32[]{:S(2)}, u32[]{:S(2)}) collective-permute-start(f32[8,1024]{1,0:T(8,128)} %get-tuple-element.123), channel_id=1, source_target_pairs={{0,1},{1,0},{2,3},{3,2},{4,5},{5,4},{6,7},{7,6},{8,9},{9,8},{10,11... | collective-permute-start | bytes 98312 | tf_op jit(solution)/shard_map/ppermute | solution.py:1617
  226.0 60.8 %collective-permute-start.3 = (bf16[1024,1024]{1,0:T(8,128)(2,1)S(1)}, bf16[1024,1024]{1,0:T(8,128)(2,1)}, u32[]{:S(2)}, u32[]{:S(2)}) collective-permute-start(bf16[1024,1024]{1,0:T(8,128)(2,1)S(1)} %copy-done.9), channel_id=1, source_target_pairs={{0,1},{1,0},{2,3},{3,2},{4,5},{5,4},{6,7},{7,6},{8,9},{9,8},{10,11... | collective-permute-start | bytes 6291464 | tf_op jit(solution)/shard_map/ppermute | solution.py:1617
  243.4 5.9 %copy-start.4 = (f32[8,1024]{1,0:T(8,128)S(1)}, f32[8,1024]{1,0:T(8,128)}, u32[]{:S(2)}) copy-start(f32[8,1024]{1,0:T(8,128)} %get-tuple-element.123) | copy-start | bytes 98308
  296.4 47.1 %collective-permute-start.5 = (bf16[1024,1024]{1,0:T(8,128)(2,1)}, bf16[1024,1024]{1,0:T(8,128)(2,1)S(1)}, u32[]{:S(2)}, u32[]{:S(2)}) collective-permute-start(bf16[1024,1024]{1,0:T(8,128)(2,1)} %get-tuple-element.133.part_ref), channel_id=1, source_target_pairs={{0,1},{1,0},{2,3},{3,2},{4,5},{5,4},{6,7},{7,6},{8,9},{9,8},{10,11... | collective-permute-start | bytes 6291464 | tf_op jit(solution)/shard_map/ppermute | solution.py:1617
  339.5 15.4 %collective-permute-start.6 = (f32[72,128]{1,0:T(8,128)}, f32[72,128]{1,0:T(8,128)S(1)}, u32[]{:S(2)}, u32[]{:S(2)}) collective-permute-start(f32[72,128]{1,0:T(8,128)} %get-tuple-element.143.total_ref), channel_id=1, source_target_pairs={{0,1},{1,0},{2,3},{3,2},{4,5},{5,4},{6,7},{7,6},{8,9},{9,8},{10,11... | collective-permute-start | bytes 110600 | tf_op jit(solution)/shard_map/ppermute | solution.py:1617
  343.5 1.4 copy-start.10
  343.5 11.4 %collective-permute-start.7 = (f32[64,256]{1,0:T(8,128)}, f32[64,256]{1,0:T(8,128)S(1)}, u32[]{:S(2)}, u32[]{:S(2)}) collective-permute-start(f32[64,256]{1,0:T(8,128)} %get-tuple-element.153.mine_ref), channel_id=1, source_target_pairs={{0,1},{1,0},{2,3},{3,2},{4,5},{5,4},{6,7},{7,6},{8,9},{9,8},{10,11... | collective-permute-start | bytes 196616 | tf_op jit(solution)/shard_map/ppermute | solution.py:1617
  354.9 0.6 copy-start.3
  355.5 0.6 copy-start.2

commit v5 on v4

--- a/solution.py
+++ b/solution.py
@@ -620,32 +620,14 @@
     return jnp.maximum(raw, 0.0) + jnp.log1p(jnp.exp(-jnp.abs(raw)))
 
 
-def shifted(values, edge, ahead):
-    span = values.shape[0]
-    moves = range(1, KCONV)
-    row, col = iota((span, span), 0), iota((span, span), 1)
-    mask = jnp.concatenate(
-        [(col == (row + move if ahead else row - move)).astype(BF16) for move in moves], axis=0
-    )
-    moved = pick_left(mask, values, 2)
-    place = iota(edge.shape, 0)
-    result = []
-    for move in moves:
-        part = moved[(move - 1) * span : move * span]
-        if ahead:
-            into = jnp.where(place >= EDGE - move, pltpu.roll(edge, EDGE - move, 0), 0.0)
-            part = jnp.concatenate([part[:-EDGE], part[-EDGE:] + into], axis=0)
-        else:
-            into = jnp.where(place < move, pltpu.roll(edge, move, 0), 0.0)
-            part = jnp.concatenate([part[:EDGE] + into, part[EDGE:]], axis=0)
-        result.append(part)
-    return result
-
-
-def apply_taps(values, moved, taps):
-    total = taps[KCONV - 1 : KCONV, :] * values
-    for move, part in enumerate(moved, 1):
-        total = total + taps[KCONV - 1 - move : KCONV - move, :] * part
+def window(buffer, start, span):
+    return buffer[start : start + span, :]
+
+
+def causal_taps(buffer, taps, span):
+    total = taps[0:1, :] * window(buffer, EDGE - KCONV + 1, span)
+    for tap in range(1, KCONV):
+        total = total + taps[tap : tap + 1, :] * window(buffer, EDGE - KCONV + 1 + tap, span)
     return total
 
 
@@ -679,7 +661,7 @@
     z_ref, x_ref, bc_ref, step_ref,
     tap_ref, tapb_ref, row_ref, shard_ref,
     y_ref, gated_ref, square_ref, enter_ref, all_ref,
-    state, edge, *sems,
+    state, buffer, *sems,
 ):
     span, channels = x_ref.shape
     ring = RingGather(devices, shard_ref, all_ref, sems)
@@ -694,14 +676,15 @@
     @pl.when(pl.program_id(0) == 0)
     def _():
         state[...] = jnp.zeros_like(state)
-        edge[...] = jnp.zeros_like(edge)
-
+        buffer[span:, :] = jnp.zeros((EDGE, buffer.shape[1]), F32)
+
+    buffer[:EDGE, :] = buffer[span:, :]
+    buffer[EDGE:, :channels] = x_ref[...]
+    buffer[EDGE:, channels:] = bc_ref[...]
     spread = head_spread(channels)
     bias, gain, biasb, stepb, decay, skip = unpack_rows(row_ref, spread)
     taps = jnp.concatenate([tap_ref[...], tapb_ref[...]], axis=1).astype(F32)
-    before = jnp.concatenate([x_ref[...], bc_ref[...]], axis=1)
-    conv = apply_taps(before, shifted(before, edge[...], False), taps)
-    edge[...] = before[-EDGE:]
+    conv = causal_taps(buffer, taps, span)
     conv = jax.nn.silu(conv + jnp.concatenate([bias, biasb], axis=1))
     inputs, shared = conv[:, :channels], conv[:, channels:]
     raw, step, cum, step_w, tails_w, grown_w = span_rates(step_ref, stepb, decay, spread, span)
@@ -748,7 +731,7 @@
     sent, refs = refs[:count], refs[count:]
     (grad_ref, gx_ref, gh_ref), refs = refs[:3], refs[3:]
     outs, refs = refs[:outs_count], refs[outs_count:]
-    (dstate, dedge, du_buf, col_buf), scratch = refs[:4], refs[4:]
+    (dstate, buffer, dbuffer, du_buf, col_buf), scratch = refs[:5], refs[5:]
     ring = RingScatter(devices, windows, pieces, sent, outs, scratch)
     span, channels = x_ref.shape
     turn = pl.program_id(0)
@@ -758,19 +741,20 @@
         ring.greet()
         ring.begin()
         dstate[...] = jnp.zeros_like(dstate)
-        dedge[...] = jnp.zeros_like(dedge)
+        dbuffer[...] = jnp.zeros_like(dbuffer)
         col_buf[...] = jnp.zeros_like(col_buf)
         gx_ref[...] = jnp.zeros_like(gx_ref)
         gh_ref[...] = jnp.zeros_like(gh_ref)
 
     inside = (turn < spans - 1).astype(F32)
-    before = jnp.concatenate([x_ref[...], bc_ref[...]], axis=1)
-    edge = jnp.concatenate([xp_ref[...], bp_ref[...]], axis=1) * inside
+    buffer[:EDGE, :channels] = xp_ref[...] * inside
+    buffer[:EDGE, channels:] = bp_ref[...] * inside
+    buffer[EDGE:, :channels] = x_ref[...]
+    buffer[EDGE:, channels:] = bc_ref[...]
     spread = head_spread(channels)
     bias, gain, biasb, stepb, decay, skip = unpack_rows(row_ref, spread)
     taps = jnp.concatenate([tap_ref[...], tapb_ref[...]], axis=1).astype(F32)
-    moved = shifted(before, edge, False)
-    conv = apply_taps(before, moved, taps) + jnp.concatenate([bias, biasb], axis=1)
+    conv = causal_taps(buffer, taps, span) + jnp.concatenate([bias, biasb], axis=1)
     sig = jax.nn.sigmoid(conv)
     swished = conv * sig
     inputs, shared = swished[:, :channels], swished[:, channels:]
@@ -787,7 +771,7 @@
     y = y_ref[...]
     scale = scale_ref[...].T[:, :1]
     normed = y * swish * scale
-    dyg = dyg_ref[...].astype(F32)
+    dyg = dyg_ref[...]
     gain_grad = jnp.sum(dyg * normed, axis=0, keepdims=True)
     dgated = scale * (dyg * gain - normed * inner_ref[...].T[:, :1])
     dy = dgated * swish
@@ -858,12 +842,14 @@
 
     dinputs = du * step_w + skip * dy
     dconv = jnp.concatenate([dinputs, db, dc], axis=1) * (sig * (1.0 + conv * (1.0 - sig)))
-    dbefore = apply_taps(dconv, shifted(dconv, dedge[...], True), taps)
-    dedge[...] = dconv[:EDGE]
-    gx_ref[KCONV - 1 : KCONV, :] += jnp.sum(dconv * before, axis=0, keepdims=True)
-    for move, part in enumerate(moved, 1):
-        tap = KCONV - 1 - move
-        gx_ref[tap : tap + 1, :] += jnp.sum(dconv * part, axis=0, keepdims=True)
+    dbuffer[span:, :] = dbuffer[:EDGE, :]
+    dbuffer[:span, :] = dconv
+    dbefore = jnp.zeros_like(dconv)
+    for tap in range(KCONV):
+        dbefore = dbefore + taps[tap : tap + 1, :] * window(dbuffer, KCONV - 1 - tap, span)
+        gx_ref[tap : tap + 1, :] += jnp.sum(
+            dconv * window(buffer, EDGE - KCONV + 1 + tap, span), axis=0, keepdims=True
+        )
     gx_ref[KCONV : KCONV + 1, :] += jnp.sum(dconv, axis=0, keepdims=True)
     gx_ref[KCONV + 1 : KCONV + 2, :channels] += gain_grad
     width = 2 * channels + 2 * NS
@@ -940,7 +926,7 @@
         ),
         scratch_shapes=[
             pltpu.VMEM((NS, channels), F32),
-            pltpu.VMEM((EDGE, channels + 2 * NS), F32),
+            pltpu.VMEM((SPAN + EDGE, channels + 2 * NS), F32),
         ]
         + gather_sems(devices),
         compiler_params=pltpu.CompilerParams(collective_id=2, has_side_effects=True),
@@ -1001,7 +987,8 @@
         + tuple(keep(item.shape) for item in shapes),
         scratch_shapes=[
             pltpu.VMEM((NS, channels), F32),
-            pltpu.VMEM((EDGE, channels + 2 * NS), F32),
+            pltpu.VMEM((SPAN + EDGE, channels + 2 * NS), F32),
+            pltpu.VMEM((SPAN + EDGE, channels + 2 * NS), F32),
             pltpu.VMEM((SPAN, channels), F32),
             pltpu.VMEM((LANES, SPAN), F32),
         ]
@@ -1489,7 +1476,7 @@
     low_ref[...] = total.astype(BF16)
     back = dot(low_ref[...], w_ref[...])
     mamba = back[:, :channels]
-    mamba_ref[...] = mamba.astype(BF16)
+    mamba_ref[...] = mamba
     attended_ref[...] = back[:, channels:].astype(BF16)
     inner_ref[...] = row_sums(mamba * gain_m_ref[...] * gated_ref[...].astype(F32)) * scale_m_ref[...]
 
@@ -1506,7 +1493,7 @@
         grid=(tokens // NBLK,),
         out_shape=(
             shape((tokens, width), BF16),
-            shape((tokens, channels), BF16),
+            shape((tokens, channels), F32),
             shape((tokens, inner - channels), BF16),
             shape((EDGE, tokens), F32),
             shape((EDGE, width), F32),
@@ -1652,10 +1639,11 @@
     )
     in_width = mixer_in.shape[1]
     (w_in,) = gather_rows([mixer_in], devices, 0, [(0, *window) for window in thirds(in_width)])
+    w_in, *small_params = lax.optimization_barrier(
+        (w_in, conv_x, conv_xb, conv_bc, conv_bcb, dt_bias, a_log, d_skip, w_mnorm)
+    )
+    params = scan_params(*small_params)
     hidden_one, proj, norms = run_project(layer_input, w_in, heads)
-    params = scan_params(
-        conv_x, conv_xb, conv_bc, conv_bcb, dt_bias, a_log, d_skip, w_mnorm
-    )
     out_shard = jnp.concatenate([w_mout.T, output_weight.reshape(attn_width, -1).T], axis=1)
     y, gated, square_sum, entering, w_out = run_scan_forward(
         proj, qkv_width, params, out_shard, devices

time: 359 us -> 356 us (level)
  local copies, waits for them, and re-layouts: 13.5 us -> 9.43 us
    concatenate x1, local copies, waits for them, and re-layouts: 4.12 us -> 0.09 us  [scan_params(): rows = jnp.concatenate(flat).astype(F32).reshape(-1, LANES)]
where the time goes in v5:
time: 356 us; the launch traced here: 355 us
  Pallas kernels  316 us (89%)
  matrix products  11.2 us (3%)
  local copies, waits for them, and re-layouts  9.43 us (3%)
  starting transfers between devices  7.78 us (2%)
  waiting for transfers between devices  6.79 us (2%)
    pallas_call x2, Pallas kernels, scatter_product(): pl.pallas_call(functools.partial(product_kernel, devices, groups, len(sha...  74.9 us
    pallas_call x2, Pallas kernels, gather_rows(): pl.pallas_call(functools.partial(gather_kernel, devices, count, windows),...  72.4 us
    pallas_call x1, Pallas kernels, run_scan_backward(): pl.pallas_call(functools.partial(scan_backward, devices, spans, windows,...  37.5 us
    pallas_call x1, Pallas kernels, run_scan_forward(): pl.pallas_call(functools.partial(scan_forward, devices, spans), grid=(spa...  24.2 us
    pallas_call x1, Pallas kernels, run_attend_backward(): pl.pallas_call(attend_backward, grid=(1,), out_shape=jax.ShapeDtypeStruct...  16.2 us
    pallas_call x1, Pallas kernels, run_feed_forward(): pl.pallas_call(feed_forward, grid=(tokens // TBLK,), out_shape=(shape((to...  16.1 us
    pallas_call x2, Pallas kernels, run_product(): pl.pallas_call(functools.partial(product_rows, dims), grid=(tokens // TBL...  12.8 us
    pallas_call x1, Pallas kernels, run_attend_forward(): pl.pallas_call(attend_forward, grid=(1,), out_shape=(jax.ShapeDtypeStruct...  12.5 us
  transfers between devices with their start and end apart: 8, of which 3 were waited for; matrix products, arithmetic and copies ran while one was open for 4% of the time, Pallas kernels for 57%

profile of v5, /device:TPU:0, one launch (start us, length us, event | category | flops | bytes accessed | tf_op | source)
XLA Modules:
  0.0 354.6 jit_solution(8274223728410740014)
XLA Ops:
  3.9 1.6 concatenate.9.refs_0_
  5.6 33.2 %gather_rows.2.w_ref = bf16[1024,2304]{1,0:T(8,128)(2,1)} custom-call(bf16[64,2304]{1,0:T(8,128)(2,1)} %concatenate.9.refs_0_), custom_call_target="tpu_custom_call" | custom-call | flops 3000000000 | tf_op jit(solution)/shard_map/gather_rows/pallas_call | solution.py:204
  40.3 10.2 %project.1 = (bf16[1024,1024]{1,0:T(8,128)(2,1)}, f32[1024,2304]{1,0:T(8,128)}, f32[8,1024]{1,0:T(8,128)}) custom-call(bf16[1024,1024]{1,0:T(8,128)(2,1)} %x_ref.7, bf16[1024,2304]{1,0:T(8,128)(2,1)} %gather_rows.2.w_ref), custom_call_target="tpu_custom_call" | custom-call | flops 8000000000 | tf_op jit(solution)/shard_map/project/pallas_call | solution.py:1352
  50.5 24.2 %scan_forward.1 = (f32[1024,768]{1,0:T(8,128)}, bf16[1024,768]{1,0:T(8,128)(2,1)}, f32[8,1024]{1,0:T(8,128)}, f32[8,128,768]{2,1,0:T(8,128)}, bf16[1024,1024]{1,0:T(8,128)(2,1)}) custom-call(f32[1024,2304]{1,0:T(8,128)} %get-tuple-element.107.z_ref.x_ref.bc_ref.step_ref.q_ref.kv_ref.xp_ref.bp_ref, ...), custom_call_target="tpu_custom_call" | custom-call | flops 20000000000 | tf_op jit(solution)/shard_map/scan_forward/pallas_call | solution.py:907
  74.7 1.5 collective-permute-start
  76.2 12.5 %attend_forward.1 = (bf16[1024,512]{1,0:T(8,128)(2,1)}, f32[8,1024]{1,0:T(8,128)}, bf16[1024,256]{1,0:T(8,128)(2,1)}) custom-call(f32[1024,2304]{1,0:T(8,128)} %get-tuple-element.107.z_ref.x_ref.bc_ref.step_ref.q_ref.kv_ref.xp_ref.bp_ref, f32[1024,2304]{1,0:T(8,128)} %get-tuple-element.107.z_ref.x_ref.bc_ref.step_ref.q_ref.kv_ref.xp_ref.bp_ref, ...), custom_call_target="tpu_custom_call" | custom-call | flops 15000000512 | tf_op jit(solution)/shard_map/attend_forward/pallas_call | solution.py:1233
  90.7 6.8 %mixer_forward.1 = (bf16[1024,1024]{1,0:T(8,128)(2,1)}, bf16[1024,1024]{1,0:T(8,128)(2,1)}) custom-call(bf16[1024,768]{1,0:T(8,128)(2,1)} %get-tuple-element.116.gated_ref, f32[8,1024]{1,0:T(8,128)} %add_rsqrt_fusion.scale_ref.scale_m_ref, f32[1,768]{1,0:T(1,128)} %reshape.65.gain_ref.gain_m_ref, bf16[1024,256]{1,0:T(8,128)(2,1)} %get-tuple-element.118.attended_ref.o_ref, ...), custom_call_target="tpu_custom_call" | custom-call | flops 5000000000 | tf_op jit(solution)/shard_map/mixer_forward/pallas_call | solution.py:1438
  98.0 39.1 %gather_rows.3 = (bf16[1024,2048]{1,0:T(8,128)(2,1)}, bf16[1024,1024]{1,0:T(8,128)(2,1)}) custom-call(bf16[64,2048]{1,0:T(8,128)(2,1)} %bitcast.29, bf16[64,1024]{1,0:T(8,128)(2,1)} %bitcast.36), custom_call_target="tpu_custom_call" | custom-call | flops 3000000000 | tf_op jit(solution)/shard_map/gather_rows/pallas_call | solution.py:204
  137.2 6.4 %product_rows.2.act_grad_ref = f32[1024,1024]{1,0:T(8,128)} custom-call(bf16[1024,1024]{1,0:T(8,128)(2,1)} %top_ref.1, bf16[1024,1024]{1,0:T(8,128)(2,1)} %get-tuple-element.133.right_ref), custom_call_target="tpu_custom_call" | custom-call | flops 4000000000 | tf_op jit(solution)/shard_map/product_rows/pallas_call | solution.py:1323
  143.5 1.8 collective-permute-done.1.other_ref
  146.6 16.1 %feed_forward.1 = (bf16[1024,1024]{1,0:T(8,128)(2,1)}, f32[1024,1]{1,0:T(8,128)}, bf16[1024,1024]{1,0:T(8,128)(2,1)}, bf16[1024,1024]{1,0:T(8,128)(2,1)}, bf16[1...) custom-call(bf16[1024,1024]{1,0:T(8,128)(2,1)} %x_ref.7, bf16[1024,1024]{1,0:T(8,128)(2,1)} %get-tuple-element.121.mixed_ref, ...), custom_call_target="tpu_custom_call" | custom-call | flops 14000000000 | tf_op jit(solution)/shard_map/feed_forward/pallas_call | solution.py:1408
  163.3 32.5 %scatter_product.2.refs_5_ = f32[64,2,1024]{2,1,0:T(2,128)} custom-call(bf16[1024,1024]{1,0:T(8,128)(2,1)} %get-tuple-element.130.left_ref, bf16[1024,2048]{1,0:T(8,128)(2,1)} %get-tuple-element.131.right_ref), custom_call_target="tpu_custom_call" | custom-call | flops 3000000000 | tf_op jit(solution)/shard_map/scatter_product/pallas_call | solution.py:573
  195.9 6.4 %product_rows.3.ffn_ref = bf16[1024,1024]{1,0:T(8,128)(2,1)} custom-call(bf16[1024,1024]{1,0:T(8,128)(2,1)} %get-tuple-element.132.left_ref, bf16[1024,1024]{1,0:T(8,128)(2,1)} %get-tuple-element.133.right_ref), custom_call_target="tpu_custom_call" | custom-call | flops 4000000000 | tf_op jit(solution)/shard_map/product_rows/pallas_call | solution.py:1323
  202.3 5.3 %convert_bitcast_fusion.refs_1_ = bf16[1024,1024]{1,0:T(8,128)(2,1)} fusion(bf16[1024,1024]{1,0:T(8,128)(2,1)} %get-tuple-element.132.left_ref, bf16[1024,1024]{1,0:T(8,128)(2,1)S(1)} %copy-done.13), kind=kOutput, calls=%fused_computation | convolution fusion | flops 2148532224 | bytes 6291456 | tf_op jit(solution)/shard_map/dot_general | solution.py:39
  207.5 2.3 collective-permute-done.2.other_ref
  209.8 11.4 %mixer_backward.1 = (bf16[1024,1024]{1,0:T(8,128)(2,1)}, f32[1024,768]{1,0:T(8,128)}, bf16[1024,256]{1,0:T(8,128)(2,1)}, f32[8,1024]{1,0:T(8,128)}, f32[8,1024]{1,0:T(8,128)}) custom-call(bf16[1024,1024]{1,0:T(8,128)(2,1)} %get-tuple-element.129.part_ref, bf16[1024,1024]{1,0:T(8,128)(2,1)} %collective-permute-done.2.other_ref, ...), custom_call_target="tpu_custom_call" | custom-call | flops 8000000000 | tf_op jit(solution)/shard_map/mixer_backward/pallas_call | solution.py:1491
  223.3 16.2 %attend_backward.1.dqkv_ref = bf16[1024,384]{1,0:T(8,128)(2,1)} custom-call(bf16[1024,512]{1,0:T(8,128)(2,1)} %get-tuple-element.142.qkv_ref, f32[8,1024]{1,0:T(8,128)} %get-tuple-element.143.lse_ref, bf16[1024,256]{1,0:T(8,128)(2,1)} %get-tuple-element.118.attended_ref.o_ref, bf16[1024,256]{1,0:T(8,128)(2,1)} %get-tuple-element.144.do_ref, ...), custom_call_target="tpu_custom_call" | custom-call | flops 16000000000 | tf_op jit(solution)/shard_map/attend_backward/pallas_call | solution.py:1265
  239.5 5.9 %convolution_convert_fusion.refs_0_ = bf16[1024,1024]{1,0:T(8,128)(2,1)} fusion(bf16[1024,1024]{1,0:T(8,128)(2,1)} %get-tuple-element.145.grad_ref, bf16[1024,1024]{1,0:T(8,128)(2,1)} %get-tuple-element.146), kind=kOutput, calls=%fused_computation.1 | convolution fusion | flops 2148532224 | bytes 6291456 | tf_op jit(solution)/shard_map/dot_general | solution.py:39
  246.1 37.5 %scan_backward.1 = (bf16[1024,2304]{1,0:T(8,128)(2,1)}, f32[8,1024]{1,0:T(8,128)}, f32[8,128]{1,0:T(8,128)}, f32[64,768]{1,0:T(8,128)}, f32[64,256]{1,0:T(8,128)}, /*index=5*/f32[64,1024]{1,0:T(8,128)}) custom-call(f32[1024,2304]{1,0:T(8,128)} %get-tuple-element.107.z_ref.x_ref.bc_ref.step_ref.q_ref.kv_ref.xp_ref.bp_ref, ...), custom_call_target="tpu_custom_call" | custom-call | flops 46999998464 | tf_op jit(solution)/shard_map/scan_backward/pallas_call | solution.py:955
  283.6 9.6 %project_back.1 = (bf16[1024,1024]{1,0:T(8,128)(2,1)}, f32[8,1024]{1,0:T(8,128)}) custom-call(bf16[1024,2304]{1,0:T(8,128)(2,1)} %get-tuple-element.153.grad_ref.right_ref, bf16[1024,2304]{1,0:T(8,128)(2,1)} %gather_rows.2.w_ref, bf16[1024,1024]{1,0:T(8,128)(2,1)} %x_ref.7), custom_call_target="tpu_custom_call" | custom-call | flops 8000000000 | tf_op jit(solution)/shard_map/project_back/pallas_call | solution.py:1385
  294.0 42.3 %scatter_product.3 = (f32[64,2,768]{2,1,0:T(2,128)}, f32[64,256]{1,0:T(8,128)}, f32[64,1,384]{2,1,0:T(1,128)}, f32[12,64]{1,0:T(8,128)}, f32[72,128]{1,0:T(8,128)}) custom-call(bf16[1024,1024]{1,0:T(8,128)(2,1)} %get-tuple-element.152.left_ref, bf16[1024,2304]{1,0:T(8,128)(2,1)} %get-tuple-element.153.grad_ref.right_ref, ...), custom_call_target="tpu_custom_call" | custom-call | flops 3000000000 | tf_op jit(solution)/shard_map/scatter_product/pallas_call | solution.py:573
  337.6 2.7 collective-permute-done.5.other_ref
  341.8 10.0 %finish_layer.1 = (f32[1024,1024]{1,0:T(8,128)}, bf16[1024,1024]{1,0:T(8,128)(2,1)}, f32[64,2,768]{2,1,0:T(2,128)}, f32[64,1,384]{2,1,0:T(1,128)}, f32[12,64]{1,...) custom-call(bf16[1024,1024]{1,0:T(8,128)(2,1)} %x_ref.7, ...), custom_call_target="tpu_custom_call" | custom-call | flops 8000000000 | tf_op jit(solution)/shard_map/finish_layer/pallas_call | solution.py:1566
  353.1 1.6 finish_shared.1
  (60 shorter events, 16.6 us)
Async XLA Ops:
  5.6 33.3 %copy-start.7 = (bf16[768]{0:T(1024)(128)(2,1)S(1)}, bf16[768]{0:T(1024)(128)(2,1)}, u32[]{:S(2)}) copy-start(bf16[768]{0:T(1024)(128)(2,1)} %param.36) | copy-start | bytes 4612
  5.6 33.4 %copy-start.8 = (bf16[768]{0:T(1024)(128)(2,1)S(1)}, bf16[768]{0:T(1024)(128)(2,1)}, u32[]{:S(2)}) copy-start(bf16[768]{0:T(1024)(128)(2,1)} %param.30) | copy-start | bytes 4612
  5.6 33.4 %copy-start.9 = (bf16[256]{0:T(256)(128)(2,1)S(1)}, bf16[256]{0:T(256)(128)(2,1)}, u32[]{:S(2)}) copy-start(bf16[256]{0:T(256)(128)(2,1)} %param.32) | copy-start | bytes 1540
  5.6 33.4 %copy-start.10 = (bf16[12]{0:T(256)(128)(2,1)S(1)}, bf16[12]{0:T(256)(128)(2,1)}, u32[]{:S(2)}) copy-start(bf16[12]{0:T(256)(128)(2,1)} %param.33) | copy-start | bytes 76
  5.6 33.4 %copy-start.11 = (bf16[12]{0:T(256)(128)(2,1)S(1)}, bf16[12]{0:T(256)(128)(2,1)}, u32[]{:S(2)}) copy-start(bf16[12]{0:T(256)(128)(2,1)} %param.34) | copy-start | bytes 76
  5.6 33.4 %copy-start.12 = (bf16[12]{0:T(256)(128)(2,1)S(1)}, bf16[12]{0:T(256)(128)(2,1)}, u32[]{:S(2)}) copy-start(bf16[12]{0:T(256)(128)(2,1)} %param.35) | copy-start | bytes 76
  5.6 34.1 %copy-start.1 = (bf16[768,64]{0,1:T(8,128)(2,1)S(1)}, bf16[768,64]{0,1:T(8,128)(2,1)}, u32[]{:S(2)}) copy-start(bf16[768,64]{0,1:T(8,128)(2,1)} %param.37) | copy-start | bytes 294916
  5.6 34.1 %copy-start.6 = (bf16[1,256,64]{1,2,0:T(8,128)(2,1)S(1)}, bf16[1,256,64]{1,2,0:T(8,128)(2,1)}, u32[]{:S(2)}) copy-start(bf16[1,256,64]{1,2,0:T(8,128)(2,1)} %param.39) | copy-start | bytes 98308
  74.7 14.6 %copy-start = (bf16[64,2,1024]{2,1,0:T(2,128)(2,1)S(1)}, bf16[64,2,1024]{2,1,0:T(2,128)(2,1)}, u32[]{:S(2)}) copy-start(bf16[64,2,1024]{2,1,0:T(2,128)(2,1)} %param.41) | copy-start | bytes 786436
  74.7 15.4 %copy-start.5 = (f32[8,1024]{1,0:T(8,128)S(1)}, f32[8,1024]{1,0:T(8,128)}, u32[]{:S(2)}) copy-start(f32[8,1024]{1,0:T(8,128)} %get-tuple-element.117) | copy-start | bytes 98308
  74.7 15.4 %collective-permute-start = (f32[8,1024]{1,0:T(8,128)}, f32[8,1024]{1,0:T(8,128)S(1)}, u32[]{:S(2)}, u32[]{:S(2)}) collective-permute-start(f32[8,1024]{1,0:T(8,128)} %get-tuple-element.117), channel_id=1, source_target_pairs={{0,1},{1,0},{2,3},{3,2},{4,5},{5,4},{6,7},{7,6},{8,9},{9,8},{10,11... | collective-permute-start | bytes 98312 | tf_op jit(solution)/shard_map/ppermute | solution.py:1604
  97.5 47.8 %collective-permute-start.1 = (bf16[1024,1024]{1,0:T(8,128)(2,1)}, bf16[1024,1024]{1,0:T(8,128)(2,1)S(1)}, u32[]{:S(2)}, u32[]{:S(2)}) collective-permute-start(bf16[1024,1024]{1,0:T(8,128)(2,1)} %get-tuple-element.121.mixed_ref), channel_id=1, source_target_pairs={{0,1},{1,0},{2,3},{3,2},{4,5},{5,4},{6,7},{7,6},{8,9},{9,8},{10,11... | collective-permute-start | bytes 6291464 | tf_op jit(solution)/shard_map/ppermute | solution.py:1604
  145.3 1.3 copy-start.16
  162.7 47.1 %collective-permute-start.2 = (bf16[1024,1024]{1,0:T(8,128)(2,1)}, bf16[1024,1024]{1,0:T(8,128)(2,1)}, u32[]{:S(2)}, u32[]{:S(2)}) collective-permute-start(bf16[1024,1024]{1,0:T(8,128)(2,1)} %get-tuple-element.129.part_ref), channel_id=1, source_target_pairs={{0,1},{1,0},{2,3},{3,2},{4,5},{5,4},{6,7},{7,6},{8,9},{9,8},{10,11... | collective-permute-start | bytes 6291464 | tf_op jit(solution)/shard_map/ppermute | solution.py:1604
  195.8 6.4 %copy-start.13 = (bf16[1024,1024]{1,0:T(8,128)(2,1)S(1)}, bf16[1024,1024]{1,0:T(8,128)(2,1)}, u32[]{:S(2)}) copy-start(bf16[1024,1024]{1,0:T(8,128)(2,1)} %top_ref.1) | copy-start | bytes 6291460
  209.8 12.3 %copy-start.14 = (bf16[1024,1024]{1,0:T(8,128)(2,1)S(1)}, bf16[1024,1024]{1,0:T(8,128)(2,1)}, u32[]{:S(2)}) copy-start(bf16[1024,1024]{1,0:T(8,128)(2,1)} %product_rows.3.ffn_ref) | copy-start | bytes 6291460
  221.2 24.2 %collective-permute-start.4 = (f32[8,1024]{1,0:T(8,128)}, f32[8,1024]{1,0:T(8,128)S(1)}, u32[]{:S(2)}, u32[]{:S(2)}) collective-permute-start(f32[8,1024]{1,0:T(8,128)} %get-tuple-element.141), channel_id=1, source_target_pairs={{0,1},{1,0},{2,3},{3,2},{4,5},{5,4},{6,7},{7,6},{8,9},{9,8},{10,11... | collective-permute-start | bytes 98312 | tf_op jit(solution)/shard_map/ppermute | solution.py:1604
  222.1 61.4 %collective-permute-start.3 = (bf16[1024,1024]{1,0:T(8,128)(2,1)S(1)}, bf16[1024,1024]{1,0:T(8,128)(2,1)}, u32[]{:S(2)}, u32[]{:S(2)}) collective-permute-start(bf16[1024,1024]{1,0:T(8,128)(2,1)S(1)} %copy-done.14), channel_id=1, source_target_pairs={{0,1},{1,0},{2,3},{3,2},{4,5},{5,4},{6,7},{7,6},{8,9},{9,8},{10,11... | collective-permute-start | bytes 6291464 | tf_op jit(solution)/shard_map/ppermute | solution.py:1604
  239.5 5.9 %copy-start.4 = (f32[8,1024]{1,0:T(8,128)S(1)}, f32[8,1024]{1,0:T(8,128)}, u32[]{:S(2)}) copy-start(f32[8,1024]{1,0:T(8,128)} %get-tuple-element.141) | copy-start | bytes 98308
  293.2 47.2 %collective-permute-start.5 = (bf16[1024,1024]{1,0:T(8,128)(2,1)}, bf16[1024,1024]{1,0:T(8,128)(2,1)S(1)}, u32[]{:S(2)}, u32[]{:S(2)}) collective-permute-start(bf16[1024,1024]{1,0:T(8,128)(2,1)} %get-tuple-element.151.part_ref), channel_id=1, source_target_pairs={{0,1},{1,0},{2,3},{3,2},{4,5},{5,4},{6,7},{7,6},{8,9},{9,8},{10,11... | collective-permute-start | bytes 6291464 | tf_op jit(solution)/shard_map/ppermute | solution.py:1604
  336.4 15.5 %collective-permute-start.6 = (f32[72,128]{1,0:T(8,128)}, f32[72,128]{1,0:T(8,128)S(1)}, u32[]{:S(2)}, u32[]{:S(2)}) collective-permute-start(f32[72,128]{1,0:T(8,128)} %get-tuple-element.161.total_ref), channel_id=1, source_target_pairs={{0,1},{1,0},{2,3},{3,2},{4,5},{5,4},{6,7},{7,6},{8,9},{9,8},{10,11... | collective-permute-start | bytes 110600 | tf_op jit(solution)/shard_map/ppermute | solution.py:1604
  340.4 1.4 copy-start.15
  340.4 11.4 %collective-permute-start.7 = (f32[64,256]{1,0:T(8,128)}, f32[64,256]{1,0:T(8,128)S(1)}, u32[]{:S(2)}, u32[]{:S(2)}) collective-permute-start(f32[64,256]{1,0:T(8,128)} %get-tuple-element.171.mine_ref), channel_id=1, source_target_pairs={{0,1},{1,0},{2,3},{3,2},{4,5},{5,4},{6,7},{7,6},{8,9},{9,8},{10,11... | collective-permute-start | bytes 196616 | tf_op jit(solution)/shard_map/ppermute | solution.py:1604
  352.4 0.6 copy-start.2
  (1 other events, 0.6 us)

commit v6 on v5

--- a/solution.py
+++ b/solution.py
@@ -8,6 +8,7 @@
 from jax.experimental import pallas as pl
 from jax.experimental.pallas import tpu as pltpu
 from jax.sharding import PartitionSpec as P
+
 
 HEAD_SIZE = 64
 MP = 64
@@ -23,7 +24,6 @@
 EDGE = 8
 
 EPSILON = 1e-05
-HIGHEST = lax.Precision.HIGHEST
 LOG_BASE = math.log(100000000000.0)
 MASKED = -1e30
 MESH = pl.DeviceIdType.MESH
@@ -55,22 +55,6 @@
     place = lax.rem(place + 4 * chips, chips)
     back = lax.div(place, chips // 2)
     return (1 - back) * (2 * place) + back * (2 * (chips - 1 - place) + 1)
-
-
-def ring_setup(chips):
-    me = lax.axis_index("dp")
-    group = lax.axis_index("tensor")
-    chip = lax.div(me, 2)
-    core = lax.rem(me, 2)
-    place = ring_place(chip, chips)
-    right = ring_chip(place + 1, chips) * 2 + core
-    left = ring_chip(place - 1, chips) * 2 + core
-    mate = chip * 2 + (1 - core)
-    barrier = pltpu.get_barrier_semaphore()
-    for other in (right, left, mate):
-        pl.semaphore_signal(barrier, inc=1, device_id=(other, group), device_id_type=MESH)
-    pl.semaphore_wait(barrier, 3)
-    return me, group, core, place, right, left, mate
 
 
 class RingGather:
@@ -213,18 +197,6 @@
     )(*shards)
 
 
-def scatter_order(chips):
-    ahead = chips // 2
-    behind = chips - 1 - ahead
-    order = []
-    for step in range(ahead):
-        order.append(-(ahead - step))
-        if step < behind:
-            order.append(behind - step)
-    order.append(0)
-    return order
-
-
 class RingScatter:
     def __init__(self, devices, windows, pieces, operands, outs, scratch):
         self.chips = devices // 2
@@ -271,7 +243,7 @@
 
     def block(self, i, slot, which):
         index = ring_chip(self.place + self.shift_of(slot), self.chips) * 2 + which
-        left, right, first, last = self.windows[i]
+        left, _, first, last = self.windows[i]
         return self.operands[left].at[self.half(index), first:last]
 
     def remote(self, source, target_ref, ssem, rsem, target):
@@ -682,12 +654,12 @@
     buffer[EDGE:, :channels] = x_ref[...]
     buffer[EDGE:, channels:] = bc_ref[...]
     spread = head_spread(channels)
-    bias, gain, biasb, stepb, decay, skip = unpack_rows(row_ref, spread)
+    bias, _, biasb, stepb, decay, skip = unpack_rows(row_ref, spread)
     taps = jnp.concatenate([tap_ref[...], tapb_ref[...]], axis=1).astype(F32)
     conv = causal_taps(buffer, taps, span)
     conv = jax.nn.silu(conv + jnp.concatenate([bias, biasb], axis=1))
     inputs, shared = conv[:, :channels], conv[:, channels:]
-    raw, step, cum, step_w, tails_w, grown_w = span_rates(step_ref, stepb, decay, spread, span)
+    _, step, cum, step_w, tails_w, grown_w = span_rates(step_ref, stepb, decay, spread, span)
     cum_rows = cum.T
     b_low = shared[:, :NS].astype(BF16)
     c_low = shared[:, NS:].astype(BF16)
@@ -713,12 +685,10 @@
     gated_ref[...] = gated.astype(BF16)
     square_ref[...] = row_sums(gated * gated)
 
-    count = spans
     for step in range(1, ring.ahead + 1):
-        pl.when(turn == min(count - 1, count * step // ring.ahead))(
-            functools.partial(ring.hop, step)
-        )
-    pl.when(turn == count - 1)(ring.finish)
+        after = spans * step // ring.ahead - (2 if step == ring.ahead else 1)
+        pl.when(turn == max(0, after))(functools.partial(ring.hop, step))
+    pl.when(turn == spans - 1)(ring.finish)
 
 
 def scan_backward(
@@ -1366,10 +1336,10 @@
     )(x, w_in)
 
 
-def project_back(grad_ref, w_ref, x_ref, part_ref, gain_grad_ref):
+def project_back(grad_ref, w_ref, x_ref, before_ref, part_ref, gain_grad_ref):
     @pl.when(pl.program_id(0) == 0)
     def _():
-        gain_grad_ref[...] = jnp.zeros_like(gain_grad_ref)
+        gain_grad_ref[...] = before_ref[...]
 
     x = x_ref[...].astype(F32)
     normed = x * lax.rsqrt(jnp.mean(x * x, axis=-1, keepdims=True) + EPSILON)
@@ -1378,26 +1348,30 @@
     gain_grad_ref[:1, :] += jnp.sum(part.astype(F32) * normed, axis=0, keepdims=True)
 
 
-def run_project_back(grads, w_in, x):
+def once(item):
+    return pl.BlockSpec(item.shape, lambda turn: (0,) * item.ndim, pipeline_mode=pl.Buffered(1))
+
+
+def run_project_back(half, grads, w_in, x, before):
     tokens, width = x.shape
     cols = w_in.shape[1]
-    rows = lambda size: pl.BlockSpec((TBLK, size), lambda turn: (turn, 0))
+    turns = tokens // TBLK // 2
+    rows = lambda size: pl.BlockSpec((TBLK, size), lambda turn: (turn + half * turns, 0))
     return pl.pallas_call(
         project_back,
-        grid=(tokens // TBLK,),
+        grid=(turns,),
         out_shape=(
-            jax.ShapeDtypeStruct((tokens, width), BF16),
+            jax.ShapeDtypeStruct((tokens // 2, width), BF16),
             jax.ShapeDtypeStruct((EDGE, width), F32),
         ),
-        in_specs=[rows(cols), once(w_in), rows(width)],
-        out_specs=(rows(width), pl.BlockSpec((EDGE, width), lambda turn: (0, 0))),
-        cost_estimate=cost(8),
+        in_specs=[rows(cols), once(w_in), rows(width), once(before)],
+        out_specs=(
+            pl.BlockSpec((TBLK, width), lambda turn: (turn, 0)),
+            pl.BlockSpec((EDGE, width), lambda turn: (0, 0)),
+        ),
+        cost_estimate=cost(5),
         name="project_back",
-    )(grads, w_in, x)
-
-
-def once(item):
-    return pl.BlockSpec(item.shape, lambda turn: (0,) * item.ndim, pipeline_mode=pl.Buffered(1))
+    )(grads, w_in, x, before)
 
 
 def run_feed_forward(x, mixed, other, act_grad, norms, w_gate_up):
@@ -1521,7 +1495,7 @@
 
 
 def finish_layer(
-    norm_at, x_ref, norms_ref, part_ref, other_ref, grad_ref, after_ref, ffn_ref, ffn_other_ref,
+    norm_at, x_ref, norms_ref, pa_ref, oa_ref, pb_ref, ob_ref, grad_ref, after_ref, ffn_ref, ffn_other_ref,
     total_ref, *refs,
 ):
     count = (len(refs) - 9) // 2
@@ -1545,7 +1519,12 @@
     x = x_ref[...].astype(F32)
     scale = lax.rsqrt(jnp.mean(x * x, axis=-1, keepdims=True) + EPSILON)
     normed = x * scale
-    weighted = (part_ref[...].astype(F32) + other_ref[...].astype(F32)) * norms_ref[0:1, :]
+    grad = jnp.where(
+        pl.program_id(0) < pl.num_programs(0) // 2,
+        pa_ref[...].astype(F32) + oa_ref[...].astype(F32),
+        pb_ref[...].astype(F32) + ob_ref[...].astype(F32),
+    )
+    weighted = grad * norms_ref[0:1, :]
     mean = jnp.mean(weighted * normed, axis=-1, keepdims=True)
     out_ref[...] = grad_ref[...].astype(F32) + scale * (weighted - normed * mean)
     ffn = ffn_ref[...].astype(F32) + ffn_other_ref[...].astype(F32)
@@ -1553,11 +1532,13 @@
 
 
 def run_finish(
-    x, norms, part, other, grad, after, ffn, ffn_other, total, passed, channels, heads, shard,
-    norm_at,
+    x, norms, halves, grad, after, ffn, ffn_other, total, passed, channels, heads, shard, norm_at
 ):
     tokens, width = x.shape
     rows = pl.BlockSpec((TBLK, width), lambda turn: (turn, 0))
+    turns = tokens // TBLK // 2
+    low_half = pl.BlockSpec((TBLK, width), lambda turn: (jnp.minimum(turn, turns - 1), 0))
+    high_half = pl.BlockSpec((TBLK, width), lambda turn: (jnp.maximum(turn - turns, 0), 0))
     shape = lambda *sizes: jax.ShapeDtypeStruct(sizes, F32)
     small = (
         shape(KCONV, channels), shape(channels), shape(channels), shape(heads), shape(heads),
@@ -1569,11 +1550,15 @@
         out_shape=(shape(tokens, width), jax.ShapeDtypeStruct((tokens, width), BF16))
         + tuple(shape(*item.shape) for item in passed)
         + small,
-        in_specs=[rows, once(norms)] + [rows] * 6 + [once(total)] + [once(item) for item in passed],
+        in_specs=[rows, once(norms)]
+        + [low_half] * 2
+        + [high_half] * 2
+        + [rows] * 4
+        + [once(total)] + [once(item) for item in passed],
         out_specs=(rows, rows) + tuple(once(item) for item in passed + small),
         cost_estimate=cost(8),
         name="finish_layer",
-    )(x, norms, part, other, grad, after, ffn, ffn_other, total, *passed)
+    )(x, norms, *halves, grad, after, ffn, ffn_other, total, *passed)
 
 
 def finish_shared(at, total_ref, cross_ref, mine_ref, other_ref, bc_ref, tap_ref, bias_ref, norm_ref, both):
@@ -1708,9 +1693,13 @@
         [grad_out, grad_down], windows, pieces, shapes, devices,
     )
     ffn_other, grad_proj = lax.optimization_barrier((ffn_other, grad_proj))
-    partial_one, grad_norm1 = run_project_back(grad_proj, w_in, layer_input)
-    partial_one, grad_proj = lax.optimization_barrier((partial_one, grad_proj))
-    other = swap(partial_one)
+    part_a, grad_norm1 = run_project_back(
+        0, grad_proj, w_in, layer_input, jnp.zeros((EDGE, width), F32)
+    )
+    other_a = swap(part_a)
+    part_b, grad_norm1 = run_project_back(1, grad_proj, w_in, layer_input, grad_norm1)
+    part_b, grad_proj = lax.optimization_barrier((part_b, grad_proj))
+    other_b = swap(part_b)
     lanes_of = lambda size, start=0: range(start, start + size, LANES)
     places = [(0, row, lane) for row in range(KCONV + 2) for lane in lanes_of(channels)]
     places += [(1, row, 0) for row in range(3)]
@@ -1720,7 +1709,6 @@
     places += [(0, row, lane) for row in range(KCONV + 1) for lane in lanes_of(2 * NS, channels)]
     places += [(3, 0, lane) for lane in lanes_of(width)]
     shared_at = 2 * channels
-    step_at = qkv_at + qkv_width
     mine_zx, mine_bc, mine_qkv, mine_step, small = scatter_product(
         hidden_one,
         grad_proj,
@@ -1747,12 +1735,12 @@
         (small_x, small_h, grad_norm2, grad_norm1),
         places,
     )
-    other, mine_bc = lax.optimization_barrier((other, mine_bc))
+    other_a, other_b, mine_bc = lax.optimization_barrier((other_a, other_b, mine_bc))
     passed = (mine_zx, mine_qkv, mine_step, mine_mout, mine_o, mine_gu, mine_down)
     cross, other_bc = swap(small), swap(mine_bc)
     grad_source, result, *rest = run_finish(
-        layer_input, norms, partial_one, other, grad_mix_low, after, ffn_part, ffn_other, small,
-        passed, channels, heads, shard, norm_at,
+        layer_input, norms, (part_a, other_a, part_b, other_b), grad_mix_low, after, ffn_part,
+        ffn_other, small, passed, channels, heads, shard, norm_at,
     )
     mine_zx, mine_qkv, mine_step, mine_mout, mine_o, mine_gu, mine_down = rest[: len(passed)]
     grad_taps, grad_bias, grad_gain, grad_steps, grad_log, grad_skip, own_norm2 = rest[len(passed) :]

time: 356 us -> 360 us (1.011)
  Pallas kernels: 316 us -> 320 us
    pallas_call x1 -> x2, Pallas kernels: 9.65 us -> 13.3 us  [run_project_back(): pl.pallas_call(project_back, grid=(turns,), out_shape=(jax.ShapeDtypeStru...]
    ppermute x8 -> x9, starting transfers between devices: 7.78 us -> 9.2 us  [swap(): return lax.ppermute(partial, 'tensor', [(0, 1), (1, 0)])]
  transfers between devices with their start and end apart: 8 -> 9, of which waited for: 3 -> 3; matrix products, arithmetic and copies ran while one was open for 4% -> 4% of each run, Pallas kernels for 57% -> 57%
where the time goes in v6:
time: 360 us; the launch traced here: 359 us
  Pallas kernels  320 us (89%)
  matrix products  11.2 us (3%)
  local copies, waits for them, and re-layouts  9.54 us (3%)
  starting transfers between devices  9.2 us (3%)
  waiting for transfers between devices  5.19 us (1%)
    pallas_call x2, Pallas kernels, scatter_product(): pl.pallas_call(functools.partial(product_kernel, devices, groups, len(sha...  75.1 us
    pallas_call x2, Pallas kernels, gather_rows(): pl.pallas_call(functools.partial(gather_kernel, devices, count, windows),...  72.6 us
    pallas_call x1, Pallas kernels, run_scan_backward(): pl.pallas_call(functools.partial(scan_backward, devices, spans, windows,...  37.4 us
    pallas_call x1, Pallas kernels, run_scan_forward(): pl.pallas_call(functools.partial(scan_forward, devices, spans), grid=(spa...  24.2 us
    pallas_call x1, Pallas kernels, run_attend_backward(): pl.pallas_call(attend_backward, grid=(1,), out_shape=jax.ShapeDtypeStruct...  16.2 us
    pallas_call x1, Pallas kernels, run_feed_forward(): pl.pallas_call(feed_forward, grid=(tokens // TBLK,), out_shape=(shape((to...  16.1 us
    pallas_call x2, Pallas kernels, run_project_back(): pl.pallas_call(project_back, grid=(turns,), out_shape=(jax.ShapeDtypeStru...  13.3 us
    pallas_call x2, Pallas kernels, run_product(): pl.pallas_call(functools.partial(product_rows, dims), grid=(tokens // TBL...  12.7 us
  transfers between devices with their start and end apart: 9, of which 3 were waited for; matrix products, arithmetic and copies ran while one was open for 4% of the time, Pallas kernels for 57%

profile of v6, /device:TPU:0, one launch (start us, length us, event | category | flops | bytes accessed | tf_op | source)
XLA Modules:
  0.0 358.9 jit_solution(14614459537793490966)
XLA Ops:
  3.9 1.6 concatenate.9.refs_0_
  5.6 33.2 %gather_rows.2.w_ref = bf16[1024,2304]{1,0:T(8,128)(2,1)} custom-call(bf16[64,2304]{1,0:T(8,128)(2,1)} %concatenate.9.refs_0_), custom_call_target="tpu_custom_call" | custom-call | flops 3000000000 | tf_op jit(solution)/shard_map/gather_rows/pallas_call | solution.py:188
  39.6 10.2 %project.1 = (bf16[1024,1024]{1,0:T(8,128)(2,1)}, f32[1024,2304]{1,0:T(8,128)}, f32[8,1024]{1,0:T(8,128)}) custom-call(bf16[1024,1024]{1,0:T(8,128)(2,1)} %x_ref.9, bf16[1024,2304]{1,0:T(8,128)(2,1)} %gather_rows.2.w_ref), custom_call_target="tpu_custom_call" | custom-call | flops 8000000000 | tf_op jit(solution)/shard_map/project/pallas_call | solution.py:1322
  50.5 24.2 %scan_forward.1 = (f32[1024,768]{1,0:T(8,128)}, bf16[1024,768]{1,0:T(8,128)(2,1)}, f32[8,1024]{1,0:T(8,128)}, f32[8,128,768]{2,1,0:T(8,128)}, bf16[1024,1024]{1,0:T(8,128)(2,1)}) custom-call(f32[1024,2304]{1,0:T(8,128)} %get-tuple-element.110.z_ref.x_ref.bc_ref.step_ref.q_ref.kv_ref.xp_ref.bp_ref, ...), custom_call_target="tpu_custom_call" | custom-call | flops 20000000000 | tf_op jit(solution)/shard_map/scan_forward/pallas_call | solution.py:877
  74.7 1.6 collective-permute-start
  76.4 12.5 %attend_forward.1 = (bf16[1024,512]{1,0:T(8,128)(2,1)}, f32[8,1024]{1,0:T(8,128)}, bf16[1024,256]{1,0:T(8,128)(2,1)}) custom-call(f32[1024,2304]{1,0:T(8,128)} %get-tuple-element.110.z_ref.x_ref.bc_ref.step_ref.q_ref.kv_ref.xp_ref.bp_ref, f32[1024,2304]{1,0:T(8,128)} %get-tuple-element.110.z_ref.x_ref.bc_ref.step_ref.q_ref.kv_ref.xp_ref.bp_ref, ...), custom_call_target="tpu_custom_call" | custom-call | flops 15000000512 | tf_op jit(solution)/shard_map/attend_forward/pallas_call | solution.py:1203
  90.8 6.7 %mixer_forward.1 = (bf16[1024,1024]{1,0:T(8,128)(2,1)}, bf16[1024,1024]{1,0:T(8,128)(2,1)}) custom-call(bf16[1024,768]{1,0:T(8,128)(2,1)} %get-tuple-element.119.gated_ref, f32[8,1024]{1,0:T(8,128)} %add_rsqrt_fusion.scale_ref.scale_m_ref, f32[1,768]{1,0:T(1,128)} %reshape.65.gain_ref.gain_m_ref, bf16[1024,256]{1,0:T(8,128)(2,1)} %get-tuple-element.121.attended_ref.o_ref, ...), custom_call_target="tpu_custom_call" | custom-call | flops 5000000000 | tf_op jit(solution)/shard_map/mixer_forward/pallas_call | solution.py:1412
  98.0 39.4 %gather_rows.3 = (bf16[1024,2048]{1,0:T(8,128)(2,1)}, bf16[1024,1024]{1,0:T(8,128)(2,1)}) custom-call(bf16[64,2048]{1,0:T(8,128)(2,1)} %bitcast.29, bf16[64,1024]{1,0:T(8,128)(2,1)} %bitcast.36), custom_call_target="tpu_custom_call" | custom-call | flops 3000000000 | tf_op jit(solution)/shard_map/gather_rows/pallas_call | solution.py:188
  137.4 6.4 %product_rows.2.act_grad_ref = f32[1024,1024]{1,0:T(8,128)} custom-call(bf16[1024,1024]{1,0:T(8,128)(2,1)} %top_ref.1, bf16[1024,1024]{1,0:T(8,128)(2,1)} %get-tuple-element.136.right_ref), custom_call_target="tpu_custom_call" | custom-call | flops 4000000000 | tf_op jit(solution)/shard_map/product_rows/pallas_call | solution.py:1293
  143.8 1.5 collective-permute-done.1.other_ref
  146.6 16.1 %feed_forward.1 = (bf16[1024,1024]{1,0:T(8,128)(2,1)}, f32[1024,1]{1,0:T(8,128)}, bf16[1024,1024]{1,0:T(8,128)(2,1)}, bf16[1024,1024]{1,0:T(8,128)(2,1)}, bf16[1...) custom-call(bf16[1024,1024]{1,0:T(8,128)(2,1)} %x_ref.9, bf16[1024,1024]{1,0:T(8,128)(2,1)} %get-tuple-element.124.mixed_ref, ...), custom_call_target="tpu_custom_call" | custom-call | flops 14000000000 | tf_op jit(solution)/shard_map/feed_forward/pallas_call | solution.py:1382
  163.2 32.6 %scatter_product.2.refs_5_ = f32[64,2,1024]{2,1,0:T(2,128)} custom-call(bf16[1024,1024]{1,0:T(8,128)(2,1)} %get-tuple-element.133.left_ref, bf16[1024,2048]{1,0:T(8,128)(2,1)} %get-tuple-element.134.right_ref), custom_call_target="tpu_custom_call" | custom-call | flops 3000000000 | tf_op jit(solution)/shard_map/scatter_product/pallas_call | solution.py:545
  195.8 6.4 %product_rows.3.ffn_ref = bf16[1024,1024]{1,0:T(8,128)(2,1)} custom-call(bf16[1024,1024]{1,0:T(8,128)(2,1)} %get-tuple-element.135.left_ref, bf16[1024,1024]{1,0:T(8,128)(2,1)} %get-tuple-element.136.right_ref), custom_call_target="tpu_custom_call" | custom-call | flops 4000000000 | tf_op jit(solution)/shard_map/product_rows/pallas_call | solution.py:1293
  202.2 5.3 %convert_bitcast_fusion.refs_1_ = bf16[1024,1024]{1,0:T(8,128)(2,1)} fusion(bf16[1024,1024]{1,0:T(8,128)(2,1)} %get-tuple-element.135.left_ref, bf16[1024,1024]{1,0:T(8,128)(2,1)S(1)} %copy-done.13), kind=kOutput, calls=%fused_computation | convolution fusion | flops 2148532224 | bytes 6291456 | tf_op jit(solution)/shard_map/dot_general | solution.py:39
  207.4 2.3 collective-permute-done.2.other_ref
  209.7 11.4 %mixer_backward.1 = (bf16[1024,1024]{1,0:T(8,128)(2,1)}, f32[1024,768]{1,0:T(8,128)}, bf16[1024,256]{1,0:T(8,128)(2,1)}, f32[8,1024]{1,0:T(8,128)}, f32[8,1024]{1,0:T(8,128)}) custom-call(bf16[1024,1024]{1,0:T(8,128)(2,1)} %get-tuple-element.132.part_ref, bf16[1024,1024]{1,0:T(8,128)(2,1)} %collective-permute-done.2.other_ref, ...), custom_call_target="tpu_custom_call" | custom-call | flops 8000000000 | tf_op jit(solution)/shard_map/mixer_backward/pallas_call | solution.py:1465
  223.2 16.2 %attend_backward.1.dqkv_ref = bf16[1024,384]{1,0:T(8,128)(2,1)} custom-call(bf16[1024,512]{1,0:T(8,128)(2,1)} %get-tuple-element.145.qkv_ref, f32[8,1024]{1,0:T(8,128)} %get-tuple-element.146.lse_ref, bf16[1024,256]{1,0:T(8,128)(2,1)} %get-tuple-element.121.attended_ref.o_ref, bf16[1024,256]{1,0:T(8,128)(2,1)} %get-tuple-element.147.do_ref, ...), custom_call_target="tpu_custom_call" | custom-call | flops 16000000000 | tf_op jit(solution)/shard_map/attend_backward/pallas_call | solution.py:1235
  239.5 5.9 %convolution_convert_fusion.refs_0_ = bf16[1024,1024]{1,0:T(8,128)(2,1)} fusion(bf16[1024,1024]{1,0:T(8,128)(2,1)} %get-tuple-element.148.grad_ref, bf16[1024,1024]{1,0:T(8,128)(2,1)} %get-tuple-element.149), kind=kOutput, calls=%fused_computation.1 | convolution fusion | flops 2148532224 | bytes 6291456 | tf_op jit(solution)/shard_map/dot_general | solution.py:39
  246.0 37.4 %scan_backward.1 = (bf16[1024,2304]{1,0:T(8,128)(2,1)}, f32[8,1024]{1,0:T(8,128)}, f32[8,128]{1,0:T(8,128)}, f32[64,768]{1,0:T(8,128)}, f32[64,256]{1,0:T(8,128)}, /*index=5*/f32[64,1024]{1,0:T(8,128)}) custom-call(f32[1024,2304]{1,0:T(8,128)} %get-tuple-element.110.z_ref.x_ref.bc_ref.step_ref.q_ref.kv_ref.xp_ref.bp_ref, ...), custom_call_target="tpu_custom_call" | custom-call | flops 46999998464 | tf_op jit(solution)/shard_map/scan_backward/pallas_call | solution.py:925
  284.1 6.6 %project_back.2 = (bf16[512,1024]{1,0:T(8,128)(2,1)}, f32[8,1024]{1,0:T(8,128)}) custom-call(bf16[1024,2304]{1,0:T(8,128)(2,1)} %get-tuple-element.158.grad_ref.right_ref, bf16[1024,2304]{1,0:T(8,128)(2,1)} %gather_rows.2.w_ref, bf16[1024,1024]{1,0:T(8,128)(2,1)} %x_ref.9, f32[8,1024]{1,0:T(8,128)} %broadcast_in_dim.30.before_ref), custom_call_target="tpu_custom_call" | custom-call | flops 5000000000 | tf_op jit(solution)/shard_map/project_back/pallas_call | solution.py:1360
  290.7 6.7 %project_back.3 = (bf16[512,1024]{1,0:T(8,128)(2,1)}, f32[8,1024]{1,0:T(8,128)}) custom-call(bf16[1024,2304]{1,0:T(8,128)(2,1)} %get-tuple-element.158.grad_ref.right_ref, bf16[1024,2304]{1,0:T(8,128)(2,1)} %gather_rows.2.w_ref, bf16[1024,1024]{1,0:T(8,128)(2,1)} %x_ref.9, f32[8,1024]{1,0:T(8,128)} %get-tuple-element.154.before_ref), custom_call_target="tpu_custom_call" | custom-call | flops 5000000000 | tf_op jit(solution)/shard_map/project_back/pallas_call | solution.py:1360
  299.4 42.6 %scatter_product.3 = (f32[64,2,768]{2,1,0:T(2,128)}, f32[64,256]{1,0:T(8,128)}, f32[64,1,384]{2,1,0:T(1,128)}, f32[12,64]{1,0:T(8,128)}, f32[72,128]{1,0:T(8,128)}) custom-call(bf16[1024,1024]{1,0:T(8,128)(2,1)} %get-tuple-element.157.left_ref, bf16[1024,2304]{1,0:T(8,128)(2,1)} %get-tuple-element.158.grad_ref.right_ref, ...), custom_call_target="tpu_custom_call" | custom-call | flops 3000000000 | tf_op jit(solution)/shard_map/scatter_product/pallas_call | solution.py:545
  345.9 10.2 %finish_layer.1 = (f32[1024,1024]{1,0:T(8,128)}, bf16[1024,1024]{1,0:T(8,128)(2,1)}, f32[64,2,768]{2,1,0:T(2,128)}, f32[64,1,384]{2,1,0:T(1,128)}, f32[12,64]{1,...) custom-call(bf16[1024,1024]{1,0:T(8,128)(2,1)} %x_ref.9, ...), custom_call_target="tpu_custom_call" | custom-call | flops 8000000000 | tf_op jit(solution)/shard_map/finish_layer/pallas_call | solution.py:1547
  357.3 1.6 finish_shared.1
  (68 shorter events, 19.4 us)
Async XLA Ops:
  5.6 33.3 %copy-start.7 = (bf16[768]{0:T(1024)(128)(2,1)S(1)}, bf16[768]{0:T(1024)(128)(2,1)}, u32[]{:S(2)}) copy-start(bf16[768]{0:T(1024)(128)(2,1)} %param.36) | copy-start | bytes 4612
  5.6 33.3 %copy-start.8 = (bf16[768]{0:T(1024)(128)(2,1)S(1)}, bf16[768]{0:T(1024)(128)(2,1)}, u32[]{:S(2)}) copy-start(bf16[768]{0:T(1024)(128)(2,1)} %param.30) | copy-start | bytes 4612
  5.6 33.3 %copy-start.9 = (bf16[256]{0:T(256)(128)(2,1)S(1)}, bf16[256]{0:T(256)(128)(2,1)}, u32[]{:S(2)}) copy-start(bf16[256]{0:T(256)(128)(2,1)} %param.32) | copy-start | bytes 1540
  5.6 33.3 %copy-start.10 = (bf16[12]{0:T(256)(128)(2,1)S(1)}, bf16[12]{0:T(256)(128)(2,1)}, u32[]{:S(2)}) copy-start(bf16[12]{0:T(256)(128)(2,1)} %param.33) | copy-start | bytes 76
  5.6 33.3 %copy-start.11 = (bf16[12]{0:T(256)(128)(2,1)S(1)}, bf16[12]{0:T(256)(128)(2,1)}, u32[]{:S(2)}) copy-start(bf16[12]{0:T(256)(128)(2,1)} %param.34) | copy-start | bytes 76
  5.6 33.3 %copy-start.12 = (bf16[12]{0:T(256)(128)(2,1)S(1)}, bf16[12]{0:T(256)(128)(2,1)}, u32[]{:S(2)}) copy-start(bf16[12]{0:T(256)(128)(2,1)} %param.35) | copy-start | bytes 76
  39.6 10.2 %copy-start.1 = (bf16[768,64]{0,1:T(8,128)(2,1)S(1)}, bf16[768,64]{0,1:T(8,128)(2,1)}, u32[]{:S(2)}) copy-start(bf16[768,64]{0,1:T(8,128)(2,1)} %param.37) | copy-start | bytes 294916
  39.6 10.2 %copy-start.6 = (bf16[1,256,64]{1,2,0:T(8,128)(2,1)S(1)}, bf16[1,256,64]{1,2,0:T(8,128)(2,1)}, u32[]{:S(2)}) copy-start(bf16[1,256,64]{1,2,0:T(8,128)(2,1)} %param.39) | copy-start | bytes 98308
  74.7 14.7 %copy-start = (bf16[64,2,1024]{2,1,0:T(2,128)(2,1)S(1)}, bf16[64,2,1024]{2,1,0:T(2,128)(2,1)}, u32[]{:S(2)}) copy-start(bf16[64,2,1024]{2,1,0:T(2,128)(2,1)} %param.41) | copy-start | bytes 786436
  74.7 15.5 %copy-start.5 = (f32[8,1024]{1,0:T(8,128)S(1)}, f32[8,1024]{1,0:T(8,128)}, u32[]{:S(2)}) copy-start(f32[8,1024]{1,0:T(8,128)} %get-tuple-element.120) | copy-start | bytes 98308
  74.7 15.5 %collective-permute-start = (f32[8,1024]{1,0:T(8,128)}, f32[8,1024]{1,0:T(8,128)S(1)}, u32[]{:S(2)}, u32[]{:S(2)}) collective-permute-start(f32[8,1024]{1,0:T(8,128)} %get-tuple-element.120), channel_id=1, source_target_pairs={{0,1},{1,0},{2,3},{3,2},{4,5},{5,4},{6,7},{7,6},{8,9},{9,8},{10,11... | collective-permute-start | bytes 98312 | tf_op jit(solution)/shard_map/ppermute | solution.py:1589
  97.6 47.7 %collective-permute-start.1 = (bf16[1024,1024]{1,0:T(8,128)(2,1)}, bf16[1024,1024]{1,0:T(8,128)(2,1)S(1)}, u32[]{:S(2)}, u32[]{:S(2)}) collective-permute-start(bf16[1024,1024]{1,0:T(8,128)(2,1)} %get-tuple-element.124.mixed_ref), channel_id=1, source_target_pairs={{0,1},{1,0},{2,3},{3,2},{4,5},{5,4},{6,7},{7,6},{8,9},{9,8},{10,11... | collective-permute-start | bytes 6291464 | tf_op jit(solution)/shard_map/ppermute | solution.py:1589
  162.7 47.0 %collective-permute-start.2 = (bf16[1024,1024]{1,0:T(8,128)(2,1)}, bf16[1024,1024]{1,0:T(8,128)(2,1)}, u32[]{:S(2)}, u32[]{:S(2)}) collective-permute-start(bf16[1024,1024]{1,0:T(8,128)(2,1)} %get-tuple-element.132.part_ref), channel_id=1, source_target_pairs={{0,1},{1,0},{2,3},{3,2},{4,5},{5,4},{6,7},{7,6},{8,9},{9,8},{10,11... | collective-permute-start | bytes 6291464 | tf_op jit(solution)/shard_map/ppermute | solution.py:1589
  195.8 6.4 %copy-start.13 = (bf16[1024,1024]{1,0:T(8,128)(2,1)S(1)}, bf16[1024,1024]{1,0:T(8,128)(2,1)}, u32[]{:S(2)}) copy-start(bf16[1024,1024]{1,0:T(8,128)(2,1)} %top_ref.1) | copy-start | bytes 6291460
  209.7 12.7 %copy-start.14 = (bf16[1024,1024]{1,0:T(8,128)(2,1)S(1)}, bf16[1024,1024]{1,0:T(8,128)(2,1)}, u32[]{:S(2)}) copy-start(bf16[1024,1024]{1,0:T(8,128)(2,1)} %product_rows.3.ffn_ref) | copy-start | bytes 6291460
  221.1 24.3 %collective-permute-start.4 = (f32[8,1024]{1,0:T(8,128)}, f32[8,1024]{1,0:T(8,128)S(1)}, u32[]{:S(2)}, u32[]{:S(2)}) collective-permute-start(f32[8,1024]{1,0:T(8,128)} %get-tuple-element.144), channel_id=1, source_target_pairs={{0,1},{1,0},{2,3},{3,2},{4,5},{5,4},{6,7},{7,6},{8,9},{9,8},{10,11... | collective-permute-start | bytes 98312 | tf_op jit(solution)/shard_map/ppermute | solution.py:1589
  222.4 61.0 %collective-permute-start.3 = (bf16[1024,1024]{1,0:T(8,128)(2,1)S(1)}, bf16[1024,1024]{1,0:T(8,128)(2,1)}, u32[]{:S(2)}, u32[]{:S(2)}) collective-permute-start(bf16[1024,1024]{1,0:T(8,128)(2,1)S(1)} %copy-done.14), channel_id=1, source_target_pairs={{0,1},{1,0},{2,3},{3,2},{4,5},{5,4},{6,7},{7,6},{8,9},{9,8},{10,11... | collective-permute-start | bytes 6291464 | tf_op jit(solution)/shard_map/ppermute | solution.py:1589
  239.5 5.9 %copy-start.4 = (f32[8,1024]{1,0:T(8,128)S(1)}, f32[8,1024]{1,0:T(8,128)}, u32[]{:S(2)}) copy-start(f32[8,1024]{1,0:T(8,128)} %get-tuple-element.144) | copy-start | bytes 98308
  290.7 7.9 %copy-start.16 = (bf16[512,1024]{1,0:T(8,128)(2,1)S(1)}, bf16[512,1024]{1,0:T(8,128)(2,1)}, u32[]{:S(2)}) copy-start(bf16[512,1024]{1,0:T(8,128)(2,1)} %get-tuple-element.153.pa_ref) | copy-start | bytes 3145732
  297.4 45.6 %collective-permute-start.6 = (bf16[512,1024]{1,0:T(8,128)(2,1)}, bf16[512,1024]{1,0:T(8,128)(2,1)S(1)}, u32[]{:S(2)}, u32[]{:S(2)}) collective-permute-start(bf16[512,1024]{1,0:T(8,128)(2,1)} %get-tuple-element.156.pb_ref), channel_id=1, source_target_pairs={{0,1},{1,0},{2,3},{3,2},{4,5},{5,4},{6,7},{7,6},{8,9},{9,8},{10,11... | collective-permute-start | bytes 3145736 | tf_op jit(solution)/shard_map/ppermute | solution.py:1589
  298.6 45.8 %collective-permute-start.5 = (bf16[512,1024]{1,0:T(8,128)(2,1)S(1)}, bf16[512,1024]{1,0:T(8,128)(2,1)S(1)}, u32[]{:S(2)}, u32[]{:S(2)}) collective-permute-start(bf16[512,1024]{1,0:T(8,128)(2,1)S(1)} %copy-done.16), channel_id=1, source_target_pairs={{0,1},{1,0},{2,3},{3,2},{4,5},{5,4},{6,7},{7,6},{8,9},{9,8},{10,11... | collective-permute-start | bytes 3145736 | tf_op jit(solution)/shard_map/ppermute | solution.py:1589
  342.0 14.1 %collective-permute-start.7 = (f32[72,128]{1,0:T(8,128)}, f32[72,128]{1,0:T(8,128)S(1)}, u32[]{:S(2)}, u32[]{:S(2)}) collective-permute-start(f32[72,128]{1,0:T(8,128)} %get-tuple-element.167.total_ref), channel_id=1, source_target_pairs={{0,1},{1,0},{2,3},{3,2},{4,5},{5,4},{6,7},{7,6},{8,9},{9,8},{10,11... | collective-permute-start | bytes 110600 | tf_op jit(solution)/shard_map/ppermute | solution.py:1589
  343.0 2.9 copy-start.17
  344.4 11.7 %collective-permute-start.8 = (f32[64,256]{1,0:T(8,128)}, f32[64,256]{1,0:T(8,128)S(1)}, u32[]{:S(2)}, u32[]{:S(2)}) collective-permute-start(f32[64,256]{1,0:T(8,128)} %get-tuple-element.177.mine_ref), channel_id=1, source_target_pairs={{0,1},{1,0},{2,3},{3,2},{4,5},{5,4},{6,7},{7,6},{8,9},{9,8},{10,11... | collective-permute-start | bytes 196616 | tf_op jit(solution)/shard_map/ppermute | solution.py:1589
  (4 other events, 4.0 us)

commit v7 on v5

--- a/solution.py
+++ b/solution.py
@@ -516,11 +516,6 @@
     ]
 
 
-def turned_copy(source, target):
-    for start in range(0, source.shape[1], LANES):
-        target[start : start + LANES, :] = source[:, start : start + LANES].T
-
-
 def product_kernel(devices, groups, outs, places, summed, left_ref, right_ref, *refs):
     values = refs[:summed]
     refs = refs[summed:]
@@ -528,7 +523,7 @@
     total = None
     if summed:
         total_out, refs = refs[0], refs[1:]
-    turned, scratch = refs[0], refs[1:]
+    scratch = refs
     if summed:
         scratch, rest = scratch[:-8], scratch[-8:]
         together = rest[0]
@@ -539,7 +534,7 @@
     each = len(scratch) // len(groups)
     rings = [
         RingScatter(
-            devices, windows, pieces, (turned, right_ref), pieces_out,
+            devices, windows, pieces, (left_ref, right_ref), pieces_out,
             scratch[place * each : (place + 1) * each],
         )
         for place, (windows, pieces) in enumerate(groups)
@@ -551,7 +546,6 @@
         total.begin()
     for ring in rings:
         ring.locate()
-    turned_copy(left_ref, turned)
     run_rings(rings, total.spread if total is not None else None)
     for ring in rings:
         ring.finish()
@@ -561,8 +555,8 @@
 
 def scatter_product(left, right, groups, shapes, devices, collective, values=(), places=()):
     vmem = pl.BlockSpec(memory_space=pltpu.VMEM)
-    rows = left.shape[1] // devices
-    scratch = [pltpu.VMEM(left.shape[::-1], BF16)]
+    rows = left.shape[0] // devices
+    scratch = []
     for windows, pieces in groups:
         scratch += scatter_scratch(windows, rows, devices)
     totals = ()
@@ -1289,7 +1283,7 @@
 
 def feed_forward(
     x_ref, mixed_ref, other_ref, act_grad_ref, norms_ref, gu_ref,
-    after_ref, scale_ref, hidden_ref, act_ref, dgu_ref, back_ref,
+    after_ref, scale_ref, turned_ref, act_ref, dgu_ref, back_ref,
 ):
     units = act_grad_ref.shape[1]
     after = x_ref[...].astype(F32) + (mixed_ref[...].astype(F32) + other_ref[...].astype(F32))
@@ -1297,7 +1291,7 @@
     scale = lax.rsqrt(jnp.mean(after * after, axis=-1, keepdims=True) + EPSILON)
     scale_ref[...] = scale
     hidden = (after * scale * norms_ref[1:2, :]).astype(BF16)
-    hidden_ref[...] = hidden
+    turned_ref[...] = hidden.T
     for start in range(0, units, UBLK):
         cols = slice(start, start + UBLK)
         up_cols = slice(units + start, units + start + UBLK)
@@ -1331,7 +1325,7 @@
     )(left, right)
 
 
-def project(heads, x_ref, w_ref, hidden_ref, proj_ref, norms_ref):
+def project(heads, x_ref, w_ref, turned_ref, proj_ref, norms_ref):
     @pl.when(pl.program_id(0) == 0)
     def _():
         gains = w_ref[:, w_ref.shape[1] - LANES :].astype(F32).T
@@ -1341,7 +1335,7 @@
     x = x_ref[...].astype(F32)
     scale = lax.rsqrt(jnp.mean(x * x, axis=-1, keepdims=True) + EPSILON)
     hidden = (x * scale * norms_ref[0:1, :]).astype(BF16)
-    hidden_ref[...] = hidden
+    turned_ref[...] = hidden.T
     proj_ref[...] = dot(hidden, w_ref[...])
 
 
@@ -1353,13 +1347,15 @@
         functools.partial(project, heads),
         grid=(tokens // TBLK,),
         out_shape=(
-            jax.ShapeDtypeStruct((tokens, width), BF16),
+            jax.ShapeDtypeStruct((width, tokens), BF16),
             jax.ShapeDtypeStruct((tokens, cols), F32),
             jax.ShapeDtypeStruct((EDGE, width), F32),
         ),
         in_specs=[rows(width), once(w_in)],
         out_specs=(
-            rows(width), rows(cols), pl.BlockSpec((EDGE, width), lambda turn: (0, 0)),
+            pl.BlockSpec((width, TBLK), lambda turn: (0, turn)),
+            rows(cols),
+            pl.BlockSpec((EDGE, width), lambda turn: (0, 0)),
         ),
         cost_estimate=cost(8),
         name="project",
@@ -1411,13 +1407,16 @@
         out_shape=(
             shape((tokens, width), BF16),
             shape((tokens, 1), F32),
-            shape((tokens, width), BF16),
+            shape((width, tokens), BF16),
             shape((tokens, units), BF16),
             shape((tokens, 2 * units), BF16),
             shape((tokens, width), BF16),
         ),
         in_specs=[rows(width)] * 3 + [rows(units), once(norms), once(w_gate_up)],
-        out_specs=(rows(width), rows(1), rows(width), rows(units), rows(2 * units), rows(width)),
+        out_specs=(
+            rows(width), rows(1), pl.BlockSpec((width, TBLK), lambda turn: (0, turn)), rows(units),
+            rows(2 * units), rows(width),
+        ),
         cost_estimate=cost(14),
         name="feed_forward",
     )(x, mixed, other, act_grad, norms, w_gate_up)
@@ -1458,7 +1457,7 @@
 def mixer_backward(
     part_ref, other_ref, after_ref, scale_ref, top_ref, norms_ref,
     w_ref, gated_ref, scale_m_ref, gain_m_ref,
-    low_ref, mamba_ref, attended_ref, inner_ref, gain_grad_ref,
+    low_ref, turned_ref, mamba_ref, attended_ref, inner_ref, gain_grad_ref,
 ):
     channels = gated_ref.shape[1]
 
@@ -1473,8 +1472,10 @@
     weighted = grad * norms_ref[1:2, :]
     mean = jnp.mean(weighted * normed, axis=-1, keepdims=True)
     total = top_ref[...].astype(F32) + scale * (weighted - normed * mean)
-    low_ref[...] = total.astype(BF16)
-    back = dot(low_ref[...], w_ref[...])
+    low = total.astype(BF16)
+    low_ref[...] = low
+    turned_ref[...] = low.T
+    back = dot(low, w_ref[...])
     mamba = back[:, :channels]
     mamba_ref[...] = mamba
     attended_ref[...] = back[:, channels:].astype(BF16)
@@ -1493,6 +1494,7 @@
         grid=(tokens // NBLK,),
         out_shape=(
             shape((tokens, width), BF16),
+            shape((width, tokens), BF16),
             shape((tokens, channels), F32),
             shape((tokens, inner - channels), BF16),
             shape((EDGE, tokens), F32),
@@ -1501,7 +1503,8 @@
         in_specs=[rows(width)] * 3
         + [rows(1), rows(width), once(norms), once(w_out), rows(channels), lanes, once(gain_m)],
         out_specs=(
-            rows(width), rows(channels), rows(inner - channels), lanes,
+            rows(width), pl.BlockSpec((width, NBLK), lambda turn: (0, turn)), rows(channels),
+            rows(inner - channels), lanes,
             pl.BlockSpec((EDGE, width), lambda turn: (0, 0)),
         ),
         cost_estimate=cost(8),
@@ -1643,7 +1646,7 @@
         (w_in, conv_x, conv_xb, conv_bc, conv_bcb, dt_bias, a_log, d_skip, w_mnorm)
     )
     params = scan_params(*small_params)
-    hidden_one, proj, norms = run_project(layer_input, w_in, heads)
+    turned_one, proj, norms = run_project(layer_input, w_in, heads)
     out_shard = jnp.concatenate([w_mout.T, output_weight.reshape(attn_width, -1).T], axis=1)
     y, gated, square_sum, entering, w_out = run_scan_forward(
         proj, qkv_width, params, out_shard, devices
@@ -1669,13 +1672,13 @@
     other, w_gate_up, w_down_t, act_grad = lax.optimization_barrier(
         (other, w_gate_up, w_down_t, act_grad)
     )
-    after, scale_two, hidden_two, activated, grad_gu_low, partial_two = run_feed_forward(
+    after, scale_two, turned_two, activated, grad_gu_low, partial_two = run_feed_forward(
         layer_input, mixed, other, act_grad, norms, w_gate_up
     )
     other = swap(partial_two)
     grad_down = dot(grad_output, activated, TN).astype(BF16)
     (mine_gu,) = scatter_product(
-        hidden_two,
+        turned_two,
         grad_gu_low,
         [
             ([(0, 1, 0, units)], [(0, 0, units, 0, 0)]),
@@ -1690,12 +1693,12 @@
         (other, mine_gu, grad_down, ffn_part)
     )
     ffn_other = swap(ffn_part)
-    grad_mix_low, grad_mamba, grad_attended, inner_m, grad_norm2 = run_mixer_backward(
+    grad_mix_low, turned_mix, grad_mamba, grad_attended, inner_m, grad_norm2 = run_mixer_backward(
         partial_two, other, after, scale_two, grad_output, norms, w_out, gated, scale_m, gain_m
     )
     inner_m = tensor_sum(inner_m) / channels_all
     dqkv = run_attend_backward(qkv, lse, attended, grad_attended, 0, tables)
-    grad_out = dot(grad_mix_low, mixer_out, TN).astype(BF16)
+    grad_out = dot(turned_mix, mixer_out).astype(BF16)
     windows = [(0, None, 0, channels + attn_width), (1, None, 0, units)]
     pieces = [
         (0, 0, channels, 0, None),
@@ -1722,7 +1725,7 @@
     shared_at = 2 * channels
     step_at = qkv_at + qkv_width
     mine_zx, mine_bc, mine_qkv, mine_step, small = scatter_product(
-        hidden_one,
+        turned_one,
         grad_proj,
         [
             ([(0, 1, 0, channels)], [(0, 0, channels, 0, 0)]),

time: 356 us -> 357 us (level)
  no operation moved by 1% of the time
where the time goes in v7:
time: 357 us; the launch traced here: 356 us
  Pallas kernels  316 us (89%)
  matrix products  11.2 us (3%)
  local copies, waits for them, and re-layouts  9.53 us (3%)
  waiting for transfers between devices  8.19 us (2%)
  starting transfers between devices  7.72 us (2%)
    pallas_call x2, Pallas kernels, scatter_product(): pl.pallas_call(functools.partial(product_kernel, devices, groups, len(sha...  73.7 us
    pallas_call x2, Pallas kernels, gather_rows(): pl.pallas_call(functools.partial(gather_kernel, devices, count, windows),...  72.4 us
    pallas_call x1, Pallas kernels, run_scan_backward(): pl.pallas_call(functools.partial(scan_backward, devices, spans, windows,...  37.3 us
    pallas_call x1, Pallas kernels, run_scan_forward(): pl.pallas_call(functools.partial(scan_forward, devices, spans), grid=(spa...  24.1 us
    pallas_call x1, Pallas kernels, run_feed_forward(): pl.pallas_call(feed_forward, grid=(tokens // TBLK,), out_shape=(shape((to...  16.3 us
    pallas_call x1, Pallas kernels, run_attend_backward(): pl.pallas_call(attend_backward, grid=(1,), out_shape=jax.ShapeDtypeStruct...  16.2 us
    pallas_call x2, Pallas kernels, run_product(): pl.pallas_call(functools.partial(product_rows, dims), grid=(tokens // TBL...  12.6 us
    pallas_call x1, Pallas kernels, run_attend_forward(): pl.pallas_call(attend_forward, grid=(1,), out_shape=(jax.ShapeDtypeStruct...  12.5 us
  transfers between devices with their start and end apart: 8, of which 3 were waited for; matrix products, arithmetic and copies ran while one was open for 4% of the time, Pallas kernels for 57%

profile of v7, /device:TPU:0, one launch (start us, length us, event | category | flops | bytes accessed | tf_op | source)
XLA Modules:
  0.0 355.7 jit_solution(17348848064542568768)
XLA Ops:
  3.9 1.6 concatenate.9.refs_0_
  5.6 33.2 %gather_rows.2.w_ref = bf16[1024,2304]{1,0:T(8,128)(2,1)} custom-call(bf16[64,2304]{1,0:T(8,128)(2,1)} %concatenate.9.refs_0_), custom_call_target="tpu_custom_call" | custom-call | flops 3000000000 | tf_op jit(solution)/shard_map/gather_rows/pallas_call | solution.py:204
  40.3 10.1 %project.1 = (bf16[1024,1024]{1,0:T(8,128)(2,1)}, f32[1024,2304]{1,0:T(8,128)}, f32[8,1024]{1,0:T(8,128)}) custom-call(bf16[1024,1024]{1,0:T(8,128)(2,1)} %x_ref.7, bf16[1024,2304]{1,0:T(8,128)(2,1)} %gather_rows.2.w_ref), custom_call_target="tpu_custom_call" | custom-call | flops 8000000000 | tf_op jit(solution)/shard_map/project/pallas_call | solution.py:1346
  50.5 24.1 %scan_forward.1 = (f32[1024,768]{1,0:T(8,128)}, bf16[1024,768]{1,0:T(8,128)(2,1)}, f32[8,1024]{1,0:T(8,128)}, f32[8,128,768]{2,1,0:T(8,128)}, bf16[1024,1024]{1,0:T(8,128)(2,1)}) custom-call(f32[1024,2304]{1,0:T(8,128)} %get-tuple-element.108.z_ref.x_ref.bc_ref.step_ref.q_ref.kv_ref.xp_ref.bp_ref, ...), custom_call_target="tpu_custom_call" | custom-call | flops 20000000000 | tf_op jit(solution)/shard_map/scan_forward/pallas_call | solution.py:901
  74.7 1.6 collective-permute-start
  76.2 12.5 %attend_forward.1 = (bf16[1024,512]{1,0:T(8,128)(2,1)}, f32[8,1024]{1,0:T(8,128)}, bf16[1024,256]{1,0:T(8,128)(2,1)}) custom-call(f32[1024,2304]{1,0:T(8,128)} %get-tuple-element.108.z_ref.x_ref.bc_ref.step_ref.q_ref.kv_ref.xp_ref.bp_ref, f32[1024,2304]{1,0:T(8,128)} %get-tuple-element.108.z_ref.x_ref.bc_ref.step_ref.q_ref.kv_ref.xp_ref.bp_ref, ...), custom_call_target="tpu_custom_call" | custom-call | flops 15000000512 | tf_op jit(solution)/shard_map/attend_forward/pallas_call | solution.py:1227
  90.7 6.8 %mixer_forward.1 = (bf16[1024,1024]{1,0:T(8,128)(2,1)}, bf16[1024,1024]{1,0:T(8,128)(2,1)}) custom-call(bf16[1024,768]{1,0:T(8,128)(2,1)} %get-tuple-element.117.gated_ref, f32[8,1024]{1,0:T(8,128)} %add_rsqrt_fusion.scale_ref.scale_m_ref, f32[1,768]{1,0:T(1,128)} %reshape.65.gain_ref.gain_m_ref, bf16[1024,256]{1,0:T(8,128)(2,1)} %get-tuple-element.119.attended_ref.o_ref, ...), custom_call_target="tpu_custom_call" | custom-call | flops 5000000000 | tf_op jit(solution)/shard_map/mixer_forward/pallas_call | solution.py:1437
  98.0 39.1 %gather_rows.3 = (bf16[1024,2048]{1,0:T(8,128)(2,1)}, bf16[1024,1024]{1,0:T(8,128)(2,1)}) custom-call(bf16[64,2048]{1,0:T(8,128)(2,1)} %bitcast.29, bf16[64,1024]{1,0:T(8,128)(2,1)} %bitcast.36), custom_call_target="tpu_custom_call" | custom-call | flops 3000000000 | tf_op jit(solution)/shard_map/gather_rows/pallas_call | solution.py:204
  137.1 6.4 %product_rows.2.act_grad_ref = f32[1024,1024]{1,0:T(8,128)} custom-call(bf16[1024,1024]{1,0:T(8,128)(2,1)} %top_ref.1, bf16[1024,1024]{1,0:T(8,128)(2,1)} %get-tuple-element.134.right_ref), custom_call_target="tpu_custom_call" | custom-call | flops 4000000000 | tf_op jit(solution)/shard_map/product_rows/pallas_call | solution.py:1317
  143.5 1.8 collective-permute-done.1.other_ref
  146.6 16.3 %feed_forward.1 = (bf16[1024,1024]{1,0:T(8,128)(2,1)}, f32[1024,1]{1,0:T(8,128)}, bf16[1024,1024]{1,0:T(8,128)(2,1)}, bf16[1024,1024]{1,0:T(8,128)(2,1)}, bf16[1...) custom-call(bf16[1024,1024]{1,0:T(8,128)(2,1)} %x_ref.7, bf16[1024,1024]{1,0:T(8,128)(2,1)} %get-tuple-element.122.mixed_ref, ...), custom_call_target="tpu_custom_call" | custom-call | flops 14000000000 | tf_op jit(solution)/shard_map/feed_forward/pallas_call | solution.py:1404
  163.6 31.9 %scatter_product.2.refs_5_ = f32[64,2,1024]{2,1,0:T(2,128)} custom-call(bf16[1024,1024]{1,0:T(8,128)(2,1)} %get-tuple-element.131.left_ref, bf16[1024,2048]{1,0:T(8,128)(2,1)} %get-tuple-element.132.right_ref), custom_call_target="tpu_custom_call" | custom-call | flops 3000000000 | tf_op jit(solution)/shard_map/scatter_product/pallas_call | solution.py:567
  195.5 6.2 %product_rows.3.ffn_ref = bf16[1024,1024]{1,0:T(8,128)(2,1)} custom-call(bf16[1024,1024]{1,0:T(8,128)(2,1)} %get-tuple-element.133.left_ref, bf16[1024,1024]{1,0:T(8,128)(2,1)} %get-tuple-element.134.right_ref), custom_call_target="tpu_custom_call" | custom-call | flops 4000000000 | tf_op jit(solution)/shard_map/product_rows/pallas_call | solution.py:1317
  201.8 5.3 %convert_bitcast_fusion.refs_1_ = bf16[1024,1024]{1,0:T(8,128)(2,1)} fusion(bf16[1024,1024]{1,0:T(8,128)(2,1)} %get-tuple-element.133.left_ref, bf16[1024,1024]{1,0:T(8,128)(2,1)S(1)} %copy-done.13), kind=kOutput, calls=%fused_computation | convolution fusion | flops 2148532224 | bytes 6291456 | tf_op jit(solution)/shard_map/dot_general | solution.py:39
  207.1 3.1 collective-permute-done.2.other_ref
  210.1 12.5 %mixer_backward.1 = (bf16[1024,1024]{1,0:T(8,128)(2,1)}, bf16[1024,1024]{1,0:T(8,128)(2,1)}, f32[1024,768]{1,0:T(8,128)}, bf16[1024,256]{1,0:T(8,128)(2,1)}, f32[8,1024]{1,0:T(8,128)}, /*index=5*/f32[8,1024]{1,0:T(8,128)}) custom-call(bf16[1024,1024]{1,0:T(8,128)(2,1)} %get-tuple-element.130.part_ref, bf16[1024,1024]{1,0:T(8,128)(2,1)} %collective-permute-done.2.other_ref, ...), custom_call_target="tpu_custom_call" | custom-call | flops 8000000000 | tf_op jit(solution)/shard_map/mixer_backward/pallas_call | solution.py:1492
  224.7 16.2 %attend_backward.1.dqkv_ref = bf16[1024,384]{1,0:T(8,128)(2,1)} custom-call(bf16[1024,512]{1,0:T(8,128)(2,1)} %get-tuple-element.143.qkv_ref, f32[8,1024]{1,0:T(8,128)} %get-tuple-element.144.lse_ref, bf16[1024,256]{1,0:T(8,128)(2,1)} %get-tuple-element.119.attended_ref.o_ref, bf16[1024,256]{1,0:T(8,128)(2,1)} %get-tuple-element.145.do_ref, ...), custom_call_target="tpu_custom_call" | custom-call | flops 16000000000 | tf_op jit(solution)/shard_map/attend_backward/pallas_call | solution.py:1259
  240.9 5.9 %convolution_convert_fusion.refs_0_ = bf16[1024,1024]{1,0:T(8,128)(2,1)} fusion(bf16[1024,1024]{1,0:T(8,128)(2,1)} %get-tuple-element.146, bf16[1024,1024]{1,0:T(8,128)(2,1)} %get-tuple-element.147), kind=kOutput, calls=%fused_computation.1 | convolution fusion | flops 2148532224 | bytes 6291456 | tf_op jit(solution)/shard_map/dot_general | solution.py:39
  247.4 37.3 %scan_backward.1 = (bf16[1024,2304]{1,0:T(8,128)(2,1)}, f32[8,1024]{1,0:T(8,128)}, f32[8,128]{1,0:T(8,128)}, f32[64,768]{1,0:T(8,128)}, f32[64,256]{1,0:T(8,128)}, /*index=5*/f32[64,1024]{1,0:T(8,128)}) custom-call(f32[1024,2304]{1,0:T(8,128)} %get-tuple-element.108.z_ref.x_ref.bc_ref.step_ref.q_ref.kv_ref.xp_ref.bp_ref, ...), custom_call_target="tpu_custom_call" | custom-call | flops 46999998464 | tf_op jit(solution)/shard_map/scan_backward/pallas_call | solution.py:949
  284.7 9.6 %project_back.1 = (bf16[1024,1024]{1,0:T(8,128)(2,1)}, f32[8,1024]{1,0:T(8,128)}) custom-call(bf16[1024,2304]{1,0:T(8,128)(2,1)} %get-tuple-element.154.grad_ref.right_ref, bf16[1024,2304]{1,0:T(8,128)(2,1)} %gather_rows.2.w_ref, bf16[1024,1024]{1,0:T(8,128)(2,1)} %x_ref.7), custom_call_target="tpu_custom_call" | custom-call | flops 8000000000 | tf_op jit(solution)/shard_map/project_back/pallas_call | solution.py:1381
  295.1 41.8 %scatter_product.3 = (f32[64,2,768]{2,1,0:T(2,128)}, f32[64,256]{1,0:T(8,128)}, f32[64,1,384]{2,1,0:T(1,128)}, f32[12,64]{1,0:T(8,128)}, f32[72,128]{1,0:T(8,128)}) custom-call(bf16[1024,1024]{1,0:T(8,128)(2,1)} %get-tuple-element.153.left_ref, bf16[1024,2304]{1,0:T(8,128)(2,1)} %get-tuple-element.154.grad_ref.right_ref, ...), custom_call_target="tpu_custom_call" | custom-call | flops 3000000000 | tf_op jit(solution)/shard_map/scatter_product/pallas_call | solution.py:567
  338.2 3.3 collective-permute-done.5.other_ref
  342.9 10.0 %finish_layer.1 = (f32[1024,1024]{1,0:T(8,128)}, bf16[1024,1024]{1,0:T(8,128)(2,1)}, f32[64,2,768]{2,1,0:T(2,128)}, f32[64,1,384]{2,1,0:T(1,128)}, f32[12,64]{1,...) custom-call(bf16[1024,1024]{1,0:T(8,128)(2,1)} %x_ref.7, ...), custom_call_target="tpu_custom_call" | custom-call | flops 8000000000 | tf_op jit(solution)/shard_map/finish_layer/pallas_call | solution.py:1569
  354.2 1.6 finish_shared.1
  (60 shorter events, 16.6 us)
Async XLA Ops:
  5.6 33.3 %copy-start.7 = (bf16[768]{0:T(1024)(128)(2,1)S(1)}, bf16[768]{0:T(1024)(128)(2,1)}, u32[]{:S(2)}) copy-start(bf16[768]{0:T(1024)(128)(2,1)} %param.36) | copy-start | bytes 4612
  5.6 33.4 %copy-start.8 = (bf16[768]{0:T(1024)(128)(2,1)S(1)}, bf16[768]{0:T(1024)(128)(2,1)}, u32[]{:S(2)}) copy-start(bf16[768]{0:T(1024)(128)(2,1)} %param.30) | copy-start | bytes 4612
  5.6 33.4 %copy-start.9 = (bf16[256]{0:T(256)(128)(2,1)S(1)}, bf16[256]{0:T(256)(128)(2,1)}, u32[]{:S(2)}) copy-start(bf16[256]{0:T(256)(128)(2,1)} %param.32) | copy-start | bytes 1540
  5.6 33.4 %copy-start.10 = (bf16[12]{0:T(256)(128)(2,1)S(1)}, bf16[12]{0:T(256)(128)(2,1)}, u32[]{:S(2)}) copy-start(bf16[12]{0:T(256)(128)(2,1)} %param.33) | copy-start | bytes 76
  5.6 33.4 %copy-start.11 = (bf16[12]{0:T(256)(128)(2,1)S(1)}, bf16[12]{0:T(256)(128)(2,1)}, u32[]{:S(2)}) copy-start(bf16[12]{0:T(256)(128)(2,1)} %param.34) | copy-start | bytes 76
  5.6 33.4 %copy-start.12 = (bf16[12]{0:T(256)(128)(2,1)S(1)}, bf16[12]{0:T(256)(128)(2,1)}, u32[]{:S(2)}) copy-start(bf16[12]{0:T(256)(128)(2,1)} %param.35) | copy-start | bytes 76
  5.6 34.1 %copy-start.1 = (bf16[768,64]{0,1:T(8,128)(2,1)S(1)}, bf16[768,64]{0,1:T(8,128)(2,1)}, u32[]{:S(2)}) copy-start(bf16[768,64]{0,1:T(8,128)(2,1)} %param.37) | copy-start | bytes 294916
  5.6 34.1 %copy-start.6 = (bf16[1,256,64]{1,2,0:T(8,128)(2,1)S(1)}, bf16[1,256,64]{1,2,0:T(8,128)(2,1)}, u32[]{:S(2)}) copy-start(bf16[1,256,64]{1,2,0:T(8,128)(2,1)} %param.39) | copy-start | bytes 98308
  74.6 14.7 %copy-start = (bf16[64,2,1024]{2,1,0:T(2,128)(2,1)S(1)}, bf16[64,2,1024]{2,1,0:T(2,128)(2,1)}, u32[]{:S(2)}) copy-start(bf16[64,2,1024]{2,1,0:T(2,128)(2,1)} %param.41) | copy-start | bytes 786436
  74.6 15.4 %copy-start.5 = (f32[8,1024]{1,0:T(8,128)S(1)}, f32[8,1024]{1,0:T(8,128)}, u32[]{:S(2)}) copy-start(f32[8,1024]{1,0:T(8,128)} %get-tuple-element.118) | copy-start | bytes 98308
  74.7 15.4 %collective-permute-start = (f32[8,1024]{1,0:T(8,128)}, f32[8,1024]{1,0:T(8,128)S(1)}, u32[]{:S(2)}, u32[]{:S(2)}) collective-permute-start(f32[8,1024]{1,0:T(8,128)} %get-tuple-element.118), channel_id=1, source_target_pairs={{0,1},{1,0},{2,3},{3,2},{4,5},{5,4},{6,7},{7,6},{8,9},{9,8},{10,11... | collective-permute-start | bytes 98312 | tf_op jit(solution)/shard_map/ppermute | solution.py:1607
  97.5 47.8 %collective-permute-start.1 = (bf16[1024,1024]{1,0:T(8,128)(2,1)}, bf16[1024,1024]{1,0:T(8,128)(2,1)S(1)}, u32[]{:S(2)}, u32[]{:S(2)}) collective-permute-start(bf16[1024,1024]{1,0:T(8,128)(2,1)} %get-tuple-element.122.mixed_ref), channel_id=1, source_target_pairs={{0,1},{1,0},{2,3},{3,2},{4,5},{5,4},{6,7},{7,6},{8,9},{9,8},{10,11... | collective-permute-start | bytes 6291464 | tf_op jit(solution)/shard_map/ppermute | solution.py:1607
  145.3 1.3 copy-start.16
  163.0 47.2 %collective-permute-start.2 = (bf16[1024,1024]{1,0:T(8,128)(2,1)}, bf16[1024,1024]{1,0:T(8,128)(2,1)}, u32[]{:S(2)}, u32[]{:S(2)}) collective-permute-start(bf16[1024,1024]{1,0:T(8,128)(2,1)} %get-tuple-element.130.part_ref), channel_id=1, source_target_pairs={{0,1},{1,0},{2,3},{3,2},{4,5},{5,4},{6,7},{7,6},{8,9},{9,8},{10,11... | collective-permute-start | bytes 6291464 | tf_op jit(solution)/shard_map/ppermute | solution.py:1607
  195.5 6.3 %copy-start.13 = (bf16[1024,1024]{1,0:T(8,128)(2,1)S(1)}, bf16[1024,1024]{1,0:T(8,128)(2,1)}, u32[]{:S(2)}) copy-start(bf16[1024,1024]{1,0:T(8,128)(2,1)} %top_ref.1) | copy-start | bytes 6291460
  210.1 13.3 %copy-start.14 = (bf16[1024,1024]{1,0:T(8,128)(2,1)S(1)}, bf16[1024,1024]{1,0:T(8,128)(2,1)}, u32[]{:S(2)}) copy-start(bf16[1024,1024]{1,0:T(8,128)(2,1)} %product_rows.3.ffn_ref) | copy-start | bytes 6291460
  222.6 24.2 %collective-permute-start.4 = (f32[8,1024]{1,0:T(8,128)}, f32[8,1024]{1,0:T(8,128)S(1)}, u32[]{:S(2)}, u32[]{:S(2)}) collective-permute-start(f32[8,1024]{1,0:T(8,128)} %get-tuple-element.142), channel_id=1, source_target_pairs={{0,1},{1,0},{2,3},{3,2},{4,5},{5,4},{6,7},{7,6},{8,9},{9,8},{10,11... | collective-permute-start | bytes 98312 | tf_op jit(solution)/shard_map/ppermute | solution.py:1607
  223.4 61.2 %collective-permute-start.3 = (bf16[1024,1024]{1,0:T(8,128)(2,1)S(1)}, bf16[1024,1024]{1,0:T(8,128)(2,1)}, u32[]{:S(2)}, u32[]{:S(2)}) collective-permute-start(bf16[1024,1024]{1,0:T(8,128)(2,1)S(1)} %copy-done.14), channel_id=1, source_target_pairs={{0,1},{1,0},{2,3},{3,2},{4,5},{5,4},{6,7},{7,6},{8,9},{9,8},{10,11... | collective-permute-start | bytes 6291464 | tf_op jit(solution)/shard_map/ppermute | solution.py:1607
  240.9 5.9 %copy-start.4 = (f32[8,1024]{1,0:T(8,128)S(1)}, f32[8,1024]{1,0:T(8,128)}, u32[]{:S(2)}) copy-start(f32[8,1024]{1,0:T(8,128)} %get-tuple-element.142) | copy-start | bytes 98308
  294.3 47.2 %collective-permute-start.5 = (bf16[1024,1024]{1,0:T(8,128)(2,1)}, bf16[1024,1024]{1,0:T(8,128)(2,1)S(1)}, u32[]{:S(2)}, u32[]{:S(2)}) collective-permute-start(bf16[1024,1024]{1,0:T(8,128)(2,1)} %get-tuple-element.152.part_ref), channel_id=1, source_target_pairs={{0,1},{1,0},{2,3},{3,2},{4,5},{5,4},{6,7},{7,6},{8,9},{9,8},{10,11... | collective-permute-start | bytes 6291464 | tf_op jit(solution)/shard_map/ppermute | solution.py:1607
  336.9 16.1 %collective-permute-start.6 = (f32[72,128]{1,0:T(8,128)}, f32[72,128]{1,0:T(8,128)S(1)}, u32[]{:S(2)}, u32[]{:S(2)}) collective-permute-start(f32[72,128]{1,0:T(8,128)} %get-tuple-element.163.total_ref), channel_id=1, source_target_pairs={{0,1},{1,0},{2,3},{3,2},{4,5},{5,4},{6,7},{7,6},{8,9},{9,8},{10,11... | collective-permute-start | bytes 110600 | tf_op jit(solution)/shard_map/ppermute | solution.py:1607
  341.5 1.4 copy-start.15
  341.5 11.4 %collective-permute-start.7 = (f32[64,256]{1,0:T(8,128)}, f32[64,256]{1,0:T(8,128)S(1)}, u32[]{:S(2)}, u32[]{:S(2)}) collective-permute-start(f32[64,256]{1,0:T(8,128)} %get-tuple-element.173.mine_ref), channel_id=1, source_target_pairs={{0,1},{1,0},{2,3},{3,2},{4,5},{5,4},{6,7},{7,6},{8,9},{9,8},{10,11... | collective-permute-start | bytes 196616 | tf_op jit(solution)/shard_map/ppermute | solution.py:1607
  353.6 0.6 copy-start.2
  (1 other events, 0.6 us)

commit v8 on v5

--- a/solution.py
+++ b/solution.py
@@ -664,13 +664,19 @@
     state, buffer, *sems,
 ):
     span, channels = x_ref.shape
-    ring = RingGather(devices, shard_ref, all_ref, sems)
+    width = shard_ref.shape[1]
+    each = len(sems) // 2
+    rings = [
+        RingGather(devices, shard_ref, all_ref, sems[:each], slice(0, width // 2)),
+        RingGather(devices, shard_ref, all_ref, sems[each:], slice(width // 2, width)),
+    ]
     turn = pl.program_id(0)
 
     @pl.when(turn == 0)
     def _():
-        ring.greet()
-        ring.begin()
+        rings[0].greet()
+        for ring in rings:
+            ring.begin()
 
 
     @pl.when(pl.program_id(0) == 0)
@@ -713,12 +719,13 @@
     gated_ref[...] = gated.astype(BF16)
     square_ref[...] = row_sums(gated * gated)
 
-    count = spans
-    for step in range(1, ring.ahead + 1):
-        pl.when(turn == min(count - 1, count * step // ring.ahead))(
-            functools.partial(ring.hop, step)
-        )
-    pl.when(turn == count - 1)(ring.finish)
+    ahead = rings[0].ahead
+    for step in range(1, ahead + 1):
+        after = max(0, spans * step // ahead - (2 if step == ahead else 1))
+        for ring in rings:
+            pl.when(turn == after)(functools.partial(ring.hop, step))
+    for ring in rings:
+        pl.when(turn == spans - 1)(ring.finish)
 
 
 def scan_backward(
@@ -928,7 +935,7 @@
             pltpu.VMEM((NS, channels), F32),
             pltpu.VMEM((SPAN + EDGE, channels + 2 * NS), F32),
         ]
-        + gather_sems(devices),
+        + gather_sems(devices) * 2,
         compiler_params=pltpu.CompilerParams(collective_id=2, has_side_effects=True),
         cost_estimate=cost(20),
         name="scan_forward",

time: 356 us -> 354 us (level)
  no operation moved by 1% of the time
where the time goes in v8:
time: 354 us; the launch traced here: 353 us
  Pallas kernels  314 us (89%)
  matrix products  11.2 us (3%)
  local copies, waits for them, and re-layouts  9.19 us (3%)
  starting transfers between devices  7.86 us (2%)
  waiting for transfers between devices  6.71 us (2%)
    pallas_call x2, Pallas kernels, scatter_product(): pl.pallas_call(functools.partial(product_kernel, devices, groups, len(sha...  75 us
    pallas_call x2, Pallas kernels, gather_rows(): pl.pallas_call(functools.partial(gather_kernel, devices, count, windows),...  72.3 us
    pallas_call x1, Pallas kernels, run_scan_backward(): pl.pallas_call(functools.partial(scan_backward, devices, spans, windows,...  37.5 us
    pallas_call x1, Pallas kernels, run_scan_forward(): pl.pallas_call(functools.partial(scan_forward, devices, spans), grid=(spa...  22.7 us
    pallas_call x1, Pallas kernels, run_attend_backward(): pl.pallas_call(attend_backward, grid=(1,), out_shape=jax.ShapeDtypeStruct...  16.2 us
    pallas_call x1, Pallas kernels, run_feed_forward(): pl.pallas_call(feed_forward, grid=(tokens // TBLK,), out_shape=(shape((to...  16.1 us
    pallas_call x2, Pallas kernels, run_product(): pl.pallas_call(functools.partial(product_rows, dims), grid=(tokens // TBL...  12.6 us
    pallas_call x1, Pallas kernels, run_attend_forward(): pl.pallas_call(attend_forward, grid=(1,), out_shape=(jax.ShapeDtypeStruct...  12.5 us
  transfers between devices with their start and end apart: 8, of which 3 were waited for; matrix products, arithmetic and copies ran while one was open for 4% of the time, Pallas kernels for 57%

profile of v8, /device:TPU:0, one launch (start us, length us, event | category | flops | bytes accessed | tf_op | source)
XLA Modules:
  0.0 352.8 jit_solution(5217536004479278667)
XLA Ops:
  3.9 1.6 concatenate.9.refs_0_
  5.6 33.2 %gather_rows.2.w_ref = bf16[1024,2304]{1,0:T(8,128)(2,1)} custom-call(bf16[64,2304]{1,0:T(8,128)(2,1)} %concatenate.9.refs_0_), custom_call_target="tpu_custom_call" | custom-call | flops 3000000000 | tf_op jit(solution)/shard_map/gather_rows/pallas_call | solution.py:204
  40.3 10.2 %project.1 = (bf16[1024,1024]{1,0:T(8,128)(2,1)}, f32[1024,2304]{1,0:T(8,128)}, f32[8,1024]{1,0:T(8,128)}) custom-call(bf16[1024,1024]{1,0:T(8,128)(2,1)} %x_ref.7, bf16[1024,2304]{1,0:T(8,128)(2,1)} %gather_rows.2.w_ref), custom_call_target="tpu_custom_call" | custom-call | flops 8000000000 | tf_op jit(solution)/shard_map/project/pallas_call | solution.py:1359
  50.5 22.7 %scan_forward.1 = (f32[1024,768]{1,0:T(8,128)}, bf16[1024,768]{1,0:T(8,128)(2,1)}, f32[8,1024]{1,0:T(8,128)}, f32[8,128,768]{2,1,0:T(8,128)}, bf16[1024,1024]{1,0:T(8,128)(2,1)}) custom-call(f32[1024,2304]{1,0:T(8,128)} %get-tuple-element.107.z_ref.x_ref.bc_ref.step_ref.q_ref.kv_ref.xp_ref.bp_ref, ...), custom_call_target="tpu_custom_call" | custom-call | flops 20000000000 | tf_op jit(solution)/shard_map/scan_forward/pallas_call | solution.py:914
  73.3 1.5 collective-permute-start
  74.8 12.5 %attend_forward.1 = (bf16[1024,512]{1,0:T(8,128)(2,1)}, f32[8,1024]{1,0:T(8,128)}, bf16[1024,256]{1,0:T(8,128)(2,1)}) custom-call(f32[1024,2304]{1,0:T(8,128)} %get-tuple-element.107.z_ref.x_ref.bc_ref.step_ref.q_ref.kv_ref.xp_ref.bp_ref, f32[1024,2304]{1,0:T(8,128)} %get-tuple-element.107.z_ref.x_ref.bc_ref.step_ref.q_ref.kv_ref.xp_ref.bp_ref, ...), custom_call_target="tpu_custom_call" | custom-call | flops 15000000512 | tf_op jit(solution)/shard_map/attend_forward/pallas_call | solution.py:1240
  89.3 6.8 %mixer_forward.1 = (bf16[1024,1024]{1,0:T(8,128)(2,1)}, bf16[1024,1024]{1,0:T(8,128)(2,1)}) custom-call(bf16[1024,768]{1,0:T(8,128)(2,1)} %get-tuple-element.116.gated_ref, f32[8,1024]{1,0:T(8,128)} %add_rsqrt_fusion.scale_ref.scale_m_ref, f32[1,768]{1,0:T(1,128)} %reshape.65.gain_ref.gain_m_ref, bf16[1024,256]{1,0:T(8,128)(2,1)} %get-tuple-element.118.attended_ref.o_ref, ...), custom_call_target="tpu_custom_call" | custom-call | flops 5000000000 | tf_op jit(solution)/shard_map/mixer_forward/pallas_call | solution.py:1445
  96.6 39.0 %gather_rows.3 = (bf16[1024,2048]{1,0:T(8,128)(2,1)}, bf16[1024,1024]{1,0:T(8,128)(2,1)}) custom-call(bf16[64,2048]{1,0:T(8,128)(2,1)} %bitcast.29, bf16[64,1024]{1,0:T(8,128)(2,1)} %bitcast.36), custom_call_target="tpu_custom_call" | custom-call | flops 3000000000 | tf_op jit(solution)/shard_map/gather_rows/pallas_call | solution.py:204
  135.7 6.4 %product_rows.2.act_grad_ref = f32[1024,1024]{1,0:T(8,128)} custom-call(bf16[1024,1024]{1,0:T(8,128)(2,1)} %top_ref.1, bf16[1024,1024]{1,0:T(8,128)(2,1)} %get-tuple-element.133.right_ref), custom_call_target="tpu_custom_call" | custom-call | flops 4000000000 | tf_op jit(solution)/shard_map/product_rows/pallas_call | solution.py:1330
  142.0 1.6 collective-permute-done.1.other_ref
  144.9 16.1 %feed_forward.1 = (bf16[1024,1024]{1,0:T(8,128)(2,1)}, f32[1024,1]{1,0:T(8,128)}, bf16[1024,1024]{1,0:T(8,128)(2,1)}, bf16[1024,1024]{1,0:T(8,128)(2,1)}, bf16[1...) custom-call(bf16[1024,1024]{1,0:T(8,128)(2,1)} %x_ref.7, bf16[1024,1024]{1,0:T(8,128)(2,1)} %get-tuple-element.121.mixed_ref, ...), custom_call_target="tpu_custom_call" | custom-call | flops 14000000000 | tf_op jit(solution)/shard_map/feed_forward/pallas_call | solution.py:1415
  161.6 32.6 %scatter_product.2.refs_5_ = f32[64,2,1024]{2,1,0:T(2,128)} custom-call(bf16[1024,1024]{1,0:T(8,128)(2,1)} %get-tuple-element.130.left_ref, bf16[1024,2048]{1,0:T(8,128)(2,1)} %get-tuple-element.131.right_ref), custom_call_target="tpu_custom_call" | custom-call | flops 3000000000 | tf_op jit(solution)/shard_map/scatter_product/pallas_call | solution.py:573
  194.2 6.2 %product_rows.3.ffn_ref = bf16[1024,1024]{1,0:T(8,128)(2,1)} custom-call(bf16[1024,1024]{1,0:T(8,128)(2,1)} %get-tuple-element.132.left_ref, bf16[1024,1024]{1,0:T(8,128)(2,1)} %get-tuple-element.133.right_ref), custom_call_target="tpu_custom_call" | custom-call | flops 4000000000 | tf_op jit(solution)/shard_map/product_rows/pallas_call | solution.py:1330
  200.5 5.3 %convert_bitcast_fusion.refs_1_ = bf16[1024,1024]{1,0:T(8,128)(2,1)} fusion(bf16[1024,1024]{1,0:T(8,128)(2,1)} %get-tuple-element.132.left_ref, bf16[1024,1024]{1,0:T(8,128)(2,1)S(1)} %copy-done.13), kind=kOutput, calls=%fused_computation | convolution fusion | flops 2148532224 | bytes 6291456 | tf_op jit(solution)/shard_map/dot_general | solution.py:39
  205.8 2.2 collective-permute-done.2.other_ref
  207.9 11.4 %mixer_backward.1 = (bf16[1024,1024]{1,0:T(8,128)(2,1)}, f32[1024,768]{1,0:T(8,128)}, bf16[1024,256]{1,0:T(8,128)(2,1)}, f32[8,1024]{1,0:T(8,128)}, f32[8,1024]{1,0:T(8,128)}) custom-call(bf16[1024,1024]{1,0:T(8,128)(2,1)} %get-tuple-element.129.part_ref, bf16[1024,1024]{1,0:T(8,128)(2,1)} %collective-permute-done.2.other_ref, ...), custom_call_target="tpu_custom_call" | custom-call | flops 8000000000 | tf_op jit(solution)/shard_map/mixer_backward/pallas_call | solution.py:1498
  221.4 16.2 %attend_backward.1.dqkv_ref = bf16[1024,384]{1,0:T(8,128)(2,1)} custom-call(bf16[1024,512]{1,0:T(8,128)(2,1)} %get-tuple-element.142.qkv_ref, f32[8,1024]{1,0:T(8,128)} %get-tuple-element.143.lse_ref, bf16[1024,256]{1,0:T(8,128)(2,1)} %get-tuple-element.118.attended_ref.o_ref, bf16[1024,256]{1,0:T(8,128)(2,1)} %get-tuple-element.144.do_ref, ...), custom_call_target="tpu_custom_call" | custom-call | flops 16000000000 | tf_op jit(solution)/shard_map/attend_backward/pallas_call | solution.py:1272
  237.6 5.9 %convolution_convert_fusion.refs_0_ = bf16[1024,1024]{1,0:T(8,128)(2,1)} fusion(bf16[1024,1024]{1,0:T(8,128)(2,1)} %get-tuple-element.145.grad_ref, bf16[1024,1024]{1,0:T(8,128)(2,1)} %get-tuple-element.146), kind=kOutput, calls=%fused_computation.1 | convolution fusion | flops 2148532224 | bytes 6291456 | tf_op jit(solution)/shard_map/dot_general | solution.py:39
  244.2 37.5 %scan_backward.1 = (bf16[1024,2304]{1,0:T(8,128)(2,1)}, f32[8,1024]{1,0:T(8,128)}, f32[8,128]{1,0:T(8,128)}, f32[64,768]{1,0:T(8,128)}, f32[64,256]{1,0:T(8,128)}, /*index=5*/f32[64,1024]{1,0:T(8,128)}) custom-call(f32[1024,2304]{1,0:T(8,128)} %get-tuple-element.107.z_ref.x_ref.bc_ref.step_ref.q_ref.kv_ref.xp_ref.bp_ref, ...), custom_call_target="tpu_custom_call" | custom-call | flops 46999998464 | tf_op jit(solution)/shard_map/scan_backward/pallas_call | solution.py:962
  281.7 9.6 %project_back.1 = (bf16[1024,1024]{1,0:T(8,128)(2,1)}, f32[8,1024]{1,0:T(8,128)}) custom-call(bf16[1024,2304]{1,0:T(8,128)(2,1)} %get-tuple-element.153.grad_ref.right_ref, bf16[1024,2304]{1,0:T(8,128)(2,1)} %gather_rows.2.w_ref, bf16[1024,1024]{1,0:T(8,128)(2,1)} %x_ref.7), custom_call_target="tpu_custom_call" | custom-call | flops 8000000000 | tf_op jit(solution)/shard_map/project_back/pallas_call | solution.py:1392
  292.5 42.4 %scatter_product.3 = (f32[64,2,768]{2,1,0:T(2,128)}, f32[64,256]{1,0:T(8,128)}, f32[64,1,384]{2,1,0:T(1,128)}, f32[12,64]{1,0:T(8,128)}, f32[72,128]{1,0:T(8,128)}) custom-call(bf16[1024,1024]{1,0:T(8,128)(2,1)} %get-tuple-element.152.left_ref, bf16[1024,2304]{1,0:T(8,128)(2,1)} %get-tuple-element.153.grad_ref.right_ref, ...), custom_call_target="tpu_custom_call" | custom-call | flops 3000000000 | tf_op jit(solution)/shard_map/scatter_product/pallas_call | solution.py:573
  335.7 2.9 collective-permute-done.5.other_ref
  340.0 10.0 %finish_layer.1 = (f32[1024,1024]{1,0:T(8,128)}, bf16[1024,1024]{1,0:T(8,128)(2,1)}, f32[64,2,768]{2,1,0:T(2,128)}, f32[64,1,384]{2,1,0:T(1,128)}, f32[12,64]{1,...) custom-call(bf16[1024,1024]{1,0:T(8,128)(2,1)} %x_ref.7, ...), custom_call_target="tpu_custom_call" | custom-call | flops 8000000000 | tf_op jit(solution)/shard_map/finish_layer/pallas_call | solution.py:1573
  351.3 1.6 finish_shared.1
  (60 shorter events, 16.4 us)
Async XLA Ops:
  5.6 33.3 %copy-start.7 = (bf16[768]{0:T(1024)(128)(2,1)S(1)}, bf16[768]{0:T(1024)(128)(2,1)}, u32[]{:S(2)}) copy-start(bf16[768]{0:T(1024)(128)(2,1)} %param.36) | copy-start | bytes 4612
  5.6 33.4 %copy-start.8 = (bf16[768]{0:T(1024)(128)(2,1)S(1)}, bf16[768]{0:T(1024)(128)(2,1)}, u32[]{:S(2)}) copy-start(bf16[768]{0:T(1024)(128)(2,1)} %param.30) | copy-start | bytes 4612
  5.6 33.4 %copy-start.9 = (bf16[256]{0:T(256)(128)(2,1)S(1)}, bf16[256]{0:T(256)(128)(2,1)}, u32[]{:S(2)}) copy-start(bf16[256]{0:T(256)(128)(2,1)} %param.32) | copy-start | bytes 1540
  5.6 33.4 %copy-start.10 = (bf16[12]{0:T(256)(128)(2,1)S(1)}, bf16[12]{0:T(256)(128)(2,1)}, u32[]{:S(2)}) copy-start(bf16[12]{0:T(256)(128)(2,1)} %param.33) | copy-start | bytes 76
  5.6 33.4 %copy-start.11 = (bf16[12]{0:T(256)(128)(2,1)S(1)}, bf16[12]{0:T(256)(128)(2,1)}, u32[]{:S(2)}) copy-start(bf16[12]{0:T(256)(128)(2,1)} %param.34) | copy-start | bytes 76
  5.6 33.4 %copy-start.12 = (bf16[12]{0:T(256)(128)(2,1)S(1)}, bf16[12]{0:T(256)(128)(2,1)}, u32[]{:S(2)}) copy-start(bf16[12]{0:T(256)(128)(2,1)} %param.35) | copy-start | bytes 76
  5.6 34.1 %copy-start.1 = (bf16[768,64]{0,1:T(8,128)(2,1)S(1)}, bf16[768,64]{0,1:T(8,128)(2,1)}, u32[]{:S(2)}) copy-start(bf16[768,64]{0,1:T(8,128)(2,1)} %param.37) | copy-start | bytes 294916
  5.6 34.1 %copy-start.6 = (bf16[1,256,64]{1,2,0:T(8,128)(2,1)S(1)}, bf16[1,256,64]{1,2,0:T(8,128)(2,1)}, u32[]{:S(2)}) copy-start(bf16[1,256,64]{1,2,0:T(8,128)(2,1)} %param.39) | copy-start | bytes 98308
  73.3 14.6 %copy-start = (bf16[64,2,1024]{2,1,0:T(2,128)(2,1)S(1)}, bf16[64,2,1024]{2,1,0:T(2,128)(2,1)}, u32[]{:S(2)}) copy-start(bf16[64,2,1024]{2,1,0:T(2,128)(2,1)} %param.41) | copy-start | bytes 786436
  73.3 15.4 %copy-start.5 = (f32[8,1024]{1,0:T(8,128)S(1)}, f32[8,1024]{1,0:T(8,128)}, u32[]{:S(2)}) copy-start(f32[8,1024]{1,0:T(8,128)} %get-tuple-element.117) | copy-start | bytes 98308
  73.3 15.4 %collective-permute-start = (f32[8,1024]{1,0:T(8,128)}, f32[8,1024]{1,0:T(8,128)S(1)}, u32[]{:S(2)}, u32[]{:S(2)}) collective-permute-start(f32[8,1024]{1,0:T(8,128)} %get-tuple-element.117), channel_id=1, source_target_pairs={{0,1},{1,0},{2,3},{3,2},{4,5},{5,4},{6,7},{7,6},{8,9},{9,8},{10,11... | collective-permute-start | bytes 98312 | tf_op jit(solution)/shard_map/ppermute | solution.py:1611
  96.1 47.6 %collective-permute-start.1 = (bf16[1024,1024]{1,0:T(8,128)(2,1)}, bf16[1024,1024]{1,0:T(8,128)(2,1)S(1)}, u32[]{:S(2)}, u32[]{:S(2)}) collective-permute-start(bf16[1024,1024]{1,0:T(8,128)(2,1)} %get-tuple-element.121.mixed_ref), channel_id=1, source_target_pairs={{0,1},{1,0},{2,3},{3,2},{4,5},{5,4},{6,7},{7,6},{8,9},{9,8},{10,11... | collective-permute-start | bytes 6291464 | tf_op jit(solution)/shard_map/ppermute | solution.py:1611
  143.7 1.3 copy-start.16
  161.0 46.9 %collective-permute-start.2 = (bf16[1024,1024]{1,0:T(8,128)(2,1)}, bf16[1024,1024]{1,0:T(8,128)(2,1)}, u32[]{:S(2)}, u32[]{:S(2)}) collective-permute-start(bf16[1024,1024]{1,0:T(8,128)(2,1)} %get-tuple-element.129.part_ref), channel_id=1, source_target_pairs={{0,1},{1,0},{2,3},{3,2},{4,5},{5,4},{6,7},{7,6},{8,9},{9,8},{10,11... | collective-permute-start | bytes 6291464 | tf_op jit(solution)/shard_map/ppermute | solution.py:1611
  194.2 6.3 %copy-start.13 = (bf16[1024,1024]{1,0:T(8,128)(2,1)S(1)}, bf16[1024,1024]{1,0:T(8,128)(2,1)}, u32[]{:S(2)}) copy-start(bf16[1024,1024]{1,0:T(8,128)(2,1)} %top_ref.1) | copy-start | bytes 6291460
  207.9 12.7 %copy-start.14 = (bf16[1024,1024]{1,0:T(8,128)(2,1)S(1)}, bf16[1024,1024]{1,0:T(8,128)(2,1)}, u32[]{:S(2)}) copy-start(bf16[1024,1024]{1,0:T(8,128)(2,1)} %product_rows.3.ffn_ref) | copy-start | bytes 6291460
  219.3 24.2 %collective-permute-start.4 = (f32[8,1024]{1,0:T(8,128)}, f32[8,1024]{1,0:T(8,128)S(1)}, u32[]{:S(2)}, u32[]{:S(2)}) collective-permute-start(f32[8,1024]{1,0:T(8,128)} %get-tuple-element.141), channel_id=1, source_target_pairs={{0,1},{1,0},{2,3},{3,2},{4,5},{5,4},{6,7},{7,6},{8,9},{9,8},{10,11... | collective-permute-start | bytes 98312 | tf_op jit(solution)/shard_map/ppermute | solution.py:1611
  220.6 61.0 %collective-permute-start.3 = (bf16[1024,1024]{1,0:T(8,128)(2,1)S(1)}, bf16[1024,1024]{1,0:T(8,128)(2,1)}, u32[]{:S(2)}, u32[]{:S(2)}) collective-permute-start(bf16[1024,1024]{1,0:T(8,128)(2,1)S(1)} %copy-done.14), channel_id=1, source_target_pairs={{0,1},{1,0},{2,3},{3,2},{4,5},{5,4},{6,7},{7,6},{8,9},{9,8},{10,11... | collective-permute-start | bytes 6291464 | tf_op jit(solution)/shard_map/ppermute | solution.py:1611
  237.6 5.9 %copy-start.4 = (f32[8,1024]{1,0:T(8,128)S(1)}, f32[8,1024]{1,0:T(8,128)}, u32[]{:S(2)}) copy-start(f32[8,1024]{1,0:T(8,128)} %get-tuple-element.141) | copy-start | bytes 98308
  291.3 47.3 %collective-permute-start.5 = (bf16[1024,1024]{1,0:T(8,128)(2,1)}, bf16[1024,1024]{1,0:T(8,128)(2,1)S(1)}, u32[]{:S(2)}, u32[]{:S(2)}) collective-permute-start(bf16[1024,1024]{1,0:T(8,128)(2,1)} %get-tuple-element.151.part_ref), channel_id=1, source_target_pairs={{0,1},{1,0},{2,3},{3,2},{4,5},{5,4},{6,7},{7,6},{8,9},{9,8},{10,11... | collective-permute-start | bytes 6291464 | tf_op jit(solution)/shard_map/ppermute | solution.py:1611
  334.9 15.1 %collective-permute-start.6 = (f32[72,128]{1,0:T(8,128)}, f32[72,128]{1,0:T(8,128)S(1)}, u32[]{:S(2)}, u32[]{:S(2)}) collective-permute-start(f32[72,128]{1,0:T(8,128)} %get-tuple-element.161.total_ref), channel_id=1, source_target_pairs={{0,1},{1,0},{2,3},{3,2},{4,5},{5,4},{6,7},{7,6},{8,9},{9,8},{10,11... | collective-permute-start | bytes 110600 | tf_op jit(solution)/shard_map/ppermute | solution.py:1611
  338.6 1.4 copy-start.15
  338.6 11.4 %collective-permute-start.7 = (f32[64,256]{1,0:T(8,128)}, f32[64,256]{1,0:T(8,128)S(1)}, u32[]{:S(2)}, u32[]{:S(2)}) collective-permute-start(f32[64,256]{1,0:T(8,128)} %get-tuple-element.171.mine_ref), channel_id=1, source_target_pairs={{0,1},{1,0},{2,3},{3,2},{4,5},{5,4},{6,7},{7,6},{8,9},{9,8},{10,11... | collective-permute-start | bytes 196616 | tf_op jit(solution)/shard_map/ppermute | solution.py:1611
  350.6 0.6 copy-start.2
  (1 other events, 0.6 us)

commit v9 on v8

--- a/solution.py
+++ b/solution.py
@@ -1619,9 +1619,9 @@
     return join(partial, swap(partial))
 
 
-def thirds(size):
-    part = size // 3
-    return [(0, part), (part, 2 * part), (2 * part, size)]
+def windows_of(size, count):
+    part = size // count // LANES * LANES
+    return [(i * part, size if i == count - 1 else (i + 1) * part) for i in range(count)]
 
 
 def local(
@@ -1645,7 +1645,7 @@
         [w_zx.reshape(shard, -1), w_bc, query_key_value_weight.reshape(shard, -1), tail], axis=1
     )
     in_width = mixer_in.shape[1]
-    (w_in,) = gather_rows([mixer_in], devices, 0, [(0, *window) for window in thirds(in_width)])
+    (w_in,) = gather_rows([mixer_in], devices, 0, [(0, *window) for window in windows_of(in_width, 6)])
     w_in, *small_params = lax.optimization_barrier(
         (w_in, conv_x, conv_xb, conv_bc, conv_bcb, dt_bias, a_log, d_skip, w_mnorm)
     )

time: 354 us -> 355 us (level)
  no operation moved by 1% of the time
where the time goes in v9:
time: 355 us; the launch traced here: 354 us
  Pallas kernels  316 us (89%)
  matrix products  11.2 us (3%)
  local copies, waits for them, and re-layouts  9.2 us (3%)
  starting transfers between devices  7.83 us (2%)
  waiting for transfers between devices  6.76 us (2%)
    pallas_call x2, Pallas kernels, scatter_product(): pl.pallas_call(functools.partial(product_kernel, devices, groups, len(sha...  74.9 us
    pallas_call x2, Pallas kernels, gather_rows(): pl.pallas_call(functools.partial(gather_kernel, devices, count, windows),...  73.5 us
    pallas_call x1, Pallas kernels, run_scan_backward(): pl.pallas_call(functools.partial(scan_backward, devices, spans, windows,...  37.5 us
    pallas_call x1, Pallas kernels, run_scan_forward(): pl.pallas_call(functools.partial(scan_forward, devices, spans), grid=(spa...  22.8 us
    pallas_call x1, Pallas kernels, run_attend_backward(): pl.pallas_call(attend_backward, grid=(1,), out_shape=jax.ShapeDtypeStruct...  16.2 us
    pallas_call x1, Pallas kernels, run_feed_forward(): pl.pallas_call(feed_forward, grid=(tokens // TBLK,), out_shape=(shape((to...  16.1 us
    pallas_call x2, Pallas kernels, run_product(): pl.pallas_call(functools.partial(product_rows, dims), grid=(tokens // TBL...  12.6 us
    pallas_call x1, Pallas kernels, run_attend_forward(): pl.pallas_call(attend_forward, grid=(1,), out_shape=(jax.ShapeDtypeStruct...  12.5 us
  transfers between devices with their start and end apart: 8, of which 3 were waited for; matrix products, arithmetic and copies ran while one was open for 4% of the time, Pallas kernels for 57%

profile of v9, /device:TPU:0, one launch (start us, length us, event | category | flops | bytes accessed | tf_op | source)
XLA Modules:
  0.0 354.1 jit_solution(17451295198316743005)
XLA Ops:
  3.9 1.6 concatenate.9.refs_0_
  5.6 34.5 %gather_rows.2.w_ref = bf16[1024,2304]{1,0:T(8,128)(2,1)} custom-call(bf16[64,2304]{1,0:T(8,128)(2,1)} %concatenate.9.refs_0_), custom_call_target="tpu_custom_call" | custom-call | flops 3000000000 | tf_op jit(solution)/shard_map/gather_rows/pallas_call | solution.py:204
  41.6 10.2 %project.1 = (bf16[1024,1024]{1,0:T(8,128)(2,1)}, f32[1024,2304]{1,0:T(8,128)}, f32[8,1024]{1,0:T(8,128)}) custom-call(bf16[1024,1024]{1,0:T(8,128)(2,1)} %x_ref.7, bf16[1024,2304]{1,0:T(8,128)(2,1)} %gather_rows.2.w_ref), custom_call_target="tpu_custom_call" | custom-call | flops 8000000000 | tf_op jit(solution)/shard_map/project/pallas_call | solution.py:1359
  51.7 22.8 %scan_forward.1 = (f32[1024,768]{1,0:T(8,128)}, bf16[1024,768]{1,0:T(8,128)(2,1)}, f32[8,1024]{1,0:T(8,128)}, f32[8,128,768]{2,1,0:T(8,128)}, bf16[1024,1024]{1,0:T(8,128)(2,1)}) custom-call(f32[1024,2304]{1,0:T(8,128)} %get-tuple-element.107.z_ref.x_ref.bc_ref.step_ref.q_ref.kv_ref.xp_ref.bp_ref, ...), custom_call_target="tpu_custom_call" | custom-call | flops 20000000000 | tf_op jit(solution)/shard_map/scan_forward/pallas_call | solution.py:914
  74.5 1.5 collective-permute-start
  76.1 12.5 %attend_forward.1 = (bf16[1024,512]{1,0:T(8,128)(2,1)}, f32[8,1024]{1,0:T(8,128)}, bf16[1024,256]{1,0:T(8,128)(2,1)}) custom-call(f32[1024,2304]{1,0:T(8,128)} %get-tuple-element.107.z_ref.x_ref.bc_ref.step_ref.q_ref.kv_ref.xp_ref.bp_ref, f32[1024,2304]{1,0:T(8,128)} %get-tuple-element.107.z_ref.x_ref.bc_ref.step_ref.q_ref.kv_ref.xp_ref.bp_ref, ...), custom_call_target="tpu_custom_call" | custom-call | flops 15000000512 | tf_op jit(solution)/shard_map/attend_forward/pallas_call | solution.py:1240
  90.6 6.8 %mixer_forward.1 = (bf16[1024,1024]{1,0:T(8,128)(2,1)}, bf16[1024,1024]{1,0:T(8,128)(2,1)}) custom-call(bf16[1024,768]{1,0:T(8,128)(2,1)} %get-tuple-element.116.gated_ref, f32[8,1024]{1,0:T(8,128)} %add_rsqrt_fusion.scale_ref.scale_m_ref, f32[1,768]{1,0:T(1,128)} %reshape.65.gain_ref.gain_m_ref, bf16[1024,256]{1,0:T(8,128)(2,1)} %get-tuple-element.118.attended_ref.o_ref, ...), custom_call_target="tpu_custom_call" | custom-call | flops 5000000000 | tf_op jit(solution)/shard_map/mixer_forward/pallas_call | solution.py:1445
  97.9 39.0 %gather_rows.3 = (bf16[1024,2048]{1,0:T(8,128)(2,1)}, bf16[1024,1024]{1,0:T(8,128)(2,1)}) custom-call(bf16[64,2048]{1,0:T(8,128)(2,1)} %bitcast.29, bf16[64,1024]{1,0:T(8,128)(2,1)} %bitcast.36), custom_call_target="tpu_custom_call" | custom-call | flops 3000000000 | tf_op jit(solution)/shard_map/gather_rows/pallas_call | solution.py:204
  136.9 6.4 %product_rows.2.act_grad_ref = f32[1024,1024]{1,0:T(8,128)} custom-call(bf16[1024,1024]{1,0:T(8,128)(2,1)} %top_ref.1, bf16[1024,1024]{1,0:T(8,128)(2,1)} %get-tuple-element.133.right_ref), custom_call_target="tpu_custom_call" | custom-call | flops 4000000000 | tf_op jit(solution)/shard_map/product_rows/pallas_call | solution.py:1330
  143.3 1.7 collective-permute-done.1.other_ref
  146.2 16.1 %feed_forward.1 = (bf16[1024,1024]{1,0:T(8,128)(2,1)}, f32[1024,1]{1,0:T(8,128)}, bf16[1024,1024]{1,0:T(8,128)(2,1)}, bf16[1024,1024]{1,0:T(8,128)(2,1)}, bf16[1...) custom-call(bf16[1024,1024]{1,0:T(8,128)(2,1)} %x_ref.7, bf16[1024,1024]{1,0:T(8,128)(2,1)} %get-tuple-element.121.mixed_ref, ...), custom_call_target="tpu_custom_call" | custom-call | flops 14000000000 | tf_op jit(solution)/shard_map/feed_forward/pallas_call | solution.py:1415
  162.9 32.6 %scatter_product.2.refs_5_ = f32[64,2,1024]{2,1,0:T(2,128)} custom-call(bf16[1024,1024]{1,0:T(8,128)(2,1)} %get-tuple-element.130.left_ref, bf16[1024,2048]{1,0:T(8,128)(2,1)} %get-tuple-element.131.right_ref), custom_call_target="tpu_custom_call" | custom-call | flops 3000000000 | tf_op jit(solution)/shard_map/scatter_product/pallas_call | solution.py:573
  195.5 6.2 %product_rows.3.ffn_ref = bf16[1024,1024]{1,0:T(8,128)(2,1)} custom-call(bf16[1024,1024]{1,0:T(8,128)(2,1)} %get-tuple-element.132.left_ref, bf16[1024,1024]{1,0:T(8,128)(2,1)} %get-tuple-element.133.right_ref), custom_call_target="tpu_custom_call" | custom-call | flops 4000000000 | tf_op jit(solution)/shard_map/product_rows/pallas_call | solution.py:1330
  201.7 5.3 %convert_bitcast_fusion.refs_1_ = bf16[1024,1024]{1,0:T(8,128)(2,1)} fusion(bf16[1024,1024]{1,0:T(8,128)(2,1)} %get-tuple-element.132.left_ref, bf16[1024,1024]{1,0:T(8,128)(2,1)S(1)} %copy-done.13), kind=kOutput, calls=%fused_computation | convolution fusion | flops 2148532224 | bytes 6291456 | tf_op jit(solution)/shard_map/dot_general | solution.py:39
  207.0 2.2 collective-permute-done.2.other_ref
  209.2 11.4 %mixer_backward.1 = (bf16[1024,1024]{1,0:T(8,128)(2,1)}, f32[1024,768]{1,0:T(8,128)}, bf16[1024,256]{1,0:T(8,128)(2,1)}, f32[8,1024]{1,0:T(8,128)}, f32[8,1024]{1,0:T(8,128)}) custom-call(bf16[1024,1024]{1,0:T(8,128)(2,1)} %get-tuple-element.129.part_ref, bf16[1024,1024]{1,0:T(8,128)(2,1)} %collective-permute-done.2.other_ref, ...), custom_call_target="tpu_custom_call" | custom-call | flops 8000000000 | tf_op jit(solution)/shard_map/mixer_backward/pallas_call | solution.py:1498
  222.7 16.2 %attend_backward.1.dqkv_ref = bf16[1024,384]{1,0:T(8,128)(2,1)} custom-call(bf16[1024,512]{1,0:T(8,128)(2,1)} %get-tuple-element.142.qkv_ref, f32[8,1024]{1,0:T(8,128)} %get-tuple-element.143.lse_ref, bf16[1024,256]{1,0:T(8,128)(2,1)} %get-tuple-element.118.attended_ref.o_ref, bf16[1024,256]{1,0:T(8,128)(2,1)} %get-tuple-element.144.do_ref, ...), custom_call_target="tpu_custom_call" | custom-call | flops 16000000000 | tf_op jit(solution)/shard_map/attend_backward/pallas_call | solution.py:1272
  238.9 5.9 %convolution_convert_fusion.refs_0_ = bf16[1024,1024]{1,0:T(8,128)(2,1)} fusion(bf16[1024,1024]{1,0:T(8,128)(2,1)} %get-tuple-element.145.grad_ref, bf16[1024,1024]{1,0:T(8,128)(2,1)} %get-tuple-element.146), kind=kOutput, calls=%fused_computation.1 | convolution fusion | flops 2148532224 | bytes 6291456 | tf_op jit(solution)/shard_map/dot_general | solution.py:39
  245.4 37.5 %scan_backward.1 = (bf16[1024,2304]{1,0:T(8,128)(2,1)}, f32[8,1024]{1,0:T(8,128)}, f32[8,128]{1,0:T(8,128)}, f32[64,768]{1,0:T(8,128)}, f32[64,256]{1,0:T(8,128)}, /*index=5*/f32[64,1024]{1,0:T(8,128)}) custom-call(f32[1024,2304]{1,0:T(8,128)} %get-tuple-element.107.z_ref.x_ref.bc_ref.step_ref.q_ref.kv_ref.xp_ref.bp_ref, ...), custom_call_target="tpu_custom_call" | custom-call | flops 46999998464 | tf_op jit(solution)/shard_map/scan_backward/pallas_call | solution.py:962
  282.9 9.6 %project_back.1 = (bf16[1024,1024]{1,0:T(8,128)(2,1)}, f32[8,1024]{1,0:T(8,128)}) custom-call(bf16[1024,2304]{1,0:T(8,128)(2,1)} %get-tuple-element.153.grad_ref.right_ref, bf16[1024,2304]{1,0:T(8,128)(2,1)} %gather_rows.2.w_ref, bf16[1024,1024]{1,0:T(8,128)(2,1)} %x_ref.7), custom_call_target="tpu_custom_call" | custom-call | flops 8000000000 | tf_op jit(solution)/shard_map/project_back/pallas_call | solution.py:1392
  293.8 42.4 %scatter_product.3 = (f32[64,2,768]{2,1,0:T(2,128)}, f32[64,256]{1,0:T(8,128)}, f32[64,1,384]{2,1,0:T(1,128)}, f32[12,64]{1,0:T(8,128)}, f32[72,128]{1,0:T(8,128)}) custom-call(bf16[1024,1024]{1,0:T(8,128)(2,1)} %get-tuple-element.152.left_ref, bf16[1024,2304]{1,0:T(8,128)(2,1)} %get-tuple-element.153.grad_ref.right_ref, ...), custom_call_target="tpu_custom_call" | custom-call | flops 3000000000 | tf_op jit(solution)/shard_map/scatter_product/pallas_call | solution.py:573
  336.9 2.9 collective-permute-done.5.other_ref
  341.2 10.0 %finish_layer.1 = (f32[1024,1024]{1,0:T(8,128)}, bf16[1024,1024]{1,0:T(8,128)(2,1)}, f32[64,2,768]{2,1,0:T(2,128)}, f32[64,1,384]{2,1,0:T(1,128)}, f32[12,64]{1,...) custom-call(bf16[1024,1024]{1,0:T(8,128)(2,1)} %x_ref.7, ...), custom_call_target="tpu_custom_call" | custom-call | flops 8000000000 | tf_op jit(solution)/shard_map/finish_layer/pallas_call | solution.py:1573
  352.5 1.6 finish_shared.1
  (60 shorter events, 16.4 us)
Async XLA Ops:
  5.6 34.6 %copy-start.7 = (bf16[768]{0:T(1024)(128)(2,1)S(1)}, bf16[768]{0:T(1024)(128)(2,1)}, u32[]{:S(2)}) copy-start(bf16[768]{0:T(1024)(128)(2,1)} %param.36) | copy-start | bytes 4612
  5.6 34.6 %copy-start.8 = (bf16[768]{0:T(1024)(128)(2,1)S(1)}, bf16[768]{0:T(1024)(128)(2,1)}, u32[]{:S(2)}) copy-start(bf16[768]{0:T(1024)(128)(2,1)} %param.30) | copy-start | bytes 4612
  5.6 34.6 %copy-start.9 = (bf16[256]{0:T(256)(128)(2,1)S(1)}, bf16[256]{0:T(256)(128)(2,1)}, u32[]{:S(2)}) copy-start(bf16[256]{0:T(256)(128)(2,1)} %param.32) | copy-start | bytes 1540
  5.6 34.6 %copy-start.10 = (bf16[12]{0:T(256)(128)(2,1)S(1)}, bf16[12]{0:T(256)(128)(2,1)}, u32[]{:S(2)}) copy-start(bf16[12]{0:T(256)(128)(2,1)} %param.33) | copy-start | bytes 76
  5.6 34.6 %copy-start.11 = (bf16[12]{0:T(256)(128)(2,1)S(1)}, bf16[12]{0:T(256)(128)(2,1)}, u32[]{:S(2)}) copy-start(bf16[12]{0:T(256)(128)(2,1)} %param.34) | copy-start | bytes 76
  5.6 34.6 %copy-start.12 = (bf16[12]{0:T(256)(128)(2,1)S(1)}, bf16[12]{0:T(256)(128)(2,1)}, u32[]{:S(2)}) copy-start(bf16[12]{0:T(256)(128)(2,1)} %param.35) | copy-start | bytes 76
  5.6 35.3 %copy-start.1 = (bf16[768,64]{0,1:T(8,128)(2,1)S(1)}, bf16[768,64]{0,1:T(8,128)(2,1)}, u32[]{:S(2)}) copy-start(bf16[768,64]{0,1:T(8,128)(2,1)} %param.37) | copy-start | bytes 294916
  5.6 35.3 %copy-start.6 = (bf16[1,256,64]{1,2,0:T(8,128)(2,1)S(1)}, bf16[1,256,64]{1,2,0:T(8,128)(2,1)}, u32[]{:S(2)}) copy-start(bf16[1,256,64]{1,2,0:T(8,128)(2,1)} %param.39) | copy-start | bytes 98308
  74.5 14.7 %copy-start = (bf16[64,2,1024]{2,1,0:T(2,128)(2,1)S(1)}, bf16[64,2,1024]{2,1,0:T(2,128)(2,1)}, u32[]{:S(2)}) copy-start(bf16[64,2,1024]{2,1,0:T(2,128)(2,1)} %param.41) | copy-start | bytes 786436
  74.5 15.4 %copy-start.5 = (f32[8,1024]{1,0:T(8,128)S(1)}, f32[8,1024]{1,0:T(8,128)}, u32[]{:S(2)}) copy-start(f32[8,1024]{1,0:T(8,128)} %get-tuple-element.117) | copy-start | bytes 98308
  74.5 15.4 %collective-permute-start = (f32[8,1024]{1,0:T(8,128)}, f32[8,1024]{1,0:T(8,128)S(1)}, u32[]{:S(2)}, u32[]{:S(2)}) collective-permute-start(f32[8,1024]{1,0:T(8,128)} %get-tuple-element.117), channel_id=1, source_target_pairs={{0,1},{1,0},{2,3},{3,2},{4,5},{5,4},{6,7},{7,6},{8,9},{9,8},{10,11... | collective-permute-start | bytes 98312 | tf_op jit(solution)/shard_map/ppermute | solution.py:1611
  97.3 47.6 %collective-permute-start.1 = (bf16[1024,1024]{1,0:T(8,128)(2,1)}, bf16[1024,1024]{1,0:T(8,128)(2,1)S(1)}, u32[]{:S(2)}, u32[]{:S(2)}) collective-permute-start(bf16[1024,1024]{1,0:T(8,128)(2,1)} %get-tuple-element.121.mixed_ref), channel_id=1, source_target_pairs={{0,1},{1,0},{2,3},{3,2},{4,5},{5,4},{6,7},{7,6},{8,9},{9,8},{10,11... | collective-permute-start | bytes 6291464 | tf_op jit(solution)/shard_map/ppermute | solution.py:1611
  144.9 1.3 copy-start.16
  162.3 46.9 %collective-permute-start.2 = (bf16[1024,1024]{1,0:T(8,128)(2,1)}, bf16[1024,1024]{1,0:T(8,128)(2,1)}, u32[]{:S(2)}, u32[]{:S(2)}) collective-permute-start(bf16[1024,1024]{1,0:T(8,128)(2,1)} %get-tuple-element.129.part_ref), channel_id=1, source_target_pairs={{0,1},{1,0},{2,3},{3,2},{4,5},{5,4},{6,7},{7,6},{8,9},{9,8},{10,11... | collective-permute-start | bytes 6291464 | tf_op jit(solution)/shard_map/ppermute | solution.py:1611
  195.5 6.3 %copy-start.13 = (bf16[1024,1024]{1,0:T(8,128)(2,1)S(1)}, bf16[1024,1024]{1,0:T(8,128)(2,1)}, u32[]{:S(2)}) copy-start(bf16[1024,1024]{1,0:T(8,128)(2,1)} %top_ref.1) | copy-start | bytes 6291460
  209.2 12.7 %copy-start.14 = (bf16[1024,1024]{1,0:T(8,128)(2,1)S(1)}, bf16[1024,1024]{1,0:T(8,128)(2,1)}, u32[]{:S(2)}) copy-start(bf16[1024,1024]{1,0:T(8,128)(2,1)} %product_rows.3.ffn_ref) | copy-start | bytes 6291460
  220.6 24.2 %collective-permute-start.4 = (f32[8,1024]{1,0:T(8,128)}, f32[8,1024]{1,0:T(8,128)S(1)}, u32[]{:S(2)}, u32[]{:S(2)}) collective-permute-start(f32[8,1024]{1,0:T(8,128)} %get-tuple-element.141), channel_id=1, source_target_pairs={{0,1},{1,0},{2,3},{3,2},{4,5},{5,4},{6,7},{7,6},{8,9},{9,8},{10,11... | collective-permute-start | bytes 98312 | tf_op jit(solution)/shard_map/ppermute | solution.py:1611
  221.9 61.1 %collective-permute-start.3 = (bf16[1024,1024]{1,0:T(8,128)(2,1)S(1)}, bf16[1024,1024]{1,0:T(8,128)(2,1)}, u32[]{:S(2)}, u32[]{:S(2)}) collective-permute-start(bf16[1024,1024]{1,0:T(8,128)(2,1)S(1)} %copy-done.14), channel_id=1, source_target_pairs={{0,1},{1,0},{2,3},{3,2},{4,5},{5,4},{6,7},{7,6},{8,9},{9,8},{10,11... | collective-permute-start | bytes 6291464 | tf_op jit(solution)/shard_map/ppermute | solution.py:1611
  238.9 5.9 %copy-start.4 = (f32[8,1024]{1,0:T(8,128)S(1)}, f32[8,1024]{1,0:T(8,128)}, u32[]{:S(2)}) copy-start(f32[8,1024]{1,0:T(8,128)} %get-tuple-element.141) | copy-start | bytes 98308
  292.6 47.3 %collective-permute-start.5 = (bf16[1024,1024]{1,0:T(8,128)(2,1)}, bf16[1024,1024]{1,0:T(8,128)(2,1)S(1)}, u32[]{:S(2)}, u32[]{:S(2)}) collective-permute-start(bf16[1024,1024]{1,0:T(8,128)(2,1)} %get-tuple-element.151.part_ref), channel_id=1, source_target_pairs={{0,1},{1,0},{2,3},{3,2},{4,5},{5,4},{6,7},{7,6},{8,9},{9,8},{10,11... | collective-permute-start | bytes 6291464 | tf_op jit(solution)/shard_map/ppermute | solution.py:1611
  336.2 15.1 %collective-permute-start.6 = (f32[72,128]{1,0:T(8,128)}, f32[72,128]{1,0:T(8,128)S(1)}, u32[]{:S(2)}, u32[]{:S(2)}) collective-permute-start(f32[72,128]{1,0:T(8,128)} %get-tuple-element.161.total_ref), channel_id=1, source_target_pairs={{0,1},{1,0},{2,3},{3,2},{4,5},{5,4},{6,7},{7,6},{8,9},{9,8},{10,11... | collective-permute-start | bytes 110600 | tf_op jit(solution)/shard_map/ppermute | solution.py:1611
  339.8 1.4 copy-start.15
  339.8 11.4 %collective-permute-start.7 = (f32[64,256]{1,0:T(8,128)}, f32[64,256]{1,0:T(8,128)S(1)}, u32[]{:S(2)}, u32[]{:S(2)}) collective-permute-start(f32[64,256]{1,0:T(8,128)} %get-tuple-element.171.mine_ref), channel_id=1, source_target_pairs={{0,1},{1,0},{2,3},{3,2},{4,5},{5,4},{6,7},{7,6},{8,9},{9,8},{10,11... | collective-permute-start | bytes 196616 | tf_op jit(solution)/shard_map/ppermute | solution.py:1611
  351.9 0.6 copy-start.2
  (1 other events, 0.6 us)
